TPU v7x, 128 devices: a whole 4x4x4 slice. The times are simulated.
128 devices in a mesh: gx: 4 (over y), gy: 4 (over z), gz: 8 (over x, core).
Axes of the slice: x: 4, y: 4, z: 4, core: 2. Of those that a mesh axis runs over, the one named last changes fastest.
Arguments:
- tokens: bfloat16 [1024, 7168], P(('gx', 'gy', 'gz')), may hold values from -6 to 6
- expert_ids: int32 [1024, 8], P(('gx', 'gy', 'gz')), may hold values from 0 to 15, as said below
- slot_ids: int32 [1024, 8], P(('gx', 'gy', 'gz')), may hold values from 0 to 7, as said below
- route_weight: bfloat16 [1024, 8], P(('gx', 'gy', 'gz')), may hold values from 0.099609375 to 0.59765625
- gate_weight: bfloat16 [16, 7168, 2048], P(('gx', 'gy'), None, 'gz'), may hold values from -0.0625 to 0.0625
- up_weight: bfloat16 [16, 7168, 2048], P(('gx', 'gy'), None, 'gz'), may hold values from -0.0625 to 0.0625
- down_weight: bfloat16 [16, 2048, 7168], P(('gx', 'gy'), 'gz'), may hold values from -0.125 to 0.125
- expert_bias: float32 [16], replicated, may hold values from -3 to 3
Outputs:
- combined: bfloat16 [1024, 7168], P(('gx', 'gy', 'gz'))
- expert_load: int32 [16], replicated
- new_bias: float32 [16], replicated
Inputs may be any that keep to these rules, and one draw needn't show every extreme that they name: `expert_ids`: the 8 experts of a token are different. Among the 8 tokens of one device no expert is named more than 8 times; one expert is named by every token of every device. `slot_ids`: for each device and expert, the routes of that device's tokens to that expert hold different slots.
All inputs are finite; a program needn't handle non-finite values.
Results may differ from a plain program's by a relative error of at most 0.015.
Values may be sent and summed in bfloat16 or wider, within the bound.
No kernel may reach another device: no remote copies, remote signals or barrier semaphores. Data moves between devices by JAX's collectives and lax.ppermute only.
A program may use at most 128 MiB of HBM per device.

v0:
```python
import functools

import jax
import jax.numpy as jnp
from jax import lax
from jax.experimental import pallas as pl
from jax.experimental.pallas import tpu as pltpu
from jax.sharding import Mesh
from jax.sharding import PartitionSpec as P

AXES = ("gx", "gy", "gz_0", "gz_1")
GZ = ("gz_0", "gz_1")
X, Y, Z = "gz_0", "gx", "gy"
EARLY = (X, Y, Z)
LATE = ((X, Y, Z), (Y, Z, X), (Z, X, Y))
INFO = 128
CUTS = (0, 2560, 4864, 7168)
COL_CUTS = (0, 2432, 4864, 7168)
BF16 = jnp.bfloat16
F32 = jnp.float32

bias_rate = 0.001


def exchange(value, axis):
    masks = (3, 1)
    pairs = [(2 * i + c, 2 * (i ^ masks[c]) + c) for i in range(4) for c in range(2)]
    return lax.ppermute(value, (axis, "gz_1"), pairs)


def direct(value, hops):
    masks = (1, 3)
    pairs = []
    for a in range(4):
        for b in range(4):
            for x in range(4):
                for c in range(2):
                    m = masks[c]
                    far = (
                        a ^ (m if Y in hops else 0),
                        b ^ (m if Z in hops else 0),
                        x ^ (m if X in hops else 0),
                    )
                    here = ((a * 4 + b) * 4 + x) * 2 + c
                    pairs.append((here, ((far[0] * 4 + far[1]) * 4 + far[2]) * 2 + c))
    return lax.ppermute(value, AXES, pairs)


def hops_of(n):
    return [axis for k, axis in enumerate(EARLY) if n >> k & 1]


def partner(value):
    return lax.ppermute(value, "gz_1", [(0, 1), (1, 0)])


def canonical(colour, place):
    bits = {LATE[colour][k]: place >> k & 1 for k in range(3)}
    return sum(bits[LATE[0][k]] << k for k in range(3))


VMEM = pl.BlockSpec(memory_space=pltpu.VMEM)
SMEM = pl.BlockSpec(memory_space=pltpu.SMEM)


def rows_kernel(experts, tokens, ids, weights, out):
    width = tokens.shape[1]
    out[:, :width] = tokens[...]
    lane = lax.broadcasted_iota(jnp.int32, (tokens.shape[0], INFO), 1)
    info = jnp.zeros((tokens.shape[0], INFO), F32)
    for k in range(ids.shape[1]):
        chosen = ids[:, k : k + 1]
        info += jnp.where(lane == chosen, weights[:, k : k + 1].astype(F32), 0.0)
        info += jnp.where(lane == chosen + experts, 1.0, 0.0)
    out[:, width:] = info.astype(BF16)


def rows_of(tokens, ids, weights, experts):
    rows, width = tokens.shape
    return pl.pallas_call(
        functools.partial(rows_kernel, experts),
        out_shape=jax.ShapeDtypeStruct((rows, width + INFO), BF16),
        in_specs=[VMEM] * 3,
        out_specs=VMEM,
        compiler_params=pltpu.CompilerParams(vmem_limit_bytes=4 << 20),
        name="token_rows",
    )(tokens, ids, weights)


def near_kernel(x0, x1, x2, w0, w1, w2, w3, acc):
    for i, x in enumerate((x0, x1, x2)):
        width = CUTS[i + 1] - CUTS[i]
        places = [canonical(i, q) for q in range(4)]
        for j, w in enumerate((w0, w1, w2, w3)):
            part = jnp.dot(
                x[:, :width], w[CUTS[i] : CUTS[i + 1], :], preferred_element_type=F32
            )
            for q, s in enumerate(places):
                rows = part[64 * q : 64 * q + 64]
                if i == 0:
                    acc[j, 64 * s : 64 * s + 64, :] = rows
                else:
                    acc[j, 64 * s : 64 * s + 64, :] += rows
            if i == 0:
                for s in range(8):
                    if s not in places:
                        acc[j, 64 * s : 64 * s + 64, :] = jnp.zeros((64, 256), F32)


def far_kernel(expert, x0, x1, x2, w0, w1, w2, w3, near_x2, acc_in, hidden, marks, acc):
    ready = {}
    for i, x in enumerate((x0, x1, x2)):
        width = CUTS[i + 1] - CUTS[i]
        places = [canonical(i, q + 4) for q in range(4)]
        for j, w in enumerate((w0, w1, w2, w3)):
            part = jnp.dot(
                x[:, :width], w[CUTS[i] : CUTS[i + 1], :], preferred_element_type=F32
            )
            for q, s in enumerate(places):
                rows = part[64 * q : 64 * q + 64]
                before = acc if (j, s) in ready else acc_in
                acc[j, 64 * s : 64 * s + 64, :] = before[j, 64 * s : 64 * s + 64, :] + rows
                ready[j, s] = True
    lane = lax.broadcasted_iota(jnp.int32, (64, INFO), 1)
    sums = jnp.zeros((8, INFO), F32)
    for place in range(8):
        s = canonical(2, place)
        source = near_x2 if place < 4 else x2
        at = 64 * (place % 4)
        info = source[at : at + 64, CUTS[3] - CUTS[2] :].astype(F32)
        sums += jnp.sum(info.reshape(8, 8, INFO), axis=0)
        scale = jnp.sum(jnp.where(lane == expert[0], info, 0.0), axis=1, keepdims=True)
        for part in range(2):
            value = acc if (part, s) in ready else acc_in
            g = value[part, 64 * s : 64 * s + 64, :]
            u = value[part + 2, 64 * s : 64 * s + 64, :]
            h = g / (1.0 + jnp.exp(-g)) * u * scale
            hidden[64 * s : 64 * s + 64, 256 * part : 256 * part + 256] = h.astype(BF16)
    marks[...] = sums


def load_kernel(*refs):
    count = (len(refs) - 1) // 2
    sem = refs[-1]
    copies = [
        pltpu.make_async_copy(refs[k], refs[count + k], sem.at[k]) for k in range(count)
    ]
    for c in copies:
        c.start()
    for c in copies:
        c.wait()


def in_vmem(*arrays):
    return pl.pallas_call(
        load_kernel,
        out_shape=tuple(jax.ShapeDtypeStruct(a.shape, a.dtype) for a in arrays),
        in_specs=[pl.BlockSpec(memory_space=pl.ANY)] * len(arrays),
        out_specs=(VMEM,) * len(arrays),
        scratch_shapes=[pltpu.SemaphoreType.DMA((len(arrays),))],
        compiler_params=pltpu.CompilerParams(vmem_limit_bytes=4 << 20),
        cost_estimate=pl.CostEstimate(flops=8 << 30, transcendentals=0, bytes_accessed=0),
        name="weights_in",
    )(*arrays)


COST = pl.CostEstimate(flops=2 * 256 * 7168 * 1024, transcendentals=0, bytes_accessed=0)


def gate_up_near(pieces, weights):
    return pl.pallas_call(
        near_kernel,
        out_shape=jax.ShapeDtypeStruct((4, 512, 256), F32),
        in_specs=[VMEM] * 7,
        out_specs=VMEM,
        cost_estimate=COST,
        compiler_params=pltpu.CompilerParams(vmem_limit_bytes=8 << 20),
        name="gate_up_near",
    )(*pieces, *weights)


def gate_up_far(expert, pieces, weights, near_x2, acc):
    return pl.pallas_call(
        far_kernel,
        out_shape=(
            jax.ShapeDtypeStruct((512, 512), BF16),
            jax.ShapeDtypeStruct((8, INFO), F32),
        ),
        in_specs=[SMEM] + [VMEM] * 9,
        out_specs=(VMEM, VMEM),
        scratch_shapes=[pltpu.VMEM((4, 512, 256), F32)],
        cost_estimate=COST,
        compiler_params=pltpu.CompilerParams(vmem_limit_bytes=10 << 20),
        name="gate_up_far",
    )(expert, *pieces, *weights, near_x2, acc)


def down_kernel(colour, far, hidden, own, other, out):
    cols = slice(COL_CUTS[colour], COL_CUTS[colour + 1])
    blocks = [canonical(colour, q + (4 if far else 0)) for q in range(4)]
    lhs = jnp.concatenate([hidden[64 * s : 64 * s + 64, :] for s in blocks], axis=0)
    total = jnp.dot(lhs[:, :256], own[:, cols], preferred_element_type=F32)
    total += jnp.dot(lhs[:, 256:], other[:, cols], preferred_element_type=F32)
    out[...] = total.astype(out.dtype)


def down_part(colour, far, hidden, own, other):
    width = COL_CUTS[colour + 1] - COL_CUTS[colour]
    return pl.pallas_call(
        functools.partial(down_kernel, colour, far),
        out_shape=jax.ShapeDtypeStruct((256, width), BF16 if far else F32),
        in_specs=[VMEM] * 3,
        out_specs=VMEM,
        cost_estimate=pl.CostEstimate(
            flops=2 * 256 * 512 * width, transcendentals=0, bytes_accessed=0
        ),
        compiler_params=pltpu.CompilerParams(vmem_limit_bytes=6 << 20),
    )(hidden, own, other)


def layer(
    tokens, expert_ids, slot_ids, route_weight, gate_weight, up_weight, down_weight, expert_bias
):
    experts = lax.axis_size("gx") * lax.axis_size("gy")
    devices = experts * lax.axis_size(GZ)
    tok_rows, width = tokens.shape
    route_count = expert_ids.shape[1]
    own_expert = lax.axis_index("gx") * lax.axis_size("gy") + lax.axis_index("gy")

    gate_own, up_own, down_own = gate_weight[0], up_weight[0], down_weight[0]
    gate_far, up_far, down_far = partner(gate_own), partner(up_own), partner(down_own)
    gate_own, gate_far, up_own, up_far = in_vmem(gate_own, gate_far, up_own, up_far)
    down_own, down_far = in_vmem(down_own, down_far)
    gate_ups = (gate_own, gate_far, up_own, up_far)

    rows = rows_of(tokens, expert_ids, route_weight, experts)
    rows = jnp.concatenate([rows] + [direct(rows, hops_of(n)) for n in range(1, 8)], axis=0)
    ends = (*CUTS[:3], width + INFO)
    pieces = [rows[:, ends[i] : ends[i + 1]] for i in range(3)]
    for step in range(2):
        pieces = [
            jnp.concatenate([p, exchange(p, LATE[i][step])], axis=0) for i, p in enumerate(pieces)
        ]
    far_pieces = [exchange(p, LATE[i][2]) for i, p in enumerate(pieces)]

    acc = gate_up_near(pieces, gate_ups)
    expert = jnp.full((1,), own_expert, jnp.int32)
    hidden, marks = gate_up_far(expert, far_pieces, gate_ups, pieces[2], acc)

    sent = [down_part(i, True, hidden, down_own, down_far) for i in range(3)]
    kept = []
    for i in range(3):
        kept.append(down_part(i, False, hidden, down_own, down_far))
    for step in (2, 1, 0):
        got = []
        for i in range(3):
            got.append(exchange(sent[i], LATE[i][step]))
        totals = [kept[i] + got[i].astype(F32) for i in range(3)]
        half = totals[0].shape[0] // 2
        if step:
            sent = [t[half:].astype(BF16) for t in totals]
            kept = [t[:half] for t in totals]
    total = jnp.concatenate(totals, axis=1)
    combined = total[:tok_rows]
    for n in range(1, 8):
        block = total[n * tok_rows : (n + 1) * tok_rows].astype(BF16)
        combined = combined + direct(block, hops_of(n)).astype(F32)

    half_load = jnp.sum(marks, axis=0)[experts : 2 * experts].astype(jnp.int32)
    other_load = partner(half_load)
    expert_load = half_load + other_load
    mean_load = tok_rows * devices * route_count // experts
    new_bias = expert_bias + bias_rate * jnp.sign((mean_load - expert_load).astype(F32))
    return (combined.astype(BF16), expert_load, new_bias)


def solution(mesh):
    finer = Mesh(mesh.devices.reshape(mesh.shape["gx"], mesh.shape["gy"], 4, 2), AXES)
    return jax.shard_map(
        layer,
        mesh=finer,
        in_specs=(
            P(AXES, None),
            P(AXES, None),
            P(AXES, None),
            P(AXES, None),
            P(("gx", "gy"), None, GZ),
            P(("gx", "gy"), None, GZ),
            P(("gx", "gy"), GZ, None),
            P(),
        ),
        out_specs=(P(AXES, None), P(), P()),
        check_vma=False,
    )
```

profile of v0, /device:TPU:2, one launch (start us, length us, event | category | flops | bytes accessed | tf_op | source)
XLA Modules:
  0.0 143.4 jit_solution(14523512053284868205)
XLA Ops:
  3.5 1.7 %collective-permute-start.1 = (bf16[8,7296]{1,0:T(8,128)(2,1)S(1)}, bf16[8,7296]{1,0:T(8,128)(2,1)S(1)}, u32[]{:S(2)}, u32[]{:S(2)}) collective-permute-start(bf16[8,7296]{1,0:T(8,128)(2,1)S(1)} %token_rows.1), channel_id=1, source_target_pairs={{0,32},{1,97},{2,34},{3,99},{4,36},{5,101},{6,38},{7,103},{8,40},{... | collective-permute-start | bytes 350216 | tf_op jit(solution)/shard_map/ppermute | solution.py:46
  5.2 1.4 collective-permute-start.2
  6.6 1.9 %collective-permute-start.3 = (bf16[8,7296]{1,0:T(8,128)(2,1)S(1)}, bf16[8,7296]{1,0:T(8,128)(2,1)S(1)}, u32[]{:S(2)}, u32[]{:S(2)}) collective-permute-start(bf16[8,7296]{1,0:T(8,128)(2,1)S(1)} %token_rows.1), channel_id=1, source_target_pairs={{0,8},{1,25},{2,10},{3,27},{4,12},{5,29},{6,14},{7,31},{8,0},{9,17... | collective-permute-start | bytes 350216 | tf_op jit(solution)/shard_map/ppermute | solution.py:46
  8.5 3.1 %collective-permute-start.5 = (bf16[8,7296]{1,0:T(8,128)(2,1)S(1)}, bf16[8,7296]{1,0:T(8,128)(2,1)S(1)}, u32[]{:S(2)}, u32[]{:S(2)}) collective-permute-start(bf16[8,7296]{1,0:T(8,128)(2,1)S(1)} %token_rows.1), channel_id=1, source_target_pairs={{0,40},{1,121},{2,42},{3,123},{4,44},{5,125},{6,46},{7,127},{8,32}... | collective-permute-start | bytes 350216 | tf_op jit(solution)/shard_map/ppermute | solution.py:46
  12.7 4.2 %collective-permute-start.16 = (bf16[7168,256]{1,0:T(8,128)(2,1)}, bf16[7168,256]{1,0:T(8,128)(2,1)}, u32[]{:S(2)}, u32[]{:S(2)}) collective-permute-start(bf16[7168,256]{1,0:T(8,128)(2,1)} %bitcast.4), channel_id=1, source_target_pairs={{0,1},{1,0},{2,3},{3,2},{4,5},{5,4},{6,7},{7,6},{8,9},{9,8},{10,11... | collective-permute-start | bytes 11010056 | tf_op jit(solution)/shard_map/ppermute | solution.py:54
  18.4 2.3 %collective-permute-start.10 = (bf16[64,2304]{1,0:T(8,128)(2,1)S(1)}, bf16[64,2304]{1,0:T(8,128)(2,1)S(1)}, u32[]{:S(2)}, u32[]{:S(2)}) collective-permute-start(bf16[64,2304]{1,0:T(8,128)(2,1)S(1)} %slice.110), channel_id=1, source_target_pairs={{0,96},{1,33},{32,64},{33,1},{64,32},{65,97},{96,0},{97,65},{2,98}... | collective-permute-start | bytes 884744 | tf_op jit(solution)/shard_map/ppermute | solution.py:28
  20.7 2.9 %collective-permute-start.13 = (bf16[64,2432]{1,0:T(8,128)(2,1)S(1)}, bf16[64,2432]{1,0:T(8,128)(2,1)S(1)}, u32[]{:S(2)}, u32[]{:S(2)}) collective-permute-start(bf16[64,2432]{1,0:T(8,128)(2,1)S(1)} %slice.111), channel_id=1, source_target_pairs={{0,24},{1,9},{8,16},{9,1},{16,8},{17,25},{24,0},{25,17},{2,26},{3,... | collective-permute-start | bytes 933896 | tf_op jit(solution)/shard_map/ppermute | solution.py:28
  23.5 2.8 %collective-permute-done.10 = bf16[64,2304]{1,0:T(8,128)(2,1)S(1)} collective-permute-done((bf16[64,2304]{1,0:T(8,128)(2,1)S(1)}, bf16[64,2304]{1,0:T(8,128)(2,1)S(1)}, u32[]{:S(2)}, u32[]{:S(2)}) %collective-permute-start.10) | collective-permute-done | bytes 294944 | tf_op jit(solution)/shard_map/ppermute | solution.py:28
  26.4 2.2 %collective-permute-start.7 = (bf16[64,2560]{1,0:T(8,128)(2,1)S(1)}, bf16[64,2560]{1,0:T(8,128)(2,1)S(1)}, u32[]{:S(2)}, u32[]{:S(2)}) collective-permute-start(bf16[64,2560]{1,0:T(8,128)(2,1)S(1)} %slice.109), channel_id=1, source_target_pairs={{0,6},{1,3},{2,4},{3,1},{4,2},{5,7},{6,0},{7,5},{8,14},{9,11},{10,... | collective-permute-start | bytes 983048 | tf_op jit(solution)/shard_map/ppermute | solution.py:28
  28.9 2.8 %collective-permute-start.11 = (bf16[128,2304]{1,0:T(8,128)(2,1)S(1)}, bf16[128,2304]{1,0:T(8,128)(2,1)S(1)}, u32[]{:S(2)}, u32[]{:S(2)}) collective-permute-start(bf16[128,2304]{1,0:T(8,128)(2,1)S(1)} %pad_maximum_fusion.6), channel_id=1, source_target_pairs={{0,24},{1,9},{8,16},{9,1},{16,8},{17,25},{24,0},{25,17},{2,26},{3,... | collective-permute-start | bytes 1769480 | tf_op jit(solution)/shard_map/ppermute | solution.py:28
  31.7 1.9 %collective-permute-done.7 = bf16[64,2560]{1,0:T(8,128)(2,1)S(1)} collective-permute-done((bf16[64,2560]{1,0:T(8,128)(2,1)S(1)}, bf16[64,2560]{1,0:T(8,128)(2,1)S(1)}, u32[]{:S(2)}, u32[]{:S(2)}) %collective-permute-start.7) | collective-permute-done | bytes 327712 | tf_op jit(solution)/shard_map/ppermute | solution.py:28
  33.6 2.0 %collective-permute-start.14 = (bf16[128,2432]{1,0:T(8,128)(2,1)S(1)}, bf16[128,2432]{1,0:T(8,128)(2,1)S(1)}, u32[]{:S(2)}, u32[]{:S(2)}) collective-permute-start(bf16[128,2432]{1,0:T(8,128)(2,1)S(1)} %pad_maximum_fusion.5), channel_id=1, source_target_pairs={{0,6},{1,3},{2,4},{3,1},{4,2},{5,7},{6,0},{7,5},{8,14},{9,11},{10,... | collective-permute-start | bytes 1867784 | tf_op jit(solution)/shard_map/ppermute | solution.py:28
  35.7 4.3 %collective-permute-done.11 = bf16[128,2304]{1,0:T(8,128)(2,1)S(1)} collective-permute-done((bf16[128,2304]{1,0:T(8,128)(2,1)S(1)}, bf16[128,2304]{1,0:T(8,128)(2,1)S(1)}, u32[]{:S(2)}, u32[]{:S(2)}) %collective-permute-start.11) | collective-permute-done | bytes 589856 | tf_op jit(solution)/shard_map/ppermute | solution.py:28
  40.0 2.0 %collective-permute-start.8 = (bf16[128,2560]{1,0:T(8,128)(2,1)S(1)}, bf16[128,2560]{1,0:T(8,128)(2,1)S(1)}, u32[]{:S(2)}, u32[]{:S(2)}) collective-permute-start(bf16[128,2560]{1,0:T(8,128)(2,1)S(1)} %pad_maximum_fusion.4), channel_id=1, source_target_pairs={{0,96},{1,33},{32,64},{33,1},{64,32},{65,97},{96,0},{97,65},{2,98}... | collective-permute-start | bytes 1966088 | tf_op jit(solution)/shard_map/ppermute | solution.py:28
  42.0 1.8 %collective-permute-done.14 = bf16[128,2432]{1,0:T(8,128)(2,1)S(1)} collective-permute-done((bf16[128,2432]{1,0:T(8,128)(2,1)S(1)}, bf16[128,2432]{1,0:T(8,128)(2,1)S(1)}, u32[]{:S(2)}, u32[]{:S(2)}) %collective-permute-start.14) | collective-permute-done | bytes 622624 | tf_op jit(solution)/shard_map/ppermute | solution.py:28
  43.8 2.0 %collective-permute-start.12 = (bf16[256,2304]{1,0:T(8,128)(2,1)S(1)}, bf16[256,2304]{1,0:T(8,128)(2,1)S(1)}, u32[]{:S(2)}, u32[]{:S(2)}) collective-permute-start(bf16[256,2304]{1,0:T(8,128)(2,1)S(1)} %pad_maximum_fusion.3.x1), channel_id=1, source_target_pairs={{0,6},{1,3},{2,4},{3,1},{4,2},{5,7},{6,0},{7,5},{8,14},{9,11},{10,... | collective-permute-start | bytes 3538952 | tf_op jit(solution)/shard_map/ppermute | solution.py:28
  45.9 5.8 %collective-permute-done.8 = bf16[128,2560]{1,0:T(8,128)(2,1)S(1)} collective-permute-done((bf16[128,2560]{1,0:T(8,128)(2,1)S(1)}, bf16[128,2560]{1,0:T(8,128)(2,1)S(1)}, u32[]{:S(2)}, u32[]{:S(2)}) %collective-permute-start.8) | collective-permute-done | bytes 655392 | tf_op jit(solution)/shard_map/ppermute | solution.py:28
  51.8 2.0 %collective-permute-start.15 = (bf16[256,2432]{1,0:T(8,128)(2,1)S(1)}, bf16[256,2432]{1,0:T(8,128)(2,1)S(1)}, u32[]{:S(2)}, u32[]{:S(2)}) collective-permute-start(bf16[256,2432]{1,0:T(8,128)(2,1)S(1)} %pad_maximum_fusion.2.x2.near_x2), channel_id=1, source_target_pairs={{0,96},{1,33},{32,64},{33,1},{64,32},{65,97},{96,0},{97,65},{2,98}... | collective-permute-start | bytes 3735560 | tf_op jit(solution)/shard_map/ppermute | solution.py:28
  53.8 2.8 %collective-permute-start.9 = (bf16[256,2560]{1,0:T(8,128)(2,1)S(1)}, bf16[256,2560]{1,0:T(8,128)(2,1)S(1)}, u32[]{:S(2)}, u32[]{:S(2)}) collective-permute-start(bf16[256,2560]{1,0:T(8,128)(2,1)S(1)} %pad_maximum_fusion.1.x0), channel_id=1, source_target_pairs={{0,24},{1,9},{8,16},{9,1},{16,8},{17,25},{24,0},{25,17},{2,26},{3,... | collective-permute-start | bytes 3932168 | tf_op jit(solution)/shard_map/ppermute | solution.py:28
  56.6 3.5 %weights_in.2 = (bf16[7168,256]{1,0:T(8,128)(2,1)S(1)}, bf16[7168,256]{1,0:T(8,128)(2,1)S(1)}, bf16[7168,256]{1,0:T(8,128)(2,1)S(1)}, bf16[7168,256]{1,0:T(8,128)(2,1)S(1)}) custom-call(bf16[7168,256]{1,0:T(8,128)(2,1)S(1)} %bitcast.5, bf16[7168,256]{1,0:T(8,128)(2,1)} %collective-permute-done.16.refs_1_, bf16[7168,256]{1,0:T(8,128)(2,1)S(1)} %bitcast.7, ...), custom_call_target="tpu_custom_call" | custom-call | flops 8589934592 | tf_op jit(solution)/shard_map/weights_in/pallas_call | solution.py:155
  60.2 3.9 %gate_up_near.1.acc_in = f32[4,512,256]{2,1,0:T(8,128)S(1)} custom-call(bf16[256,2560]{1,0:T(8,128)(2,1)S(1)} %pad_maximum_fusion.1.x0, bf16[256,2304]{1,0:T(8,128)(2,1)S(1)} %pad_maximum_fusion.3.x1, bf16[256,2432]{1,0:T(8,128)(2,1)S(1)} %pad_maximum_fusion.2.x2.near_x2, bf16[7168,256]{1,0:T(8,128)(2,1)S(1)} %get-tuple-element.11.w0, ...), custom_call_target="tpu_custom_call" | custom-call | flops 3758096384 | tf_op jit(solution)/shard_map/gate_up_near/pallas_call | solution.py:171
  64.1 2.3 %weights_in.3 = (bf16[256,7168]{1,0:T(8,128)(2,1)S(1)}, bf16[256,7168]{1,0:T(8,128)(2,1)S(1)}) custom-call(bf16[256,7168]{1,0:T(8,128)(2,1)S(1)} %bitcast.9, bf16[256,7168]{1,0:T(8,128)(2,1)} %collective-permute-done.18.refs_1_), custom_call_target="tpu_custom_call" | custom-call | flops 8589934592 | tf_op jit(solution)/shard_map/weights_in/pallas_call | solution.py:155
  66.5 3.4 %collective-permute-done.15.x2 = bf16[256,2432]{1,0:T(8,128)(2,1)S(1)} collective-permute-done((bf16[256,2432]{1,0:T(8,128)(2,1)S(1)}, bf16[256,2432]{1,0:T(8,128)(2,1)S(1)}, u32[]{:S(2)}, u32[]{:S(2)}) %collective-permute-start.15) | collective-permute-done | bytes 1245216 | tf_op jit(solution)/shard_map/ppermute | solution.py:28
  69.9 3.0 %collective-permute-done.9.x0 = bf16[256,2560]{1,0:T(8,128)(2,1)S(1)} collective-permute-done((bf16[256,2560]{1,0:T(8,128)(2,1)S(1)}, bf16[256,2560]{1,0:T(8,128)(2,1)S(1)}, u32[]{:S(2)}, u32[]{:S(2)}) %collective-permute-start.9) | collective-permute-done | bytes 1310752 | tf_op jit(solution)/shard_map/ppermute | solution.py:28
  72.9 4.0 %gate_up_far.1 = (bf16[512,512]{1,0:T(8,128)(2,1)S(1)}, f32[8,128]{1,0:T(8,128)S(1)}) custom-call(s32[1]{0:T(128)} %bitcast.expert, bf16[256,2560]{1,0:T(8,128)(2,1)S(1)} %collective-permute-done.9.x0, bf16[256,2304]{1,0:T(8,128)(2,1)S(1)} %collective-permute-done.12.x1, bf16[256,2432]{1,0:T(8,128)(2,1)S(1)} %collective-permute-done.15.x2, ...), custom_call_target="tpu_custom_call" | custom-call | flops 3758096384 | tf_op jit(solution)/shard_map/gate_up_far/pallas_call | solution.py:183
  76.9 1.8 %shard_map.99 = bf16[256,2304]{1,0:T(8,128)(2,1)} custom-call(bf16[512,512]{1,0:T(8,128)(2,1)S(1)} %get-tuple-element.15.hidden, bf16[256,7168]{1,0:T(8,128)(2,1)S(1)} %get-tuple-element.16.own, bf16[256,7168]{1,0:T(8,128)(2,1)S(1)} %get-tuple-element.17.other), custom_call_target="tpu_custom_call" | custom-call | flops 603979776 | tf_op jit(solution)/shard_map/pallas_call | solution.py:209
  80.9 2.9 %collective-permute-start.19 = (bf16[256,2432]{1,0:T(8,128)(2,1)S(1)}, bf16[256,2432]{1,0:T(8,128)(2,1)}, u32[]{:S(2)}, u32[]{:S(2)}) collective-permute-start(bf16[256,2432]{1,0:T(8,128)(2,1)S(1)} %shard_map.95), channel_id=1, source_target_pairs={{0,24},{1,9},{8,16},{9,1},{16,8},{17,25},{24,0},{25,17},{2,26},{3,... | collective-permute-start | bytes 3735560 | tf_op jit(solution)/shard_map/ppermute | solution.py:28
  84.6 2.0 %collective-permute-start.22 = (bf16[256,2432]{1,0:T(8,128)(2,1)S(1)}, bf16[256,2432]{1,0:T(8,128)(2,1)}, u32[]{:S(2)}, u32[]{:S(2)}) collective-permute-start(bf16[256,2432]{1,0:T(8,128)(2,1)S(1)} %shard_map.97), channel_id=1, source_target_pairs={{0,6},{1,3},{2,4},{3,1},{4,2},{5,7},{6,0},{7,5},{8,14},{9,11},{10,... | collective-permute-start | bytes 3735560 | tf_op jit(solution)/shard_map/ppermute | solution.py:28
  86.7 2.0 %copy-done.1 = bf16[256,7168]{1,0:T(8,128)(2,1)S(1)} copy-done((bf16[256,7168]{1,0:T(8,128)(2,1)S(1)}, bf16[256,7168]{1,0:T(8,128)(2,1)}, u32[]{:S(2)}) %copy-start.1) | copy-done | bytes 3670040
  88.7 2.0 %copy-done.3 = bf16[256,7168]{1,0:T(8,128)(2,1)S(1)} copy-done((bf16[256,7168]{1,0:T(8,128)(2,1)S(1)}, bf16[256,7168]{1,0:T(8,128)(2,1)}, u32[]{:S(2)}) %copy-start.3) | copy-done | bytes 3670040
  93.2 3.2 %collective-permute-done.25 = bf16[256,2304]{1,0:T(8,128)(2,1)} collective-permute-done((bf16[256,2304]{1,0:T(8,128)(2,1)}, bf16[256,2304]{1,0:T(8,128)(2,1)}, u32[]{:S(2)}, u32[]{:S(2)}) %collective-permute-start.25) | collective-permute-done | bytes 1179680 | tf_op jit(solution)/shard_map/ppermute | solution.py:28
  96.5 1.5 %convert_add_fusion.2 = f32[256,2304]{1,0:T(8,128)S(1)} fusion(f32[256,2304]{1,0:T(8,128)S(1)} %shard_map.98, bf16[256,2304]{1,0:T(8,128)(2,1)} %collective-permute-done.25), kind=kLoop, calls=%fused_computation.2 | loop fusion | flops 1179648 | bytes 5898240 | tf_op jit(solution)/shard_map/add | solution.py:258
  98.1 1.3 collective-permute-start.26
  99.4 1.6 %convert_add_fusion.1 = f32[256,2432]{1,0:T(8,128)S(1)} fusion(f32[256,2432]{1,0:T(8,128)S(1)} %shard_map.94, bf16[256,2432]{1,0:T(8,128)(2,1)} %collective-permute-done.19), kind=kLoop, calls=%fused_computation.1 | loop fusion | flops 1245184 | bytes 6225920 | tf_op jit(solution)/shard_map/add | solution.py:258
  101.0 2.5 %collective-permute-start.20 = (bf16[128,2432]{1,0:T(8,128)(2,1)S(1)}, bf16[128,2432]{1,0:T(8,128)(2,1)S(1)}, u32[]{:S(2)}, u32[]{:S(2)}) collective-permute-start(bf16[128,2432]{1,0:T(8,128)(2,1)S(1)} %slice.163), channel_id=1, source_target_pairs={{0,96},{1,33},{32,64},{33,1},{64,32},{65,97},{96,0},{97,65},{2,98}... | collective-permute-start | bytes 1867784 | tf_op jit(solution)/shard_map/ppermute | solution.py:28
  103.5 1.6 %convert_add_fusion = f32[256,2432]{1,0:T(8,128)S(1)} fusion(f32[256,2432]{1,0:T(8,128)S(1)} %shard_map.96, bf16[256,2432]{1,0:T(8,128)(2,1)} %collective-permute-done.22), kind=kLoop, calls=%fused_computation | loop fusion | flops 1245184 | bytes 6225920 | tf_op jit(solution)/shard_map/add | solution.py:258
  105.2 2.6 %collective-permute-start.23 = (bf16[128,2432]{1,0:T(8,128)(2,1)S(1)}, bf16[128,2432]{1,0:T(8,128)(2,1)S(1)}, u32[]{:S(2)}, u32[]{:S(2)}) collective-permute-start(bf16[128,2432]{1,0:T(8,128)(2,1)S(1)} %slice.162), channel_id=1, source_target_pairs={{0,24},{1,9},{8,16},{9,1},{16,8},{17,25},{24,0},{25,17},{2,26},{3,... | collective-permute-start | bytes 1867784 | tf_op jit(solution)/shard_map/ppermute | solution.py:28
  108.2 2.6 %collective-permute-start.27 = (bf16[64,2304]{1,0:T(8,128)(2,1)S(1)}, bf16[64,2304]{1,0:T(8,128)(2,1)S(1)}, u32[]{:S(2)}, u32[]{:S(2)}) collective-permute-start(bf16[64,2304]{1,0:T(8,128)(2,1)S(1)} %slice.167), channel_id=1, source_target_pairs={{0,24},{1,9},{8,16},{9,1},{16,8},{17,25},{24,0},{25,17},{2,26},{3,... | collective-permute-start | bytes 884744 | tf_op jit(solution)/shard_map/ppermute | solution.py:28
  110.8 2.0 %collective-permute-done.20 = bf16[128,2432]{1,0:T(8,128)(2,1)S(1)} collective-permute-done((bf16[128,2432]{1,0:T(8,128)(2,1)S(1)}, bf16[128,2432]{1,0:T(8,128)(2,1)S(1)}, u32[]{:S(2)}, u32[]{:S(2)}) %collective-permute-start.20) | collective-permute-done | bytes 622624 | tf_op jit(solution)/shard_map/ppermute | solution.py:28
  112.9 2.0 %collective-permute-start.21 = (bf16[64,2432]{1,0:T(8,128)(2,1)S(1)}, bf16[64,2432]{1,0:T(8,128)(2,1)S(1)}, u32[]{:S(2)}, u32[]{:S(2)}) collective-permute-start(bf16[64,2432]{1,0:T(8,128)(2,1)S(1)} %slice.166), channel_id=1, source_target_pairs={{0,6},{1,3},{2,4},{3,1},{4,2},{5,7},{6,0},{7,5},{8,14},{9,11},{10,... | collective-permute-start | bytes 933896 | tf_op jit(solution)/shard_map/ppermute | solution.py:28
  114.9 1.7 %collective-permute-done.23 = bf16[128,2432]{1,0:T(8,128)(2,1)S(1)} collective-permute-done((bf16[128,2432]{1,0:T(8,128)(2,1)S(1)}, bf16[128,2432]{1,0:T(8,128)(2,1)S(1)}, u32[]{:S(2)}, u32[]{:S(2)}) %collective-permute-start.23) | collective-permute-done | bytes 622624 | tf_op jit(solution)/shard_map/ppermute | solution.py:28
  118.0 1.9 %collective-permute-done.27 = bf16[64,2304]{1,0:T(8,128)(2,1)S(1)} collective-permute-done((bf16[64,2304]{1,0:T(8,128)(2,1)S(1)}, bf16[64,2304]{1,0:T(8,128)(2,1)S(1)}, u32[]{:S(2)}, u32[]{:S(2)}) %collective-permute-start.27) | collective-permute-done | bytes 294944 | tf_op jit(solution)/shard_map/ppermute | solution.py:28
  120.0 7.5 %collective-permute-done.24 = bf16[64,2432]{1,0:T(8,128)(2,1)S(1)} collective-permute-done((bf16[64,2432]{1,0:T(8,128)(2,1)S(1)}, bf16[64,2432]{1,0:T(8,128)(2,1)S(1)}, u32[]{:S(2)}, u32[]{:S(2)}) %collective-permute-start.24) | collective-permute-done | bytes 311328 | tf_op jit(solution)/shard_map/ppermute | solution.py:28
  127.7 2.4 %collective-permute-start.28 = (bf16[8,7168]{1,0:T(8,128)(2,1)S(1)}, bf16[8,7168]{1,0:T(8,128)(2,1)S(1)}, u32[]{:S(2)}, u32[]{:S(2)}) collective-permute-start(bf16[8,7168]{1,0:T(8,128)(2,1)S(1)} %get-tuple-element.21), channel_id=1, source_target_pairs={{0,2},{1,7},{2,0},{3,5},{4,6},{5,3},{6,4},{7,1},{8,10},{9,15},{10,... | collective-permute-start | bytes 344072 | tf_op jit(solution)/shard_map/ppermute | solution.py:46
  130.8 1.5 %collective-permute-start.30 = (bf16[8,7168]{1,0:T(8,128)(2,1)S(1)}, bf16[8,7168]{1,0:T(8,128)(2,1)S(1)}, u32[]{:S(2)}, u32[]{:S(2)}) collective-permute-start(bf16[8,7168]{1,0:T(8,128)(2,1)S(1)} %get-tuple-element.26), channel_id=1, source_target_pairs={{0,34},{1,103},{2,32},{3,101},{4,38},{5,99},{6,36},{7,97},{8,42},{... | collective-permute-start | bytes 344072 | tf_op jit(solution)/shard_map/ppermute | solution.py:46
  132.3 3.4 %collective-permute-start.32 = (bf16[8,7168]{1,0:T(8,128)(2,1)S(1)}, bf16[8,7168]{1,0:T(8,128)(2,1)S(1)}, u32[]{:S(2)}, u32[]{:S(2)}) collective-permute-start(bf16[8,7168]{1,0:T(8,128)(2,1)S(1)} %get-tuple-element.24), channel_id=1, source_target_pairs={{0,10},{1,31},{2,8},{3,29},{4,14},{5,27},{6,12},{7,25},{8,2},{9,23... | collective-permute-start | bytes 344072 | tf_op jit(solution)/shard_map/ppermute | solution.py:46
  135.7 2.5 %collective-permute-start.34 = (bf16[8,7168]{1,0:T(8,128)(2,1)S(1)}, bf16[8,7168]{1,0:T(8,128)(2,1)S(1)}, u32[]{:S(2)}, u32[]{:S(2)}) collective-permute-start(bf16[8,7168]{1,0:T(8,128)(2,1)S(1)} %get-tuple-element.22), channel_id=1, source_target_pairs={{0,42},{1,127},{2,40},{3,125},{4,46},{5,123},{6,44},{7,121},{8,34}... | collective-permute-start | bytes 344072 | tf_op jit(solution)/shard_map/ppermute | solution.py:46
  138.5 4.2 %collective-permute-done.33 = bf16[8,7168]{1,0:T(8,128)(2,1)S(1)} collective-permute-done((bf16[8,7168]{1,0:T(8,128)(2,1)S(1)}, bf16[8,7168]{1,0:T(8,128)(2,1)S(1)}, u32[]{:S(2)}, u32[]{:S(2)}) %collective-permute-start.33) | collective-permute-done | bytes 114720 | tf_op jit(solution)/shard_map/ppermute | solution.py:46
  (96 shorter events, 15.7 us)
Async XLA Ops:
  0.6 0.9 copy-start.4
  1.5 0.7 copy-start.5
  2.2 0.7 copy-start.6
  3.0 5.5 %collective-permute-start = (bf16[8,7296]{1,0:T(8,128)(2,1)S(1)}, bf16[8,7296]{1,0:T(8,128)(2,1)S(1)}, u32[]{:S(2)}, u32[]{:S(2)}) collective-permute-start(bf16[8,7296]{1,0:T(8,128)(2,1)S(1)} %token_rows.1), channel_id=1, source_target_pairs={{0,2},{1,7},{2,0},{3,5},{4,6},{5,3},{6,4},{7,1},{8,10},{9,15},{10,... | collective-permute-start | bytes 350216 | tf_op jit(solution)/shard_map/ppermute | solution.py:46
  3.5 8.1 %collective-permute-start.1 = (bf16[8,7296]{1,0:T(8,128)(2,1)S(1)}, bf16[8,7296]{1,0:T(8,128)(2,1)S(1)}, u32[]{:S(2)}, u32[]{:S(2)}) collective-permute-start(bf16[8,7296]{1,0:T(8,128)(2,1)S(1)} %token_rows.1), channel_id=1, source_target_pairs={{0,32},{1,97},{2,34},{3,99},{4,36},{5,101},{6,38},{7,103},{8,40},{... | collective-permute-start | bytes 350216 | tf_op jit(solution)/shard_map/ppermute | solution.py:46
  5.2 7.5 %collective-permute-start.2 = (bf16[8,7296]{1,0:T(8,128)(2,1)S(1)}, bf16[8,7296]{1,0:T(8,128)(2,1)S(1)}, u32[]{:S(2)}, u32[]{:S(2)}) collective-permute-start(bf16[8,7296]{1,0:T(8,128)(2,1)S(1)} %token_rows.1), channel_id=1, source_target_pairs={{0,34},{1,103},{2,32},{3,101},{4,38},{5,99},{6,36},{7,97},{8,42},{... | collective-permute-start | bytes 350216 | tf_op jit(solution)/shard_map/ppermute | solution.py:46
  6.6 10.4 %collective-permute-start.3 = (bf16[8,7296]{1,0:T(8,128)(2,1)S(1)}, bf16[8,7296]{1,0:T(8,128)(2,1)S(1)}, u32[]{:S(2)}, u32[]{:S(2)}) collective-permute-start(bf16[8,7296]{1,0:T(8,128)(2,1)S(1)} %token_rows.1), channel_id=1, source_target_pairs={{0,8},{1,25},{2,10},{3,27},{4,12},{5,29},{6,14},{7,31},{8,0},{9,17... | collective-permute-start | bytes 350216 | tf_op jit(solution)/shard_map/ppermute | solution.py:46
  8.5 8.6 %collective-permute-start.4 = (bf16[8,7296]{1,0:T(8,128)(2,1)S(1)}, bf16[8,7296]{1,0:T(8,128)(2,1)S(1)}, u32[]{:S(2)}, u32[]{:S(2)}) collective-permute-start(bf16[8,7296]{1,0:T(8,128)(2,1)S(1)} %token_rows.1), channel_id=1, source_target_pairs={{0,10},{1,31},{2,8},{3,29},{4,14},{5,27},{6,12},{7,25},{8,2},{9,23... | collective-permute-start | bytes 350216 | tf_op jit(solution)/shard_map/ppermute | solution.py:46
  8.5 9.1 %collective-permute-start.5 = (bf16[8,7296]{1,0:T(8,128)(2,1)S(1)}, bf16[8,7296]{1,0:T(8,128)(2,1)S(1)}, u32[]{:S(2)}, u32[]{:S(2)}) collective-permute-start(bf16[8,7296]{1,0:T(8,128)(2,1)S(1)} %token_rows.1), channel_id=1, source_target_pairs={{0,40},{1,121},{2,42},{3,123},{4,44},{5,125},{6,46},{7,127},{8,32}... | collective-permute-start | bytes 350216 | tf_op jit(solution)/shard_map/ppermute | solution.py:46
  11.6 6.7 %collective-permute-start.6 = (bf16[8,7296]{1,0:T(8,128)(2,1)S(1)}, bf16[8,7296]{1,0:T(8,128)(2,1)S(1)}, u32[]{:S(2)}, u32[]{:S(2)}) collective-permute-start(bf16[8,7296]{1,0:T(8,128)(2,1)S(1)} %token_rows.1), channel_id=1, source_target_pairs={{0,42},{1,127},{2,40},{3,125},{4,46},{5,123},{6,44},{7,121},{8,34}... | collective-permute-start | bytes 350216 | tf_op jit(solution)/shard_map/ppermute | solution.py:46
  12.7 41.2 %collective-permute-start.16 = (bf16[7168,256]{1,0:T(8,128)(2,1)}, bf16[7168,256]{1,0:T(8,128)(2,1)}, u32[]{:S(2)}, u32[]{:S(2)}) collective-permute-start(bf16[7168,256]{1,0:T(8,128)(2,1)} %bitcast.4), channel_id=1, source_target_pairs={{0,1},{1,0},{2,3},{3,2},{4,5},{5,4},{6,7},{7,6},{8,9},{9,8},{10,11... | collective-permute-start | bytes 11010056 | tf_op jit(solution)/shard_map/ppermute | solution.py:54
  16.9 39.7 %collective-permute-start.17 = (bf16[7168,256]{1,0:T(8,128)(2,1)}, bf16[7168,256]{1,0:T(8,128)(2,1)}, u32[]{:S(2)}, u32[]{:S(2)}) collective-permute-start(bf16[7168,256]{1,0:T(8,128)(2,1)} %bitcast.6), channel_id=1, source_target_pairs={{0,1},{1,0},{2,3},{3,2},{4,5},{5,4},{6,7},{7,6},{8,9},{9,8},{10,11... | collective-permute-start | bytes 11010056 | tf_op jit(solution)/shard_map/ppermute | solution.py:54
  17.1 47.0 %collective-permute-start.18 = (bf16[256,7168]{1,0:T(8,128)(2,1)}, bf16[256,7168]{1,0:T(8,128)(2,1)}, u32[]{:S(2)}, u32[]{:S(2)}) collective-permute-start(bf16[256,7168]{1,0:T(8,128)(2,1)} %bitcast.8), channel_id=1, source_target_pairs={{0,1},{1,0},{2,3},{3,2},{4,5},{5,4},{6,7},{7,6},{8,9},{9,8},{10,11... | collective-permute-start | bytes 11010056 | tf_op jit(solution)/shard_map/ppermute | solution.py:54
  18.4 8.0 %collective-permute-start.10 = (bf16[64,2304]{1,0:T(8,128)(2,1)S(1)}, bf16[64,2304]{1,0:T(8,128)(2,1)S(1)}, u32[]{:S(2)}, u32[]{:S(2)}) collective-permute-start(bf16[64,2304]{1,0:T(8,128)(2,1)S(1)} %slice.110), channel_id=1, source_target_pairs={{0,96},{1,33},{32,64},{33,1},{64,32},{65,97},{96,0},{97,65},{2,98}... | collective-permute-start | bytes 884744 | tf_op jit(solution)/shard_map/ppermute | solution.py:28
  20.7 8.2 %collective-permute-start.13 = (bf16[64,2432]{1,0:T(8,128)(2,1)S(1)}, bf16[64,2432]{1,0:T(8,128)(2,1)S(1)}, u32[]{:S(2)}, u32[]{:S(2)}) collective-permute-start(bf16[64,2432]{1,0:T(8,128)(2,1)S(1)} %slice.111), channel_id=1, source_target_pairs={{0,24},{1,9},{8,16},{9,1},{16,8},{17,25},{24,0},{25,17},{2,26},{3,... | collective-permute-start | bytes 933896 | tf_op jit(solution)/shard_map/ppermute | solution.py:28
  26.4 7.2 %collective-permute-start.7 = (bf16[64,2560]{1,0:T(8,128)(2,1)S(1)}, bf16[64,2560]{1,0:T(8,128)(2,1)S(1)}, u32[]{:S(2)}, u32[]{:S(2)}) collective-permute-start(bf16[64,2560]{1,0:T(8,128)(2,1)S(1)} %slice.109), channel_id=1, source_target_pairs={{0,6},{1,3},{2,4},{3,1},{4,2},{5,7},{6,0},{7,5},{8,14},{9,11},{10,... | collective-permute-start | bytes 983048 | tf_op jit(solution)/shard_map/ppermute | solution.py:28
  28.9 11.1 %collective-permute-start.11 = (bf16[128,2304]{1,0:T(8,128)(2,1)S(1)}, bf16[128,2304]{1,0:T(8,128)(2,1)S(1)}, u32[]{:S(2)}, u32[]{:S(2)}) collective-permute-start(bf16[128,2304]{1,0:T(8,128)(2,1)S(1)} %pad_maximum_fusion.6), channel_id=1, source_target_pairs={{0,24},{1,9},{8,16},{9,1},{16,8},{17,25},{24,0},{25,17},{2,26},{3,... | collective-permute-start | bytes 1769480 | tf_op jit(solution)/shard_map/ppermute | solution.py:28
  33.6 10.2 %collective-permute-start.14 = (bf16[128,2432]{1,0:T(8,128)(2,1)S(1)}, bf16[128,2432]{1,0:T(8,128)(2,1)S(1)}, u32[]{:S(2)}, u32[]{:S(2)}) collective-permute-start(bf16[128,2432]{1,0:T(8,128)(2,1)S(1)} %pad_maximum_fusion.5), channel_id=1, source_target_pairs={{0,6},{1,3},{2,4},{3,1},{4,2},{5,7},{6,0},{7,5},{8,14},{9,11},{10,... | collective-permute-start | bytes 1867784 | tf_op jit(solution)/shard_map/ppermute | solution.py:28
  40.0 11.8 %collective-permute-start.8 = (bf16[128,2560]{1,0:T(8,128)(2,1)S(1)}, bf16[128,2560]{1,0:T(8,128)(2,1)S(1)}, u32[]{:S(2)}, u32[]{:S(2)}) collective-permute-start(bf16[128,2560]{1,0:T(8,128)(2,1)S(1)} %pad_maximum_fusion.4), channel_id=1, source_target_pairs={{0,96},{1,33},{32,64},{33,1},{64,32},{65,97},{96,0},{97,65},{2,98}... | collective-permute-start | bytes 1966088 | tf_op jit(solution)/shard_map/ppermute | solution.py:28
  41.9 14.7 %copy-start.8 = (bf16[1,7168,256]{2,1,0:T(8,128)(2,1)S(1)}, bf16[1,7168,256]{2,1,0:T(8,128)(2,1)}, u32[]{:S(2)}) copy-start(bf16[1,7168,256]{2,1,0:T(8,128)(2,1)} %param.12) | copy-start | bytes 11010052
  43.8 22.6 %collective-permute-start.12 = (bf16[256,2304]{1,0:T(8,128)(2,1)S(1)}, bf16[256,2304]{1,0:T(8,128)(2,1)S(1)}, u32[]{:S(2)}, u32[]{:S(2)}) collective-permute-start(bf16[256,2304]{1,0:T(8,128)(2,1)S(1)} %pad_maximum_fusion.3.x1), channel_id=1, source_target_pairs={{0,6},{1,3},{2,4},{3,1},{4,2},{5,7},{6,0},{7,5},{8,14},{9,11},{10,... | collective-permute-start | bytes 3538952 | tf_op jit(solution)/shard_map/ppermute | solution.py:28
  45.8 10.8 %copy-start.7 = (bf16[1,7168,256]{2,1,0:T(8,128)(2,1)S(1)}, bf16[1,7168,256]{2,1,0:T(8,128)(2,1)}, u32[]{:S(2)}) copy-start(bf16[1,7168,256]{2,1,0:T(8,128)(2,1)} %param.11) | copy-start | bytes 11010052
  51.8 18.1 %collective-permute-start.15 = (bf16[256,2432]{1,0:T(8,128)(2,1)S(1)}, bf16[256,2432]{1,0:T(8,128)(2,1)S(1)}, u32[]{:S(2)}, u32[]{:S(2)}) collective-permute-start(bf16[256,2432]{1,0:T(8,128)(2,1)S(1)} %pad_maximum_fusion.2.x2.near_x2), channel_id=1, source_target_pairs={{0,96},{1,33},{32,64},{33,1},{64,32},{65,97},{96,0},{97,65},{2,98}... | collective-permute-start | bytes 3735560 | tf_op jit(solution)/shard_map/ppermute | solution.py:28
  53.8 19.1 %collective-permute-start.9 = (bf16[256,2560]{1,0:T(8,128)(2,1)S(1)}, bf16[256,2560]{1,0:T(8,128)(2,1)S(1)}, u32[]{:S(2)}, u32[]{:S(2)}) collective-permute-start(bf16[256,2560]{1,0:T(8,128)(2,1)S(1)} %pad_maximum_fusion.1.x0), channel_id=1, source_target_pairs={{0,24},{1,9},{8,16},{9,1},{16,8},{17,25},{24,0},{25,17},{2,26},{3,... | collective-permute-start | bytes 3932168 | tf_op jit(solution)/shard_map/ppermute | solution.py:28
  60.1 4.0 %copy-start.9 = (bf16[1,256,7168]{2,1,0:T(8,128)(2,1)S(1)}, bf16[1,256,7168]{2,1,0:T(8,128)(2,1)}, u32[]{:S(2)}) copy-start(bf16[1,256,7168]{2,1,0:T(8,128)(2,1)} %param.13) | copy-start | bytes 11010052
  66.4 17.3 %copy-start = (bf16[256,7168]{1,0:T(8,128)(2,1)}, bf16[256,7168]{1,0:T(8,128)(2,1)S(1)}, u32[]{:S(2)}) copy-start(bf16[256,7168]{1,0:T(8,128)(2,1)S(1)} %get-tuple-element.16.own) | copy-start | bytes 11010052
  66.5 17.3 %copy-start.2 = (bf16[256,7168]{1,0:T(8,128)(2,1)}, bf16[256,7168]{1,0:T(8,128)(2,1)S(1)}, u32[]{:S(2)}) copy-start(bf16[256,7168]{1,0:T(8,128)(2,1)S(1)} %get-tuple-element.17.other) | copy-start | bytes 11010052
  78.8 17.7 %collective-permute-start.25 = (bf16[256,2304]{1,0:T(8,128)(2,1)}, bf16[256,2304]{1,0:T(8,128)(2,1)}, u32[]{:S(2)}, u32[]{:S(2)}) collective-permute-start(bf16[256,2304]{1,0:T(8,128)(2,1)} %shard_map.99), channel_id=1, source_target_pairs={{0,96},{1,33},{32,64},{33,1},{64,32},{65,97},{96,0},{97,65},{2,98}... | collective-permute-start | bytes 3538952 | tf_op jit(solution)/shard_map/ppermute | solution.py:28
  80.9 18.5 %collective-permute-start.19 = (bf16[256,2432]{1,0:T(8,128)(2,1)S(1)}, bf16[256,2432]{1,0:T(8,128)(2,1)}, u32[]{:S(2)}, u32[]{:S(2)}) collective-permute-start(bf16[256,2432]{1,0:T(8,128)(2,1)S(1)} %shard_map.95), channel_id=1, source_target_pairs={{0,24},{1,9},{8,16},{9,1},{16,8},{17,25},{24,0},{25,17},{2,26},{3,... | collective-permute-start | bytes 3735560 | tf_op jit(solution)/shard_map/ppermute | solution.py:28
  84.6 18.9 %collective-permute-start.22 = (bf16[256,2432]{1,0:T(8,128)(2,1)S(1)}, bf16[256,2432]{1,0:T(8,128)(2,1)}, u32[]{:S(2)}, u32[]{:S(2)}) collective-permute-start(bf16[256,2432]{1,0:T(8,128)(2,1)S(1)} %shard_map.97), channel_id=1, source_target_pairs={{0,6},{1,3},{2,4},{3,1},{4,2},{5,7},{6,0},{7,5},{8,14},{9,11},{10,... | collective-permute-start | bytes 3735560 | tf_op jit(solution)/shard_map/ppermute | solution.py:28
  86.7 43.5 %collective-permute-start.35 = (s32[16]{0:T(128)S(1)}, s32[16]{0:T(128)S(1)}, u32[]{:S(2)}, u32[]{:S(2)}) collective-permute-start(s32[16]{0:T(128)S(1)} %slice_convert_fusion.6), channel_id=1, source_target_pairs={{0,1},{1,0},{2,3},{3,2},{4,5},{5,4},{6,7},{7,6},{8,9},{9,8},{10,11... | collective-permute-start | bytes 200 | tf_op jit(solution)/shard_map/ppermute | solution.py:54
  86.7 2.0 %copy-start.1 = (bf16[256,7168]{1,0:T(8,128)(2,1)S(1)}, bf16[256,7168]{1,0:T(8,128)(2,1)}, u32[]{:S(2)}) copy-start(bf16[256,7168]{1,0:T(8,128)(2,1)} %copy-done) | copy-start | bytes 11010052
  88.7 2.0 %copy-start.3 = (bf16[256,7168]{1,0:T(8,128)(2,1)S(1)}, bf16[256,7168]{1,0:T(8,128)(2,1)}, u32[]{:S(2)}) copy-start(bf16[256,7168]{1,0:T(8,128)(2,1)} %copy-done.2) | copy-start | bytes 11010052
  98.1 10.0 %collective-permute-start.26 = (bf16[128,2304]{1,0:T(8,128)(2,1)S(1)}, bf16[128,2304]{1,0:T(8,128)(2,1)S(1)}, u32[]{:S(2)}, u32[]{:S(2)}) collective-permute-start(bf16[128,2304]{1,0:T(8,128)(2,1)S(1)} %slice.164), channel_id=1, source_target_pairs={{0,6},{1,3},{2,4},{3,1},{4,2},{5,7},{6,0},{7,5},{8,14},{9,11},{10,... | collective-permute-start | bytes 1769480 | tf_op jit(solution)/shard_map/ppermute | solution.py:28
  101.0 11.7 %collective-permute-start.20 = (bf16[128,2432]{1,0:T(8,128)(2,1)S(1)}, bf16[128,2432]{1,0:T(8,128)(2,1)S(1)}, u32[]{:S(2)}, u32[]{:S(2)}) collective-permute-start(bf16[128,2432]{1,0:T(8,128)(2,1)S(1)} %slice.163), channel_id=1, source_target_pairs={{0,96},{1,33},{32,64},{33,1},{64,32},{65,97},{96,0},{97,65},{2,98}... | collective-permute-start | bytes 1867784 | tf_op jit(solution)/shard_map/ppermute | solution.py:28
  105.2 11.5 %collective-permute-start.23 = (bf16[128,2432]{1,0:T(8,128)(2,1)S(1)}, bf16[128,2432]{1,0:T(8,128)(2,1)S(1)}, u32[]{:S(2)}, u32[]{:S(2)}) collective-permute-start(bf16[128,2432]{1,0:T(8,128)(2,1)S(1)} %slice.162), channel_id=1, source_target_pairs={{0,24},{1,9},{8,16},{9,1},{16,8},{17,25},{24,0},{25,17},{2,26},{3,... | collective-permute-start | bytes 1867784 | tf_op jit(solution)/shard_map/ppermute | solution.py:28
  108.2 11.7 %collective-permute-start.27 = (bf16[64,2304]{1,0:T(8,128)(2,1)S(1)}, bf16[64,2304]{1,0:T(8,128)(2,1)S(1)}, u32[]{:S(2)}, u32[]{:S(2)}) collective-permute-start(bf16[64,2304]{1,0:T(8,128)(2,1)S(1)} %slice.167), channel_id=1, source_target_pairs={{0,24},{1,9},{8,16},{9,1},{16,8},{17,25},{24,0},{25,17},{2,26},{3,... | collective-permute-start | bytes 884744 | tf_op jit(solution)/shard_map/ppermute | solution.py:28
  112.9 7.0 %collective-permute-start.21 = (bf16[64,2432]{1,0:T(8,128)(2,1)S(1)}, bf16[64,2432]{1,0:T(8,128)(2,1)S(1)}, u32[]{:S(2)}, u32[]{:S(2)}) collective-permute-start(bf16[64,2432]{1,0:T(8,128)(2,1)S(1)} %slice.166), channel_id=1, source_target_pairs={{0,6},{1,3},{2,4},{3,1},{4,2},{5,7},{6,0},{7,5},{8,14},{9,11},{10,... | collective-permute-start | bytes 933896 | tf_op jit(solution)/shard_map/ppermute | solution.py:28
  116.8 10.6 %collective-permute-start.24 = (bf16[64,2432]{1,0:T(8,128)(2,1)S(1)}, bf16[64,2432]{1,0:T(8,128)(2,1)S(1)}, u32[]{:S(2)}, u32[]{:S(2)}) collective-permute-start(bf16[64,2432]{1,0:T(8,128)(2,1)S(1)} %slice.165), channel_id=1, source_target_pairs={{0,96},{1,33},{32,64},{33,1},{64,32},{65,97},{96,0},{97,65},{2,98}... | collective-permute-start | bytes 933896 | tf_op jit(solution)/shard_map/ppermute | solution.py:28
  127.5 2.6 %copy-start.10 = (f32[16]{0:T(128)S(1)}, f32[16]{0:T(128)}, u32[]{:S(2)}) copy-start(f32[16]{0:T(128)} %param.14) | copy-start | bytes 196
  127.7 8.0 %collective-permute-start.28 = (bf16[8,7168]{1,0:T(8,128)(2,1)S(1)}, bf16[8,7168]{1,0:T(8,128)(2,1)S(1)}, u32[]{:S(2)}, u32[]{:S(2)}) collective-permute-start(bf16[8,7168]{1,0:T(8,128)(2,1)S(1)} %get-tuple-element.21), channel_id=1, source_target_pairs={{0,2},{1,7},{2,0},{3,5},{4,6},{5,3},{6,4},{7,1},{8,10},{9,15},{10,... | collective-permute-start | bytes 344072 | tf_op jit(solution)/shard_map/ppermute | solution.py:46
  130.2 5.6 %collective-permute-start.29 = (bf16[8,7168]{1,0:T(8,128)(2,1)S(1)}, bf16[8,7168]{1,0:T(8,128)(2,1)S(1)}, u32[]{:S(2)}, u32[]{:S(2)}) collective-permute-start(bf16[8,7168]{1,0:T(8,128)(2,1)S(1)} %get-tuple-element.27), channel_id=1, source_target_pairs={{0,32},{1,97},{2,34},{3,99},{4,36},{5,101},{6,38},{7,103},{8,40},{... | collective-permute-start | bytes 344072 | tf_op jit(solution)/shard_map/ppermute | solution.py:46
  130.8 7.5 %collective-permute-start.30 = (bf16[8,7168]{1,0:T(8,128)(2,1)S(1)}, bf16[8,7168]{1,0:T(8,128)(2,1)S(1)}, u32[]{:S(2)}, u32[]{:S(2)}) collective-permute-start(bf16[8,7168]{1,0:T(8,128)(2,1)S(1)} %get-tuple-element.26), channel_id=1, source_target_pairs={{0,34},{1,103},{2,32},{3,101},{4,38},{5,99},{6,36},{7,97},{8,42},{... | collective-permute-start | bytes 344072 | tf_op jit(solution)/shard_map/ppermute | solution.py:46
  132.3 6.0 %collective-permute-start.31 = (bf16[8,7168]{1,0:T(8,128)(2,1)S(1)}, bf16[8,7168]{1,0:T(8,128)(2,1)S(1)}, u32[]{:S(2)}, u32[]{:S(2)}) collective-permute-start(bf16[8,7168]{1,0:T(8,128)(2,1)S(1)} %get-tuple-element.25), channel_id=1, source_target_pairs={{0,8},{1,25},{2,10},{3,27},{4,12},{5,29},{6,14},{7,31},{8,0},{9,17... | collective-permute-start | bytes 344072 | tf_op jit(solution)/shard_map/ppermute | solution.py:46
  132.3 6.2 %collective-permute-start.32 = (bf16[8,7168]{1,0:T(8,128)(2,1)S(1)}, bf16[8,7168]{1,0:T(8,128)(2,1)S(1)}, u32[]{:S(2)}, u32[]{:S(2)}) collective-permute-start(bf16[8,7168]{1,0:T(8,128)(2,1)S(1)} %get-tuple-element.24), channel_id=1, source_target_pairs={{0,10},{1,31},{2,8},{3,29},{4,14},{5,27},{6,12},{7,25},{8,2},{9,23... | collective-permute-start | bytes 344072 | tf_op jit(solution)/shard_map/ppermute | solution.py:46
  135.7 6.9 %collective-permute-start.33 = (bf16[8,7168]{1,0:T(8,128)(2,1)S(1)}, bf16[8,7168]{1,0:T(8,128)(2,1)S(1)}, u32[]{:S(2)}, u32[]{:S(2)}) collective-permute-start(bf16[8,7168]{1,0:T(8,128)(2,1)S(1)} %get-tuple-element.23), channel_id=1, source_target_pairs={{0,40},{1,121},{2,42},{3,123},{4,44},{5,125},{6,46},{7,127},{8,32}... | collective-permute-start | bytes 344072 | tf_op jit(solution)/shard_map/ppermute | solution.py:46
  135.7 6.9 %collective-permute-start.34 = (bf16[8,7168]{1,0:T(8,128)(2,1)S(1)}, bf16[8,7168]{1,0:T(8,128)(2,1)S(1)}, u32[]{:S(2)}, u32[]{:S(2)}) collective-permute-start(bf16[8,7168]{1,0:T(8,128)(2,1)S(1)} %get-tuple-element.22), channel_id=1, source_target_pairs={{0,42},{1,127},{2,40},{3,125},{4,46},{5,123},{6,44},{7,121},{8,34}... | collective-permute-start | bytes 344072 | tf_op jit(solution)/shard_map/ppermute | solution.py:46
where the time goes:
time: 144 us; the launch traced here: 143 us
  starting transfers between devices  63.4 us (44%)
  waiting for transfers between devices  45 us (31%)
  Pallas kernels  19.8 us (14%)
  other arithmetic  7.19 us (5%)
  local copies, waits for them, and re-layouts  6.9 us (5%)
    ppermute x18, waiting for transfers between devices, exchange(): return lax.ppermute(value, (axis, 'gz_1'), pairs)  40 us
    ppermute x18, starting transfers between devices, exchange(): return lax.ppermute(value, (axis, 'gz_1'), pairs)  39.1 us
    ppermute x14, starting transfers between devices, direct(): return lax.ppermute(value, AXES, pairs)  19.4 us
    unnamed x29, local copies, waits for them, and re-layouts  6.46 us
    pallas_call x6, Pallas kernels, down_part(): pl.pallas_call(functools.partial(down_kernel, colour, far), out_shape=jax...  6.01 us
    pallas_call x2, Pallas kernels, in_vmem(): pl.pallas_call(load_kernel, out_shape=tuple((jax.ShapeDtypeStruct(a.shape...  5.8 us
    add x9, other arithmetic, layer(): totals = [kept[i] + got[i].astype(F32) for i in range(3)]  5.14 us
    ppermute x14, waiting for transfers between devices, direct(): return lax.ppermute(value, AXES, pairs)  4.98 us
  transfers between devices with their start and end apart: 36, of which 17 were waited for; matrix products, arithmetic and copies ran while one was open for 5% of the time, Pallas kernels for 10%

commit v1 on v0

--- a/solution.py
+++ b/solution.py
@@ -63,9 +63,17 @@
 SMEM = pl.BlockSpec(memory_space=pltpu.SMEM)
 
 
-def rows_kernel(experts, tokens, ids, weights, out):
+def rows_kernel(experts, tokens, ids_in, weights_in, out, ids, weights, sem):
     width = tokens.shape[1]
-    out[:, :width] = tokens[...]
+    copies = (
+        pltpu.make_async_copy(ids_in, ids, sem.at[0]),
+        pltpu.make_async_copy(weights_in, weights, sem.at[1]),
+        pltpu.make_async_copy(tokens, out.at[:, pl.ds(0, width)], sem.at[2]),
+    )
+    for c in copies:
+        c.start()
+    copies[0].wait()
+    copies[1].wait()
     lane = lax.broadcasted_iota(jnp.int32, (tokens.shape[0], INFO), 1)
     info = jnp.zeros((tokens.shape[0], INFO), F32)
     for k in range(ids.shape[1]):
@@ -73,6 +81,7 @@
         info += jnp.where(lane == chosen, weights[:, k : k + 1].astype(F32), 0.0)
         info += jnp.where(lane == chosen + experts, 1.0, 0.0)
     out[:, width:] = info.astype(BF16)
+    copies[2].wait()
 
 
 def rows_of(tokens, ids, weights, experts):
@@ -80,8 +89,13 @@
     return pl.pallas_call(
         functools.partial(rows_kernel, experts),
         out_shape=jax.ShapeDtypeStruct((rows, width + INFO), BF16),
-        in_specs=[VMEM] * 3,
+        in_specs=[pl.BlockSpec(memory_space=pltpu.HBM)] * 3,
         out_specs=VMEM,
+        scratch_shapes=[
+            pltpu.VMEM(ids.shape, ids.dtype),
+            pltpu.VMEM(weights.shape, weights.dtype),
+            pltpu.SemaphoreType.DMA((3,)),
+        ],
         compiler_params=pltpu.CompilerParams(vmem_limit_bytes=4 << 20),
         name="token_rows",
     )(tokens, ids, weights)
@@ -107,36 +121,44 @@
                         acc[j, 64 * s : 64 * s + 64, :] = jnp.zeros((64, 256), F32)
 
 
-def far_kernel(expert, x0, x1, x2, w0, w1, w2, w3, near_x2, acc_in, hidden, marks, acc):
-    ready = {}
-    for i, x in enumerate((x0, x1, x2)):
-        width = CUTS[i + 1] - CUTS[i]
-        places = [canonical(i, q + 4) for q in range(4)]
-        for j, w in enumerate((w0, w1, w2, w3)):
-            part = jnp.dot(
-                x[:, :width], w[CUTS[i] : CUTS[i + 1], :], preferred_element_type=F32
-            )
-            for q, s in enumerate(places):
-                rows = part[64 * q : 64 * q + 64]
-                before = acc if (j, s) in ready else acc_in
-                acc[j, 64 * s : 64 * s + 64, :] = before[j, 64 * s : 64 * s + 64, :] + rows
-                ready[j, s] = True
+def far_part_kernel(colour, x, w0, w1, w2, w3, out):
+    rows = slice(CUTS[colour], CUTS[colour + 1])
+    width = CUTS[colour + 1] - CUTS[colour]
+    for j, w in enumerate((w0, w1, w2, w3)):
+        out[j] = jnp.dot(x[:, :width], w[rows, :], preferred_element_type=F32)
+
+
+def far_last_kernel(
+    expert, x0, w0, w1, w2, w3, part1, part2, near_x2, far_x2, acc_in, hidden, marks, acc
+):
+    far_places = [{canonical(i, q + 4): 64 * q for q in range(4)} for i in range(3)]
+    for j, w in enumerate((w0, w1, w2, w3)):
+        mine = jnp.dot(x0[...], w[: CUTS[1], :], preferred_element_type=F32)
+        for s in range(8):
+            rows = acc_in[j, 64 * s : 64 * s + 64, :]
+            if s in far_places[0]:
+                at = far_places[0][s]
+                rows += mine[at : at + 64]
+            for i, part in ((1, part1), (2, part2)):
+                if s in far_places[i]:
+                    at = far_places[i][s]
+                    rows += part[j, at : at + 64, :]
+            acc[j, 64 * s : 64 * s + 64, :] = rows
     lane = lax.broadcasted_iota(jnp.int32, (64, INFO), 1)
     sums = jnp.zeros((8, INFO), F32)
     for place in range(8):
         s = canonical(2, place)
-        source = near_x2 if place < 4 else x2
+        source = near_x2 if place < 4 else far_x2
         at = 64 * (place % 4)
         info = source[at : at + 64, CUTS[3] - CUTS[2] :].astype(F32)
         sums += jnp.sum(info.reshape(8, 8, INFO), axis=0)
         scale = jnp.sum(jnp.where(lane == expert[0], info, 0.0), axis=1, keepdims=True)
         for part in range(2):
-            value = acc if (part, s) in ready else acc_in
-            g = value[part, 64 * s : 64 * s + 64, :]
-            u = value[part + 2, 64 * s : 64 * s + 64, :]
+            g = acc[part, 64 * s : 64 * s + 64, :]
+            u = acc[part + 2, 64 * s : 64 * s + 64, :]
             h = g / (1.0 + jnp.exp(-g)) * u * scale
             hidden[64 * s : 64 * s + 64, 256 * part : 256 * part + 256] = h.astype(BF16)
-    marks[...] = sums
+    marks[...] = jnp.sum(sums, axis=0, keepdims=True).astype(jnp.int32)
 
 
 def load_kernel(*refs):
@@ -164,7 +186,10 @@
     )(*arrays)
 
 
-COST = pl.CostEstimate(flops=2 * 256 * 7168 * 1024, transcendentals=0, bytes_accessed=0)
+def cost(parts):
+    return pl.CostEstimate(
+        flops=2 * 256 * 2389 * 1024 * parts, transcendentals=0, bytes_accessed=0
+    )
 
 
 def gate_up_near(pieces, weights):
@@ -173,26 +198,37 @@
         out_shape=jax.ShapeDtypeStruct((4, 512, 256), F32),
         in_specs=[VMEM] * 7,
         out_specs=VMEM,
-        cost_estimate=COST,
+        cost_estimate=cost(3),
         compiler_params=pltpu.CompilerParams(vmem_limit_bytes=8 << 20),
         name="gate_up_near",
     )(*pieces, *weights)
 
 
-def gate_up_far(expert, pieces, weights, near_x2, acc):
-    return pl.pallas_call(
-        far_kernel,
+def gate_up_far_part(colour, piece, weights):
+    return pl.pallas_call(
+        functools.partial(far_part_kernel, colour),
+        out_shape=jax.ShapeDtypeStruct((4, 256, 256), F32),
+        in_specs=[VMEM] * 5,
+        out_specs=VMEM,
+        cost_estimate=cost(1),
+        compiler_params=pltpu.CompilerParams(vmem_limit_bytes=6 << 20),
+    )(piece, *weights)
+
+
+def gate_up_last(expert, piece, weights, parts, near_x2, far_x2, acc):
+    return pl.pallas_call(
+        far_last_kernel,
         out_shape=(
             jax.ShapeDtypeStruct((512, 512), BF16),
-            jax.ShapeDtypeStruct((8, INFO), F32),
+            jax.ShapeDtypeStruct((1, INFO), jnp.int32),
         ),
-        in_specs=[SMEM] + [VMEM] * 9,
+        in_specs=[SMEM] + [VMEM] * 10,
         out_specs=(VMEM, VMEM),
         scratch_shapes=[pltpu.VMEM((4, 512, 256), F32)],
-        cost_estimate=COST,
+        cost_estimate=cost(1),
         compiler_params=pltpu.CompilerParams(vmem_limit_bytes=10 << 20),
-        name="gate_up_far",
-    )(expert, *pieces, *weights, near_x2, acc)
+        name="gate_up_far_0",
+    )(expert, piece, *weights, *parts, near_x2, far_x2, acc)
 
 
 def down_kernel(colour, far, hidden, own, other, out):
@@ -228,7 +264,9 @@
     own_expert = lax.axis_index("gx") * lax.axis_size("gy") + lax.axis_index("gy")
 
     gate_own, up_own, down_own = gate_weight[0], up_weight[0], down_weight[0]
-    gate_far, up_far, down_far = partner(gate_own), partner(up_own), partner(down_own)
+    gate_far = partner(gate_own)
+    up_far = partner(up_own)
+    down_far = partner(down_own)
     gate_own, gate_far, up_own, up_far = in_vmem(gate_own, gate_far, up_own, up_far)
     down_own, down_far = in_vmem(down_own, down_far)
     gate_ups = (gate_own, gate_far, up_own, up_far)
@@ -237,15 +275,19 @@
     rows = jnp.concatenate([rows] + [direct(rows, hops_of(n)) for n in range(1, 8)], axis=0)
     ends = (*CUTS[:3], width + INFO)
     pieces = [rows[:, ends[i] : ends[i + 1]] for i in range(3)]
-    for step in range(2):
-        pieces = [
-            jnp.concatenate([p, exchange(p, LATE[i][step])], axis=0) for i, p in enumerate(pieces)
-        ]
-    far_pieces = [exchange(p, LATE[i][2]) for i, p in enumerate(pieces)]
+    for step in range(3):
+        far_pieces = []
+        for i, p in enumerate(pieces):
+            far_pieces.append(exchange(p, LATE[i][step]))
+        if step < 2:
+            pieces = [jnp.concatenate(pair, axis=0) for pair in zip(pieces, far_pieces)]
 
     acc = gate_up_near(pieces, gate_ups)
     expert = jnp.full((1,), own_expert, jnp.int32)
-    hidden, marks = gate_up_far(expert, far_pieces, gate_ups, pieces[2], acc)
+    parts = [gate_up_far_part(i, far_pieces[i], gate_ups) for i in (1, 2)]
+    hidden, marks = gate_up_last(
+        expert, far_pieces[0], gate_ups, parts, pieces[2], far_pieces[2], acc
+    )
 
     sent = [down_part(i, True, hidden, down_own, down_far) for i in range(3)]
     kept = []
@@ -266,9 +308,8 @@
         block = total[n * tok_rows : (n + 1) * tok_rows].astype(BF16)
         combined = combined + direct(block, hops_of(n)).astype(F32)
 
-    half_load = jnp.sum(marks, axis=0)[experts : 2 * experts].astype(jnp.int32)
-    other_load = partner(half_load)
-    expert_load = half_load + other_load
+    other_marks = partner(marks)
+    expert_load = (marks + other_marks)[0, experts : 2 * experts]
     mean_load = tok_rows * devices * route_count // experts
     new_bias = expert_bias + bias_rate * jnp.sign((mean_load - expert_load).astype(F32))
     return (combined.astype(BF16), expert_load, new_bias)

time: 144 us -> 150 us (1.042)
  the two profiles are of different devices: /device:TPU:2 before, /device:TPU:1 now
where the time goes in v1:
time: 150 us
  waiting for transfers between devices  81.1 us (54%)
  starting transfers between devices  42.1 us (28%)
  Pallas kernels  19.6 us (13%)
  other arithmetic  3.05 us (2%)
  local copies, waits for them, and re-layouts  2.83 us (2%)
    ppermute x18, waiting for transfers between devices, exchange(): return lax.ppermute(value, (axis, 'gz_1'), pairs)  69.9 us
    ppermute x14, starting transfers between devices, direct(): return lax.ppermute(value, AXES, pairs)  31.9 us
    ppermute x14, waiting for transfers between devices, direct(): return lax.ppermute(value, AXES, pairs)  11.1 us
    ppermute x4, starting transfers between devices, partner(): return lax.ppermute(value, 'gz_1', [(0, 1), (1, 0)])  8.32 us
    pallas_call x2, Pallas kernels, in_vmem(): pl.pallas_call(load_kernel, out_shape=tuple((jax.ShapeDtypeStruct(a.shape...  5.8 us
    pallas_call x6, Pallas kernels, down_part(): pl.pallas_call(functools.partial(down_kernel, colour, far), out_shape=jax...  5.08 us
    pallas_call x1, Pallas kernels, gate_up_near(): pl.pallas_call(near_kernel, out_shape=jax.ShapeDtypeStruct((4, 512, 256),...  3.96 us
  transfers between devices with their start and end apart: 36, of which 18 were waited for; matrix products, arithmetic and copies ran while one was open for 2% of the time, Pallas kernels for 11%

profile of v1, /device:TPU:1, one launch (start us, length us, event | category | flops | bytes accessed | tf_op | source)
XLA Modules:
  0.0 149.8 jit_solution(12449689026514724995)
XLA Ops:
  0.6 0.9 copy-done
  1.5 0.7 copy-done.1
  2.2 0.7 copy-done.2
  3.2 3.4 %collective-permute-start = (bf16[8,7296]{1,0:T(8,128)(2,1)S(1)}, bf16[8,7296]{1,0:T(8,128)(2,1)S(1)}, u32[]{:S(2)}, u32[]{:S(2)}) collective-permute-start(bf16[8,7296]{1,0:T(8,128)(2,1)S(1)} %token_rows.1), channel_id=1, source_target_pairs={{0,2},{1,7},{2,0},{3,5},{4,6},{5,3},{6,4},{7,1},{8,10},{9,15},{10,... | collective-permute-start | bytes 350216 | tf_op jit(solution)/shard_map/ppermute | solution.py:46
  6.5 2.7 %collective-permute-start.1 = (bf16[8,7296]{1,0:T(8,128)(2,1)S(1)}, bf16[8,7296]{1,0:T(8,128)(2,1)S(1)}, u32[]{:S(2)}, u32[]{:S(2)}) collective-permute-start(bf16[8,7296]{1,0:T(8,128)(2,1)S(1)} %token_rows.1), channel_id=1, source_target_pairs={{0,32},{1,97},{2,34},{3,99},{4,36},{5,101},{6,38},{7,103},{8,40},{... | collective-permute-start | bytes 350216 | tf_op jit(solution)/shard_map/ppermute | solution.py:46
  9.3 3.8 %collective-permute-start.3 = (bf16[8,7296]{1,0:T(8,128)(2,1)S(1)}, bf16[8,7296]{1,0:T(8,128)(2,1)S(1)}, u32[]{:S(2)}, u32[]{:S(2)}) collective-permute-start(bf16[8,7296]{1,0:T(8,128)(2,1)S(1)} %token_rows.1), channel_id=1, source_target_pairs={{0,8},{1,25},{2,10},{3,27},{4,12},{5,29},{6,14},{7,31},{8,0},{9,17... | collective-permute-start | bytes 350216 | tf_op jit(solution)/shard_map/ppermute | solution.py:46
  13.0 2.1 %collective-permute-start.4 = (bf16[8,7296]{1,0:T(8,128)(2,1)S(1)}, bf16[8,7296]{1,0:T(8,128)(2,1)S(1)}, u32[]{:S(2)}, u32[]{:S(2)}) collective-permute-start(bf16[8,7296]{1,0:T(8,128)(2,1)S(1)} %token_rows.1), channel_id=1, source_target_pairs={{0,10},{1,31},{2,8},{3,29},{4,14},{5,27},{6,12},{7,25},{8,2},{9,23... | collective-permute-start | bytes 350216 | tf_op jit(solution)/shard_map/ppermute | solution.py:46
  15.2 5.1 %collective-permute-start.5 = (bf16[8,7296]{1,0:T(8,128)(2,1)S(1)}, bf16[8,7296]{1,0:T(8,128)(2,1)S(1)}, u32[]{:S(2)}, u32[]{:S(2)}) collective-permute-start(bf16[8,7296]{1,0:T(8,128)(2,1)S(1)} %token_rows.1), channel_id=1, source_target_pairs={{0,40},{1,121},{2,42},{3,123},{4,44},{5,125},{6,46},{7,127},{8,32}... | collective-permute-start | bytes 350216 | tf_op jit(solution)/shard_map/ppermute | solution.py:46
  20.6 0.6 collective-permute-start.11
  21.2 1.3 collective-permute-done.5
  22.5 7.1 %collective-permute-done.6 = bf16[8,7296]{1,0:T(8,128)(2,1)S(1)} collective-permute-done((bf16[8,7296]{1,0:T(8,128)(2,1)S(1)}, bf16[8,7296]{1,0:T(8,128)(2,1)S(1)}, u32[]{:S(2)}, u32[]{:S(2)}) %collective-permute-start.6) | collective-permute-done | bytes 116768 | tf_op jit(solution)/shard_map/ppermute | solution.py:46
  30.0 5.6 %collective-permute-done.12 = bf16[64,2304]{1,0:T(8,128)(2,1)S(1)} collective-permute-done((bf16[64,2304]{1,0:T(8,128)(2,1)S(1)}, bf16[64,2304]{1,0:T(8,128)(2,1)S(1)}, u32[]{:S(2)}, u32[]{:S(2)}) %collective-permute-start.12) | collective-permute-done | bytes 294944 | tf_op jit(solution)/shard_map/ppermute | solution.py:28
  35.7 5.7 %collective-permute-done.15 = bf16[64,2432]{1,0:T(8,128)(2,1)S(1)} collective-permute-done((bf16[64,2432]{1,0:T(8,128)(2,1)S(1)}, bf16[64,2432]{1,0:T(8,128)(2,1)S(1)}, u32[]{:S(2)}, u32[]{:S(2)}) %collective-permute-start.15) | collective-permute-done | bytes 311328 | tf_op jit(solution)/shard_map/ppermute | solution.py:28
  41.9 8.5 %collective-permute-done.13 = bf16[128,2304]{1,0:T(8,128)(2,1)S(1)} collective-permute-done((bf16[128,2304]{1,0:T(8,128)(2,1)S(1)}, bf16[128,2304]{1,0:T(8,128)(2,1)S(1)}, u32[]{:S(2)}, u32[]{:S(2)}) %collective-permute-start.13) | collective-permute-done | bytes 589856 | tf_op jit(solution)/shard_map/ppermute | solution.py:28
  50.5 0.7 collective-permute-done.16
  51.3 8.8 %collective-permute-done.8 = bf16[128,2560]{1,0:T(8,128)(2,1)S(1)} collective-permute-done((bf16[128,2560]{1,0:T(8,128)(2,1)S(1)}, bf16[128,2560]{1,0:T(8,128)(2,1)S(1)}, u32[]{:S(2)}, u32[]{:S(2)}) %collective-permute-start.8) | collective-permute-done | bytes 655392 | tf_op jit(solution)/shard_map/ppermute | solution.py:28
  60.5 3.5 %weights_in.4 = (bf16[7168,256]{1,0:T(8,128)(2,1)S(1)}, bf16[7168,256]{1,0:T(8,128)(2,1)S(1)}, bf16[7168,256]{1,0:T(8,128)(2,1)S(1)}, bf16[7168,256]{1,0:T(8,128)(2,1)S(1)}) custom-call(bf16[7168,256]{1,0:T(8,128)(2,1)S(1)} %bitcast.8, bf16[7168,256]{1,0:T(8,128)(2,1)} %collective-permute-done.10.refs_1_, bf16[7168,256]{1,0:T(8,128)(2,1)S(1)} %bitcast.10, ...), custom_call_target="tpu_custom_call" | custom-call | flops 8589934592 | tf_op jit(solution)/shard_map/weights_in/pallas_call | solution.py:177
  64.0 2.5 %collective-permute-done.14.x = bf16[256,2304]{1,0:T(8,128)(2,1)S(1)} collective-permute-done((bf16[256,2304]{1,0:T(8,128)(2,1)S(1)}, bf16[256,2304]{1,0:T(8,128)(2,1)S(1)}, u32[]{:S(2)}, u32[]{:S(2)}) %collective-permute-start.14) | collective-permute-done | bytes 1179680 | tf_op jit(solution)/shard_map/ppermute | solution.py:28
  66.5 1.4 shard_map.94.part1
  67.9 8.3 %collective-permute-done.17.x.far_x2 = bf16[256,2432]{1,0:T(8,128)(2,1)S(1)} collective-permute-done((bf16[256,2432]{1,0:T(8,128)(2,1)S(1)}, bf16[256,2432]{1,0:T(8,128)(2,1)S(1)}, u32[]{:S(2)}, u32[]{:S(2)}) %collective-permute-start.17) | collective-permute-done | bytes 1245216 | tf_op jit(solution)/shard_map/ppermute | solution.py:28
  76.2 1.4 shard_map.95.part2
  77.6 4.0 %gate_up_near.1.acc_in = f32[4,512,256]{2,1,0:T(8,128)S(1)} custom-call(bf16[256,2560]{1,0:T(8,128)(2,1)S(1)} %pad_maximum_fusion.1.x0, bf16[256,2304]{1,0:T(8,128)(2,1)S(1)} %pad_maximum_fusion.3.x1, bf16[256,2432]{1,0:T(8,128)(2,1)S(1)} %pad_maximum_fusion.2.x2.near_x2, bf16[7168,256]{1,0:T(8,128)(2,1)S(1)} %get-tuple-element.11.w0, ...), custom_call_target="tpu_custom_call" | custom-call | flops 3757572096 | tf_op jit(solution)/shard_map/gate_up_near/pallas_call | solution.py:196
  81.6 2.3 %weights_in.5 = (bf16[256,7168]{1,0:T(8,128)(2,1)S(1)}, bf16[256,7168]{1,0:T(8,128)(2,1)S(1)}) custom-call(bf16[256,7168]{1,0:T(8,128)(2,1)S(1)} %bitcast.12, bf16[256,7168]{1,0:T(8,128)(2,1)} %collective-permute-done.18.refs_1_), custom_call_target="tpu_custom_call" | custom-call | flops 8589934592 | tf_op jit(solution)/shard_map/weights_in/pallas_call | solution.py:177
  83.9 1.7 %gate_up_far_0.1 = (bf16[512,512]{1,0:T(8,128)(2,1)S(1)}, s32[1,128]{1,0:T(1,128)S(1)}) custom-call(s32[1]{0:T(128)} %bitcast.expert, bf16[256,2560]{1,0:T(8,128)(2,1)S(1)} %collective-permute-done.9.x0, bf16[7168,256]{1,0:T(8,128)(2,1)S(1)} %get-tuple-element.11.w0, bf16[7168,256]{1,0:T(8,128)(2,1)S(1)} %get-tuple-element.12.w1, ...), custom_call_target="tpu_custom_call" | custom-call | flops 1252524032 | tf_op jit(solution)/shard_map/gate_up_far_0/pallas_call | solution.py:219
  85.6 0.8 shard_map.101
  86.5 0.9 shard_map.99
  87.5 7.6 %collective-permute-start.35 = (s32[1,128]{1,0:T(1,128)S(1)}, s32[1,128]{1,0:T(1,128)S(1)}, u32[]{:S(2)}, u32[]{:S(2)}) collective-permute-start(s32[1,128]{1,0:T(1,128)S(1)} %get-tuple-element.18), channel_id=1, source_target_pairs={{0,1},{1,0},{2,3},{3,2},{4,5},{5,4},{6,7},{7,6},{8,9},{9,8},{10,11... | collective-permute-start | bytes 1544 | tf_op jit(solution)/shard_map/ppermute | solution.py:54
  95.0 0.9 shard_map.98
  95.9 0.9 shard_map.96
  96.8 0.9 shard_map.97
  97.7 0.8 shard_map.100
  98.6 3.2 %collective-permute-done.25 = bf16[256,2304]{1,0:T(8,128)(2,1)S(1)} collective-permute-done((bf16[256,2304]{1,0:T(8,128)(2,1)S(1)}, bf16[256,2304]{1,0:T(8,128)(2,1)S(1)}, u32[]{:S(2)}, u32[]{:S(2)}) %collective-permute-start.25) | collective-permute-done | bytes 1179680 | tf_op jit(solution)/shard_map/ppermute | solution.py:28
  102.4 1.1 collective-permute-done.22
  103.9 10.7 %collective-permute-done.19 = bf16[256,2432]{1,0:T(8,128)(2,1)S(1)} collective-permute-done((bf16[256,2432]{1,0:T(8,128)(2,1)S(1)}, bf16[256,2432]{1,0:T(8,128)(2,1)S(1)}, u32[]{:S(2)}, u32[]{:S(2)}) %collective-permute-start.19) | collective-permute-done | bytes 1245216 | tf_op jit(solution)/shard_map/ppermute | solution.py:28
  115.2 6.0 %collective-permute-done.23 = bf16[128,2432]{1,0:T(8,128)(2,1)S(1)} collective-permute-done((bf16[128,2432]{1,0:T(8,128)(2,1)S(1)}, bf16[128,2432]{1,0:T(8,128)(2,1)S(1)}, u32[]{:S(2)}, u32[]{:S(2)}) %collective-permute-start.23) | collective-permute-done | bytes 622624 | tf_op jit(solution)/shard_map/ppermute | solution.py:28
  121.5 2.8 %collective-permute-done.20 = bf16[128,2432]{1,0:T(8,128)(2,1)S(1)} collective-permute-done((bf16[128,2432]{1,0:T(8,128)(2,1)S(1)}, bf16[128,2432]{1,0:T(8,128)(2,1)S(1)}, u32[]{:S(2)}, u32[]{:S(2)}) %collective-permute-start.20) | collective-permute-done | bytes 622624 | tf_op jit(solution)/shard_map/ppermute | solution.py:28
  124.7 3.0 %collective-permute-done.24 = bf16[64,2432]{1,0:T(8,128)(2,1)S(1)} collective-permute-done((bf16[64,2432]{1,0:T(8,128)(2,1)S(1)}, bf16[64,2432]{1,0:T(8,128)(2,1)S(1)}, u32[]{:S(2)}, u32[]{:S(2)}) %collective-permute-start.24) | collective-permute-done | bytes 311328 | tf_op jit(solution)/shard_map/ppermute | solution.py:28
  127.7 2.9 %collective-permute-done.21 = bf16[64,2432]{1,0:T(8,128)(2,1)S(1)} collective-permute-done((bf16[64,2432]{1,0:T(8,128)(2,1)S(1)}, bf16[64,2432]{1,0:T(8,128)(2,1)S(1)}, u32[]{:S(2)}, u32[]{:S(2)}) %collective-permute-start.21) | collective-permute-done | bytes 311328 | tf_op jit(solution)/shard_map/ppermute | solution.py:28
  130.9 3.7 %collective-permute-start.34 = (bf16[8,7168]{1,0:T(8,128)(2,1)S(1)}, bf16[8,7168]{1,0:T(8,128)(2,1)S(1)}, u32[]{:S(2)}, u32[]{:S(2)}) collective-permute-start(bf16[8,7168]{1,0:T(8,128)(2,1)S(1)} %get-tuple-element.22), channel_id=1, source_target_pairs={{0,42},{1,127},{2,40},{3,125},{4,46},{5,123},{6,44},{7,121},{8,34}... | collective-permute-start | bytes 344072 | tf_op jit(solution)/shard_map/ppermute | solution.py:46
  134.6 1.2 collective-permute-start.33
  135.8 0.6 multiply_add_fusion
  136.3 4.8 %collective-permute-start.32 = (bf16[8,7168]{1,0:T(8,128)(2,1)S(1)}, bf16[8,7168]{1,0:T(8,128)(2,1)S(1)}, u32[]{:S(2)}, u32[]{:S(2)}) collective-permute-start(bf16[8,7168]{1,0:T(8,128)(2,1)S(1)} %get-tuple-element.24), channel_id=1, source_target_pairs={{0,10},{1,31},{2,8},{3,29},{4,14},{5,27},{6,12},{7,25},{8,2},{9,23... | collective-permute-start | bytes 344072 | tf_op jit(solution)/shard_map/ppermute | solution.py:46
  141.1 1.8 %collective-permute-start.30 = (bf16[8,7168]{1,0:T(8,128)(2,1)S(1)}, bf16[8,7168]{1,0:T(8,128)(2,1)S(1)}, u32[]{:S(2)}, u32[]{:S(2)}) collective-permute-start(bf16[8,7168]{1,0:T(8,128)(2,1)S(1)} %get-tuple-element.26), channel_id=1, source_target_pairs={{0,34},{1,103},{2,32},{3,101},{4,38},{5,99},{6,36},{7,97},{8,42},{... | collective-permute-start | bytes 344072 | tf_op jit(solution)/shard_map/ppermute | solution.py:46
  143.0 0.8 collective-permute-start.29
  143.8 2.4 %collective-permute-start.28 = (bf16[8,7168]{1,0:T(8,128)(2,1)S(1)}, bf16[8,7168]{1,0:T(8,128)(2,1)S(1)}, u32[]{:S(2)}, u32[]{:S(2)}) collective-permute-start(bf16[8,7168]{1,0:T(8,128)(2,1)S(1)} %get-tuple-element.21), channel_id=1, source_target_pairs={{0,2},{1,7},{2,0},{3,5},{4,6},{5,3},{6,4},{7,1},{8,10},{9,15},{10,... | collective-permute-start | bytes 344072 | tf_op jit(solution)/shard_map/ppermute | solution.py:46
  146.4 1.8 %collective-permute-done.30 = bf16[8,7168]{1,0:T(8,128)(2,1)S(1)} collective-permute-done((bf16[8,7168]{1,0:T(8,128)(2,1)S(1)}, bf16[8,7168]{1,0:T(8,128)(2,1)S(1)}, u32[]{:S(2)}, u32[]{:S(2)}) %collective-permute-start.30) | collective-permute-done | bytes 114720 | tf_op jit(solution)/shard_map/ppermute | solution.py:46
  148.2 0.9 collective-permute-done.29
  149.1 0.8 fusion.6
  (89 shorter events, 4.7 us)
Async XLA Ops:
  0.6 0.9 copy-start
  1.5 0.7 copy-start.1
  2.2 0.7 copy-start.2
  3.2 12.0 %collective-permute-start = (bf16[8,7296]{1,0:T(8,128)(2,1)S(1)}, bf16[8,7296]{1,0:T(8,128)(2,1)S(1)}, u32[]{:S(2)}, u32[]{:S(2)}) collective-permute-start(bf16[8,7296]{1,0:T(8,128)(2,1)S(1)} %token_rows.1), channel_id=1, source_target_pairs={{0,2},{1,7},{2,0},{3,5},{4,6},{5,3},{6,4},{7,1},{8,10},{9,15},{10,... | collective-permute-start | bytes 350216 | tf_op jit(solution)/shard_map/ppermute | solution.py:46
  6.5 13.8 %collective-permute-start.1 = (bf16[8,7296]{1,0:T(8,128)(2,1)S(1)}, bf16[8,7296]{1,0:T(8,128)(2,1)S(1)}, u32[]{:S(2)}, u32[]{:S(2)}) collective-permute-start(bf16[8,7296]{1,0:T(8,128)(2,1)S(1)} %token_rows.1), channel_id=1, source_target_pairs={{0,32},{1,97},{2,34},{3,99},{4,36},{5,101},{6,38},{7,103},{8,40},{... | collective-permute-start | bytes 350216 | tf_op jit(solution)/shard_map/ppermute | solution.py:46
  9.3 11.2 %collective-permute-start.2 = (bf16[8,7296]{1,0:T(8,128)(2,1)S(1)}, bf16[8,7296]{1,0:T(8,128)(2,1)S(1)}, u32[]{:S(2)}, u32[]{:S(2)}) collective-permute-start(bf16[8,7296]{1,0:T(8,128)(2,1)S(1)} %token_rows.1), channel_id=1, source_target_pairs={{0,34},{1,103},{2,32},{3,101},{4,38},{5,99},{6,36},{7,97},{8,42},{... | collective-permute-start | bytes 350216 | tf_op jit(solution)/shard_map/ppermute | solution.py:46
  9.3 11.3 %collective-permute-start.3 = (bf16[8,7296]{1,0:T(8,128)(2,1)S(1)}, bf16[8,7296]{1,0:T(8,128)(2,1)S(1)}, u32[]{:S(2)}, u32[]{:S(2)}) collective-permute-start(bf16[8,7296]{1,0:T(8,128)(2,1)S(1)} %token_rows.1), channel_id=1, source_target_pairs={{0,8},{1,25},{2,10},{3,27},{4,12},{5,29},{6,14},{7,31},{8,0},{9,17... | collective-permute-start | bytes 350216 | tf_op jit(solution)/shard_map/ppermute | solution.py:46
  13.0 8.1 %collective-permute-start.4 = (bf16[8,7296]{1,0:T(8,128)(2,1)S(1)}, bf16[8,7296]{1,0:T(8,128)(2,1)S(1)}, u32[]{:S(2)}, u32[]{:S(2)}) collective-permute-start(bf16[8,7296]{1,0:T(8,128)(2,1)S(1)} %token_rows.1), channel_id=1, source_target_pairs={{0,10},{1,31},{2,8},{3,29},{4,14},{5,27},{6,12},{7,25},{8,2},{9,23... | collective-permute-start | bytes 350216 | tf_op jit(solution)/shard_map/ppermute | solution.py:46
  15.2 7.3 %collective-permute-start.5 = (bf16[8,7296]{1,0:T(8,128)(2,1)S(1)}, bf16[8,7296]{1,0:T(8,128)(2,1)S(1)}, u32[]{:S(2)}, u32[]{:S(2)}) collective-permute-start(bf16[8,7296]{1,0:T(8,128)(2,1)S(1)} %token_rows.1), channel_id=1, source_target_pairs={{0,40},{1,121},{2,42},{3,123},{4,44},{5,125},{6,46},{7,127},{8,32}... | collective-permute-start | bytes 350216 | tf_op jit(solution)/shard_map/ppermute | solution.py:46
  20.3 9.3 %collective-permute-start.6 = (bf16[8,7296]{1,0:T(8,128)(2,1)S(1)}, bf16[8,7296]{1,0:T(8,128)(2,1)S(1)}, u32[]{:S(2)}, u32[]{:S(2)}) collective-permute-start(bf16[8,7296]{1,0:T(8,128)(2,1)S(1)} %token_rows.1), channel_id=1, source_target_pairs={{0,42},{1,127},{2,40},{3,125},{4,46},{5,123},{6,44},{7,121},{8,34}... | collective-permute-start | bytes 350216 | tf_op jit(solution)/shard_map/ppermute | solution.py:46
  20.5 39.7 %collective-permute-start.10 = (bf16[7168,256]{1,0:T(8,128)(2,1)}, bf16[7168,256]{1,0:T(8,128)(2,1)}, u32[]{:S(2)}, u32[]{:S(2)}) collective-permute-start(bf16[7168,256]{1,0:T(8,128)(2,1)} %bitcast.7), channel_id=1, source_target_pairs={{0,1},{1,0},{2,3},{3,2},{4,5},{5,4},{6,7},{7,6},{8,9},{9,8},{10,11... | collective-permute-start | bytes 11010056 | tf_op jit(solution)/shard_map/ppermute | solution.py:54
  20.6 39.9 %collective-permute-start.11 = (bf16[7168,256]{1,0:T(8,128)(2,1)}, bf16[7168,256]{1,0:T(8,128)(2,1)}, u32[]{:S(2)}, u32[]{:S(2)}) collective-permute-start(bf16[7168,256]{1,0:T(8,128)(2,1)} %bitcast.9), channel_id=1, source_target_pairs={{0,1},{1,0},{2,3},{3,2},{4,5},{5,4},{6,7},{7,6},{8,9},{9,8},{10,11... | collective-permute-start | bytes 11010056 | tf_op jit(solution)/shard_map/ppermute | solution.py:54
  29.7 5.9 %collective-permute-start.12 = (bf16[64,2304]{1,0:T(8,128)(2,1)S(1)}, bf16[64,2304]{1,0:T(8,128)(2,1)S(1)}, u32[]{:S(2)}, u32[]{:S(2)}) collective-permute-start(bf16[64,2304]{1,0:T(8,128)(2,1)S(1)} %slice.110), channel_id=1, source_target_pairs={{0,96},{1,33},{32,64},{33,1},{64,32},{65,97},{96,0},{97,65},{2,98}... | collective-permute-start | bytes 884744 | tf_op jit(solution)/shard_map/ppermute | solution.py:28
  29.8 51.8 %collective-permute-start.18 = (bf16[256,7168]{1,0:T(8,128)(2,1)}, bf16[256,7168]{1,0:T(8,128)(2,1)}, u32[]{:S(2)}, u32[]{:S(2)}) collective-permute-start(bf16[256,7168]{1,0:T(8,128)(2,1)} %bitcast.11), channel_id=1, source_target_pairs={{0,1},{1,0},{2,3},{3,2},{4,5},{5,4},{6,7},{7,6},{8,9},{9,8},{10,11... | collective-permute-start | bytes 11010056 | tf_op jit(solution)/shard_map/ppermute | solution.py:54
  29.9 11.8 %collective-permute-start.7 = (bf16[64,2560]{1,0:T(8,128)(2,1)S(1)}, bf16[64,2560]{1,0:T(8,128)(2,1)S(1)}, u32[]{:S(2)}, u32[]{:S(2)}) collective-permute-start(bf16[64,2560]{1,0:T(8,128)(2,1)S(1)} %slice.109), channel_id=1, source_target_pairs={{0,6},{1,3},{2,4},{3,1},{4,2},{5,7},{6,0},{7,5},{8,14},{9,11},{10,... | collective-permute-start | bytes 983048 | tf_op jit(solution)/shard_map/ppermute | solution.py:28
  35.6 5.7 %collective-permute-start.15 = (bf16[64,2432]{1,0:T(8,128)(2,1)S(1)}, bf16[64,2432]{1,0:T(8,128)(2,1)S(1)}, u32[]{:S(2)}, u32[]{:S(2)}) collective-permute-start(bf16[64,2432]{1,0:T(8,128)(2,1)S(1)} %slice.111), channel_id=1, source_target_pairs={{0,24},{1,9},{8,16},{9,1},{16,8},{17,25},{24,0},{25,17},{2,26},{3,... | collective-permute-start | bytes 933896 | tf_op jit(solution)/shard_map/ppermute | solution.py:28
  41.4 9.0 %collective-permute-start.13 = (bf16[128,2304]{1,0:T(8,128)(2,1)S(1)}, bf16[128,2304]{1,0:T(8,128)(2,1)S(1)}, u32[]{:S(2)}, u32[]{:S(2)}) collective-permute-start(bf16[128,2304]{1,0:T(8,128)(2,1)S(1)} %pad_maximum_fusion.6), channel_id=1, source_target_pairs={{0,24},{1,9},{8,16},{9,1},{16,8},{17,25},{24,0},{25,17},{2,26},{3,... | collective-permute-start | bytes 1769480 | tf_op jit(solution)/shard_map/ppermute | solution.py:28
  41.7 9.5 %collective-permute-start.16 = (bf16[128,2432]{1,0:T(8,128)(2,1)S(1)}, bf16[128,2432]{1,0:T(8,128)(2,1)S(1)}, u32[]{:S(2)}, u32[]{:S(2)}) collective-permute-start(bf16[128,2432]{1,0:T(8,128)(2,1)S(1)} %pad_maximum_fusion.5), channel_id=1, source_target_pairs={{0,6},{1,3},{2,4},{3,1},{4,2},{5,7},{6,0},{7,5},{8,14},{9,11},{10,... | collective-permute-start | bytes 1867784 | tf_op jit(solution)/shard_map/ppermute | solution.py:28
  50.4 9.7 %collective-permute-start.8 = (bf16[128,2560]{1,0:T(8,128)(2,1)S(1)}, bf16[128,2560]{1,0:T(8,128)(2,1)S(1)}, u32[]{:S(2)}, u32[]{:S(2)}) collective-permute-start(bf16[128,2560]{1,0:T(8,128)(2,1)S(1)} %pad_maximum_fusion.4), channel_id=1, source_target_pairs={{0,96},{1,33},{32,64},{33,1},{64,32},{65,97},{96,0},{97,65},{2,98}... | collective-permute-start | bytes 1966088 | tf_op jit(solution)/shard_map/ppermute | solution.py:28
  50.4 10.1 %copy-start.4 = (bf16[1,7168,256]{2,1,0:T(8,128)(2,1)S(1)}, bf16[1,7168,256]{2,1,0:T(8,128)(2,1)}, u32[]{:S(2)}) copy-start(bf16[1,7168,256]{2,1,0:T(8,128)(2,1)} %param.12) | copy-start | bytes 11010052
  51.2 15.3 %collective-permute-start.14 = (bf16[256,2304]{1,0:T(8,128)(2,1)S(1)}, bf16[256,2304]{1,0:T(8,128)(2,1)S(1)}, u32[]{:S(2)}, u32[]{:S(2)}) collective-permute-start(bf16[256,2304]{1,0:T(8,128)(2,1)S(1)} %pad_maximum_fusion.3.x1), channel_id=1, source_target_pairs={{0,6},{1,3},{2,4},{3,1},{4,2},{5,7},{6,0},{7,5},{8,14},{9,11},{10,... | collective-permute-start | bytes 3538952 | tf_op jit(solution)/shard_map/ppermute | solution.py:28
  51.2 9.3 %copy-start.3 = (bf16[1,7168,256]{2,1,0:T(8,128)(2,1)S(1)}, bf16[1,7168,256]{2,1,0:T(8,128)(2,1)}, u32[]{:S(2)}) copy-start(bf16[1,7168,256]{2,1,0:T(8,128)(2,1)} %param.11) | copy-start | bytes 11010052
  60.1 16.1 %collective-permute-start.17 = (bf16[256,2432]{1,0:T(8,128)(2,1)S(1)}, bf16[256,2432]{1,0:T(8,128)(2,1)S(1)}, u32[]{:S(2)}, u32[]{:S(2)}) collective-permute-start(bf16[256,2432]{1,0:T(8,128)(2,1)S(1)} %pad_maximum_fusion.2.x2.near_x2), channel_id=1, source_target_pairs={{0,96},{1,33},{32,64},{33,1},{64,32},{65,97},{96,0},{97,65},{2,98}... | collective-permute-start | bytes 3735560 | tf_op jit(solution)/shard_map/ppermute | solution.py:28
  60.2 23.7 %collective-permute-start.9 = (bf16[256,2560]{1,0:T(8,128)(2,1)S(1)}, bf16[256,2560]{1,0:T(8,128)(2,1)S(1)}, u32[]{:S(2)}, u32[]{:S(2)}) collective-permute-start(bf16[256,2560]{1,0:T(8,128)(2,1)S(1)} %pad_maximum_fusion.1.x0), channel_id=1, source_target_pairs={{0,24},{1,9},{8,16},{9,1},{16,8},{17,25},{24,0},{25,17},{2,26},{3,... | collective-permute-start | bytes 3932168 | tf_op jit(solution)/shard_map/ppermute | solution.py:28
  77.6 4.0 %copy-start.5 = (bf16[1,256,7168]{2,1,0:T(8,128)(2,1)S(1)}, bf16[1,256,7168]{2,1,0:T(8,128)(2,1)}, u32[]{:S(2)}) copy-start(bf16[1,256,7168]{2,1,0:T(8,128)(2,1)} %param.13) | copy-start | bytes 11010052
  86.4 15.4 %collective-permute-start.25 = (bf16[256,2304]{1,0:T(8,128)(2,1)S(1)}, bf16[256,2304]{1,0:T(8,128)(2,1)S(1)}, u32[]{:S(2)}, u32[]{:S(2)}) collective-permute-start(bf16[256,2304]{1,0:T(8,128)(2,1)S(1)} %shard_map.101), channel_id=1, source_target_pairs={{0,96},{1,33},{32,64},{33,1},{64,32},{65,97},{96,0},{97,65},{2,98}... | collective-permute-start | bytes 3538952 | tf_op jit(solution)/shard_map/ppermute | solution.py:28
  87.4 16.1 %collective-permute-start.22 = (bf16[256,2432]{1,0:T(8,128)(2,1)S(1)}, bf16[256,2432]{1,0:T(8,128)(2,1)S(1)}, u32[]{:S(2)}, u32[]{:S(2)}) collective-permute-start(bf16[256,2432]{1,0:T(8,128)(2,1)S(1)} %shard_map.99), channel_id=1, source_target_pairs={{0,6},{1,3},{2,4},{3,1},{4,2},{5,7},{6,0},{7,5},{8,14},{9,11},{10,... | collective-permute-start | bytes 3735560 | tf_op jit(solution)/shard_map/ppermute | solution.py:28
  87.5 11.1 %collective-permute-start.35 = (s32[1,128]{1,0:T(1,128)S(1)}, s32[1,128]{1,0:T(1,128)S(1)}, u32[]{:S(2)}, u32[]{:S(2)}) collective-permute-start(s32[1,128]{1,0:T(1,128)S(1)} %get-tuple-element.18), channel_id=1, source_target_pairs={{0,1},{1,0},{2,3},{3,2},{4,5},{5,4},{6,7},{7,6},{8,9},{9,8},{10,11... | collective-permute-start | bytes 1544 | tf_op jit(solution)/shard_map/ppermute | solution.py:54
  98.5 16.1 %collective-permute-start.19 = (bf16[256,2432]{1,0:T(8,128)(2,1)S(1)}, bf16[256,2432]{1,0:T(8,128)(2,1)S(1)}, u32[]{:S(2)}, u32[]{:S(2)}) collective-permute-start(bf16[256,2432]{1,0:T(8,128)(2,1)S(1)} %shard_map.97), channel_id=1, source_target_pairs={{0,24},{1,9},{8,16},{9,1},{16,8},{17,25},{24,0},{25,17},{2,26},{3,... | collective-permute-start | bytes 3735560 | tf_op jit(solution)/shard_map/ppermute | solution.py:28
  102.1 12.9 %collective-permute-start.26 = (bf16[128,2304]{1,0:T(8,128)(2,1)S(1)}, bf16[128,2304]{1,0:T(8,128)(2,1)S(1)}, u32[]{:S(2)}, u32[]{:S(2)}) collective-permute-start(bf16[128,2304]{1,0:T(8,128)(2,1)S(1)} %slice.162), channel_id=1, source_target_pairs={{0,6},{1,3},{2,4},{3,1},{4,2},{5,7},{6,0},{7,5},{8,14},{9,11},{10,... | collective-permute-start | bytes 1769480 | tf_op jit(solution)/shard_map/ppermute | solution.py:28
  103.8 17.5 %collective-permute-start.23 = (bf16[128,2432]{1,0:T(8,128)(2,1)S(1)}, bf16[128,2432]{1,0:T(8,128)(2,1)S(1)}, u32[]{:S(2)}, u32[]{:S(2)}) collective-permute-start(bf16[128,2432]{1,0:T(8,128)(2,1)S(1)} %slice.160), channel_id=1, source_target_pairs={{0,24},{1,9},{8,16},{9,1},{16,8},{17,25},{24,0},{25,17},{2,26},{3,... | collective-permute-start | bytes 1867784 | tf_op jit(solution)/shard_map/ppermute | solution.py:28
  114.9 9.5 %collective-permute-start.20 = (bf16[128,2432]{1,0:T(8,128)(2,1)S(1)}, bf16[128,2432]{1,0:T(8,128)(2,1)S(1)}, u32[]{:S(2)}, u32[]{:S(2)}) collective-permute-start(bf16[128,2432]{1,0:T(8,128)(2,1)S(1)} %slice.161), channel_id=1, source_target_pairs={{0,96},{1,33},{32,64},{33,1},{64,32},{65,97},{96,0},{97,65},{2,98}... | collective-permute-start | bytes 1867784 | tf_op jit(solution)/shard_map/ppermute | solution.py:28
  115.1 9.5 %collective-permute-start.27 = (bf16[64,2304]{1,0:T(8,128)(2,1)S(1)}, bf16[64,2304]{1,0:T(8,128)(2,1)S(1)}, u32[]{:S(2)}, u32[]{:S(2)}) collective-permute-start(bf16[64,2304]{1,0:T(8,128)(2,1)S(1)} %slice.165), channel_id=1, source_target_pairs={{0,24},{1,9},{8,16},{9,1},{16,8},{17,25},{24,0},{25,17},{2,26},{3,... | collective-permute-start | bytes 884744 | tf_op jit(solution)/shard_map/ppermute | solution.py:28
  121.4 6.3 %collective-permute-start.24 = (bf16[64,2432]{1,0:T(8,128)(2,1)S(1)}, bf16[64,2432]{1,0:T(8,128)(2,1)S(1)}, u32[]{:S(2)}, u32[]{:S(2)}) collective-permute-start(bf16[64,2432]{1,0:T(8,128)(2,1)S(1)} %slice.163), channel_id=1, source_target_pairs={{0,96},{1,33},{32,64},{33,1},{64,32},{65,97},{96,0},{97,65},{2,98}... | collective-permute-start | bytes 933896 | tf_op jit(solution)/shard_map/ppermute | solution.py:28
  124.5 6.1 %collective-permute-start.21 = (bf16[64,2432]{1,0:T(8,128)(2,1)S(1)}, bf16[64,2432]{1,0:T(8,128)(2,1)S(1)}, u32[]{:S(2)}, u32[]{:S(2)}) collective-permute-start(bf16[64,2432]{1,0:T(8,128)(2,1)S(1)} %slice.164), channel_id=1, source_target_pairs={{0,6},{1,3},{2,4},{3,1},{4,2},{5,7},{6,0},{7,5},{8,14},{9,11},{10,... | collective-permute-start | bytes 933896 | tf_op jit(solution)/shard_map/ppermute | solution.py:28
  130.7 5.1 %copy-start.6 = (f32[16]{0:T(128)S(1)}, f32[16]{0:T(128)}, u32[]{:S(2)}) copy-start(f32[16]{0:T(128)} %param.14) | copy-start | bytes 196
  130.9 12.1 %collective-permute-start.34 = (bf16[8,7168]{1,0:T(8,128)(2,1)S(1)}, bf16[8,7168]{1,0:T(8,128)(2,1)S(1)}, u32[]{:S(2)}, u32[]{:S(2)}) collective-permute-start(bf16[8,7168]{1,0:T(8,128)(2,1)S(1)} %get-tuple-element.22), channel_id=1, source_target_pairs={{0,42},{1,127},{2,40},{3,125},{4,46},{5,123},{6,44},{7,121},{8,34}... | collective-permute-start | bytes 344072 | tf_op jit(solution)/shard_map/ppermute | solution.py:46
  134.6 9.2 %collective-permute-start.33 = (bf16[8,7168]{1,0:T(8,128)(2,1)S(1)}, bf16[8,7168]{1,0:T(8,128)(2,1)S(1)}, u32[]{:S(2)}, u32[]{:S(2)}) collective-permute-start(bf16[8,7168]{1,0:T(8,128)(2,1)S(1)} %get-tuple-element.23), channel_id=1, source_target_pairs={{0,40},{1,121},{2,42},{3,123},{4,44},{5,125},{6,46},{7,127},{8,32}... | collective-permute-start | bytes 344072 | tf_op jit(solution)/shard_map/ppermute | solution.py:46
  136.3 10.0 %collective-permute-start.32 = (bf16[8,7168]{1,0:T(8,128)(2,1)S(1)}, bf16[8,7168]{1,0:T(8,128)(2,1)S(1)}, u32[]{:S(2)}, u32[]{:S(2)}) collective-permute-start(bf16[8,7168]{1,0:T(8,128)(2,1)S(1)} %get-tuple-element.24), channel_id=1, source_target_pairs={{0,10},{1,31},{2,8},{3,29},{4,14},{5,27},{6,12},{7,25},{8,2},{9,23... | collective-permute-start | bytes 344072 | tf_op jit(solution)/shard_map/ppermute | solution.py:46
  141.1 5.2 %collective-permute-start.31 = (bf16[8,7168]{1,0:T(8,128)(2,1)S(1)}, bf16[8,7168]{1,0:T(8,128)(2,1)S(1)}, u32[]{:S(2)}, u32[]{:S(2)}) collective-permute-start(bf16[8,7168]{1,0:T(8,128)(2,1)S(1)} %get-tuple-element.25), channel_id=1, source_target_pairs={{0,8},{1,25},{2,10},{3,27},{4,12},{5,29},{6,14},{7,31},{8,0},{9,17... | collective-permute-start | bytes 344072 | tf_op jit(solution)/shard_map/ppermute | solution.py:46
  141.1 7.1 %collective-permute-start.30 = (bf16[8,7168]{1,0:T(8,128)(2,1)S(1)}, bf16[8,7168]{1,0:T(8,128)(2,1)S(1)}, u32[]{:S(2)}, u32[]{:S(2)}) collective-permute-start(bf16[8,7168]{1,0:T(8,128)(2,1)S(1)} %get-tuple-element.26), channel_id=1, source_target_pairs={{0,34},{1,103},{2,32},{3,101},{4,38},{5,99},{6,36},{7,97},{8,42},{... | collective-permute-start | bytes 344072 | tf_op jit(solution)/shard_map/ppermute | solution.py:46
  143.0 6.1 %collective-permute-start.29 = (bf16[8,7168]{1,0:T(8,128)(2,1)S(1)}, bf16[8,7168]{1,0:T(8,128)(2,1)S(1)}, u32[]{:S(2)}, u32[]{:S(2)}) collective-permute-start(bf16[8,7168]{1,0:T(8,128)(2,1)S(1)} %get-tuple-element.27), channel_id=1, source_target_pairs={{0,32},{1,97},{2,34},{3,99},{4,36},{5,101},{6,38},{7,103},{8,40},{... | collective-permute-start | bytes 344072 | tf_op jit(solution)/shard_map/ppermute | solution.py:46
  143.8 5.2 %collective-permute-start.28 = (bf16[8,7168]{1,0:T(8,128)(2,1)S(1)}, bf16[8,7168]{1,0:T(8,128)(2,1)S(1)}, u32[]{:S(2)}, u32[]{:S(2)}) collective-permute-start(bf16[8,7168]{1,0:T(8,128)(2,1)S(1)} %get-tuple-element.21), channel_id=1, source_target_pairs={{0,2},{1,7},{2,0},{3,5},{4,6},{5,3},{6,4},{7,1},{8,10},{9,15},{10,... | collective-permute-start | bytes 344072 | tf_op jit(solution)/shard_map/ppermute | solution.py:46

commit v2 on v1

--- a/solution.py
+++ b/solution.py
@@ -272,7 +272,10 @@
     gate_ups = (gate_own, gate_far, up_own, up_far)
 
     rows = rows_of(tokens, expert_ids, route_weight, experts)
-    rows = jnp.concatenate([rows] + [direct(rows, hops_of(n)) for n in range(1, 8)], axis=0)
+    blocks = [rows]
+    for n in range(1, 8):
+        blocks.append(direct(rows, hops_of(n)))
+    rows = jnp.concatenate(blocks, axis=0)
     ends = (*CUTS[:3], width + INFO)
     pieces = [rows[:, ends[i] : ends[i + 1]] for i in range(3)]
     for step in range(3):
@@ -306,7 +309,8 @@
     combined = total[:tok_rows]
     for n in range(1, 8):
         block = total[n * tok_rows : (n + 1) * tok_rows].astype(BF16)
-        combined = combined + direct(block, hops_of(n)).astype(F32)
+        block = direct(block, hops_of(n))
+        combined = combined + block.astype(F32)
 
     other_marks = partner(marks)
     expert_load = (marks + other_marks)[0, experts : 2 * experts]

time: 150 us -> 150 us (level)
  no operation moved by 1% of the time
where the time goes in v2:
time: 150 us
  waiting for transfers between devices  81.1 us (54%)
  starting transfers between devices  42.1 us (28%)
  Pallas kernels  19.6 us (13%)
  other arithmetic  3.05 us (2%)
  local copies, waits for them, and re-layouts  2.83 us (2%)
    ppermute x18, waiting for transfers between devices, exchange(): return lax.ppermute(value, (axis, 'gz_1'), pairs)  69.9 us
    ppermute x14, starting transfers between devices, direct(): return lax.ppermute(value, AXES, pairs)  31.9 us
    ppermute x14, waiting for transfers between devices, direct(): return lax.ppermute(value, AXES, pairs)  11.1 us
    ppermute x4, starting transfers between devices, partner(): return lax.ppermute(value, 'gz_1', [(0, 1), (1, 0)])  8.32 us
    pallas_call x2, Pallas kernels, in_vmem(): pl.pallas_call(load_kernel, out_shape=tuple((jax.ShapeDtypeStruct(a.shape...  5.8 us
    pallas_call x6, Pallas kernels, down_part(): pl.pallas_call(functools.partial(down_kernel, colour, far), out_shape=jax...  5.08 us
    pallas_call x1, Pallas kernels, gate_up_near(): pl.pallas_call(near_kernel, out_shape=jax.ShapeDtypeStruct((4, 512, 256),...  3.96 us
  transfers between devices with their start and end apart: 36, of which 18 were waited for; matrix products, arithmetic and copies ran while one was open for 2% of the time, Pallas kernels for 11%

profile of v2, /device:TPU:1, one launch (start us, length us, event | category | flops | bytes accessed | tf_op | source)
XLA Modules:
  0.0 149.8 jit_solution(12449689026514724995)
XLA Ops:
  0.6 0.9 copy-done
  1.5 0.7 copy-done.1
  2.2 0.7 copy-done.2
  3.2 3.4 %collective-permute-start = (bf16[8,7296]{1,0:T(8,128)(2,1)S(1)}, bf16[8,7296]{1,0:T(8,128)(2,1)S(1)}, u32[]{:S(2)}, u32[]{:S(2)}) collective-permute-start(bf16[8,7296]{1,0:T(8,128)(2,1)S(1)} %token_rows.1), channel_id=1, source_target_pairs={{0,2},{1,7},{2,0},{3,5},{4,6},{5,3},{6,4},{7,1},{8,10},{9,15},{10,... | collective-permute-start | bytes 350216 | tf_op jit(solution)/shard_map/ppermute | solution.py:46
  6.5 2.7 %collective-permute-start.1 = (bf16[8,7296]{1,0:T(8,128)(2,1)S(1)}, bf16[8,7296]{1,0:T(8,128)(2,1)S(1)}, u32[]{:S(2)}, u32[]{:S(2)}) collective-permute-start(bf16[8,7296]{1,0:T(8,128)(2,1)S(1)} %token_rows.1), channel_id=1, source_target_pairs={{0,32},{1,97},{2,34},{3,99},{4,36},{5,101},{6,38},{7,103},{8,40},{... | collective-permute-start | bytes 350216 | tf_op jit(solution)/shard_map/ppermute | solution.py:46
  9.3 3.8 %collective-permute-start.3 = (bf16[8,7296]{1,0:T(8,128)(2,1)S(1)}, bf16[8,7296]{1,0:T(8,128)(2,1)S(1)}, u32[]{:S(2)}, u32[]{:S(2)}) collective-permute-start(bf16[8,7296]{1,0:T(8,128)(2,1)S(1)} %token_rows.1), channel_id=1, source_target_pairs={{0,8},{1,25},{2,10},{3,27},{4,12},{5,29},{6,14},{7,31},{8,0},{9,17... | collective-permute-start | bytes 350216 | tf_op jit(solution)/shard_map/ppermute | solution.py:46
  13.0 2.1 %collective-permute-start.4 = (bf16[8,7296]{1,0:T(8,128)(2,1)S(1)}, bf16[8,7296]{1,0:T(8,128)(2,1)S(1)}, u32[]{:S(2)}, u32[]{:S(2)}) collective-permute-start(bf16[8,7296]{1,0:T(8,128)(2,1)S(1)} %token_rows.1), channel_id=1, source_target_pairs={{0,10},{1,31},{2,8},{3,29},{4,14},{5,27},{6,12},{7,25},{8,2},{9,23... | collective-permute-start | bytes 350216 | tf_op jit(solution)/shard_map/ppermute | solution.py:46
  15.2 5.1 %collective-permute-start.5 = (bf16[8,7296]{1,0:T(8,128)(2,1)S(1)}, bf16[8,7296]{1,0:T(8,128)(2,1)S(1)}, u32[]{:S(2)}, u32[]{:S(2)}) collective-permute-start(bf16[8,7296]{1,0:T(8,128)(2,1)S(1)} %token_rows.1), channel_id=1, source_target_pairs={{0,40},{1,121},{2,42},{3,123},{4,44},{5,125},{6,46},{7,127},{8,32}... | collective-permute-start | bytes 350216 | tf_op jit(solution)/shard_map/ppermute | solution.py:46
  20.6 0.6 collective-permute-start.11
  21.2 1.3 collective-permute-done.5
  22.5 7.1 %collective-permute-done.6 = bf16[8,7296]{1,0:T(8,128)(2,1)S(1)} collective-permute-done((bf16[8,7296]{1,0:T(8,128)(2,1)S(1)}, bf16[8,7296]{1,0:T(8,128)(2,1)S(1)}, u32[]{:S(2)}, u32[]{:S(2)}) %collective-permute-start.6) | collective-permute-done | bytes 116768 | tf_op jit(solution)/shard_map/ppermute | solution.py:46
  30.0 5.6 %collective-permute-done.12 = bf16[64,2304]{1,0:T(8,128)(2,1)S(1)} collective-permute-done((bf16[64,2304]{1,0:T(8,128)(2,1)S(1)}, bf16[64,2304]{1,0:T(8,128)(2,1)S(1)}, u32[]{:S(2)}, u32[]{:S(2)}) %collective-permute-start.12) | collective-permute-done | bytes 294944 | tf_op jit(solution)/shard_map/ppermute | solution.py:28
  35.7 5.7 %collective-permute-done.15 = bf16[64,2432]{1,0:T(8,128)(2,1)S(1)} collective-permute-done((bf16[64,2432]{1,0:T(8,128)(2,1)S(1)}, bf16[64,2432]{1,0:T(8,128)(2,1)S(1)}, u32[]{:S(2)}, u32[]{:S(2)}) %collective-permute-start.15) | collective-permute-done | bytes 311328 | tf_op jit(solution)/shard_map/ppermute | solution.py:28
  41.9 8.5 %collective-permute-done.13 = bf16[128,2304]{1,0:T(8,128)(2,1)S(1)} collective-permute-done((bf16[128,2304]{1,0:T(8,128)(2,1)S(1)}, bf16[128,2304]{1,0:T(8,128)(2,1)S(1)}, u32[]{:S(2)}, u32[]{:S(2)}) %collective-permute-start.13) | collective-permute-done | bytes 589856 | tf_op jit(solution)/shard_map/ppermute | solution.py:28
  50.5 0.7 collective-permute-done.16
  51.3 8.8 %collective-permute-done.8 = bf16[128,2560]{1,0:T(8,128)(2,1)S(1)} collective-permute-done((bf16[128,2560]{1,0:T(8,128)(2,1)S(1)}, bf16[128,2560]{1,0:T(8,128)(2,1)S(1)}, u32[]{:S(2)}, u32[]{:S(2)}) %collective-permute-start.8) | collective-permute-done | bytes 655392 | tf_op jit(solution)/shard_map/ppermute | solution.py:28
  60.5 3.5 %weights_in.4 = (bf16[7168,256]{1,0:T(8,128)(2,1)S(1)}, bf16[7168,256]{1,0:T(8,128)(2,1)S(1)}, bf16[7168,256]{1,0:T(8,128)(2,1)S(1)}, bf16[7168,256]{1,0:T(8,128)(2,1)S(1)}) custom-call(bf16[7168,256]{1,0:T(8,128)(2,1)S(1)} %bitcast.8, bf16[7168,256]{1,0:T(8,128)(2,1)} %collective-permute-done.10.refs_1_, bf16[7168,256]{1,0:T(8,128)(2,1)S(1)} %bitcast.10, ...), custom_call_target="tpu_custom_call" | custom-call | flops 8589934592 | tf_op jit(solution)/shard_map/weights_in/pallas_call | solution.py:177
  64.0 2.5 %collective-permute-done.14.x = bf16[256,2304]{1,0:T(8,128)(2,1)S(1)} collective-permute-done((bf16[256,2304]{1,0:T(8,128)(2,1)S(1)}, bf16[256,2304]{1,0:T(8,128)(2,1)S(1)}, u32[]{:S(2)}, u32[]{:S(2)}) %collective-permute-start.14) | collective-permute-done | bytes 1179680 | tf_op jit(solution)/shard_map/ppermute | solution.py:28
  66.5 1.4 shard_map.94.part1
  67.9 8.3 %collective-permute-done.17.x.far_x2 = bf16[256,2432]{1,0:T(8,128)(2,1)S(1)} collective-permute-done((bf16[256,2432]{1,0:T(8,128)(2,1)S(1)}, bf16[256,2432]{1,0:T(8,128)(2,1)S(1)}, u32[]{:S(2)}, u32[]{:S(2)}) %collective-permute-start.17) | collective-permute-done | bytes 1245216 | tf_op jit(solution)/shard_map/ppermute | solution.py:28
  76.2 1.4 shard_map.95.part2
  77.6 4.0 %gate_up_near.1.acc_in = f32[4,512,256]{2,1,0:T(8,128)S(1)} custom-call(bf16[256,2560]{1,0:T(8,128)(2,1)S(1)} %pad_maximum_fusion.1.x0, bf16[256,2304]{1,0:T(8,128)(2,1)S(1)} %pad_maximum_fusion.3.x1, bf16[256,2432]{1,0:T(8,128)(2,1)S(1)} %pad_maximum_fusion.2.x2.near_x2, bf16[7168,256]{1,0:T(8,128)(2,1)S(1)} %get-tuple-element.11.w0, ...), custom_call_target="tpu_custom_call" | custom-call | flops 3757572096 | tf_op jit(solution)/shard_map/gate_up_near/pallas_call | solution.py:196
  81.6 2.3 %weights_in.5 = (bf16[256,7168]{1,0:T(8,128)(2,1)S(1)}, bf16[256,7168]{1,0:T(8,128)(2,1)S(1)}) custom-call(bf16[256,7168]{1,0:T(8,128)(2,1)S(1)} %bitcast.12, bf16[256,7168]{1,0:T(8,128)(2,1)} %collective-permute-done.18.refs_1_), custom_call_target="tpu_custom_call" | custom-call | flops 8589934592 | tf_op jit(solution)/shard_map/weights_in/pallas_call | solution.py:177
  83.9 1.7 %gate_up_far_0.1 = (bf16[512,512]{1,0:T(8,128)(2,1)S(1)}, s32[1,128]{1,0:T(1,128)S(1)}) custom-call(s32[1]{0:T(128)} %bitcast.expert, bf16[256,2560]{1,0:T(8,128)(2,1)S(1)} %collective-permute-done.9.x0, bf16[7168,256]{1,0:T(8,128)(2,1)S(1)} %get-tuple-element.11.w0, bf16[7168,256]{1,0:T(8,128)(2,1)S(1)} %get-tuple-element.12.w1, ...), custom_call_target="tpu_custom_call" | custom-call | flops 1252524032 | tf_op jit(solution)/shard_map/gate_up_far_0/pallas_call | solution.py:219
  85.6 0.8 shard_map.101
  86.5 0.9 shard_map.99
  87.5 7.6 %collective-permute-start.35 = (s32[1,128]{1,0:T(1,128)S(1)}, s32[1,128]{1,0:T(1,128)S(1)}, u32[]{:S(2)}, u32[]{:S(2)}) collective-permute-start(s32[1,128]{1,0:T(1,128)S(1)} %get-tuple-element.18), channel_id=1, source_target_pairs={{0,1},{1,0},{2,3},{3,2},{4,5},{5,4},{6,7},{7,6},{8,9},{9,8},{10,11... | collective-permute-start | bytes 1544 | tf_op jit(solution)/shard_map/ppermute | solution.py:54
  95.0 0.9 shard_map.98
  95.9 0.9 shard_map.96
  96.8 0.9 shard_map.97
  97.7 0.8 shard_map.100
  98.6 3.2 %collective-permute-done.25 = bf16[256,2304]{1,0:T(8,128)(2,1)S(1)} collective-permute-done((bf16[256,2304]{1,0:T(8,128)(2,1)S(1)}, bf16[256,2304]{1,0:T(8,128)(2,1)S(1)}, u32[]{:S(2)}, u32[]{:S(2)}) %collective-permute-start.25) | collective-permute-done | bytes 1179680 | tf_op jit(solution)/shard_map/ppermute | solution.py:28
  102.4 1.1 collective-permute-done.22
  103.9 10.7 %collective-permute-done.19 = bf16[256,2432]{1,0:T(8,128)(2,1)S(1)} collective-permute-done((bf16[256,2432]{1,0:T(8,128)(2,1)S(1)}, bf16[256,2432]{1,0:T(8,128)(2,1)S(1)}, u32[]{:S(2)}, u32[]{:S(2)}) %collective-permute-start.19) | collective-permute-done | bytes 1245216 | tf_op jit(solution)/shard_map/ppermute | solution.py:28
  115.2 6.0 %collective-permute-done.23 = bf16[128,2432]{1,0:T(8,128)(2,1)S(1)} collective-permute-done((bf16[128,2432]{1,0:T(8,128)(2,1)S(1)}, bf16[128,2432]{1,0:T(8,128)(2,1)S(1)}, u32[]{:S(2)}, u32[]{:S(2)}) %collective-permute-start.23) | collective-permute-done | bytes 622624 | tf_op jit(solution)/shard_map/ppermute | solution.py:28
  121.5 2.8 %collective-permute-done.20 = bf16[128,2432]{1,0:T(8,128)(2,1)S(1)} collective-permute-done((bf16[128,2432]{1,0:T(8,128)(2,1)S(1)}, bf16[128,2432]{1,0:T(8,128)(2,1)S(1)}, u32[]{:S(2)}, u32[]{:S(2)}) %collective-permute-start.20) | collective-permute-done | bytes 622624 | tf_op jit(solution)/shard_map/ppermute | solution.py:28
  124.7 3.0 %collective-permute-done.24 = bf16[64,2432]{1,0:T(8,128)(2,1)S(1)} collective-permute-done((bf16[64,2432]{1,0:T(8,128)(2,1)S(1)}, bf16[64,2432]{1,0:T(8,128)(2,1)S(1)}, u32[]{:S(2)}, u32[]{:S(2)}) %collective-permute-start.24) | collective-permute-done | bytes 311328 | tf_op jit(solution)/shard_map/ppermute | solution.py:28
  127.7 2.9 %collective-permute-done.21 = bf16[64,2432]{1,0:T(8,128)(2,1)S(1)} collective-permute-done((bf16[64,2432]{1,0:T(8,128)(2,1)S(1)}, bf16[64,2432]{1,0:T(8,128)(2,1)S(1)}, u32[]{:S(2)}, u32[]{:S(2)}) %collective-permute-start.21) | collective-permute-done | bytes 311328 | tf_op jit(solution)/shard_map/ppermute | solution.py:28
  130.9 3.7 %collective-permute-start.34 = (bf16[8,7168]{1,0:T(8,128)(2,1)S(1)}, bf16[8,7168]{1,0:T(8,128)(2,1)S(1)}, u32[]{:S(2)}, u32[]{:S(2)}) collective-permute-start(bf16[8,7168]{1,0:T(8,128)(2,1)S(1)} %get-tuple-element.22), channel_id=1, source_target_pairs={{0,42},{1,127},{2,40},{3,125},{4,46},{5,123},{6,44},{7,121},{8,34}... | collective-permute-start | bytes 344072 | tf_op jit(solution)/shard_map/ppermute | solution.py:46
  134.6 1.2 collective-permute-start.33
  135.8 0.6 multiply_add_fusion
  136.3 4.8 %collective-permute-start.32 = (bf16[8,7168]{1,0:T(8,128)(2,1)S(1)}, bf16[8,7168]{1,0:T(8,128)(2,1)S(1)}, u32[]{:S(2)}, u32[]{:S(2)}) collective-permute-start(bf16[8,7168]{1,0:T(8,128)(2,1)S(1)} %get-tuple-element.24), channel_id=1, source_target_pairs={{0,10},{1,31},{2,8},{3,29},{4,14},{5,27},{6,12},{7,25},{8,2},{9,23... | collective-permute-start | bytes 344072 | tf_op jit(solution)/shard_map/ppermute | solution.py:46
  141.1 1.8 %collective-permute-start.30 = (bf16[8,7168]{1,0:T(8,128)(2,1)S(1)}, bf16[8,7168]{1,0:T(8,128)(2,1)S(1)}, u32[]{:S(2)}, u32[]{:S(2)}) collective-permute-start(bf16[8,7168]{1,0:T(8,128)(2,1)S(1)} %get-tuple-element.26), channel_id=1, source_target_pairs={{0,34},{1,103},{2,32},{3,101},{4,38},{5,99},{6,36},{7,97},{8,42},{... | collective-permute-start | bytes 344072 | tf_op jit(solution)/shard_map/ppermute | solution.py:46
  143.0 0.8 collective-permute-start.29
  143.8 2.4 %collective-permute-start.28 = (bf16[8,7168]{1,0:T(8,128)(2,1)S(1)}, bf16[8,7168]{1,0:T(8,128)(2,1)S(1)}, u32[]{:S(2)}, u32[]{:S(2)}) collective-permute-start(bf16[8,7168]{1,0:T(8,128)(2,1)S(1)} %get-tuple-element.21), channel_id=1, source_target_pairs={{0,2},{1,7},{2,0},{3,5},{4,6},{5,3},{6,4},{7,1},{8,10},{9,15},{10,... | collective-permute-start | bytes 344072 | tf_op jit(solution)/shard_map/ppermute | solution.py:46
  146.4 1.8 %collective-permute-done.30 = bf16[8,7168]{1,0:T(8,128)(2,1)S(1)} collective-permute-done((bf16[8,7168]{1,0:T(8,128)(2,1)S(1)}, bf16[8,7168]{1,0:T(8,128)(2,1)S(1)}, u32[]{:S(2)}, u32[]{:S(2)}) %collective-permute-start.30) | collective-permute-done | bytes 114720 | tf_op jit(solution)/shard_map/ppermute | solution.py:46
  148.2 0.9 collective-permute-done.29
  149.1 0.8 fusion.6
  (89 shorter events, 4.7 us)
Async XLA Ops:
  0.6 0.9 copy-start
  1.5 0.7 copy-start.1
  2.2 0.7 copy-start.2
  3.2 12.0 %collective-permute-start = (bf16[8,7296]{1,0:T(8,128)(2,1)S(1)}, bf16[8,7296]{1,0:T(8,128)(2,1)S(1)}, u32[]{:S(2)}, u32[]{:S(2)}) collective-permute-start(bf16[8,7296]{1,0:T(8,128)(2,1)S(1)} %token_rows.1), channel_id=1, source_target_pairs={{0,2},{1,7},{2,0},{3,5},{4,6},{5,3},{6,4},{7,1},{8,10},{9,15},{10,... | collective-permute-start | bytes 350216 | tf_op jit(solution)/shard_map/ppermute | solution.py:46
  6.5 13.8 %collective-permute-start.1 = (bf16[8,7296]{1,0:T(8,128)(2,1)S(1)}, bf16[8,7296]{1,0:T(8,128)(2,1)S(1)}, u32[]{:S(2)}, u32[]{:S(2)}) collective-permute-start(bf16[8,7296]{1,0:T(8,128)(2,1)S(1)} %token_rows.1), channel_id=1, source_target_pairs={{0,32},{1,97},{2,34},{3,99},{4,36},{5,101},{6,38},{7,103},{8,40},{... | collective-permute-start | bytes 350216 | tf_op jit(solution)/shard_map/ppermute | solution.py:46
  9.3 11.2 %collective-permute-start.2 = (bf16[8,7296]{1,0:T(8,128)(2,1)S(1)}, bf16[8,7296]{1,0:T(8,128)(2,1)S(1)}, u32[]{:S(2)}, u32[]{:S(2)}) collective-permute-start(bf16[8,7296]{1,0:T(8,128)(2,1)S(1)} %token_rows.1), channel_id=1, source_target_pairs={{0,34},{1,103},{2,32},{3,101},{4,38},{5,99},{6,36},{7,97},{8,42},{... | collective-permute-start | bytes 350216 | tf_op jit(solution)/shard_map/ppermute | solution.py:46
  9.3 11.3 %collective-permute-start.3 = (bf16[8,7296]{1,0:T(8,128)(2,1)S(1)}, bf16[8,7296]{1,0:T(8,128)(2,1)S(1)}, u32[]{:S(2)}, u32[]{:S(2)}) collective-permute-start(bf16[8,7296]{1,0:T(8,128)(2,1)S(1)} %token_rows.1), channel_id=1, source_target_pairs={{0,8},{1,25},{2,10},{3,27},{4,12},{5,29},{6,14},{7,31},{8,0},{9,17... | collective-permute-start | bytes 350216 | tf_op jit(solution)/shard_map/ppermute | solution.py:46
  13.0 8.1 %collective-permute-start.4 = (bf16[8,7296]{1,0:T(8,128)(2,1)S(1)}, bf16[8,7296]{1,0:T(8,128)(2,1)S(1)}, u32[]{:S(2)}, u32[]{:S(2)}) collective-permute-start(bf16[8,7296]{1,0:T(8,128)(2,1)S(1)} %token_rows.1), channel_id=1, source_target_pairs={{0,10},{1,31},{2,8},{3,29},{4,14},{5,27},{6,12},{7,25},{8,2},{9,23... | collective-permute-start | bytes 350216 | tf_op jit(solution)/shard_map/ppermute | solution.py:46
  15.2 7.3 %collective-permute-start.5 = (bf16[8,7296]{1,0:T(8,128)(2,1)S(1)}, bf16[8,7296]{1,0:T(8,128)(2,1)S(1)}, u32[]{:S(2)}, u32[]{:S(2)}) collective-permute-start(bf16[8,7296]{1,0:T(8,128)(2,1)S(1)} %token_rows.1), channel_id=1, source_target_pairs={{0,40},{1,121},{2,42},{3,123},{4,44},{5,125},{6,46},{7,127},{8,32}... | collective-permute-start | bytes 350216 | tf_op jit(solution)/shard_map/ppermute | solution.py:46
  20.3 9.3 %collective-permute-start.6 = (bf16[8,7296]{1,0:T(8,128)(2,1)S(1)}, bf16[8,7296]{1,0:T(8,128)(2,1)S(1)}, u32[]{:S(2)}, u32[]{:S(2)}) collective-permute-start(bf16[8,7296]{1,0:T(8,128)(2,1)S(1)} %token_rows.1), channel_id=1, source_target_pairs={{0,42},{1,127},{2,40},{3,125},{4,46},{5,123},{6,44},{7,121},{8,34}... | collective-permute-start | bytes 350216 | tf_op jit(solution)/shard_map/ppermute | solution.py:46
  20.5 39.7 %collective-permute-start.10 = (bf16[7168,256]{1,0:T(8,128)(2,1)}, bf16[7168,256]{1,0:T(8,128)(2,1)}, u32[]{:S(2)}, u32[]{:S(2)}) collective-permute-start(bf16[7168,256]{1,0:T(8,128)(2,1)} %bitcast.7), channel_id=1, source_target_pairs={{0,1},{1,0},{2,3},{3,2},{4,5},{5,4},{6,7},{7,6},{8,9},{9,8},{10,11... | collective-permute-start | bytes 11010056 | tf_op jit(solution)/shard_map/ppermute | solution.py:54
  20.6 39.9 %collective-permute-start.11 = (bf16[7168,256]{1,0:T(8,128)(2,1)}, bf16[7168,256]{1,0:T(8,128)(2,1)}, u32[]{:S(2)}, u32[]{:S(2)}) collective-permute-start(bf16[7168,256]{1,0:T(8,128)(2,1)} %bitcast.9), channel_id=1, source_target_pairs={{0,1},{1,0},{2,3},{3,2},{4,5},{5,4},{6,7},{7,6},{8,9},{9,8},{10,11... | collective-permute-start | bytes 11010056 | tf_op jit(solution)/shard_map/ppermute | solution.py:54
  29.7 5.9 %collective-permute-start.12 = (bf16[64,2304]{1,0:T(8,128)(2,1)S(1)}, bf16[64,2304]{1,0:T(8,128)(2,1)S(1)}, u32[]{:S(2)}, u32[]{:S(2)}) collective-permute-start(bf16[64,2304]{1,0:T(8,128)(2,1)S(1)} %slice.110), channel_id=1, source_target_pairs={{0,96},{1,33},{32,64},{33,1},{64,32},{65,97},{96,0},{97,65},{2,98}... | collective-permute-start | bytes 884744 | tf_op jit(solution)/shard_map/ppermute | solution.py:28
  29.8 51.8 %collective-permute-start.18 = (bf16[256,7168]{1,0:T(8,128)(2,1)}, bf16[256,7168]{1,0:T(8,128)(2,1)}, u32[]{:S(2)}, u32[]{:S(2)}) collective-permute-start(bf16[256,7168]{1,0:T(8,128)(2,1)} %bitcast.11), channel_id=1, source_target_pairs={{0,1},{1,0},{2,3},{3,2},{4,5},{5,4},{6,7},{7,6},{8,9},{9,8},{10,11... | collective-permute-start | bytes 11010056 | tf_op jit(solution)/shard_map/ppermute | solution.py:54
  29.9 11.8 %collective-permute-start.7 = (bf16[64,2560]{1,0:T(8,128)(2,1)S(1)}, bf16[64,2560]{1,0:T(8,128)(2,1)S(1)}, u32[]{:S(2)}, u32[]{:S(2)}) collective-permute-start(bf16[64,2560]{1,0:T(8,128)(2,1)S(1)} %slice.109), channel_id=1, source_target_pairs={{0,6},{1,3},{2,4},{3,1},{4,2},{5,7},{6,0},{7,5},{8,14},{9,11},{10,... | collective-permute-start | bytes 983048 | tf_op jit(solution)/shard_map/ppermute | solution.py:28
  35.6 5.7 %collective-permute-start.15 = (bf16[64,2432]{1,0:T(8,128)(2,1)S(1)}, bf16[64,2432]{1,0:T(8,128)(2,1)S(1)}, u32[]{:S(2)}, u32[]{:S(2)}) collective-permute-start(bf16[64,2432]{1,0:T(8,128)(2,1)S(1)} %slice.111), channel_id=1, source_target_pairs={{0,24},{1,9},{8,16},{9,1},{16,8},{17,25},{24,0},{25,17},{2,26},{3,... | collective-permute-start | bytes 933896 | tf_op jit(solution)/shard_map/ppermute | solution.py:28
  41.4 9.0 %collective-permute-start.13 = (bf16[128,2304]{1,0:T(8,128)(2,1)S(1)}, bf16[128,2304]{1,0:T(8,128)(2,1)S(1)}, u32[]{:S(2)}, u32[]{:S(2)}) collective-permute-start(bf16[128,2304]{1,0:T(8,128)(2,1)S(1)} %pad_maximum_fusion.6), channel_id=1, source_target_pairs={{0,24},{1,9},{8,16},{9,1},{16,8},{17,25},{24,0},{25,17},{2,26},{3,... | collective-permute-start | bytes 1769480 | tf_op jit(solution)/shard_map/ppermute | solution.py:28
  41.7 9.5 %collective-permute-start.16 = (bf16[128,2432]{1,0:T(8,128)(2,1)S(1)}, bf16[128,2432]{1,0:T(8,128)(2,1)S(1)}, u32[]{:S(2)}, u32[]{:S(2)}) collective-permute-start(bf16[128,2432]{1,0:T(8,128)(2,1)S(1)} %pad_maximum_fusion.5), channel_id=1, source_target_pairs={{0,6},{1,3},{2,4},{3,1},{4,2},{5,7},{6,0},{7,5},{8,14},{9,11},{10,... | collective-permute-start | bytes 1867784 | tf_op jit(solution)/shard_map/ppermute | solution.py:28
  50.4 9.7 %collective-permute-start.8 = (bf16[128,2560]{1,0:T(8,128)(2,1)S(1)}, bf16[128,2560]{1,0:T(8,128)(2,1)S(1)}, u32[]{:S(2)}, u32[]{:S(2)}) collective-permute-start(bf16[128,2560]{1,0:T(8,128)(2,1)S(1)} %pad_maximum_fusion.4), channel_id=1, source_target_pairs={{0,96},{1,33},{32,64},{33,1},{64,32},{65,97},{96,0},{97,65},{2,98}... | collective-permute-start | bytes 1966088 | tf_op jit(solution)/shard_map/ppermute | solution.py:28
  50.4 10.1 %copy-start.4 = (bf16[1,7168,256]{2,1,0:T(8,128)(2,1)S(1)}, bf16[1,7168,256]{2,1,0:T(8,128)(2,1)}, u32[]{:S(2)}) copy-start(bf16[1,7168,256]{2,1,0:T(8,128)(2,1)} %param.12) | copy-start | bytes 11010052
  51.2 15.3 %collective-permute-start.14 = (bf16[256,2304]{1,0:T(8,128)(2,1)S(1)}, bf16[256,2304]{1,0:T(8,128)(2,1)S(1)}, u32[]{:S(2)}, u32[]{:S(2)}) collective-permute-start(bf16[256,2304]{1,0:T(8,128)(2,1)S(1)} %pad_maximum_fusion.3.x1), channel_id=1, source_target_pairs={{0,6},{1,3},{2,4},{3,1},{4,2},{5,7},{6,0},{7,5},{8,14},{9,11},{10,... | collective-permute-start | bytes 3538952 | tf_op jit(solution)/shard_map/ppermute | solution.py:28
  51.2 9.3 %copy-start.3 = (bf16[1,7168,256]{2,1,0:T(8,128)(2,1)S(1)}, bf16[1,7168,256]{2,1,0:T(8,128)(2,1)}, u32[]{:S(2)}) copy-start(bf16[1,7168,256]{2,1,0:T(8,128)(2,1)} %param.11) | copy-start | bytes 11010052
  60.1 16.1 %collective-permute-start.17 = (bf16[256,2432]{1,0:T(8,128)(2,1)S(1)}, bf16[256,2432]{1,0:T(8,128)(2,1)S(1)}, u32[]{:S(2)}, u32[]{:S(2)}) collective-permute-start(bf16[256,2432]{1,0:T(8,128)(2,1)S(1)} %pad_maximum_fusion.2.x2.near_x2), channel_id=1, source_target_pairs={{0,96},{1,33},{32,64},{33,1},{64,32},{65,97},{96,0},{97,65},{2,98}... | collective-permute-start | bytes 3735560 | tf_op jit(solution)/shard_map/ppermute | solution.py:28
  60.2 23.7 %collective-permute-start.9 = (bf16[256,2560]{1,0:T(8,128)(2,1)S(1)}, bf16[256,2560]{1,0:T(8,128)(2,1)S(1)}, u32[]{:S(2)}, u32[]{:S(2)}) collective-permute-start(bf16[256,2560]{1,0:T(8,128)(2,1)S(1)} %pad_maximum_fusion.1.x0), channel_id=1, source_target_pairs={{0,24},{1,9},{8,16},{9,1},{16,8},{17,25},{24,0},{25,17},{2,26},{3,... | collective-permute-start | bytes 3932168 | tf_op jit(solution)/shard_map/ppermute | solution.py:28
  77.6 4.0 %copy-start.5 = (bf16[1,256,7168]{2,1,0:T(8,128)(2,1)S(1)}, bf16[1,256,7168]{2,1,0:T(8,128)(2,1)}, u32[]{:S(2)}) copy-start(bf16[1,256,7168]{2,1,0:T(8,128)(2,1)} %param.13) | copy-start | bytes 11010052
  86.4 15.4 %collective-permute-start.25 = (bf16[256,2304]{1,0:T(8,128)(2,1)S(1)}, bf16[256,2304]{1,0:T(8,128)(2,1)S(1)}, u32[]{:S(2)}, u32[]{:S(2)}) collective-permute-start(bf16[256,2304]{1,0:T(8,128)(2,1)S(1)} %shard_map.101), channel_id=1, source_target_pairs={{0,96},{1,33},{32,64},{33,1},{64,32},{65,97},{96,0},{97,65},{2,98}... | collective-permute-start | bytes 3538952 | tf_op jit(solution)/shard_map/ppermute | solution.py:28
  87.4 16.1 %collective-permute-start.22 = (bf16[256,2432]{1,0:T(8,128)(2,1)S(1)}, bf16[256,2432]{1,0:T(8,128)(2,1)S(1)}, u32[]{:S(2)}, u32[]{:S(2)}) collective-permute-start(bf16[256,2432]{1,0:T(8,128)(2,1)S(1)} %shard_map.99), channel_id=1, source_target_pairs={{0,6},{1,3},{2,4},{3,1},{4,2},{5,7},{6,0},{7,5},{8,14},{9,11},{10,... | collective-permute-start | bytes 3735560 | tf_op jit(solution)/shard_map/ppermute | solution.py:28
  87.5 11.1 %collective-permute-start.35 = (s32[1,128]{1,0:T(1,128)S(1)}, s32[1,128]{1,0:T(1,128)S(1)}, u32[]{:S(2)}, u32[]{:S(2)}) collective-permute-start(s32[1,128]{1,0:T(1,128)S(1)} %get-tuple-element.18), channel_id=1, source_target_pairs={{0,1},{1,0},{2,3},{3,2},{4,5},{5,4},{6,7},{7,6},{8,9},{9,8},{10,11... | collective-permute-start | bytes 1544 | tf_op jit(solution)/shard_map/ppermute | solution.py:54
  98.5 16.1 %collective-permute-start.19 = (bf16[256,2432]{1,0:T(8,128)(2,1)S(1)}, bf16[256,2432]{1,0:T(8,128)(2,1)S(1)}, u32[]{:S(2)}, u32[]{:S(2)}) collective-permute-start(bf16[256,2432]{1,0:T(8,128)(2,1)S(1)} %shard_map.97), channel_id=1, source_target_pairs={{0,24},{1,9},{8,16},{9,1},{16,8},{17,25},{24,0},{25,17},{2,26},{3,... | collective-permute-start | bytes 3735560 | tf_op jit(solution)/shard_map/ppermute | solution.py:28
  102.1 12.9 %collective-permute-start.26 = (bf16[128,2304]{1,0:T(8,128)(2,1)S(1)}, bf16[128,2304]{1,0:T(8,128)(2,1)S(1)}, u32[]{:S(2)}, u32[]{:S(2)}) collective-permute-start(bf16[128,2304]{1,0:T(8,128)(2,1)S(1)} %slice.162), channel_id=1, source_target_pairs={{0,6},{1,3},{2,4},{3,1},{4,2},{5,7},{6,0},{7,5},{8,14},{9,11},{10,... | collective-permute-start | bytes 1769480 | tf_op jit(solution)/shard_map/ppermute | solution.py:28
  103.8 17.5 %collective-permute-start.23 = (bf16[128,2432]{1,0:T(8,128)(2,1)S(1)}, bf16[128,2432]{1,0:T(8,128)(2,1)S(1)}, u32[]{:S(2)}, u32[]{:S(2)}) collective-permute-start(bf16[128,2432]{1,0:T(8,128)(2,1)S(1)} %slice.160), channel_id=1, source_target_pairs={{0,24},{1,9},{8,16},{9,1},{16,8},{17,25},{24,0},{25,17},{2,26},{3,... | collective-permute-start | bytes 1867784 | tf_op jit(solution)/shard_map/ppermute | solution.py:28
  114.9 9.5 %collective-permute-start.20 = (bf16[128,2432]{1,0:T(8,128)(2,1)S(1)}, bf16[128,2432]{1,0:T(8,128)(2,1)S(1)}, u32[]{:S(2)}, u32[]{:S(2)}) collective-permute-start(bf16[128,2432]{1,0:T(8,128)(2,1)S(1)} %slice.161), channel_id=1, source_target_pairs={{0,96},{1,33},{32,64},{33,1},{64,32},{65,97},{96,0},{97,65},{2,98}... | collective-permute-start | bytes 1867784 | tf_op jit(solution)/shard_map/ppermute | solution.py:28
  115.1 9.5 %collective-permute-start.27 = (bf16[64,2304]{1,0:T(8,128)(2,1)S(1)}, bf16[64,2304]{1,0:T(8,128)(2,1)S(1)}, u32[]{:S(2)}, u32[]{:S(2)}) collective-permute-start(bf16[64,2304]{1,0:T(8,128)(2,1)S(1)} %slice.165), channel_id=1, source_target_pairs={{0,24},{1,9},{8,16},{9,1},{16,8},{17,25},{24,0},{25,17},{2,26},{3,... | collective-permute-start | bytes 884744 | tf_op jit(solution)/shard_map/ppermute | solution.py:28
  121.4 6.3 %collective-permute-start.24 = (bf16[64,2432]{1,0:T(8,128)(2,1)S(1)}, bf16[64,2432]{1,0:T(8,128)(2,1)S(1)}, u32[]{:S(2)}, u32[]{:S(2)}) collective-permute-start(bf16[64,2432]{1,0:T(8,128)(2,1)S(1)} %slice.163), channel_id=1, source_target_pairs={{0,96},{1,33},{32,64},{33,1},{64,32},{65,97},{96,0},{97,65},{2,98}... | collective-permute-start | bytes 933896 | tf_op jit(solution)/shard_map/ppermute | solution.py:28
  124.5 6.1 %collective-permute-start.21 = (bf16[64,2432]{1,0:T(8,128)(2,1)S(1)}, bf16[64,2432]{1,0:T(8,128)(2,1)S(1)}, u32[]{:S(2)}, u32[]{:S(2)}) collective-permute-start(bf16[64,2432]{1,0:T(8,128)(2,1)S(1)} %slice.164), channel_id=1, source_target_pairs={{0,6},{1,3},{2,4},{3,1},{4,2},{5,7},{6,0},{7,5},{8,14},{9,11},{10,... | collective-permute-start | bytes 933896 | tf_op jit(solution)/shard_map/ppermute | solution.py:28
  130.7 5.1 %copy-start.6 = (f32[16]{0:T(128)S(1)}, f32[16]{0:T(128)}, u32[]{:S(2)}) copy-start(f32[16]{0:T(128)} %param.14) | copy-start | bytes 196
  130.9 12.1 %collective-permute-start.34 = (bf16[8,7168]{1,0:T(8,128)(2,1)S(1)}, bf16[8,7168]{1,0:T(8,128)(2,1)S(1)}, u32[]{:S(2)}, u32[]{:S(2)}) collective-permute-start(bf16[8,7168]{1,0:T(8,128)(2,1)S(1)} %get-tuple-element.22), channel_id=1, source_target_pairs={{0,42},{1,127},{2,40},{3,125},{4,46},{5,123},{6,44},{7,121},{8,34}... | collective-permute-start | bytes 344072 | tf_op jit(solution)/shard_map/ppermute | solution.py:46
  134.6 9.2 %collective-permute-start.33 = (bf16[8,7168]{1,0:T(8,128)(2,1)S(1)}, bf16[8,7168]{1,0:T(8,128)(2,1)S(1)}, u32[]{:S(2)}, u32[]{:S(2)}) collective-permute-start(bf16[8,7168]{1,0:T(8,128)(2,1)S(1)} %get-tuple-element.23), channel_id=1, source_target_pairs={{0,40},{1,121},{2,42},{3,123},{4,44},{5,125},{6,46},{7,127},{8,32}... | collective-permute-start | bytes 344072 | tf_op jit(solution)/shard_map/ppermute | solution.py:46
  136.3 10.0 %collective-permute-start.32 = (bf16[8,7168]{1,0:T(8,128)(2,1)S(1)}, bf16[8,7168]{1,0:T(8,128)(2,1)S(1)}, u32[]{:S(2)}, u32[]{:S(2)}) collective-permute-start(bf16[8,7168]{1,0:T(8,128)(2,1)S(1)} %get-tuple-element.24), channel_id=1, source_target_pairs={{0,10},{1,31},{2,8},{3,29},{4,14},{5,27},{6,12},{7,25},{8,2},{9,23... | collective-permute-start | bytes 344072 | tf_op jit(solution)/shard_map/ppermute | solution.py:46
  141.1 5.2 %collective-permute-start.31 = (bf16[8,7168]{1,0:T(8,128)(2,1)S(1)}, bf16[8,7168]{1,0:T(8,128)(2,1)S(1)}, u32[]{:S(2)}, u32[]{:S(2)}) collective-permute-start(bf16[8,7168]{1,0:T(8,128)(2,1)S(1)} %get-tuple-element.25), channel_id=1, source_target_pairs={{0,8},{1,25},{2,10},{3,27},{4,12},{5,29},{6,14},{7,31},{8,0},{9,17... | collective-permute-start | bytes 344072 | tf_op jit(solution)/shard_map/ppermute | solution.py:46
  141.1 7.1 %collective-permute-start.30 = (bf16[8,7168]{1,0:T(8,128)(2,1)S(1)}, bf16[8,7168]{1,0:T(8,128)(2,1)S(1)}, u32[]{:S(2)}, u32[]{:S(2)}) collective-permute-start(bf16[8,7168]{1,0:T(8,128)(2,1)S(1)} %get-tuple-element.26), channel_id=1, source_target_pairs={{0,34},{1,103},{2,32},{3,101},{4,38},{5,99},{6,36},{7,97},{8,42},{... | collective-permute-start | bytes 344072 | tf_op jit(solution)/shard_map/ppermute | solution.py:46
  143.0 6.1 %collective-permute-start.29 = (bf16[8,7168]{1,0:T(8,128)(2,1)S(1)}, bf16[8,7168]{1,0:T(8,128)(2,1)S(1)}, u32[]{:S(2)}, u32[]{:S(2)}) collective-permute-start(bf16[8,7168]{1,0:T(8,128)(2,1)S(1)} %get-tuple-element.27), channel_id=1, source_target_pairs={{0,32},{1,97},{2,34},{3,99},{4,36},{5,101},{6,38},{7,103},{8,40},{... | collective-permute-start | bytes 344072 | tf_op jit(solution)/shard_map/ppermute | solution.py:46
  143.8 5.2 %collective-permute-start.28 = (bf16[8,7168]{1,0:T(8,128)(2,1)S(1)}, bf16[8,7168]{1,0:T(8,128)(2,1)S(1)}, u32[]{:S(2)}, u32[]{:S(2)}) collective-permute-start(bf16[8,7168]{1,0:T(8,128)(2,1)S(1)} %get-tuple-element.21), channel_id=1, source_target_pairs={{0,2},{1,7},{2,0},{3,5},{4,6},{5,3},{6,4},{7,1},{8,10},{9,15},{10,... | collective-permute-start | bytes 344072 | tf_op jit(solution)/shard_map/ppermute | solution.py:46

commit v3 on v2

--- a/solution.py
+++ b/solution.py
@@ -14,7 +14,7 @@
 EARLY = (X, Y, Z)
 LATE = ((X, Y, Z), (Y, Z, X), (Z, X, Y))
 INFO = 128
-CUTS = (0, 2560, 4864, 7168)
+CUTS = (0, 2432, 4864, 7168)
 COL_CUTS = (0, 2432, 4864, 7168)
 BF16 = jnp.bfloat16
 F32 = jnp.float32
@@ -128,34 +128,29 @@
         out[j] = jnp.dot(x[:, :width], w[rows, :], preferred_element_type=F32)
 
 
-def far_last_kernel(
-    expert, x0, w0, w1, w2, w3, part1, part2, near_x2, far_x2, acc_in, hidden, marks, acc
-):
+def hidden_kernel(expert, part0, part1, part2, near_x2, x2, acc, hidden, marks):
+    parts = (part0, part1, part2)
     far_places = [{canonical(i, q + 4): 64 * q for q in range(4)} for i in range(3)]
-    for j, w in enumerate((w0, w1, w2, w3)):
-        mine = jnp.dot(x0[...], w[: CUTS[1], :], preferred_element_type=F32)
-        for s in range(8):
-            rows = acc_in[j, 64 * s : 64 * s + 64, :]
-            if s in far_places[0]:
-                at = far_places[0][s]
-                rows += mine[at : at + 64]
-            for i, part in ((1, part1), (2, part2)):
-                if s in far_places[i]:
-                    at = far_places[i][s]
-                    rows += part[j, at : at + 64, :]
-            acc[j, 64 * s : 64 * s + 64, :] = rows
+
+    def total(j, s):
+        rows = acc[j, 64 * s : 64 * s + 64, :]
+        for i in range(3):
+            if s in far_places[i]:
+                at = far_places[i][s]
+                rows += parts[i][j, at : at + 64, :]
+        return rows
+
     lane = lax.broadcasted_iota(jnp.int32, (64, INFO), 1)
     sums = jnp.zeros((8, INFO), F32)
     for place in range(8):
         s = canonical(2, place)
-        source = near_x2 if place < 4 else far_x2
+        source = near_x2 if place < 4 else x2
         at = 64 * (place % 4)
         info = source[at : at + 64, CUTS[3] - CUTS[2] :].astype(F32)
         sums += jnp.sum(info.reshape(8, 8, INFO), axis=0)
         scale = jnp.sum(jnp.where(lane == expert[0], info, 0.0), axis=1, keepdims=True)
         for part in range(2):
-            g = acc[part, 64 * s : 64 * s + 64, :]
-            u = acc[part + 2, 64 * s : 64 * s + 64, :]
+            g, u = total(part, s), total(part + 2, s)
             h = g / (1.0 + jnp.exp(-g)) * u * scale
             hidden[64 * s : 64 * s + 64, 256 * part : 256 * part + 256] = h.astype(BF16)
     marks[...] = jnp.sum(sums, axis=0, keepdims=True).astype(jnp.int32)
@@ -215,20 +210,19 @@
     )(piece, *weights)
 
 
-def gate_up_last(expert, piece, weights, parts, near_x2, far_x2, acc):
-    return pl.pallas_call(
-        far_last_kernel,
+def hidden_of(expert, parts, near_x2, far_x2, acc):
+    return pl.pallas_call(
+        hidden_kernel,
         out_shape=(
             jax.ShapeDtypeStruct((512, 512), BF16),
             jax.ShapeDtypeStruct((1, INFO), jnp.int32),
         ),
-        in_specs=[SMEM] + [VMEM] * 10,
+        in_specs=[SMEM] + [VMEM] * 6,
         out_specs=(VMEM, VMEM),
-        scratch_shapes=[pltpu.VMEM((4, 512, 256), F32)],
         cost_estimate=cost(1),
-        compiler_params=pltpu.CompilerParams(vmem_limit_bytes=10 << 20),
-        name="gate_up_far_0",
-    )(expert, piece, *weights, *parts, near_x2, far_x2, acc)
+        compiler_params=pltpu.CompilerParams(vmem_limit_bytes=6 << 20),
+        name="hidden",
+    )(expert, *parts, near_x2, far_x2, acc)
 
 
 def down_kernel(colour, far, hidden, own, other, out):
@@ -287,10 +281,8 @@
 
     acc = gate_up_near(pieces, gate_ups)
     expert = jnp.full((1,), own_expert, jnp.int32)
-    parts = [gate_up_far_part(i, far_pieces[i], gate_ups) for i in (1, 2)]
-    hidden, marks = gate_up_last(
-        expert, far_pieces[0], gate_ups, parts, pieces[2], far_pieces[2], acc
-    )
+    parts = [gate_up_far_part(i, far_pieces[i], gate_ups) for i in range(3)]
+    hidden, marks = hidden_of(expert, parts, pieces[2], far_pieces[2], acc)
 
     sent = [down_part(i, True, hidden, down_own, down_far) for i in range(3)]
     kept = []

time: 150 us -> 157 us (1.047); the launches traced: 150 us -> 155 us
  waiting for transfers between devices: 81.1 us -> 61.7 us
  starting transfers between devices: 42.1 us -> 50.7 us
  local copies, waits for them, and re-layouts: 2.83 us -> 10.8 us
  Pallas kernels: 19.6 us -> 26.6 us
    ppermute x18, waiting for transfers between devices: 69.9 us -> 50.2 us  [exchange(): return lax.ppermute(value, (axis, 'gz_1'), pairs)]
    unnamed x21 -> x23, local copies, waits for them, and re-layouts: 2.38 us -> 10.4 us
    ppermute x18, starting transfers between devices: 1.83 us -> 8.11 us  [exchange(): return lax.ppermute(value, (axis, 'gz_1'), pairs)]
    pallas_call x2 -> x3, Pallas kernels: 2.78 us -> 8.27 us  [gate_up_far_part(): pl.pallas_call(functools.partial(far_part_kernel, colour), out_shape=jax....]
    ppermute x4, starting transfers between devices: 8.32 us -> 10.5 us  [partner(): return lax.ppermute(value, 'gz_1', [(0, 1), (1, 0)])]
  transfers between devices with their start and end apart: 36 -> 36, of which waited for: 18 -> 19; matrix products, arithmetic and copies ran while one was open for 2% -> 2% of each run, Pallas kernels for 11% -> 13%
where the time goes in v3:
time: 157 us; the launch traced here: 155 us
  waiting for transfers between devices  61.7 us (39%)
  starting transfers between devices  50.7 us (32%)
  Pallas kernels  26.6 us (17%)
  local copies, waits for them, and re-layouts  10.8 us (7%)
  other arithmetic  4.21 us (3%)
    ppermute x18, waiting for transfers between devices, exchange(): return lax.ppermute(value, (axis, 'gz_1'), pairs)  50.2 us
    ppermute x14, starting transfers between devices, direct(): return lax.ppermute(value, AXES, pairs)  32 us
    ppermute x14, waiting for transfers between devices, direct(): return lax.ppermute(value, AXES, pairs)  11.5 us
    ppermute x4, starting transfers between devices, partner(): return lax.ppermute(value, 'gz_1', [(0, 1), (1, 0)])  10.5 us
    unnamed x23, local copies, waits for them, and re-layouts  10.4 us
    pallas_call x3, Pallas kernels, gate_up_far_part(): pl.pallas_call(functools.partial(far_part_kernel, colour), out_shape=jax....  8.27 us
    ppermute x18, starting transfers between devices, exchange(): return lax.ppermute(value, (axis, 'gz_1'), pairs)  8.11 us
    pallas_call x2, Pallas kernels, in_vmem(): pl.pallas_call(load_kernel, out_shape=tuple((jax.ShapeDtypeStruct(a.shape...  5.98 us
  transfers between devices with their start and end apart: 36, of which 19 were waited for; matrix products, arithmetic and copies ran while one was open for 2% of the time, Pallas kernels for 13%

profile of v3, /device:TPU:1, one launch (start us, length us, event | category | flops | bytes accessed | tf_op | source)
XLA Modules:
  0.0 155.2 jit_solution(3405132482524540832)
XLA Ops:
  0.6 0.9 copy-done
  3.2 3.4 %collective-permute-start = (bf16[8,7296]{1,0:T(8,128)(2,1)S(1)}, bf16[8,7296]{1,0:T(8,128)(2,1)S(1)}, u32[]{:S(2)}, u32[]{:S(2)}) collective-permute-start(bf16[8,7296]{1,0:T(8,128)(2,1)S(1)} %token_rows.1), channel_id=1, source_target_pairs={{0,2},{1,7},{2,0},{3,5},{4,6},{5,3},{6,4},{7,1},{8,10},{9,15},{10,... | collective-permute-start | bytes 350216 | tf_op jit(solution)/shard_map/ppermute | solution.py:46
  6.5 2.7 %collective-permute-start.1 = (bf16[8,7296]{1,0:T(8,128)(2,1)S(1)}, bf16[8,7296]{1,0:T(8,128)(2,1)S(1)}, u32[]{:S(2)}, u32[]{:S(2)}) collective-permute-start(bf16[8,7296]{1,0:T(8,128)(2,1)S(1)} %token_rows.1), channel_id=1, source_target_pairs={{0,32},{1,97},{2,34},{3,99},{4,36},{5,101},{6,38},{7,103},{8,40},{... | collective-permute-start | bytes 350216 | tf_op jit(solution)/shard_map/ppermute | solution.py:46
  9.3 3.8 %collective-permute-start.3 = (bf16[8,7296]{1,0:T(8,128)(2,1)S(1)}, bf16[8,7296]{1,0:T(8,128)(2,1)S(1)}, u32[]{:S(2)}, u32[]{:S(2)}) collective-permute-start(bf16[8,7296]{1,0:T(8,128)(2,1)S(1)} %token_rows.1), channel_id=1, source_target_pairs={{0,8},{1,25},{2,10},{3,27},{4,12},{5,29},{6,14},{7,31},{8,0},{9,17... | collective-permute-start | bytes 350216 | tf_op jit(solution)/shard_map/ppermute | solution.py:46
  13.0 2.1 %collective-permute-start.4 = (bf16[8,7296]{1,0:T(8,128)(2,1)S(1)}, bf16[8,7296]{1,0:T(8,128)(2,1)S(1)}, u32[]{:S(2)}, u32[]{:S(2)}) collective-permute-start(bf16[8,7296]{1,0:T(8,128)(2,1)S(1)} %token_rows.1), channel_id=1, source_target_pairs={{0,10},{1,31},{2,8},{3,29},{4,14},{5,27},{6,12},{7,25},{8,2},{9,23... | collective-permute-start | bytes 350216 | tf_op jit(solution)/shard_map/ppermute | solution.py:46
  15.2 5.1 %collective-permute-start.5 = (bf16[8,7296]{1,0:T(8,128)(2,1)S(1)}, bf16[8,7296]{1,0:T(8,128)(2,1)S(1)}, u32[]{:S(2)}, u32[]{:S(2)}) collective-permute-start(bf16[8,7296]{1,0:T(8,128)(2,1)S(1)} %token_rows.1), channel_id=1, source_target_pairs={{0,40},{1,121},{2,42},{3,123},{4,44},{5,125},{6,46},{7,127},{8,32}... | collective-permute-start | bytes 350216 | tf_op jit(solution)/shard_map/ppermute | solution.py:46
  21.2 1.3 collective-permute-done.5
  22.5 7.0 %collective-permute-done.6 = bf16[8,7296]{1,0:T(8,128)(2,1)S(1)} collective-permute-done((bf16[8,7296]{1,0:T(8,128)(2,1)S(1)}, bf16[8,7296]{1,0:T(8,128)(2,1)S(1)}, u32[]{:S(2)}, u32[]{:S(2)}) %collective-permute-start.6) | collective-permute-done | bytes 116768 | tf_op jit(solution)/shard_map/ppermute | solution.py:46
  29.9 5.8 %collective-permute-done.7 = bf16[64,2432]{1,0:T(8,128)(2,1)S(1)} collective-permute-done((bf16[64,2432]{1,0:T(8,128)(2,1)S(1)}, bf16[64,2432]{1,0:T(8,128)(2,1)S(1)}, u32[]{:S(2)}, u32[]{:S(2)}) %collective-permute-start.7) | collective-permute-done | bytes 311328 | tf_op jit(solution)/shard_map/ppermute | solution.py:28
  36.0 5.5 %collective-permute-done.15 = bf16[64,2432]{1,0:T(8,128)(2,1)S(1)} collective-permute-done((bf16[64,2432]{1,0:T(8,128)(2,1)S(1)}, bf16[64,2432]{1,0:T(8,128)(2,1)S(1)}, u32[]{:S(2)}, u32[]{:S(2)}) %collective-permute-start.15) | collective-permute-done | bytes 311328 | tf_op jit(solution)/shard_map/ppermute | solution.py:28
  41.8 3.5 %collective-permute-done.8 = bf16[128,2432]{1,0:T(8,128)(2,1)S(1)} collective-permute-done((bf16[128,2432]{1,0:T(8,128)(2,1)S(1)}, bf16[128,2432]{1,0:T(8,128)(2,1)S(1)}, u32[]{:S(2)}, u32[]{:S(2)}) %collective-permute-start.8) | collective-permute-done | bytes 622624 | tf_op jit(solution)/shard_map/ppermute | solution.py:28
  45.3 1.3 collective-permute-start.16
  46.7 3.9 %collective-permute-done.13 = bf16[128,2432]{1,0:T(8,128)(2,1)S(1)} collective-permute-done((bf16[128,2432]{1,0:T(8,128)(2,1)S(1)}, bf16[128,2432]{1,0:T(8,128)(2,1)S(1)}, u32[]{:S(2)}, u32[]{:S(2)}) %collective-permute-start.13) | collective-permute-done | bytes 622624 | tf_op jit(solution)/shard_map/ppermute | solution.py:28
  51.3 1.2 pad_maximum_fusion.2.x1
  52.4 2.2 %collective-permute-done.16 = bf16[128,2432]{1,0:T(8,128)(2,1)S(1)} collective-permute-done((bf16[128,2432]{1,0:T(8,128)(2,1)S(1)}, bf16[128,2432]{1,0:T(8,128)(2,1)S(1)}, u32[]{:S(2)}, u32[]{:S(2)}) %collective-permute-start.16) | collective-permute-done | bytes 622624 | tf_op jit(solution)/shard_map/ppermute | solution.py:28
  54.7 1.3 collective-permute-start.14
  56.1 1.9 %copy-done.5 = bf16[7168,256]{1,0:T(8,128)(2,1)} copy-done((bf16[7168,256]{1,0:T(8,128)(2,1)}, bf16[7168,256]{1,0:T(8,128)(2,1)S(1)}, u32[]{:S(2)}) %copy-start.5) | copy-done | bytes 3670040
  58.1 2.0 %copy-done.3 = bf16[1,7168,256]{2,1,0:T(8,128)(2,1)S(1)} copy-done((bf16[1,7168,256]{2,1,0:T(8,128)(2,1)S(1)}, bf16[1,7168,256]{2,1,0:T(8,128)(2,1)}, u32[]{:S(2)}) %copy-start.3) | copy-done | bytes 3670040
  60.1 2.0 %copy-done.4 = bf16[1,7168,256]{2,1,0:T(8,128)(2,1)S(1)} copy-done((bf16[1,7168,256]{2,1,0:T(8,128)(2,1)S(1)}, bf16[1,7168,256]{2,1,0:T(8,128)(2,1)}, u32[]{:S(2)}) %copy-start.4) | copy-done | bytes 3670040
  62.2 2.0 %copy-done.6 = bf16[7168,256]{1,0:T(8,128)(2,1)S(1)} copy-done((bf16[7168,256]{1,0:T(8,128)(2,1)S(1)}, bf16[7168,256]{1,0:T(8,128)(2,1)}, u32[]{:S(2)}) %copy-start.6) | copy-done | bytes 3670040
  64.2 2.8 %weights_in.4 = (bf16[7168,256]{1,0:T(8,128)(2,1)S(1)}, bf16[7168,256]{1,0:T(8,128)(2,1)S(1)}, bf16[7168,256]{1,0:T(8,128)(2,1)S(1)}, bf16[7168,256]{1,0:T(8,128)(2,1)S(1)}) custom-call(bf16[7168,256]{1,0:T(8,128)(2,1)S(1)} %bitcast.8, bf16[7168,256]{1,0:T(8,128)(2,1)S(1)} %copy-done.6, bf16[7168,256]{1,0:T(8,128)(2,1)S(1)} %bitcast.10, ...), custom_call_target="tpu_custom_call" | custom-call | flops 8589934592 | tf_op jit(solution)/shard_map/weights_in/pallas_call | solution.py:172
  67.0 2.8 %shard_map.94.part0 = f32[4,256,256]{2,1,0:T(8,128)S(1)} custom-call(bf16[256,2432]{1,0:T(8,128)(2,1)} %collective-permute-done.9.x, bf16[7168,256]{1,0:T(8,128)(2,1)S(1)} %get-tuple-element.11.w0, bf16[7168,256]{1,0:T(8,128)(2,1)S(1)} %get-tuple-element.12.w1, bf16[7168,256]{1,0:T(8,128)(2,1)S(1)} %get-tuple-element.13.w2, ...), custom_call_target="tpu_custom_call" | custom-call | flops 1252524032 | tf_op jit(solution)/shard_map/pallas_call | solution.py:203
  69.8 1.2 collective-permute-done.14.x
  71.1 2.8 %shard_map.95.part1 = f32[4,256,256]{2,1,0:T(8,128)S(1)} custom-call(bf16[256,2432]{1,0:T(8,128)(2,1)} %collective-permute-done.14.x, bf16[7168,256]{1,0:T(8,128)(2,1)S(1)} %get-tuple-element.11.w0, bf16[7168,256]{1,0:T(8,128)(2,1)S(1)} %get-tuple-element.12.w1, bf16[7168,256]{1,0:T(8,128)(2,1)S(1)} %get-tuple-element.13.w2, ...), custom_call_target="tpu_custom_call" | custom-call | flops 1252524032 | tf_op jit(solution)/shard_map/pallas_call | solution.py:203
  74.1 2.7 %shard_map.96.part2 = f32[4,256,256]{2,1,0:T(8,128)S(1)} custom-call(bf16[256,2432]{1,0:T(8,128)(2,1)} %collective-permute-done.17.x.x2, bf16[7168,256]{1,0:T(8,128)(2,1)S(1)} %get-tuple-element.11.w0, bf16[7168,256]{1,0:T(8,128)(2,1)S(1)} %get-tuple-element.12.w1, bf16[7168,256]{1,0:T(8,128)(2,1)S(1)} %get-tuple-element.13.w2, ...), custom_call_target="tpu_custom_call" | custom-call | flops 1252524032 | tf_op jit(solution)/shard_map/pallas_call | solution.py:203
  76.8 5.4 %gate_up_near.1.acc = f32[4,512,256]{2,1,0:T(8,128)S(1)} custom-call(bf16[256,2432]{1,0:T(8,128)(2,1)S(1)} %pad_maximum_fusion.1.x0, bf16[256,2432]{1,0:T(8,128)(2,1)} %pad_maximum_fusion.2.x1, bf16[256,2432]{1,0:T(8,128)(2,1)S(1)} %pad_maximum_fusion.3.x2.near_x2, bf16[7168,256]{1,0:T(8,128)(2,1)S(1)} %get-tuple-element.11.w0, ...), custom_call_target="tpu_custom_call" | custom-call | flops 3757572096 | tf_op jit(solution)/shard_map/gate_up_near/pallas_call | solution.py:191
  82.2 3.2 %weights_in.5 = (bf16[256,7168]{1,0:T(8,128)(2,1)S(1)}, bf16[256,7168]{1,0:T(8,128)(2,1)S(1)}) custom-call(bf16[256,7168]{1,0:T(8,128)(2,1)} %bitcast.3.refs_0_, bf16[256,7168]{1,0:T(8,128)(2,1)} %collective-permute-done.18.refs_1_), custom_call_target="tpu_custom_call" | custom-call | flops 8589934592 | tf_op jit(solution)/shard_map/weights_in/pallas_call | solution.py:172
  85.4 1.8 %hidden.1 = (bf16[512,512]{1,0:T(8,128)(2,1)S(1)}, s32[1,128]{1,0:T(1,128)S(1)}) custom-call(s32[1]{0:T(128)} %bitcast.expert, f32[4,256,256]{2,1,0:T(8,128)S(1)} %shard_map.94.part0, f32[4,256,256]{2,1,0:T(8,128)S(1)} %shard_map.95.part1, f32[4,256,256]{2,1,0:T(8,128)S(1)} %shard_map.96.part2, bf16[256,2432]{1,0:T(8,128)(2,1)S(1)} %pad_maximum_fusion.3.x2.near_x2, ...), custom_call_target="tpu_custom_call" | custom-call | flops 1252524032 | tf_op jit(solution)/shard_map/hidden/pallas_call | solution.py:214
  88.1 0.8 shard_map.100
  89.0 1.1 collective-permute-start.22
  90.1 9.8 %collective-permute-start.35 = (s32[1,128]{1,0:T(1,128)S(1)}, s32[1,128]{1,0:T(1,128)S(1)}, u32[]{:S(2)}, u32[]{:S(2)}) collective-permute-start(s32[1,128]{1,0:T(1,128)S(1)} %get-tuple-element.18), channel_id=1, source_target_pairs={{0,1},{1,0},{2,3},{3,2},{4,5},{5,4},{6,7},{7,6},{8,9},{9,8},{10,11... | collective-permute-start | bytes 1544 | tf_op jit(solution)/shard_map/ppermute | solution.py:54
  100.7 0.8 shard_map.97
  101.6 0.8 shard_map.98
  103.6 1.3 collective-permute-start.26
  105.4 1.2 collective-permute-start.23
  106.6 12.7 %collective-permute-done.19 = bf16[256,2432]{1,0:T(8,128)(2,1)S(1)} collective-permute-done((bf16[256,2432]{1,0:T(8,128)(2,1)S(1)}, bf16[256,2432]{1,0:T(8,128)(2,1)S(1)}, u32[]{:S(2)}, u32[]{:S(2)}) %collective-permute-start.19) | collective-permute-done | bytes 1245216 | tf_op jit(solution)/shard_map/ppermute | solution.py:28
  120.1 6.0 %collective-permute-done.23 = bf16[128,2432]{1,0:T(8,128)(2,1)S(1)} collective-permute-done((bf16[128,2432]{1,0:T(8,128)(2,1)S(1)}, bf16[128,2432]{1,0:T(8,128)(2,1)S(1)}, u32[]{:S(2)}, u32[]{:S(2)}) %collective-permute-start.23) | collective-permute-done | bytes 622624 | tf_op jit(solution)/shard_map/ppermute | solution.py:28
  126.3 2.9 %collective-permute-done.20 = bf16[128,2432]{1,0:T(8,128)(2,1)S(1)} collective-permute-done((bf16[128,2432]{1,0:T(8,128)(2,1)S(1)}, bf16[128,2432]{1,0:T(8,128)(2,1)S(1)}, u32[]{:S(2)}, u32[]{:S(2)}) %collective-permute-start.20) | collective-permute-done | bytes 622624 | tf_op jit(solution)/shard_map/ppermute | solution.py:28
  129.5 3.0 %collective-permute-done.24 = bf16[64,2432]{1,0:T(8,128)(2,1)S(1)} collective-permute-done((bf16[64,2432]{1,0:T(8,128)(2,1)S(1)}, bf16[64,2432]{1,0:T(8,128)(2,1)S(1)}, u32[]{:S(2)}, u32[]{:S(2)}) %collective-permute-start.24) | collective-permute-done | bytes 311328 | tf_op jit(solution)/shard_map/ppermute | solution.py:28
  132.5 2.9 %collective-permute-done.21 = bf16[64,2432]{1,0:T(8,128)(2,1)S(1)} collective-permute-done((bf16[64,2432]{1,0:T(8,128)(2,1)S(1)}, bf16[64,2432]{1,0:T(8,128)(2,1)S(1)}, u32[]{:S(2)}, u32[]{:S(2)}) %collective-permute-start.21) | collective-permute-done | bytes 311328 | tf_op jit(solution)/shard_map/ppermute | solution.py:28
  135.7 2.9 %collective-permute-start.34 = (bf16[8,7168]{1,0:T(8,128)(2,1)S(1)}, bf16[8,7168]{1,0:T(8,128)(2,1)S(1)}, u32[]{:S(2)}, u32[]{:S(2)}) collective-permute-start(bf16[8,7168]{1,0:T(8,128)(2,1)S(1)} %get-tuple-element.25), channel_id=1, source_target_pairs={{0,42},{1,127},{2,40},{3,125},{4,46},{5,123},{6,44},{7,121},{8,34}... | collective-permute-start | bytes 344072 | tf_op jit(solution)/shard_map/ppermute | solution.py:46
  138.6 2.4 %collective-permute-start.33 = (bf16[8,7168]{1,0:T(8,128)(2,1)S(1)}, bf16[8,7168]{1,0:T(8,128)(2,1)S(1)}, u32[]{:S(2)}, u32[]{:S(2)}) collective-permute-start(bf16[8,7168]{1,0:T(8,128)(2,1)S(1)} %get-tuple-element.26), channel_id=1, source_target_pairs={{0,40},{1,121},{2,42},{3,123},{4,44},{5,125},{6,46},{7,127},{8,32}... | collective-permute-start | bytes 344072 | tf_op jit(solution)/shard_map/ppermute | solution.py:46
  141.6 2.0 %collective-permute-start.32 = (bf16[8,7168]{1,0:T(8,128)(2,1)S(1)}, bf16[8,7168]{1,0:T(8,128)(2,1)S(1)}, u32[]{:S(2)}, u32[]{:S(2)}) collective-permute-start(bf16[8,7168]{1,0:T(8,128)(2,1)S(1)} %get-tuple-element.27), channel_id=1, source_target_pairs={{0,10},{1,31},{2,8},{3,29},{4,14},{5,27},{6,12},{7,25},{8,2},{9,23... | collective-permute-start | bytes 344072 | tf_op jit(solution)/shard_map/ppermute | solution.py:46
  143.5 2.4 %collective-permute-start.31 = (bf16[8,7168]{1,0:T(8,128)(2,1)S(1)}, bf16[8,7168]{1,0:T(8,128)(2,1)S(1)}, u32[]{:S(2)}, u32[]{:S(2)}) collective-permute-start(bf16[8,7168]{1,0:T(8,128)(2,1)S(1)} %get-tuple-element.28), channel_id=1, source_target_pairs={{0,8},{1,25},{2,10},{3,27},{4,12},{5,29},{6,14},{7,31},{8,0},{9,17... | collective-permute-start | bytes 344072 | tf_op jit(solution)/shard_map/ppermute | solution.py:46
  145.9 3.1 %collective-permute-start.30 = (bf16[8,7168]{1,0:T(8,128)(2,1)S(1)}, bf16[8,7168]{1,0:T(8,128)(2,1)S(1)}, u32[]{:S(2)}, u32[]{:S(2)}) collective-permute-start(bf16[8,7168]{1,0:T(8,128)(2,1)S(1)} %get-tuple-element.29), channel_id=1, source_target_pairs={{0,34},{1,103},{2,32},{3,101},{4,38},{5,99},{6,36},{7,97},{8,42},{... | collective-permute-start | bytes 344072 | tf_op jit(solution)/shard_map/ppermute | solution.py:46
  149.1 2.0 %collective-permute-start.28 = (bf16[8,7168]{1,0:T(8,128)(2,1)S(1)}, bf16[8,7168]{1,0:T(8,128)(2,1)S(1)}, u32[]{:S(2)}, u32[]{:S(2)}) collective-permute-start(bf16[8,7168]{1,0:T(8,128)(2,1)S(1)} %get-tuple-element.24), channel_id=1, source_target_pairs={{0,2},{1,7},{2,0},{3,5},{4,6},{5,3},{6,4},{7,1},{8,10},{9,15},{10,... | collective-permute-start | bytes 344072 | tf_op jit(solution)/shard_map/ppermute | solution.py:46
  151.2 1.7 %collective-permute-done.30 = bf16[8,7168]{1,0:T(8,128)(2,1)S(1)} collective-permute-done((bf16[8,7168]{1,0:T(8,128)(2,1)S(1)}, bf16[8,7168]{1,0:T(8,128)(2,1)S(1)}, u32[]{:S(2)}, u32[]{:S(2)}) %collective-permute-start.30) | collective-permute-done | bytes 114720 | tf_op jit(solution)/shard_map/ppermute | solution.py:46
  152.9 1.2 collective-permute-done.29
  (90 shorter events, 11.3 us)
Async XLA Ops:
  0.6 0.9 copy-start
  1.5 0.7 copy-start.1
  2.2 0.7 copy-start.2
  3.2 12.0 %collective-permute-start = (bf16[8,7296]{1,0:T(8,128)(2,1)S(1)}, bf16[8,7296]{1,0:T(8,128)(2,1)S(1)}, u32[]{:S(2)}, u32[]{:S(2)}) collective-permute-start(bf16[8,7296]{1,0:T(8,128)(2,1)S(1)} %token_rows.1), channel_id=1, source_target_pairs={{0,2},{1,7},{2,0},{3,5},{4,6},{5,3},{6,4},{7,1},{8,10},{9,15},{10,... | collective-permute-start | bytes 350216 | tf_op jit(solution)/shard_map/ppermute | solution.py:46
  6.5 13.8 %collective-permute-start.1 = (bf16[8,7296]{1,0:T(8,128)(2,1)S(1)}, bf16[8,7296]{1,0:T(8,128)(2,1)S(1)}, u32[]{:S(2)}, u32[]{:S(2)}) collective-permute-start(bf16[8,7296]{1,0:T(8,128)(2,1)S(1)} %token_rows.1), channel_id=1, source_target_pairs={{0,32},{1,97},{2,34},{3,99},{4,36},{5,101},{6,38},{7,103},{8,40},{... | collective-permute-start | bytes 350216 | tf_op jit(solution)/shard_map/ppermute | solution.py:46
  9.3 11.2 %collective-permute-start.2 = (bf16[8,7296]{1,0:T(8,128)(2,1)S(1)}, bf16[8,7296]{1,0:T(8,128)(2,1)S(1)}, u32[]{:S(2)}, u32[]{:S(2)}) collective-permute-start(bf16[8,7296]{1,0:T(8,128)(2,1)S(1)} %token_rows.1), channel_id=1, source_target_pairs={{0,34},{1,103},{2,32},{3,101},{4,38},{5,99},{6,36},{7,97},{8,42},{... | collective-permute-start | bytes 350216 | tf_op jit(solution)/shard_map/ppermute | solution.py:46
  9.3 11.3 %collective-permute-start.3 = (bf16[8,7296]{1,0:T(8,128)(2,1)S(1)}, bf16[8,7296]{1,0:T(8,128)(2,1)S(1)}, u32[]{:S(2)}, u32[]{:S(2)}) collective-permute-start(bf16[8,7296]{1,0:T(8,128)(2,1)S(1)} %token_rows.1), channel_id=1, source_target_pairs={{0,8},{1,25},{2,10},{3,27},{4,12},{5,29},{6,14},{7,31},{8,0},{9,17... | collective-permute-start | bytes 350216 | tf_op jit(solution)/shard_map/ppermute | solution.py:46
  13.0 8.1 %collective-permute-start.4 = (bf16[8,7296]{1,0:T(8,128)(2,1)S(1)}, bf16[8,7296]{1,0:T(8,128)(2,1)S(1)}, u32[]{:S(2)}, u32[]{:S(2)}) collective-permute-start(bf16[8,7296]{1,0:T(8,128)(2,1)S(1)} %token_rows.1), channel_id=1, source_target_pairs={{0,10},{1,31},{2,8},{3,29},{4,14},{5,27},{6,12},{7,25},{8,2},{9,23... | collective-permute-start | bytes 350216 | tf_op jit(solution)/shard_map/ppermute | solution.py:46
  15.2 7.3 %collective-permute-start.5 = (bf16[8,7296]{1,0:T(8,128)(2,1)S(1)}, bf16[8,7296]{1,0:T(8,128)(2,1)S(1)}, u32[]{:S(2)}, u32[]{:S(2)}) collective-permute-start(bf16[8,7296]{1,0:T(8,128)(2,1)S(1)} %token_rows.1), channel_id=1, source_target_pairs={{0,40},{1,121},{2,42},{3,123},{4,44},{5,125},{6,46},{7,127},{8,32}... | collective-permute-start | bytes 350216 | tf_op jit(solution)/shard_map/ppermute | solution.py:46
  20.3 9.2 %collective-permute-start.6 = (bf16[8,7296]{1,0:T(8,128)(2,1)S(1)}, bf16[8,7296]{1,0:T(8,128)(2,1)S(1)}, u32[]{:S(2)}, u32[]{:S(2)}) collective-permute-start(bf16[8,7296]{1,0:T(8,128)(2,1)S(1)} %token_rows.1), channel_id=1, source_target_pairs={{0,42},{1,127},{2,40},{3,125},{4,46},{5,123},{6,44},{7,121},{8,34}... | collective-permute-start | bytes 350216 | tf_op jit(solution)/shard_map/ppermute | solution.py:46
  20.5 35.6 %collective-permute-start.10 = (bf16[7168,256]{1,0:T(8,128)(2,1)}, bf16[7168,256]{1,0:T(8,128)(2,1)S(1)}, u32[]{:S(2)}, u32[]{:S(2)}) collective-permute-start(bf16[7168,256]{1,0:T(8,128)(2,1)} %bitcast.7), channel_id=1, source_target_pairs={{0,1},{1,0},{2,3},{3,2},{4,5},{5,4},{6,7},{7,6},{8,9},{9,8},{10,11... | collective-permute-start | bytes 11010056 | tf_op jit(solution)/shard_map/ppermute | solution.py:54
  20.6 37.5 %collective-permute-start.11 = (bf16[7168,256]{1,0:T(8,128)(2,1)}, bf16[7168,256]{1,0:T(8,128)(2,1)}, u32[]{:S(2)}, u32[]{:S(2)}) collective-permute-start(bf16[7168,256]{1,0:T(8,128)(2,1)} %bitcast.9), channel_id=1, source_target_pairs={{0,1},{1,0},{2,3},{3,2},{4,5},{5,4},{6,7},{7,6},{8,9},{9,8},{10,11... | collective-permute-start | bytes 11010056 | tf_op jit(solution)/shard_map/ppermute | solution.py:54
  29.6 6.1 %collective-permute-start.7 = (bf16[64,2432]{1,0:T(8,128)(2,1)S(1)}, bf16[64,2432]{1,0:T(8,128)(2,1)S(1)}, u32[]{:S(2)}, u32[]{:S(2)}) collective-permute-start(bf16[64,2432]{1,0:T(8,128)(2,1)S(1)} %get-tuple-element.23), channel_id=1, source_target_pairs={{0,6},{1,3},{2,4},{3,1},{4,2},{5,7},{6,0},{7,5},{8,14},{9,11},{10,... | collective-permute-start | bytes 933896 | tf_op jit(solution)/shard_map/ppermute | solution.py:28
  29.7 52.5 %collective-permute-start.18 = (bf16[256,7168]{1,0:T(8,128)(2,1)}, bf16[256,7168]{1,0:T(8,128)(2,1)}, u32[]{:S(2)}, u32[]{:S(2)}) collective-permute-start(bf16[256,7168]{1,0:T(8,128)(2,1)} %bitcast.3.refs_0_), channel_id=1, source_target_pairs={{0,1},{1,0},{2,3},{3,2},{4,5},{5,4},{6,7},{7,6},{8,9},{9,8},{10,11... | collective-permute-start | bytes 11010056 | tf_op jit(solution)/shard_map/ppermute | solution.py:54
  29.8 6.1 %collective-permute-start.12 = (bf16[64,2432]{1,0:T(8,128)(2,1)S(1)}, bf16[64,2432]{1,0:T(8,128)(2,1)S(1)}, u32[]{:S(2)}, u32[]{:S(2)}) collective-permute-start(bf16[64,2432]{1,0:T(8,128)(2,1)S(1)} %get-tuple-element.22), channel_id=1, source_target_pairs={{0,96},{1,33},{32,64},{33,1},{64,32},{65,97},{96,0},{97,65},{2,98}... | collective-permute-start | bytes 933896 | tf_op jit(solution)/shard_map/ppermute | solution.py:28
  35.7 5.7 %collective-permute-start.15 = (bf16[64,2432]{1,0:T(8,128)(2,1)S(1)}, bf16[64,2432]{1,0:T(8,128)(2,1)S(1)}, u32[]{:S(2)}, u32[]{:S(2)}) collective-permute-start(bf16[64,2432]{1,0:T(8,128)(2,1)S(1)} %get-tuple-element.21), channel_id=1, source_target_pairs={{0,24},{1,9},{8,16},{9,1},{16,8},{17,25},{24,0},{25,17},{2,26},{3,... | collective-permute-start | bytes 933896 | tf_op jit(solution)/shard_map/ppermute | solution.py:28
  35.9 9.4 %collective-permute-start.8 = (bf16[128,2432]{1,0:T(8,128)(2,1)S(1)}, bf16[128,2432]{1,0:T(8,128)(2,1)S(1)}, u32[]{:S(2)}, u32[]{:S(2)}) collective-permute-start(bf16[128,2432]{1,0:T(8,128)(2,1)S(1)} %pad_maximum_fusion.4), channel_id=1, source_target_pairs={{0,96},{1,33},{32,64},{33,1},{64,32},{65,97},{96,0},{97,65},{2,98}... | collective-permute-start | bytes 1867784 | tf_op jit(solution)/shard_map/ppermute | solution.py:28
  41.5 9.1 %collective-permute-start.13 = (bf16[128,2432]{1,0:T(8,128)(2,1)S(1)}, bf16[128,2432]{1,0:T(8,128)(2,1)S(1)}, u32[]{:S(2)}, u32[]{:S(2)}) collective-permute-start(bf16[128,2432]{1,0:T(8,128)(2,1)S(1)} %pad_maximum_fusion.5), channel_id=1, source_target_pairs={{0,24},{1,9},{8,16},{9,1},{16,8},{17,25},{24,0},{25,17},{2,26},{3,... | collective-permute-start | bytes 1867784 | tf_op jit(solution)/shard_map/ppermute | solution.py:28
  45.3 9.4 %collective-permute-start.16 = (bf16[128,2432]{1,0:T(8,128)(2,1)S(1)}, bf16[128,2432]{1,0:T(8,128)(2,1)S(1)}, u32[]{:S(2)}, u32[]{:S(2)}) collective-permute-start(bf16[128,2432]{1,0:T(8,128)(2,1)S(1)} %pad_maximum_fusion.6), channel_id=1, source_target_pairs={{0,6},{1,3},{2,4},{3,1},{4,2},{5,7},{6,0},{7,5},{8,14},{9,11},{10,... | collective-permute-start | bytes 1867784 | tf_op jit(solution)/shard_map/ppermute | solution.py:28
  50.6 16.5 %collective-permute-start.9 = (bf16[256,2432]{1,0:T(8,128)(2,1)S(1)}, bf16[256,2432]{1,0:T(8,128)(2,1)}, u32[]{:S(2)}, u32[]{:S(2)}) collective-permute-start(bf16[256,2432]{1,0:T(8,128)(2,1)S(1)} %pad_maximum_fusion.1.x0), channel_id=1, source_target_pairs={{0,24},{1,9},{8,16},{9,1},{16,8},{17,25},{24,0},{25,17},{2,26},{3,... | collective-permute-start | bytes 3735560 | tf_op jit(solution)/shard_map/ppermute | solution.py:28
  54.7 16.4 %collective-permute-start.14 = (bf16[256,2432]{1,0:T(8,128)(2,1)}, bf16[256,2432]{1,0:T(8,128)(2,1)}, u32[]{:S(2)}, u32[]{:S(2)}) collective-permute-start(bf16[256,2432]{1,0:T(8,128)(2,1)} %pad_maximum_fusion.2.x1), channel_id=1, source_target_pairs={{0,6},{1,3},{2,4},{3,1},{4,2},{5,7},{6,0},{7,5},{8,14},{9,11},{10,... | collective-permute-start | bytes 3735560 | tf_op jit(solution)/shard_map/ppermute | solution.py:28
  56.1 1.9 %copy-start.5 = (bf16[7168,256]{1,0:T(8,128)(2,1)}, bf16[7168,256]{1,0:T(8,128)(2,1)S(1)}, u32[]{:S(2)}) copy-start(bf16[7168,256]{1,0:T(8,128)(2,1)S(1)} %collective-permute-done.10.refs_1_) | copy-start | bytes 11010052
  58.0 16.2 %collective-permute-start.17 = (bf16[256,2432]{1,0:T(8,128)(2,1)S(1)}, bf16[256,2432]{1,0:T(8,128)(2,1)}, u32[]{:S(2)}, u32[]{:S(2)}) collective-permute-start(bf16[256,2432]{1,0:T(8,128)(2,1)S(1)} %pad_maximum_fusion.3.x2.near_x2), channel_id=1, source_target_pairs={{0,96},{1,33},{32,64},{33,1},{64,32},{65,97},{96,0},{97,65},{2,98}... | collective-permute-start | bytes 3735560 | tf_op jit(solution)/shard_map/ppermute | solution.py:28
  58.1 2.0 %copy-start.3 = (bf16[1,7168,256]{2,1,0:T(8,128)(2,1)S(1)}, bf16[1,7168,256]{2,1,0:T(8,128)(2,1)}, u32[]{:S(2)}) copy-start(bf16[1,7168,256]{2,1,0:T(8,128)(2,1)} %param.11) | copy-start | bytes 11010052
  60.1 2.0 %copy-start.4 = (bf16[1,7168,256]{2,1,0:T(8,128)(2,1)S(1)}, bf16[1,7168,256]{2,1,0:T(8,128)(2,1)}, u32[]{:S(2)}) copy-start(bf16[1,7168,256]{2,1,0:T(8,128)(2,1)} %param.12) | copy-start | bytes 11010052
  62.2 2.0 %copy-start.6 = (bf16[7168,256]{1,0:T(8,128)(2,1)S(1)}, bf16[7168,256]{1,0:T(8,128)(2,1)}, u32[]{:S(2)}) copy-start(bf16[7168,256]{1,0:T(8,128)(2,1)} %copy-done.5) | copy-start | bytes 11010052
  87.9 15.4 %collective-permute-start.25 = (bf16[256,2304]{1,0:T(8,128)(2,1)S(1)}, bf16[256,2304]{1,0:T(8,128)(2,1)S(1)}, u32[]{:S(2)}, u32[]{:S(2)}) collective-permute-start(bf16[256,2304]{1,0:T(8,128)(2,1)S(1)} %shard_map.102), channel_id=1, source_target_pairs={{0,96},{1,33},{32,64},{33,1},{64,32},{65,97},{96,0},{97,65},{2,98}... | collective-permute-start | bytes 3538952 | tf_op jit(solution)/shard_map/ppermute | solution.py:28
  89.0 16.1 %collective-permute-start.22 = (bf16[256,2432]{1,0:T(8,128)(2,1)S(1)}, bf16[256,2432]{1,0:T(8,128)(2,1)S(1)}, u32[]{:S(2)}, u32[]{:S(2)}) collective-permute-start(bf16[256,2432]{1,0:T(8,128)(2,1)S(1)} %shard_map.100), channel_id=1, source_target_pairs={{0,6},{1,3},{2,4},{3,1},{4,2},{5,7},{6,0},{7,5},{8,14},{9,11},{10,... | collective-permute-start | bytes 3735560 | tf_op jit(solution)/shard_map/ppermute | solution.py:28
  90.1 13.2 %collective-permute-start.35 = (s32[1,128]{1,0:T(1,128)S(1)}, s32[1,128]{1,0:T(1,128)S(1)}, u32[]{:S(2)}, u32[]{:S(2)}) collective-permute-start(s32[1,128]{1,0:T(1,128)S(1)} %get-tuple-element.18), channel_id=1, source_target_pairs={{0,1},{1,0},{2,3},{3,2},{4,5},{5,4},{6,7},{7,6},{8,9},{9,8},{10,11... | collective-permute-start | bytes 1544 | tf_op jit(solution)/shard_map/ppermute | solution.py:54
  103.2 16.1 %collective-permute-start.19 = (bf16[256,2432]{1,0:T(8,128)(2,1)S(1)}, bf16[256,2432]{1,0:T(8,128)(2,1)S(1)}, u32[]{:S(2)}, u32[]{:S(2)}) collective-permute-start(bf16[256,2432]{1,0:T(8,128)(2,1)S(1)} %shard_map.98), channel_id=1, source_target_pairs={{0,24},{1,9},{8,16},{9,1},{16,8},{17,25},{24,0},{25,17},{2,26},{3,... | collective-permute-start | bytes 3735560 | tf_op jit(solution)/shard_map/ppermute | solution.py:28
  103.6 16.2 %collective-permute-start.26 = (bf16[128,2304]{1,0:T(8,128)(2,1)S(1)}, bf16[128,2304]{1,0:T(8,128)(2,1)S(1)}, u32[]{:S(2)}, u32[]{:S(2)}) collective-permute-start(bf16[128,2304]{1,0:T(8,128)(2,1)S(1)} %slice.162), channel_id=1, source_target_pairs={{0,6},{1,3},{2,4},{3,1},{4,2},{5,7},{6,0},{7,5},{8,14},{9,11},{10,... | collective-permute-start | bytes 1769480 | tf_op jit(solution)/shard_map/ppermute | solution.py:28
  105.4 20.6 %collective-permute-start.23 = (bf16[128,2432]{1,0:T(8,128)(2,1)S(1)}, bf16[128,2432]{1,0:T(8,128)(2,1)S(1)}, u32[]{:S(2)}, u32[]{:S(2)}) collective-permute-start(bf16[128,2432]{1,0:T(8,128)(2,1)S(1)} %slice.160), channel_id=1, source_target_pairs={{0,24},{1,9},{8,16},{9,1},{16,8},{17,25},{24,0},{25,17},{2,26},{3,... | collective-permute-start | bytes 1867784 | tf_op jit(solution)/shard_map/ppermute | solution.py:28
  119.7 9.5 %collective-permute-start.20 = (bf16[128,2432]{1,0:T(8,128)(2,1)S(1)}, bf16[128,2432]{1,0:T(8,128)(2,1)S(1)}, u32[]{:S(2)}, u32[]{:S(2)}) collective-permute-start(bf16[128,2432]{1,0:T(8,128)(2,1)S(1)} %slice.161), channel_id=1, source_target_pairs={{0,96},{1,33},{32,64},{33,1},{64,32},{65,97},{96,0},{97,65},{2,98}... | collective-permute-start | bytes 1867784 | tf_op jit(solution)/shard_map/ppermute | solution.py:28
  120.0 9.4 %collective-permute-start.27 = (bf16[64,2304]{1,0:T(8,128)(2,1)S(1)}, bf16[64,2304]{1,0:T(8,128)(2,1)S(1)}, u32[]{:S(2)}, u32[]{:S(2)}) collective-permute-start(bf16[64,2304]{1,0:T(8,128)(2,1)S(1)} %slice.165), channel_id=1, source_target_pairs={{0,24},{1,9},{8,16},{9,1},{16,8},{17,25},{24,0},{25,17},{2,26},{3,... | collective-permute-start | bytes 884744 | tf_op jit(solution)/shard_map/ppermute | solution.py:28
  126.2 6.3 %collective-permute-start.24 = (bf16[64,2432]{1,0:T(8,128)(2,1)S(1)}, bf16[64,2432]{1,0:T(8,128)(2,1)S(1)}, u32[]{:S(2)}, u32[]{:S(2)}) collective-permute-start(bf16[64,2432]{1,0:T(8,128)(2,1)S(1)} %slice.163), channel_id=1, source_target_pairs={{0,96},{1,33},{32,64},{33,1},{64,32},{65,97},{96,0},{97,65},{2,98}... | collective-permute-start | bytes 933896 | tf_op jit(solution)/shard_map/ppermute | solution.py:28
  129.3 6.1 %collective-permute-start.21 = (bf16[64,2432]{1,0:T(8,128)(2,1)S(1)}, bf16[64,2432]{1,0:T(8,128)(2,1)S(1)}, u32[]{:S(2)}, u32[]{:S(2)}) collective-permute-start(bf16[64,2432]{1,0:T(8,128)(2,1)S(1)} %slice.164), channel_id=1, source_target_pairs={{0,6},{1,3},{2,4},{3,1},{4,2},{5,7},{6,0},{7,5},{8,14},{9,11},{10,... | collective-permute-start | bytes 933896 | tf_op jit(solution)/shard_map/ppermute | solution.py:28
  135.5 5.5 %copy-start.7 = (f32[16]{0:T(128)S(1)}, f32[16]{0:T(128)}, u32[]{:S(2)}) copy-start(f32[16]{0:T(128)} %param.14) | copy-start | bytes 196
  135.7 13.4 %collective-permute-start.34 = (bf16[8,7168]{1,0:T(8,128)(2,1)S(1)}, bf16[8,7168]{1,0:T(8,128)(2,1)S(1)}, u32[]{:S(2)}, u32[]{:S(2)}) collective-permute-start(bf16[8,7168]{1,0:T(8,128)(2,1)S(1)} %get-tuple-element.25), channel_id=1, source_target_pairs={{0,42},{1,127},{2,40},{3,125},{4,46},{5,123},{6,44},{7,121},{8,34}... | collective-permute-start | bytes 344072 | tf_op jit(solution)/shard_map/ppermute | solution.py:46
  138.6 10.5 %collective-permute-start.33 = (bf16[8,7168]{1,0:T(8,128)(2,1)S(1)}, bf16[8,7168]{1,0:T(8,128)(2,1)S(1)}, u32[]{:S(2)}, u32[]{:S(2)}) collective-permute-start(bf16[8,7168]{1,0:T(8,128)(2,1)S(1)} %get-tuple-element.26), channel_id=1, source_target_pairs={{0,40},{1,121},{2,42},{3,123},{4,44},{5,125},{6,46},{7,127},{8,32}... | collective-permute-start | bytes 344072 | tf_op jit(solution)/shard_map/ppermute | solution.py:46
  141.6 9.6 %collective-permute-start.32 = (bf16[8,7168]{1,0:T(8,128)(2,1)S(1)}, bf16[8,7168]{1,0:T(8,128)(2,1)S(1)}, u32[]{:S(2)}, u32[]{:S(2)}) collective-permute-start(bf16[8,7168]{1,0:T(8,128)(2,1)S(1)} %get-tuple-element.27), channel_id=1, source_target_pairs={{0,10},{1,31},{2,8},{3,29},{4,14},{5,27},{6,12},{7,25},{8,2},{9,23... | collective-permute-start | bytes 344072 | tf_op jit(solution)/shard_map/ppermute | solution.py:46
  143.5 7.7 %collective-permute-start.31 = (bf16[8,7168]{1,0:T(8,128)(2,1)S(1)}, bf16[8,7168]{1,0:T(8,128)(2,1)S(1)}, u32[]{:S(2)}, u32[]{:S(2)}) collective-permute-start(bf16[8,7168]{1,0:T(8,128)(2,1)S(1)} %get-tuple-element.28), channel_id=1, source_target_pairs={{0,8},{1,25},{2,10},{3,27},{4,12},{5,29},{6,14},{7,31},{8,0},{9,17... | collective-permute-start | bytes 344072 | tf_op jit(solution)/shard_map/ppermute | solution.py:46
  145.9 7.0 %collective-permute-start.30 = (bf16[8,7168]{1,0:T(8,128)(2,1)S(1)}, bf16[8,7168]{1,0:T(8,128)(2,1)S(1)}, u32[]{:S(2)}, u32[]{:S(2)}) collective-permute-start(bf16[8,7168]{1,0:T(8,128)(2,1)S(1)} %get-tuple-element.29), channel_id=1, source_target_pairs={{0,34},{1,103},{2,32},{3,101},{4,38},{5,99},{6,36},{7,97},{8,42},{... | collective-permute-start | bytes 344072 | tf_op jit(solution)/shard_map/ppermute | solution.py:46
  149.0 5.1 %collective-permute-start.29 = (bf16[8,7168]{1,0:T(8,128)(2,1)S(1)}, bf16[8,7168]{1,0:T(8,128)(2,1)S(1)}, u32[]{:S(2)}, u32[]{:S(2)}) collective-permute-start(bf16[8,7168]{1,0:T(8,128)(2,1)S(1)} %get-tuple-element.30), channel_id=1, source_target_pairs={{0,32},{1,97},{2,34},{3,99},{4,36},{5,101},{6,38},{7,103},{8,40},{... | collective-permute-start | bytes 344072 | tf_op jit(solution)/shard_map/ppermute | solution.py:46
  149.1 5.3 %collective-permute-start.28 = (bf16[8,7168]{1,0:T(8,128)(2,1)S(1)}, bf16[8,7168]{1,0:T(8,128)(2,1)S(1)}, u32[]{:S(2)}, u32[]{:S(2)}) collective-permute-start(bf16[8,7168]{1,0:T(8,128)(2,1)S(1)} %get-tuple-element.24), channel_id=1, source_target_pairs={{0,2},{1,7},{2,0},{3,5},{4,6},{5,3},{6,4},{7,1},{8,10},{9,15},{10,... | collective-permute-start | bytes 344072 | tf_op jit(solution)/shard_map/ppermute | solution.py:46

commit v4 on v3

--- a/solution.py
+++ b/solution.py
@@ -23,13 +23,13 @@
 
 
 def exchange(value, axis):
-    masks = (3, 1)
+    masks = (1, 3)
     pairs = [(2 * i + c, 2 * (i ^ masks[c]) + c) for i in range(4) for c in range(2)]
     return lax.ppermute(value, (axis, "gz_1"), pairs)
 
 
 def direct(value, hops):
-    masks = (1, 3)
+    masks = (3, 1)
     pairs = []
     for a in range(4):
         for b in range(4):
@@ -261,8 +261,9 @@
     gate_far = partner(gate_own)
     up_far = partner(up_own)
     down_far = partner(down_own)
-    gate_own, gate_far, up_own, up_far = in_vmem(gate_own, gate_far, up_own, up_far)
-    down_own, down_far = in_vmem(down_own, down_far)
+    gate_own, up_own, down_own = in_vmem(gate_own, up_own, down_own)
+    gate_far, up_far = in_vmem(gate_far, up_far)
+    (down_far,) = in_vmem(down_far)
     gate_ups = (gate_own, gate_far, up_own, up_far)
 
     rows = rows_of(tokens, expert_ids, route_weight, experts)

time: 157 us -> 162 us (1.032)
  the two profiles are of different devices: /device:TPU:1 before, /device:TPU:0 now
where the time goes in v4:
time: 162 us
  waiting for transfers between devices  69.2 us (43%)
  starting transfers between devices  45.1 us (28%)
  Pallas kernels  27.8 us (17%)
  local copies, waits for them, and re-layouts  14.5 us (9%)
  other arithmetic  4.24 us (3%)
    ppermute x18, waiting for transfers between devices, exchange(): return lax.ppermute(value, (axis, 'gz_1'), pairs)  56 us
    ppermute x14, starting transfers between devices, direct(): return lax.ppermute(value, AXES, pairs)  34.9 us
    unnamed x35, local copies, waits for them, and re-layouts  14 us
    ppermute x14, waiting for transfers between devices, direct(): return lax.ppermute(value, AXES, pairs)  13.2 us
    pallas_call x3, Pallas kernels, gate_up_far_part(): pl.pallas_call(functools.partial(far_part_kernel, colour), out_shape=jax....  8.28 us
    ppermute x18, starting transfers between devices, exchange(): return lax.ppermute(value, (axis, 'gz_1'), pairs)  7.57 us
    pallas_call x3, Pallas kernels, in_vmem(): pl.pallas_call(load_kernel, out_shape=tuple((jax.ShapeDtypeStruct(a.shape...  7.05 us
    pallas_call x1, Pallas kernels, gate_up_near(): pl.pallas_call(near_kernel, out_shape=jax.ShapeDtypeStruct((4, 512, 256),...  5.38 us
  transfers between devices with their start and end apart: 36, of which 18 were waited for; matrix products, arithmetic and copies ran while one was open for 2% of the time, Pallas kernels for 14%

profile of v4, /device:TPU:0, one launch (start us, length us, event | category | flops | bytes accessed | tf_op | source)
XLA Modules:
  0.0 161.9 jit_solution(17401466265419693492)
XLA Ops:
  0.6 0.9 copy-done.6
  3.2 2.9 %collective-permute-start = (bf16[8,7296]{1,0:T(8,128)(2,1)S(1)}, bf16[8,7296]{1,0:T(8,128)(2,1)S(1)}, u32[]{:S(2)}, u32[]{:S(2)}) collective-permute-start(bf16[8,7296]{1,0:T(8,128)(2,1)S(1)} %token_rows.1), channel_id=1, source_target_pairs={{0,6},{1,3},{2,4},{3,1},{4,2},{5,7},{6,0},{7,5},{8,14},{9,11},{10,... | collective-permute-start | bytes 350216 | tf_op jit(solution)/shard_map/ppermute | solution.py:46
  6.1 3.0 %collective-permute-start.1 = (bf16[8,7296]{1,0:T(8,128)(2,1)S(1)}, bf16[8,7296]{1,0:T(8,128)(2,1)S(1)}, u32[]{:S(2)}, u32[]{:S(2)}) collective-permute-start(bf16[8,7296]{1,0:T(8,128)(2,1)S(1)} %token_rows.1), channel_id=1, source_target_pairs={{0,96},{1,33},{2,98},{3,35},{4,100},{5,37},{6,102},{7,39},{8,104},... | collective-permute-start | bytes 350216 | tf_op jit(solution)/shard_map/ppermute | solution.py:46
  9.2 4.1 %collective-permute-start.3 = (bf16[8,7296]{1,0:T(8,128)(2,1)S(1)}, bf16[8,7296]{1,0:T(8,128)(2,1)S(1)}, u32[]{:S(2)}, u32[]{:S(2)}) collective-permute-start(bf16[8,7296]{1,0:T(8,128)(2,1)S(1)} %token_rows.1), channel_id=1, source_target_pairs={{0,24},{1,9},{2,26},{3,11},{4,28},{5,13},{6,30},{7,15},{8,16},{9,1... | collective-permute-start | bytes 350216 | tf_op jit(solution)/shard_map/ppermute | solution.py:46
  13.3 2.2 %collective-permute-start.4 = (bf16[8,7296]{1,0:T(8,128)(2,1)S(1)}, bf16[8,7296]{1,0:T(8,128)(2,1)S(1)}, u32[]{:S(2)}, u32[]{:S(2)}) collective-permute-start(bf16[8,7296]{1,0:T(8,128)(2,1)S(1)} %token_rows.1), channel_id=1, source_target_pairs={{0,30},{1,11},{2,28},{3,9},{4,26},{5,15},{6,24},{7,13},{8,22},{9,3... | collective-permute-start | bytes 350216 | tf_op jit(solution)/shard_map/ppermute | solution.py:46
  15.5 5.8 %collective-permute-start.5 = (bf16[8,7296]{1,0:T(8,128)(2,1)S(1)}, bf16[8,7296]{1,0:T(8,128)(2,1)S(1)}, u32[]{:S(2)}, u32[]{:S(2)}) collective-permute-start(bf16[8,7296]{1,0:T(8,128)(2,1)S(1)} %token_rows.1), channel_id=1, source_target_pairs={{0,120},{1,41},{2,122},{3,43},{4,124},{5,45},{6,126},{7,47},{8,112... | collective-permute-start | bytes 350216 | tf_op jit(solution)/shard_map/ppermute | solution.py:46
  22.2 1.9 %collective-permute-done.5 = bf16[8,7296]{1,0:T(8,128)(2,1)S(1)} collective-permute-done((bf16[8,7296]{1,0:T(8,128)(2,1)S(1)}, bf16[8,7296]{1,0:T(8,128)(2,1)S(1)}, u32[]{:S(2)}, u32[]{:S(2)}) %collective-permute-start.5) | collective-permute-done | bytes 116768 | tf_op jit(solution)/shard_map/ppermute | solution.py:46
  24.1 8.3 %collective-permute-done.6 = bf16[8,7296]{1,0:T(8,128)(2,1)S(1)} collective-permute-done((bf16[8,7296]{1,0:T(8,128)(2,1)S(1)}, bf16[8,7296]{1,0:T(8,128)(2,1)S(1)}, u32[]{:S(2)}, u32[]{:S(2)}) %collective-permute-start.6) | collective-permute-done | bytes 116768 | tf_op jit(solution)/shard_map/ppermute | solution.py:46
  32.8 6.7 %collective-permute-done.7 = bf16[64,2432]{1,0:T(8,128)(2,1)S(1)} collective-permute-done((bf16[64,2432]{1,0:T(8,128)(2,1)S(1)}, bf16[64,2432]{1,0:T(8,128)(2,1)S(1)}, u32[]{:S(2)}, u32[]{:S(2)}) %collective-permute-start.7) | collective-permute-done | bytes 311328 | tf_op jit(solution)/shard_map/ppermute | solution.py:28
  39.7 6.7 %collective-permute-done.15 = bf16[64,2432]{1,0:T(8,128)(2,1)S(1)} collective-permute-done((bf16[64,2432]{1,0:T(8,128)(2,1)S(1)}, bf16[64,2432]{1,0:T(8,128)(2,1)S(1)}, u32[]{:S(2)}, u32[]{:S(2)}) %collective-permute-start.15) | collective-permute-done | bytes 311328 | tf_op jit(solution)/shard_map/ppermute | solution.py:28
  46.4 3.5 %collective-permute-done.8 = bf16[128,2432]{1,0:T(8,128)(2,1)S(1)} collective-permute-done((bf16[128,2432]{1,0:T(8,128)(2,1)S(1)}, bf16[128,2432]{1,0:T(8,128)(2,1)S(1)}, u32[]{:S(2)}, u32[]{:S(2)}) %collective-permute-start.8) | collective-permute-done | bytes 622624 | tf_op jit(solution)/shard_map/ppermute | solution.py:28
  49.9 1.8 %collective-permute-start.16 = (bf16[128,2432]{1,0:T(8,128)(2,1)S(1)}, bf16[128,2432]{1,0:T(8,128)(2,1)S(1)}, u32[]{:S(2)}, u32[]{:S(2)}) collective-permute-start(bf16[128,2432]{1,0:T(8,128)(2,1)S(1)} %pad_maximum_fusion.6), channel_id=1, source_target_pairs={{0,2},{1,7},{2,0},{3,5},{4,6},{5,3},{6,4},{7,1},{8,10},{9,15},{10,... | collective-permute-start | bytes 1867784 | tf_op jit(solution)/shard_map/ppermute | solution.py:28
  51.8 4.8 %collective-permute-done.13 = bf16[128,2432]{1,0:T(8,128)(2,1)S(1)} collective-permute-done((bf16[128,2432]{1,0:T(8,128)(2,1)S(1)}, bf16[128,2432]{1,0:T(8,128)(2,1)S(1)}, u32[]{:S(2)}, u32[]{:S(2)}) %collective-permute-start.13) | collective-permute-done | bytes 622624 | tf_op jit(solution)/shard_map/ppermute | solution.py:28
  56.6 1.1 pad_maximum_fusion.2.x1
  57.7 2.4 %collective-permute-done.16 = bf16[128,2432]{1,0:T(8,128)(2,1)S(1)} collective-permute-done((bf16[128,2432]{1,0:T(8,128)(2,1)S(1)}, bf16[128,2432]{1,0:T(8,128)(2,1)S(1)}, u32[]{:S(2)}, u32[]{:S(2)}) %collective-permute-start.16) | collective-permute-done | bytes 622624 | tf_op jit(solution)/shard_map/ppermute | solution.py:28
  60.1 1.8 %collective-permute-start.14 = (bf16[256,2432]{1,0:T(8,128)(2,1)}, bf16[256,2432]{1,0:T(8,128)(2,1)}, u32[]{:S(2)}, u32[]{:S(2)}) collective-permute-start(bf16[256,2432]{1,0:T(8,128)(2,1)} %pad_maximum_fusion.2.x1), channel_id=1, source_target_pairs={{0,2},{1,7},{2,0},{3,5},{4,6},{5,3},{6,4},{7,1},{8,10},{9,15},{10,... | collective-permute-start | bytes 3735560 | tf_op jit(solution)/shard_map/ppermute | solution.py:28
  62.1 1.9 %copy-done.11 = bf16[7168,256]{1,0:T(8,128)(2,1)} copy-done((bf16[7168,256]{1,0:T(8,128)(2,1)}, bf16[7168,256]{1,0:T(8,128)(2,1)S(1)}, u32[]{:S(2)}) %copy-start.11) | copy-done | bytes 3670040
  63.9 2.6 %weights_in.5 = (bf16[7168,256]{1,0:T(8,128)(2,1)S(1)}, bf16[7168,256]{1,0:T(8,128)(2,1)S(1)}, bf16[256,7168]{1,0:T(8,128)(2,1)S(1)}) custom-call(bf16[7168,256]{1,0:T(8,128)(2,1)S(1)} %bitcast.8, bf16[7168,256]{1,0:T(8,128)(2,1)S(1)} %bitcast.10, bf16[256,7168]{1,0:T(8,128)(2,1)} %bitcast.3.refs_2_), custom_call_target="tpu_custom_call" | custom-call | flops 8589934592 | tf_op jit(solution)/shard_map/weights_in/pallas_call | solution.py:172
  66.5 1.8 %copy-done = bf16[256,7168]{1,0:T(8,128)(2,1)} copy-done((bf16[256,7168]{1,0:T(8,128)(2,1)}, bf16[256,7168]{1,0:T(8,128)(2,1)S(1)}, u32[]{:S(2)}) %copy-start) | copy-done | bytes 3670040
  68.3 1.8 %copy-done.2 = bf16[7168,256]{1,0:T(8,128)(2,1)} copy-done((bf16[7168,256]{1,0:T(8,128)(2,1)}, bf16[7168,256]{1,0:T(8,128)(2,1)S(1)}, u32[]{:S(2)}) %copy-start.2) | copy-done | bytes 3670040
  70.1 1.9 %copy-done.4 = bf16[7168,256]{1,0:T(8,128)(2,1)} copy-done((bf16[7168,256]{1,0:T(8,128)(2,1)}, bf16[7168,256]{1,0:T(8,128)(2,1)S(1)}, u32[]{:S(2)}) %copy-start.4) | copy-done | bytes 3670040
  72.0 2.0 %copy-done.12 = bf16[7168,256]{1,0:T(8,128)(2,1)S(1)} copy-done((bf16[7168,256]{1,0:T(8,128)(2,1)S(1)}, bf16[7168,256]{1,0:T(8,128)(2,1)}, u32[]{:S(2)}) %copy-start.12) | copy-done | bytes 3670040
  74.0 2.4 %weights_in.6 = (bf16[7168,256]{1,0:T(8,128)(2,1)S(1)}, bf16[7168,256]{1,0:T(8,128)(2,1)S(1)}) custom-call(bf16[7168,256]{1,0:T(8,128)(2,1)S(1)} %copy-done.12, bf16[7168,256]{1,0:T(8,128)(2,1)} %collective-permute-done.11.refs_1_), custom_call_target="tpu_custom_call" | custom-call | flops 8589934592 | tf_op jit(solution)/shard_map/weights_in/pallas_call | solution.py:172
  77.1 1.1 copy-done.5
  78.3 2.8 %shard_map.94.part0 = f32[4,256,256]{2,1,0:T(8,128)S(1)} custom-call(bf16[256,2432]{1,0:T(8,128)(2,1)} %collective-permute-done.9.x, bf16[7168,256]{1,0:T(8,128)(2,1)S(1)} %copy-done.3, bf16[7168,256]{1,0:T(8,128)(2,1)S(1)} %get-tuple-element.11.w1, bf16[7168,256]{1,0:T(8,128)(2,1)S(1)} %copy-done.5, bf16[7168,256]{1,0:T(8,128)(2,1)S(1)} %get-tuple-element.13.w3), custom_call_target="tpu_custom_call" | custom-call | flops 1252524032 | tf_op jit(solution)/shard_map/pallas_call | solution.py:203
  81.1 2.8 %shard_map.95.part1 = f32[4,256,256]{2,1,0:T(8,128)S(1)} custom-call(bf16[256,2432]{1,0:T(8,128)(2,1)} %collective-permute-done.14.x, bf16[7168,256]{1,0:T(8,128)(2,1)S(1)} %copy-done.3, bf16[7168,256]{1,0:T(8,128)(2,1)S(1)} %get-tuple-element.11.w1, bf16[7168,256]{1,0:T(8,128)(2,1)S(1)} %copy-done.5, bf16[7168,256]{1,0:T(8,128)(2,1)S(1)} %get-tuple-element.13.w3), custom_call_target="tpu_custom_call" | custom-call | flops 1252524032 | tf_op jit(solution)/shard_map/pallas_call | solution.py:203
  83.9 2.7 %shard_map.96.part2 = f32[4,256,256]{2,1,0:T(8,128)S(1)} custom-call(bf16[256,2432]{1,0:T(8,128)(2,1)} %collective-permute-done.17.x.x2, bf16[7168,256]{1,0:T(8,128)(2,1)S(1)} %copy-done.3, bf16[7168,256]{1,0:T(8,128)(2,1)S(1)} %get-tuple-element.11.w1, bf16[7168,256]{1,0:T(8,128)(2,1)S(1)} %copy-done.5, bf16[7168,256]{1,0:T(8,128)(2,1)S(1)} %get-tuple-element.13.w3), custom_call_target="tpu_custom_call" | custom-call | flops 1252524032 | tf_op jit(solution)/shard_map/pallas_call | solution.py:203
  86.6 5.4 %gate_up_near.1.acc = f32[4,512,256]{2,1,0:T(8,128)S(1)} custom-call(bf16[256,2432]{1,0:T(8,128)(2,1)S(1)} %pad_maximum_fusion.1.x0, bf16[256,2432]{1,0:T(8,128)(2,1)} %pad_maximum_fusion.2.x1, bf16[256,2432]{1,0:T(8,128)(2,1)S(1)} %pad_maximum_fusion.3.x2.near_x2, bf16[7168,256]{1,0:T(8,128)(2,1)S(1)} %copy-done.3, ...), custom_call_target="tpu_custom_call" | custom-call | flops 3757572096 | tf_op jit(solution)/shard_map/gate_up_near/pallas_call | solution.py:191
  92.0 2.0 %weights_in.7.other = bf16[256,7168]{1,0:T(8,128)(2,1)S(1)} custom-call(bf16[256,7168]{1,0:T(8,128)(2,1)} %collective-permute-done.18.refs_0_), custom_call_target="tpu_custom_call" | custom-call | flops 8589934592 | tf_op jit(solution)/shard_map/weights_in/pallas_call | solution.py:172
  94.0 1.9 %hidden.1 = (bf16[512,512]{1,0:T(8,128)(2,1)S(1)}, s32[1,128]{1,0:T(1,128)S(1)}) custom-call(s32[1]{0:T(128)} %bitcast.expert, f32[4,256,256]{2,1,0:T(8,128)S(1)} %shard_map.94.part0, f32[4,256,256]{2,1,0:T(8,128)S(1)} %shard_map.95.part1, f32[4,256,256]{2,1,0:T(8,128)S(1)} %shard_map.96.part2, bf16[256,2432]{1,0:T(8,128)(2,1)S(1)} %pad_maximum_fusion.3.x2.near_x2, ...), custom_call_target="tpu_custom_call" | custom-call | flops 1252524032 | tf_op jit(solution)/shard_map/hidden/pallas_call | solution.py:214
  97.2 2.1 %collective-permute-start.25 = (bf16[256,2304]{1,0:T(8,128)(2,1)S(1)}, bf16[256,2304]{1,0:T(8,128)(2,1)S(1)}, u32[]{:S(2)}, u32[]{:S(2)}) collective-permute-start(bf16[256,2304]{1,0:T(8,128)(2,1)S(1)} %shard_map.102), channel_id=1, source_target_pairs={{0,32},{1,97},{32,0},{33,65},{64,96},{65,33},{96,64},{97,1},{2,34}... | collective-permute-start | bytes 3538952 | tf_op jit(solution)/shard_map/ppermute | solution.py:28
  99.3 0.8 shard_map.100
  100.5 1.9 %collective-permute-start.35 = (s32[1,128]{1,0:T(1,128)S(1)}, s32[1,128]{1,0:T(1,128)S(1)}, u32[]{:S(2)}, u32[]{:S(2)}) collective-permute-start(s32[1,128]{1,0:T(1,128)S(1)} %get-tuple-element.16), channel_id=1, source_target_pairs={{0,1},{1,0},{2,3},{3,2},{4,5},{5,4},{6,7},{7,6},{8,9},{9,8},{10,11... | collective-permute-start | bytes 1544 | tf_op jit(solution)/shard_map/ppermute | solution.py:54
  103.2 0.8 shard_map.97
  105.9 7.7 %collective-permute-done.25 = bf16[256,2304]{1,0:T(8,128)(2,1)S(1)} collective-permute-done((bf16[256,2304]{1,0:T(8,128)(2,1)S(1)}, bf16[256,2304]{1,0:T(8,128)(2,1)S(1)}, u32[]{:S(2)}, u32[]{:S(2)}) %collective-permute-start.25) | collective-permute-done | bytes 1179680 | tf_op jit(solution)/shard_map/ppermute | solution.py:28
  114.3 2.9 %collective-permute-done.22 = bf16[256,2432]{1,0:T(8,128)(2,1)S(1)} collective-permute-done((bf16[256,2432]{1,0:T(8,128)(2,1)S(1)}, bf16[256,2432]{1,0:T(8,128)(2,1)S(1)}, u32[]{:S(2)}, u32[]{:S(2)}) %collective-permute-start.22) | collective-permute-done | bytes 1245216 | tf_op jit(solution)/shard_map/ppermute | solution.py:28
  117.7 5.0 %collective-permute-done.19 = bf16[256,2432]{1,0:T(8,128)(2,1)S(1)} collective-permute-done((bf16[256,2432]{1,0:T(8,128)(2,1)S(1)}, bf16[256,2432]{1,0:T(8,128)(2,1)S(1)}, u32[]{:S(2)}, u32[]{:S(2)}) %collective-permute-start.19) | collective-permute-done | bytes 1245216 | tf_op jit(solution)/shard_map/ppermute | solution.py:28
  124.3 5.0 %collective-permute-done.23 = bf16[128,2432]{1,0:T(8,128)(2,1)S(1)} collective-permute-done((bf16[128,2432]{1,0:T(8,128)(2,1)S(1)}, bf16[128,2432]{1,0:T(8,128)(2,1)S(1)}, u32[]{:S(2)}, u32[]{:S(2)}) %collective-permute-start.23) | collective-permute-done | bytes 622624 | tf_op jit(solution)/shard_map/ppermute | solution.py:28
  129.6 3.7 %collective-permute-done.20 = bf16[128,2432]{1,0:T(8,128)(2,1)S(1)} collective-permute-done((bf16[128,2432]{1,0:T(8,128)(2,1)S(1)}, bf16[128,2432]{1,0:T(8,128)(2,1)S(1)}, u32[]{:S(2)}, u32[]{:S(2)}) %collective-permute-start.20) | collective-permute-done | bytes 622624 | tf_op jit(solution)/shard_map/ppermute | solution.py:28
  133.7 3.0 %collective-permute-done.24 = bf16[64,2432]{1,0:T(8,128)(2,1)S(1)} collective-permute-done((bf16[64,2432]{1,0:T(8,128)(2,1)S(1)}, bf16[64,2432]{1,0:T(8,128)(2,1)S(1)}, u32[]{:S(2)}, u32[]{:S(2)}) %collective-permute-start.24) | collective-permute-done | bytes 311328 | tf_op jit(solution)/shard_map/ppermute | solution.py:28
  136.7 3.8 %collective-permute-done.21 = bf16[64,2432]{1,0:T(8,128)(2,1)S(1)} collective-permute-done((bf16[64,2432]{1,0:T(8,128)(2,1)S(1)}, bf16[64,2432]{1,0:T(8,128)(2,1)S(1)}, u32[]{:S(2)}, u32[]{:S(2)}) %collective-permute-start.21) | collective-permute-done | bytes 311328 | tf_op jit(solution)/shard_map/ppermute | solution.py:28
  140.8 5.1 %collective-permute-start.33 = (bf16[8,7168]{1,0:T(8,128)(2,1)S(1)}, bf16[8,7168]{1,0:T(8,128)(2,1)S(1)}, u32[]{:S(2)}, u32[]{:S(2)}) collective-permute-start(bf16[8,7168]{1,0:T(8,128)(2,1)S(1)} %get-tuple-element.24), channel_id=1, source_target_pairs={{0,120},{1,41},{2,122},{3,43},{4,124},{5,45},{6,126},{7,47},{8,112... | collective-permute-start | bytes 344072 | tf_op jit(solution)/shard_map/ppermute | solution.py:46
  146.6 2.2 %collective-permute-start.32 = (bf16[8,7168]{1,0:T(8,128)(2,1)S(1)}, bf16[8,7168]{1,0:T(8,128)(2,1)S(1)}, u32[]{:S(2)}, u32[]{:S(2)}) collective-permute-start(bf16[8,7168]{1,0:T(8,128)(2,1)S(1)} %get-tuple-element.25), channel_id=1, source_target_pairs={{0,30},{1,11},{2,28},{3,9},{4,26},{5,15},{6,24},{7,13},{8,22},{9,3... | collective-permute-start | bytes 344072 | tf_op jit(solution)/shard_map/ppermute | solution.py:46
  148.8 3.3 %collective-permute-start.31 = (bf16[8,7168]{1,0:T(8,128)(2,1)S(1)}, bf16[8,7168]{1,0:T(8,128)(2,1)S(1)}, u32[]{:S(2)}, u32[]{:S(2)}) collective-permute-start(bf16[8,7168]{1,0:T(8,128)(2,1)S(1)} %get-tuple-element.26), channel_id=1, source_target_pairs={{0,24},{1,9},{2,26},{3,11},{4,28},{5,13},{6,30},{7,15},{8,16},{9,1... | collective-permute-start | bytes 344072 | tf_op jit(solution)/shard_map/ppermute | solution.py:46
  152.2 2.9 %collective-permute-start.29 = (bf16[8,7168]{1,0:T(8,128)(2,1)S(1)}, bf16[8,7168]{1,0:T(8,128)(2,1)S(1)}, u32[]{:S(2)}, u32[]{:S(2)}) collective-permute-start(bf16[8,7168]{1,0:T(8,128)(2,1)S(1)} %get-tuple-element.28), channel_id=1, source_target_pairs={{0,96},{1,33},{2,98},{3,35},{4,100},{5,37},{6,102},{7,39},{8,104},... | collective-permute-start | bytes 344072 | tf_op jit(solution)/shard_map/ppermute | solution.py:46
  155.2 2.9 %collective-permute-start.28 = (bf16[8,7168]{1,0:T(8,128)(2,1)S(1)}, bf16[8,7168]{1,0:T(8,128)(2,1)S(1)}, u32[]{:S(2)}, u32[]{:S(2)}) collective-permute-start(bf16[8,7168]{1,0:T(8,128)(2,1)S(1)} %get-tuple-element.22), channel_id=1, source_target_pairs={{0,6},{1,3},{2,4},{3,1},{4,2},{5,7},{6,0},{7,5},{8,14},{9,11},{10,... | collective-permute-start | bytes 344072 | tf_op jit(solution)/shard_map/ppermute | solution.py:46
  158.2 2.1 %collective-permute-done.30 = bf16[8,7168]{1,0:T(8,128)(2,1)S(1)} collective-permute-done((bf16[8,7168]{1,0:T(8,128)(2,1)S(1)}, bf16[8,7168]{1,0:T(8,128)(2,1)S(1)}, u32[]{:S(2)}, u32[]{:S(2)}) %collective-permute-start.30) | collective-permute-done | bytes 114720 | tf_op jit(solution)/shard_map/ppermute | solution.py:46
  160.2 0.9 collective-permute-done.28
  (103 shorter events, 13.6 us)
Async XLA Ops:
  0.6 0.9 copy-start.6
  3.2 12.4 %collective-permute-start = (bf16[8,7296]{1,0:T(8,128)(2,1)S(1)}, bf16[8,7296]{1,0:T(8,128)(2,1)S(1)}, u32[]{:S(2)}, u32[]{:S(2)}) collective-permute-start(bf16[8,7296]{1,0:T(8,128)(2,1)S(1)} %token_rows.1), channel_id=1, source_target_pairs={{0,6},{1,3},{2,4},{3,1},{4,2},{5,7},{6,0},{7,5},{8,14},{9,11},{10,... | collective-permute-start | bytes 350216 | tf_op jit(solution)/shard_map/ppermute | solution.py:46
  6.1 15.2 %collective-permute-start.1 = (bf16[8,7296]{1,0:T(8,128)(2,1)S(1)}, bf16[8,7296]{1,0:T(8,128)(2,1)S(1)}, u32[]{:S(2)}, u32[]{:S(2)}) collective-permute-start(bf16[8,7296]{1,0:T(8,128)(2,1)S(1)} %token_rows.1), channel_id=1, source_target_pairs={{0,96},{1,33},{2,98},{3,35},{4,100},{5,37},{6,102},{7,39},{8,104},... | collective-permute-start | bytes 350216 | tf_op jit(solution)/shard_map/ppermute | solution.py:46
  9.1 12.3 %collective-permute-start.2 = (bf16[8,7296]{1,0:T(8,128)(2,1)S(1)}, bf16[8,7296]{1,0:T(8,128)(2,1)S(1)}, u32[]{:S(2)}, u32[]{:S(2)}) collective-permute-start(bf16[8,7296]{1,0:T(8,128)(2,1)S(1)} %token_rows.1), channel_id=1, source_target_pairs={{0,102},{1,35},{2,100},{3,33},{4,98},{5,39},{6,96},{7,37},{8,110},... | collective-permute-start | bytes 350216 | tf_op jit(solution)/shard_map/ppermute | solution.py:46
  9.2 12.4 %collective-permute-start.3 = (bf16[8,7296]{1,0:T(8,128)(2,1)S(1)}, bf16[8,7296]{1,0:T(8,128)(2,1)S(1)}, u32[]{:S(2)}, u32[]{:S(2)}) collective-permute-start(bf16[8,7296]{1,0:T(8,128)(2,1)S(1)} %token_rows.1), channel_id=1, source_target_pairs={{0,24},{1,9},{2,26},{3,11},{4,28},{5,13},{6,30},{7,15},{8,16},{9,1... | collective-permute-start | bytes 350216 | tf_op jit(solution)/shard_map/ppermute | solution.py:46
  13.3 8.8 %collective-permute-start.4 = (bf16[8,7296]{1,0:T(8,128)(2,1)S(1)}, bf16[8,7296]{1,0:T(8,128)(2,1)S(1)}, u32[]{:S(2)}, u32[]{:S(2)}) collective-permute-start(bf16[8,7296]{1,0:T(8,128)(2,1)S(1)} %token_rows.1), channel_id=1, source_target_pairs={{0,30},{1,11},{2,28},{3,9},{4,26},{5,15},{6,24},{7,13},{8,22},{9,3... | collective-permute-start | bytes 350216 | tf_op jit(solution)/shard_map/ppermute | solution.py:46
  15.5 8.6 %collective-permute-start.5 = (bf16[8,7296]{1,0:T(8,128)(2,1)S(1)}, bf16[8,7296]{1,0:T(8,128)(2,1)S(1)}, u32[]{:S(2)}, u32[]{:S(2)}) collective-permute-start(bf16[8,7296]{1,0:T(8,128)(2,1)S(1)} %token_rows.1), channel_id=1, source_target_pairs={{0,120},{1,41},{2,122},{3,43},{4,124},{5,45},{6,126},{7,47},{8,112... | collective-permute-start | bytes 350216 | tf_op jit(solution)/shard_map/ppermute | solution.py:46
  21.3 11.1 %collective-permute-start.6 = (bf16[8,7296]{1,0:T(8,128)(2,1)S(1)}, bf16[8,7296]{1,0:T(8,128)(2,1)S(1)}, u32[]{:S(2)}, u32[]{:S(2)}) collective-permute-start(bf16[8,7296]{1,0:T(8,128)(2,1)S(1)} %token_rows.1), channel_id=1, source_target_pairs={{0,126},{1,43},{2,124},{3,41},{4,122},{5,47},{6,120},{7,45},{8,118... | collective-permute-start | bytes 350216 | tf_op jit(solution)/shard_map/ppermute | solution.py:46
  21.4 40.6 %collective-permute-start.10 = (bf16[7168,256]{1,0:T(8,128)(2,1)}, bf16[7168,256]{1,0:T(8,128)(2,1)S(1)}, u32[]{:S(2)}, u32[]{:S(2)}) collective-permute-start(bf16[7168,256]{1,0:T(8,128)(2,1)} %bitcast.7), channel_id=1, source_target_pairs={{0,1},{1,0},{2,3},{3,2},{4,5},{5,4},{6,7},{7,6},{8,9},{9,8},{10,11... | collective-permute-start | bytes 11010056 | tf_op jit(solution)/shard_map/ppermute | solution.py:54
  21.6 50.4 %collective-permute-start.11 = (bf16[7168,256]{1,0:T(8,128)(2,1)}, bf16[7168,256]{1,0:T(8,128)(2,1)}, u32[]{:S(2)}, u32[]{:S(2)}) collective-permute-start(bf16[7168,256]{1,0:T(8,128)(2,1)} %bitcast.9), channel_id=1, source_target_pairs={{0,1},{1,0},{2,3},{3,2},{4,5},{5,4},{6,7},{7,6},{8,9},{9,8},{10,11... | collective-permute-start | bytes 11010056 | tf_op jit(solution)/shard_map/ppermute | solution.py:54
  32.5 7.0 %collective-permute-start.7 = (bf16[64,2432]{1,0:T(8,128)(2,1)S(1)}, bf16[64,2432]{1,0:T(8,128)(2,1)S(1)}, u32[]{:S(2)}, u32[]{:S(2)}) collective-permute-start(bf16[64,2432]{1,0:T(8,128)(2,1)S(1)} %get-tuple-element.21), channel_id=1, source_target_pairs={{0,2},{1,7},{2,0},{3,5},{4,6},{5,3},{6,4},{7,1},{8,10},{9,15},{10,... | collective-permute-start | bytes 933896 | tf_op jit(solution)/shard_map/ppermute | solution.py:28
  32.6 59.4 %collective-permute-start.18 = (bf16[256,7168]{1,0:T(8,128)(2,1)}, bf16[256,7168]{1,0:T(8,128)(2,1)}, u32[]{:S(2)}, u32[]{:S(2)}) collective-permute-start(bf16[256,7168]{1,0:T(8,128)(2,1)} %bitcast.3.refs_2_), channel_id=1, source_target_pairs={{0,1},{1,0},{2,3},{3,2},{4,5},{5,4},{6,7},{7,6},{8,9},{9,8},{10,11... | collective-permute-start | bytes 11010056 | tf_op jit(solution)/shard_map/ppermute | solution.py:54
  32.7 7.0 %collective-permute-start.12 = (bf16[64,2432]{1,0:T(8,128)(2,1)S(1)}, bf16[64,2432]{1,0:T(8,128)(2,1)S(1)}, u32[]{:S(2)}, u32[]{:S(2)}) collective-permute-start(bf16[64,2432]{1,0:T(8,128)(2,1)S(1)} %get-tuple-element.20), channel_id=1, source_target_pairs={{0,32},{1,97},{32,0},{33,65},{64,96},{65,33},{96,64},{97,1},{2,34}... | collective-permute-start | bytes 933896 | tf_op jit(solution)/shard_map/ppermute | solution.py:28
  39.5 6.9 %collective-permute-start.15 = (bf16[64,2432]{1,0:T(8,128)(2,1)S(1)}, bf16[64,2432]{1,0:T(8,128)(2,1)S(1)}, u32[]{:S(2)}, u32[]{:S(2)}) collective-permute-start(bf16[64,2432]{1,0:T(8,128)(2,1)S(1)} %get-tuple-element.19), channel_id=1, source_target_pairs={{0,8},{1,25},{8,0},{9,17},{16,24},{17,9},{24,16},{25,1},{2,10},{3,... | collective-permute-start | bytes 933896 | tf_op jit(solution)/shard_map/ppermute | solution.py:28
  39.6 10.2 %collective-permute-start.8 = (bf16[128,2432]{1,0:T(8,128)(2,1)S(1)}, bf16[128,2432]{1,0:T(8,128)(2,1)S(1)}, u32[]{:S(2)}, u32[]{:S(2)}) collective-permute-start(bf16[128,2432]{1,0:T(8,128)(2,1)S(1)} %pad_maximum_fusion.4), channel_id=1, source_target_pairs={{0,32},{1,97},{32,0},{33,65},{64,96},{65,33},{96,64},{97,1},{2,34}... | collective-permute-start | bytes 1867784 | tf_op jit(solution)/shard_map/ppermute | solution.py:28
  46.4 10.2 %collective-permute-start.13 = (bf16[128,2432]{1,0:T(8,128)(2,1)S(1)}, bf16[128,2432]{1,0:T(8,128)(2,1)S(1)}, u32[]{:S(2)}, u32[]{:S(2)}) collective-permute-start(bf16[128,2432]{1,0:T(8,128)(2,1)S(1)} %pad_maximum_fusion.5), channel_id=1, source_target_pairs={{0,8},{1,25},{8,0},{9,17},{16,24},{17,9},{24,16},{25,1},{2,10},{3,... | collective-permute-start | bytes 1867784 | tf_op jit(solution)/shard_map/ppermute | solution.py:28
  49.9 10.2 %collective-permute-start.16 = (bf16[128,2432]{1,0:T(8,128)(2,1)S(1)}, bf16[128,2432]{1,0:T(8,128)(2,1)S(1)}, u32[]{:S(2)}, u32[]{:S(2)}) collective-permute-start(bf16[128,2432]{1,0:T(8,128)(2,1)S(1)} %pad_maximum_fusion.6), channel_id=1, source_target_pairs={{0,2},{1,7},{2,0},{3,5},{4,6},{5,3},{6,4},{7,1},{8,10},{9,15},{10,... | collective-permute-start | bytes 1867784 | tf_op jit(solution)/shard_map/ppermute | solution.py:28
  51.7 12.2 %copy-start.10 = (bf16[1,7168,256]{2,1,0:T(8,128)(2,1)S(1)}, bf16[1,7168,256]{2,1,0:T(8,128)(2,1)}, u32[]{:S(2)}) copy-start(bf16[1,7168,256]{2,1,0:T(8,128)(2,1)} %param.12) | copy-start | bytes 11010052
  56.6 19.9 %collective-permute-start.9 = (bf16[256,2432]{1,0:T(8,128)(2,1)S(1)}, bf16[256,2432]{1,0:T(8,128)(2,1)}, u32[]{:S(2)}, u32[]{:S(2)}) collective-permute-start(bf16[256,2432]{1,0:T(8,128)(2,1)S(1)} %pad_maximum_fusion.1.x0), channel_id=1, source_target_pairs={{0,8},{1,25},{8,0},{9,17},{16,24},{17,9},{24,16},{25,1},{2,10},{3,... | collective-permute-start | bytes 3735560 | tf_op jit(solution)/shard_map/ppermute | solution.py:28
  56.6 7.3 %copy-start.9 = (bf16[1,7168,256]{2,1,0:T(8,128)(2,1)S(1)}, bf16[1,7168,256]{2,1,0:T(8,128)(2,1)}, u32[]{:S(2)}) copy-start(bf16[1,7168,256]{2,1,0:T(8,128)(2,1)} %param.11) | copy-start | bytes 11010052
  60.1 21.0 %collective-permute-start.14 = (bf16[256,2432]{1,0:T(8,128)(2,1)}, bf16[256,2432]{1,0:T(8,128)(2,1)}, u32[]{:S(2)}, u32[]{:S(2)}) collective-permute-start(bf16[256,2432]{1,0:T(8,128)(2,1)} %pad_maximum_fusion.2.x1), channel_id=1, source_target_pairs={{0,2},{1,7},{2,0},{3,5},{4,6},{5,3},{6,4},{7,1},{8,10},{9,15},{10,... | collective-permute-start | bytes 3735560 | tf_op jit(solution)/shard_map/ppermute | solution.py:28
  62.1 1.9 %copy-start.11 = (bf16[7168,256]{1,0:T(8,128)(2,1)}, bf16[7168,256]{1,0:T(8,128)(2,1)S(1)}, u32[]{:S(2)}) copy-start(bf16[7168,256]{1,0:T(8,128)(2,1)S(1)} %collective-permute-done.10.refs_0_) | copy-start | bytes 11010052
  63.9 20.0 %collective-permute-start.17 = (bf16[256,2432]{1,0:T(8,128)(2,1)S(1)}, bf16[256,2432]{1,0:T(8,128)(2,1)}, u32[]{:S(2)}, u32[]{:S(2)}) collective-permute-start(bf16[256,2432]{1,0:T(8,128)(2,1)S(1)} %pad_maximum_fusion.3.x2.near_x2), channel_id=1, source_target_pairs={{0,32},{1,97},{32,0},{33,65},{64,96},{65,33},{96,64},{97,1},{2,34}... | collective-permute-start | bytes 3735560 | tf_op jit(solution)/shard_map/ppermute | solution.py:28
  66.5 1.8 %copy-start = (bf16[256,7168]{1,0:T(8,128)(2,1)}, bf16[256,7168]{1,0:T(8,128)(2,1)S(1)}, u32[]{:S(2)}) copy-start(bf16[256,7168]{1,0:T(8,128)(2,1)S(1)} %get-tuple-element.15.own) | copy-start | bytes 11010052
  68.3 1.8 %copy-start.2 = (bf16[7168,256]{1,0:T(8,128)(2,1)}, bf16[7168,256]{1,0:T(8,128)(2,1)S(1)}, u32[]{:S(2)}) copy-start(bf16[7168,256]{1,0:T(8,128)(2,1)S(1)} %get-tuple-element.10.w0) | copy-start | bytes 11010052
  70.1 1.9 %copy-start.4 = (bf16[7168,256]{1,0:T(8,128)(2,1)}, bf16[7168,256]{1,0:T(8,128)(2,1)S(1)}, u32[]{:S(2)}) copy-start(bf16[7168,256]{1,0:T(8,128)(2,1)S(1)} %get-tuple-element.12.w2) | copy-start | bytes 11010052
  72.0 2.0 %copy-start.12 = (bf16[7168,256]{1,0:T(8,128)(2,1)S(1)}, bf16[7168,256]{1,0:T(8,128)(2,1)}, u32[]{:S(2)}) copy-start(bf16[7168,256]{1,0:T(8,128)(2,1)} %copy-done.11) | copy-start | bytes 11010052
  74.0 3.1 %copy-start.3 = (bf16[7168,256]{1,0:T(8,128)(2,1)S(1)}, bf16[7168,256]{1,0:T(8,128)(2,1)}, u32[]{:S(2)}) copy-start(bf16[7168,256]{1,0:T(8,128)(2,1)} %copy-done.2) | copy-start | bytes 11010052
  74.0 4.3 %copy-start.5 = (bf16[7168,256]{1,0:T(8,128)(2,1)S(1)}, bf16[7168,256]{1,0:T(8,128)(2,1)}, u32[]{:S(2)}) copy-start(bf16[7168,256]{1,0:T(8,128)(2,1)} %copy-done.4) | copy-start | bytes 11010052
  94.0 2.4 %copy-start.1 = (bf16[256,7168]{1,0:T(8,128)(2,1)S(1)}, bf16[256,7168]{1,0:T(8,128)(2,1)}, u32[]{:S(2)}) copy-start(bf16[256,7168]{1,0:T(8,128)(2,1)} %copy-done) | copy-start | bytes 11010052
  97.2 16.3 %collective-permute-start.25 = (bf16[256,2304]{1,0:T(8,128)(2,1)S(1)}, bf16[256,2304]{1,0:T(8,128)(2,1)S(1)}, u32[]{:S(2)}, u32[]{:S(2)}) collective-permute-start(bf16[256,2304]{1,0:T(8,128)(2,1)S(1)} %shard_map.102), channel_id=1, source_target_pairs={{0,32},{1,97},{32,0},{33,65},{64,96},{65,33},{96,64},{97,1},{2,34}... | collective-permute-start | bytes 3538952 | tf_op jit(solution)/shard_map/ppermute | solution.py:28
  100.2 17.0 %collective-permute-start.22 = (bf16[256,2432]{1,0:T(8,128)(2,1)S(1)}, bf16[256,2432]{1,0:T(8,128)(2,1)S(1)}, u32[]{:S(2)}, u32[]{:S(2)}) collective-permute-start(bf16[256,2432]{1,0:T(8,128)(2,1)S(1)} %shard_map.100), channel_id=1, source_target_pairs={{0,2},{1,7},{2,0},{3,5},{4,6},{5,3},{6,4},{7,1},{8,10},{9,15},{10,... | collective-permute-start | bytes 3735560 | tf_op jit(solution)/shard_map/ppermute | solution.py:28
  100.5 5.4 %collective-permute-start.35 = (s32[1,128]{1,0:T(1,128)S(1)}, s32[1,128]{1,0:T(1,128)S(1)}, u32[]{:S(2)}, u32[]{:S(2)}) collective-permute-start(s32[1,128]{1,0:T(1,128)S(1)} %get-tuple-element.16), channel_id=1, source_target_pairs={{0,1},{1,0},{2,3},{3,2},{4,5},{5,4},{6,7},{7,6},{8,9},{9,8},{10,11... | collective-permute-start | bytes 1544 | tf_op jit(solution)/shard_map/ppermute | solution.py:54
  105.7 17.0 %collective-permute-start.19 = (bf16[256,2432]{1,0:T(8,128)(2,1)S(1)}, bf16[256,2432]{1,0:T(8,128)(2,1)S(1)}, u32[]{:S(2)}, u32[]{:S(2)}) collective-permute-start(bf16[256,2432]{1,0:T(8,128)(2,1)S(1)} %shard_map.98), channel_id=1, source_target_pairs={{0,8},{1,25},{8,0},{9,17},{16,24},{17,9},{24,16},{25,1},{2,10},{3,... | collective-permute-start | bytes 3735560 | tf_op jit(solution)/shard_map/ppermute | solution.py:28
  113.8 10.2 %collective-permute-start.26 = (bf16[128,2304]{1,0:T(8,128)(2,1)S(1)}, bf16[128,2304]{1,0:T(8,128)(2,1)S(1)}, u32[]{:S(2)}, u32[]{:S(2)}) collective-permute-start(bf16[128,2304]{1,0:T(8,128)(2,1)S(1)} %slice.162), channel_id=1, source_target_pairs={{0,2},{1,7},{2,0},{3,5},{4,6},{5,3},{6,4},{7,1},{8,10},{9,15},{10,... | collective-permute-start | bytes 1769480 | tf_op jit(solution)/shard_map/ppermute | solution.py:28
  117.5 11.9 %collective-permute-start.23 = (bf16[128,2432]{1,0:T(8,128)(2,1)S(1)}, bf16[128,2432]{1,0:T(8,128)(2,1)S(1)}, u32[]{:S(2)}, u32[]{:S(2)}) collective-permute-start(bf16[128,2432]{1,0:T(8,128)(2,1)S(1)} %slice.160), channel_id=1, source_target_pairs={{0,8},{1,25},{8,0},{9,17},{16,24},{17,9},{24,16},{25,1},{2,10},{3,... | collective-permute-start | bytes 1867784 | tf_op jit(solution)/shard_map/ppermute | solution.py:28
  123.0 10.3 %collective-permute-start.20 = (bf16[128,2432]{1,0:T(8,128)(2,1)S(1)}, bf16[128,2432]{1,0:T(8,128)(2,1)S(1)}, u32[]{:S(2)}, u32[]{:S(2)}) collective-permute-start(bf16[128,2432]{1,0:T(8,128)(2,1)S(1)} %slice.161), channel_id=1, source_target_pairs={{0,32},{1,97},{32,0},{33,65},{64,96},{65,33},{96,64},{97,1},{2,34}... | collective-permute-start | bytes 1867784 | tf_op jit(solution)/shard_map/ppermute | solution.py:28
  124.1 9.5 %collective-permute-start.27 = (bf16[64,2304]{1,0:T(8,128)(2,1)S(1)}, bf16[64,2304]{1,0:T(8,128)(2,1)S(1)}, u32[]{:S(2)}, u32[]{:S(2)}) collective-permute-start(bf16[64,2304]{1,0:T(8,128)(2,1)S(1)} %slice.165), channel_id=1, source_target_pairs={{0,8},{1,25},{8,0},{9,17},{16,24},{17,9},{24,16},{25,1},{2,10},{3,... | collective-permute-start | bytes 884744 | tf_op jit(solution)/shard_map/ppermute | solution.py:28
  129.5 7.2 %collective-permute-start.24 = (bf16[64,2432]{1,0:T(8,128)(2,1)S(1)}, bf16[64,2432]{1,0:T(8,128)(2,1)S(1)}, u32[]{:S(2)}, u32[]{:S(2)}) collective-permute-start(bf16[64,2432]{1,0:T(8,128)(2,1)S(1)} %slice.163), channel_id=1, source_target_pairs={{0,32},{1,97},{32,0},{33,65},{64,96},{65,33},{96,64},{97,1},{2,34}... | collective-permute-start | bytes 933896 | tf_op jit(solution)/shard_map/ppermute | solution.py:28
  133.5 7.0 %collective-permute-start.21 = (bf16[64,2432]{1,0:T(8,128)(2,1)S(1)}, bf16[64,2432]{1,0:T(8,128)(2,1)S(1)}, u32[]{:S(2)}, u32[]{:S(2)}) collective-permute-start(bf16[64,2432]{1,0:T(8,128)(2,1)S(1)} %slice.164), channel_id=1, source_target_pairs={{0,2},{1,7},{2,0},{3,5},{4,6},{5,3},{6,4},{7,1},{8,10},{9,15},{10,... | collective-permute-start | bytes 933896 | tf_op jit(solution)/shard_map/ppermute | solution.py:28
  140.6 5.4 %copy-start.13 = (f32[16]{0:T(128)S(1)}, f32[16]{0:T(128)}, u32[]{:S(2)}) copy-start(f32[16]{0:T(128)} %param.14) | copy-start | bytes 196
  140.8 11.5 %collective-permute-start.34 = (bf16[8,7168]{1,0:T(8,128)(2,1)S(1)}, bf16[8,7168]{1,0:T(8,128)(2,1)S(1)}, u32[]{:S(2)}, u32[]{:S(2)}) collective-permute-start(bf16[8,7168]{1,0:T(8,128)(2,1)S(1)} %get-tuple-element.23), channel_id=1, source_target_pairs={{0,126},{1,43},{2,124},{3,41},{4,122},{5,47},{6,120},{7,45},{8,118... | collective-permute-start | bytes 344072 | tf_op jit(solution)/shard_map/ppermute | solution.py:46
  140.8 14.3 %collective-permute-start.33 = (bf16[8,7168]{1,0:T(8,128)(2,1)S(1)}, bf16[8,7168]{1,0:T(8,128)(2,1)S(1)}, u32[]{:S(2)}, u32[]{:S(2)}) collective-permute-start(bf16[8,7168]{1,0:T(8,128)(2,1)S(1)} %get-tuple-element.24), channel_id=1, source_target_pairs={{0,120},{1,41},{2,122},{3,43},{4,124},{5,45},{6,126},{7,47},{8,112... | collective-permute-start | bytes 344072 | tf_op jit(solution)/shard_map/ppermute | solution.py:46
  146.6 11.6 %collective-permute-start.32 = (bf16[8,7168]{1,0:T(8,128)(2,1)S(1)}, bf16[8,7168]{1,0:T(8,128)(2,1)S(1)}, u32[]{:S(2)}, u32[]{:S(2)}) collective-permute-start(bf16[8,7168]{1,0:T(8,128)(2,1)S(1)} %get-tuple-element.25), channel_id=1, source_target_pairs={{0,30},{1,11},{2,28},{3,9},{4,26},{5,15},{6,24},{7,13},{8,22},{9,3... | collective-permute-start | bytes 344072 | tf_op jit(solution)/shard_map/ppermute | solution.py:46
  148.8 9.4 %collective-permute-start.31 = (bf16[8,7168]{1,0:T(8,128)(2,1)S(1)}, bf16[8,7168]{1,0:T(8,128)(2,1)S(1)}, u32[]{:S(2)}, u32[]{:S(2)}) collective-permute-start(bf16[8,7168]{1,0:T(8,128)(2,1)S(1)} %get-tuple-element.26), channel_id=1, source_target_pairs={{0,24},{1,9},{2,26},{3,11},{4,28},{5,13},{6,30},{7,15},{8,16},{9,1... | collective-permute-start | bytes 344072 | tf_op jit(solution)/shard_map/ppermute | solution.py:46
  152.1 8.1 %collective-permute-start.30 = (bf16[8,7168]{1,0:T(8,128)(2,1)S(1)}, bf16[8,7168]{1,0:T(8,128)(2,1)S(1)}, u32[]{:S(2)}, u32[]{:S(2)}) collective-permute-start(bf16[8,7168]{1,0:T(8,128)(2,1)S(1)} %get-tuple-element.27), channel_id=1, source_target_pairs={{0,102},{1,35},{2,100},{3,33},{4,98},{5,39},{6,96},{7,37},{8,110},... | collective-permute-start | bytes 344072 | tf_op jit(solution)/shard_map/ppermute | solution.py:46
  152.2 8.0 %collective-permute-start.29 = (bf16[8,7168]{1,0:T(8,128)(2,1)S(1)}, bf16[8,7168]{1,0:T(8,128)(2,1)S(1)}, u32[]{:S(2)}, u32[]{:S(2)}) collective-permute-start(bf16[8,7168]{1,0:T(8,128)(2,1)S(1)} %get-tuple-element.28), channel_id=1, source_target_pairs={{0,96},{1,33},{2,98},{3,35},{4,100},{5,37},{6,102},{7,39},{8,104},... | collective-permute-start | bytes 344072 | tf_op jit(solution)/shard_map/ppermute | solution.py:46
  155.2 6.0 %collective-permute-start.28 = (bf16[8,7168]{1,0:T(8,128)(2,1)S(1)}, bf16[8,7168]{1,0:T(8,128)(2,1)S(1)}, u32[]{:S(2)}, u32[]{:S(2)}) collective-permute-start(bf16[8,7168]{1,0:T(8,128)(2,1)S(1)} %get-tuple-element.22), channel_id=1, source_target_pairs={{0,6},{1,3},{2,4},{3,1},{4,2},{5,7},{6,0},{7,5},{8,14},{9,11},{10,... | collective-permute-start | bytes 344072 | tf_op jit(solution)/shard_map/ppermute | solution.py:46
  (2 other events, 1.4 us)

commit v5 on v4

--- a/solution.py
+++ b/solution.py
@@ -14,8 +14,8 @@
 EARLY = (X, Y, Z)
 LATE = ((X, Y, Z), (Y, Z, X), (Z, X, Y))
 INFO = 128
-CUTS = (0, 2432, 4864, 7168)
-COL_CUTS = (0, 2432, 4864, 7168)
+CUTS = (0, 2560, 4992, 7168)
+COL_CUTS = (0, 2176, 4608, 7168)
 BF16 = jnp.bfloat16
 F32 = jnp.float32
 
@@ -23,13 +23,13 @@
 
 
 def exchange(value, axis):
-    masks = (1, 3)
+    masks = (3, 1)
     pairs = [(2 * i + c, 2 * (i ^ masks[c]) + c) for i in range(4) for c in range(2)]
     return lax.ppermute(value, (axis, "gz_1"), pairs)
 
 
 def direct(value, hops):
-    masks = (3, 1)
+    masks = (1, 3)
     pairs = []
     for a in range(4):
         for b in range(4):
@@ -278,14 +278,21 @@
         for i, p in enumerate(pieces):
             far_pieces.append(exchange(p, LATE[i][step]))
         if step < 2:
-            pieces = [jnp.concatenate(pair, axis=0) for pair in zip(pieces, far_pieces)]
+            joined = []
+            for i in range(3):
+                joined.append(jnp.concatenate([pieces[i], far_pieces[i]], axis=0))
+            pieces = joined
 
     acc = gate_up_near(pieces, gate_ups)
     expert = jnp.full((1,), own_expert, jnp.int32)
-    parts = [gate_up_far_part(i, far_pieces[i], gate_ups) for i in range(3)]
+    parts = []
+    for i in range(3):
+        parts.append(gate_up_far_part(i, far_pieces[i], gate_ups))
     hidden, marks = hidden_of(expert, parts, pieces[2], far_pieces[2], acc)
 
-    sent = [down_part(i, True, hidden, down_own, down_far) for i in range(3)]
+    sent = []
+    for i in range(3):
+        sent.append(down_part(i, True, hidden, down_own, down_far))
     kept = []
     for i in range(3):
         kept.append(down_part(i, False, hidden, down_own, down_far))
@@ -293,7 +300,9 @@
         got = []
         for i in range(3):
             got.append(exchange(sent[i], LATE[i][step]))
-        totals = [kept[i] + got[i].astype(F32) for i in range(3)]
+        totals = []
+        for i in range(3):
+            totals.append(kept[i] + got[i].astype(F32))
         half = totals[0].shape[0] // 2
         if step:
             sent = [t[half:].astype(BF16) for t in totals]

time: 162 us -> 168 us (1.037)
  the two profiles are of different devices: /device:TPU:0 before, /device:TPU:1 now
where the time goes in v5:
time: 168 us
  waiting for transfers between devices  77.1 us (46%)
  starting transfers between devices  46.4 us (28%)
  Pallas kernels  26 us (15%)
  local copies, waits for them, and re-layouts  12.7 us (8%)
  other arithmetic  4.31 us (3%)
    ppermute x18, waiting for transfers between devices, exchange(): return lax.ppermute(value, (axis, 'gz_1'), pairs)  65.4 us
    ppermute x14, starting transfers between devices, direct(): return lax.ppermute(value, AXES, pairs)  31.9 us
    unnamed x37, local copies, waits for them, and re-layouts  12.3 us
    ppermute x14, waiting for transfers between devices, direct(): return lax.ppermute(value, AXES, pairs)  11.7 us
    ppermute x4, starting transfers between devices, partner(): return lax.ppermute(value, 'gz_1', [(0, 1), (1, 0)])  8.68 us
    pallas_call x3, Pallas kernels, gate_up_far_part(): pl.pallas_call(functools.partial(far_part_kernel, colour), out_shape=jax....  8.28 us
    ppermute x18, starting transfers between devices, exchange(): return lax.ppermute(value, (axis, 'gz_1'), pairs)  5.8 us
    pallas_call x1, Pallas kernels, gate_up_near(): pl.pallas_call(near_kernel, out_shape=jax.ShapeDtypeStruct((4, 512, 256),...  5.38 us
  transfers between devices with their start and end apart: 36, of which 17 were waited for; matrix products, arithmetic and copies ran while one was open for 2% of the time, Pallas kernels for 13%

profile of v5, /device:TPU:1, one launch (start us, length us, event | category | flops | bytes accessed | tf_op | source)
XLA Modules:
  0.0 167.7 jit_solution(17699406760147155733)
XLA Ops:
  0.6 0.9 copy-done.6
  3.2 3.4 %collective-permute-start = (bf16[8,7296]{1,0:T(8,128)(2,1)S(1)}, bf16[8,7296]{1,0:T(8,128)(2,1)S(1)}, u32[]{:S(2)}, u32[]{:S(2)}) collective-permute-start(bf16[8,7296]{1,0:T(8,128)(2,1)S(1)} %token_rows.1), channel_id=1, source_target_pairs={{0,2},{1,7},{2,0},{3,5},{4,6},{5,3},{6,4},{7,1},{8,10},{9,15},{10,... | collective-permute-start | bytes 350216 | tf_op jit(solution)/shard_map/ppermute | solution.py:46
  6.5 2.7 %collective-permute-start.1 = (bf16[8,7296]{1,0:T(8,128)(2,1)S(1)}, bf16[8,7296]{1,0:T(8,128)(2,1)S(1)}, u32[]{:S(2)}, u32[]{:S(2)}) collective-permute-start(bf16[8,7296]{1,0:T(8,128)(2,1)S(1)} %token_rows.1), channel_id=1, source_target_pairs={{0,32},{1,97},{2,34},{3,99},{4,36},{5,101},{6,38},{7,103},{8,40},{... | collective-permute-start | bytes 350216 | tf_op jit(solution)/shard_map/ppermute | solution.py:46
  9.3 3.8 %collective-permute-start.3 = (bf16[8,7296]{1,0:T(8,128)(2,1)S(1)}, bf16[8,7296]{1,0:T(8,128)(2,1)S(1)}, u32[]{:S(2)}, u32[]{:S(2)}) collective-permute-start(bf16[8,7296]{1,0:T(8,128)(2,1)S(1)} %token_rows.1), channel_id=1, source_target_pairs={{0,8},{1,25},{2,10},{3,27},{4,12},{5,29},{6,14},{7,31},{8,0},{9,17... | collective-permute-start | bytes 350216 | tf_op jit(solution)/shard_map/ppermute | solution.py:46
  13.0 2.1 %collective-permute-start.4 = (bf16[8,7296]{1,0:T(8,128)(2,1)S(1)}, bf16[8,7296]{1,0:T(8,128)(2,1)S(1)}, u32[]{:S(2)}, u32[]{:S(2)}) collective-permute-start(bf16[8,7296]{1,0:T(8,128)(2,1)S(1)} %token_rows.1), channel_id=1, source_target_pairs={{0,10},{1,31},{2,8},{3,29},{4,14},{5,27},{6,12},{7,25},{8,2},{9,23... | collective-permute-start | bytes 350216 | tf_op jit(solution)/shard_map/ppermute | solution.py:46
  15.2 5.1 %collective-permute-start.5 = (bf16[8,7296]{1,0:T(8,128)(2,1)S(1)}, bf16[8,7296]{1,0:T(8,128)(2,1)S(1)}, u32[]{:S(2)}, u32[]{:S(2)}) collective-permute-start(bf16[8,7296]{1,0:T(8,128)(2,1)S(1)} %token_rows.1), channel_id=1, source_target_pairs={{0,40},{1,121},{2,42},{3,123},{4,44},{5,125},{6,46},{7,127},{8,32}... | collective-permute-start | bytes 350216 | tf_op jit(solution)/shard_map/ppermute | solution.py:46
  21.2 1.3 collective-permute-done.5
  22.5 7.1 %collective-permute-done.6 = bf16[8,7296]{1,0:T(8,128)(2,1)S(1)} collective-permute-done((bf16[8,7296]{1,0:T(8,128)(2,1)S(1)}, bf16[8,7296]{1,0:T(8,128)(2,1)S(1)}, u32[]{:S(2)}, u32[]{:S(2)}) %collective-permute-start.6) | collective-permute-done | bytes 116768 | tf_op jit(solution)/shard_map/ppermute | solution.py:46
  30.0 5.6 %collective-permute-done.15 = bf16[64,2304]{1,0:T(8,128)(2,1)S(1)} collective-permute-done((bf16[64,2304]{1,0:T(8,128)(2,1)S(1)}, bf16[64,2304]{1,0:T(8,128)(2,1)S(1)}, u32[]{:S(2)}, u32[]{:S(2)}) %collective-permute-start.15) | collective-permute-done | bytes 294944 | tf_op jit(solution)/shard_map/ppermute | solution.py:28
  35.7 5.7 %collective-permute-done.12 = bf16[64,2432]{1,0:T(8,128)(2,1)S(1)} collective-permute-done((bf16[64,2432]{1,0:T(8,128)(2,1)S(1)}, bf16[64,2432]{1,0:T(8,128)(2,1)S(1)}, u32[]{:S(2)}, u32[]{:S(2)}) %collective-permute-start.12) | collective-permute-done | bytes 311328 | tf_op jit(solution)/shard_map/ppermute | solution.py:28
  41.6 8.8 %collective-permute-done.16 = bf16[128,2304]{1,0:T(8,128)(2,1)S(1)} collective-permute-done((bf16[128,2304]{1,0:T(8,128)(2,1)S(1)}, bf16[128,2304]{1,0:T(8,128)(2,1)S(1)}, u32[]{:S(2)}, u32[]{:S(2)}) %collective-permute-start.16) | collective-permute-done | bytes 589856 | tf_op jit(solution)/shard_map/ppermute | solution.py:28
  50.9 1.1 collective-permute-start.17
  52.0 1.2 pad_maximum_fusion.2.x1
  53.2 6.9 %collective-permute-done.8 = bf16[128,2560]{1,0:T(8,128)(2,1)S(1)} collective-permute-done((bf16[128,2560]{1,0:T(8,128)(2,1)S(1)}, bf16[128,2560]{1,0:T(8,128)(2,1)S(1)}, u32[]{:S(2)}, u32[]{:S(2)}) %collective-permute-start.8) | collective-permute-done | bytes 655392 | tf_op jit(solution)/shard_map/ppermute | solution.py:28
  60.3 1.9 %copy-done.12 = bf16[7168,256]{1,0:T(8,128)(2,1)} copy-done((bf16[7168,256]{1,0:T(8,128)(2,1)}, bf16[7168,256]{1,0:T(8,128)(2,1)S(1)}, u32[]{:S(2)}) %copy-start.12) | copy-done | bytes 3670040
  63.0 1.8 %copy-done = bf16[256,7168]{1,0:T(8,128)(2,1)} copy-done((bf16[256,7168]{1,0:T(8,128)(2,1)}, bf16[256,7168]{1,0:T(8,128)(2,1)S(1)}, u32[]{:S(2)}) %copy-start) | copy-done | bytes 3670040
  64.8 1.8 %copy-done.2 = bf16[7168,256]{1,0:T(8,128)(2,1)} copy-done((bf16[7168,256]{1,0:T(8,128)(2,1)}, bf16[7168,256]{1,0:T(8,128)(2,1)S(1)}, u32[]{:S(2)}) %copy-start.2) | copy-done | bytes 3670040
  66.6 1.9 %copy-done.4 = bf16[7168,256]{1,0:T(8,128)(2,1)} copy-done((bf16[7168,256]{1,0:T(8,128)(2,1)}, bf16[7168,256]{1,0:T(8,128)(2,1)S(1)}, u32[]{:S(2)}) %copy-start.4) | copy-done | bytes 3670040
  68.5 2.0 %copy-done.13 = bf16[7168,256]{1,0:T(8,128)(2,1)S(1)} copy-done((bf16[7168,256]{1,0:T(8,128)(2,1)S(1)}, bf16[7168,256]{1,0:T(8,128)(2,1)}, u32[]{:S(2)}) %copy-start.13) | copy-done | bytes 3670040
  70.5 2.4 %weights_in.6 = (bf16[7168,256]{1,0:T(8,128)(2,1)S(1)}, bf16[7168,256]{1,0:T(8,128)(2,1)S(1)}) custom-call(bf16[7168,256]{1,0:T(8,128)(2,1)S(1)} %copy-done.13, bf16[7168,256]{1,0:T(8,128)(2,1)} %collective-permute-done.11.refs_1_), custom_call_target="tpu_custom_call" | custom-call | flops 8589934592 | tf_op jit(solution)/shard_map/weights_in/pallas_call | solution.py:172
  73.0 6.1 %collective-permute-done.9.x = bf16[256,2560]{1,0:T(8,128)(2,1)} collective-permute-done((bf16[256,2560]{1,0:T(8,128)(2,1)S(1)}, bf16[256,2560]{1,0:T(8,128)(2,1)}, u32[]{:S(2)}, u32[]{:S(2)}) %collective-permute-start.9) | collective-permute-done | bytes 1310752 | tf_op jit(solution)/shard_map/ppermute | solution.py:28
  79.1 2.8 %shard_map.94.part0 = f32[4,256,256]{2,1,0:T(8,128)S(1)} custom-call(bf16[256,2560]{1,0:T(8,128)(2,1)} %collective-permute-done.9.x, bf16[7168,256]{1,0:T(8,128)(2,1)S(1)} %copy-done.3, bf16[7168,256]{1,0:T(8,128)(2,1)S(1)} %get-tuple-element.11.w1, bf16[7168,256]{1,0:T(8,128)(2,1)S(1)} %copy-done.5, bf16[7168,256]{1,0:T(8,128)(2,1)S(1)} %get-tuple-element.13.w3), custom_call_target="tpu_custom_call" | custom-call | flops 1252524032 | tf_op jit(solution)/shard_map/pallas_call | solution.py:203
  81.9 2.8 %shard_map.95.part1 = f32[4,256,256]{2,1,0:T(8,128)S(1)} custom-call(bf16[256,2432]{1,0:T(8,128)(2,1)} %collective-permute-done.14.x, bf16[7168,256]{1,0:T(8,128)(2,1)S(1)} %copy-done.3, bf16[7168,256]{1,0:T(8,128)(2,1)S(1)} %get-tuple-element.11.w1, bf16[7168,256]{1,0:T(8,128)(2,1)S(1)} %copy-done.5, bf16[7168,256]{1,0:T(8,128)(2,1)S(1)} %get-tuple-element.13.w3), custom_call_target="tpu_custom_call" | custom-call | flops 1252524032 | tf_op jit(solution)/shard_map/pallas_call | solution.py:203
  84.7 2.6 %shard_map.96.part2 = f32[4,256,256]{2,1,0:T(8,128)S(1)} custom-call(bf16[256,2304]{1,0:T(8,128)(2,1)} %collective-permute-done.17.x.x2, bf16[7168,256]{1,0:T(8,128)(2,1)S(1)} %copy-done.3, bf16[7168,256]{1,0:T(8,128)(2,1)S(1)} %get-tuple-element.11.w1, bf16[7168,256]{1,0:T(8,128)(2,1)S(1)} %copy-done.5, bf16[7168,256]{1,0:T(8,128)(2,1)S(1)} %get-tuple-element.13.w3), custom_call_target="tpu_custom_call" | custom-call | flops 1252524032 | tf_op jit(solution)/shard_map/pallas_call | solution.py:203
  87.4 5.4 %gate_up_near.1.acc = f32[4,512,256]{2,1,0:T(8,128)S(1)} custom-call(bf16[256,2560]{1,0:T(8,128)(2,1)S(1)} %pad_maximum_fusion.1.x0, bf16[256,2432]{1,0:T(8,128)(2,1)} %pad_maximum_fusion.2.x1, bf16[256,2304]{1,0:T(8,128)(2,1)S(1)} %pad_maximum_fusion.3.x2.near_x2, bf16[7168,256]{1,0:T(8,128)(2,1)S(1)} %copy-done.3, ...), custom_call_target="tpu_custom_call" | custom-call | flops 3757572096 | tf_op jit(solution)/shard_map/gate_up_near/pallas_call | solution.py:191
  92.8 2.0 %weights_in.7.other = bf16[256,7168]{1,0:T(8,128)(2,1)S(1)} custom-call(bf16[256,7168]{1,0:T(8,128)(2,1)} %collective-permute-done.18.refs_0_), custom_call_target="tpu_custom_call" | custom-call | flops 8589934592 | tf_op jit(solution)/shard_map/weights_in/pallas_call | solution.py:172
  94.8 1.9 %hidden.1 = (bf16[512,512]{1,0:T(8,128)(2,1)S(1)}, s32[1,128]{1,0:T(1,128)S(1)}) custom-call(s32[1]{0:T(128)} %bitcast.expert, f32[4,256,256]{2,1,0:T(8,128)S(1)} %shard_map.94.part0, f32[4,256,256]{2,1,0:T(8,128)S(1)} %shard_map.95.part1, f32[4,256,256]{2,1,0:T(8,128)S(1)} %shard_map.96.part2, bf16[256,2304]{1,0:T(8,128)(2,1)S(1)} %pad_maximum_fusion.3.x2.near_x2, ...), custom_call_target="tpu_custom_call" | custom-call | flops 1252524032 | tf_op jit(solution)/shard_map/hidden/pallas_call | solution.py:214
  98.1 0.8 shard_map.100
  99.0 1.4 collective-permute-start.22
  100.4 7.9 %collective-permute-start.35 = (s32[1,128]{1,0:T(1,128)S(1)}, s32[1,128]{1,0:T(1,128)S(1)}, u32[]{:S(2)}, u32[]{:S(2)}) collective-permute-start(s32[1,128]{1,0:T(1,128)S(1)} %get-tuple-element.16), channel_id=1, source_target_pairs={{0,1},{1,0},{2,3},{3,2},{4,5},{5,4},{6,7},{7,6},{8,9},{9,8},{10,11... | collective-permute-start | bytes 1544 | tf_op jit(solution)/shard_map/ppermute | solution.py:54
  108.3 0.8 shard_map.99
  109.2 0.8 shard_map.101
  110.0 0.8 shard_map.102
  111.8 0.9 collective-permute-done.19
  113.8 1.3 collective-permute-done.22
  115.4 1.5 collective-permute-start.23
  116.9 11.6 %collective-permute-done.25 = bf16[256,2560]{1,0:T(8,128)(2,1)S(1)} collective-permute-done((bf16[256,2560]{1,0:T(8,128)(2,1)S(1)}, bf16[256,2560]{1,0:T(8,128)(2,1)S(1)}, u32[]{:S(2)}, u32[]{:S(2)}) %collective-permute-start.25) | collective-permute-done | bytes 1310752 | tf_op jit(solution)/shard_map/ppermute | solution.py:28
  129.0 5.5 %collective-permute-done.20 = bf16[128,2176]{1,0:T(8,128)(2,1)S(1)} collective-permute-done((bf16[128,2176]{1,0:T(8,128)(2,1)S(1)}, bf16[128,2176]{1,0:T(8,128)(2,1)S(1)}, u32[]{:S(2)}, u32[]{:S(2)}) %collective-permute-start.20) | collective-permute-done | bytes 557088 | tf_op jit(solution)/shard_map/ppermute | solution.py:28
  135.0 6.7 %collective-permute-done.21 = bf16[64,2176]{1,0:T(8,128)(2,1)S(1)} collective-permute-done((bf16[64,2176]{1,0:T(8,128)(2,1)S(1)}, bf16[64,2176]{1,0:T(8,128)(2,1)S(1)}, u32[]{:S(2)}, u32[]{:S(2)}) %collective-permute-start.21) | collective-permute-done | bytes 278560 | tf_op jit(solution)/shard_map/ppermute | solution.py:28
  142.1 5.8 %collective-permute-done.27 = bf16[64,2560]{1,0:T(8,128)(2,1)S(1)} collective-permute-done((bf16[64,2560]{1,0:T(8,128)(2,1)S(1)}, bf16[64,2560]{1,0:T(8,128)(2,1)S(1)}, u32[]{:S(2)}, u32[]{:S(2)}) %collective-permute-start.27) | collective-permute-done | bytes 327712 | tf_op jit(solution)/shard_map/ppermute | solution.py:28
  148.2 3.3 %collective-permute-start.34 = (bf16[8,7168]{1,0:T(8,128)(2,1)S(1)}, bf16[8,7168]{1,0:T(8,128)(2,1)S(1)}, u32[]{:S(2)}, u32[]{:S(2)}) collective-permute-start(bf16[8,7168]{1,0:T(8,128)(2,1)S(1)} %get-tuple-element.20), channel_id=1, source_target_pairs={{0,42},{1,127},{2,40},{3,125},{4,46},{5,123},{6,44},{7,121},{8,34}... | collective-permute-start | bytes 344072 | tf_op jit(solution)/shard_map/ppermute | solution.py:46
  151.6 2.4 %collective-permute-start.33 = (bf16[8,7168]{1,0:T(8,128)(2,1)S(1)}, bf16[8,7168]{1,0:T(8,128)(2,1)S(1)}, u32[]{:S(2)}, u32[]{:S(2)}) collective-permute-start(bf16[8,7168]{1,0:T(8,128)(2,1)S(1)} %get-tuple-element.21), channel_id=1, source_target_pairs={{0,40},{1,121},{2,42},{3,123},{4,44},{5,125},{6,46},{7,127},{8,32}... | collective-permute-start | bytes 344072 | tf_op jit(solution)/shard_map/ppermute | solution.py:46
  154.5 1.9 %collective-permute-start.32 = (bf16[8,7168]{1,0:T(8,128)(2,1)S(1)}, bf16[8,7168]{1,0:T(8,128)(2,1)S(1)}, u32[]{:S(2)}, u32[]{:S(2)}) collective-permute-start(bf16[8,7168]{1,0:T(8,128)(2,1)S(1)} %get-tuple-element.22), channel_id=1, source_target_pairs={{0,10},{1,31},{2,8},{3,29},{4,14},{5,27},{6,12},{7,25},{8,2},{9,23... | collective-permute-start | bytes 344072 | tf_op jit(solution)/shard_map/ppermute | solution.py:46
  156.5 2.0 %collective-permute-start.31 = (bf16[8,7168]{1,0:T(8,128)(2,1)S(1)}, bf16[8,7168]{1,0:T(8,128)(2,1)S(1)}, u32[]{:S(2)}, u32[]{:S(2)}) collective-permute-start(bf16[8,7168]{1,0:T(8,128)(2,1)S(1)} %get-tuple-element.23), channel_id=1, source_target_pairs={{0,8},{1,25},{2,10},{3,27},{4,12},{5,29},{6,14},{7,31},{8,0},{9,17... | collective-permute-start | bytes 344072 | tf_op jit(solution)/shard_map/ppermute | solution.py:46
  158.5 3.5 %collective-permute-start.30 = (bf16[8,7168]{1,0:T(8,128)(2,1)S(1)}, bf16[8,7168]{1,0:T(8,128)(2,1)S(1)}, u32[]{:S(2)}, u32[]{:S(2)}) collective-permute-start(bf16[8,7168]{1,0:T(8,128)(2,1)S(1)} %get-tuple-element.24), channel_id=1, source_target_pairs={{0,34},{1,103},{2,32},{3,101},{4,38},{5,99},{6,36},{7,97},{8,42},{... | collective-permute-start | bytes 344072 | tf_op jit(solution)/shard_map/ppermute | solution.py:46
  162.0 1.5 collective-permute-start.28
  163.7 1.7 %collective-permute-done.30 = bf16[8,7168]{1,0:T(8,128)(2,1)S(1)} collective-permute-done((bf16[8,7168]{1,0:T(8,128)(2,1)S(1)}, bf16[8,7168]{1,0:T(8,128)(2,1)S(1)}, u32[]{:S(2)}, u32[]{:S(2)}) %collective-permute-start.30) | collective-permute-done | bytes 114720 | tf_op jit(solution)/shard_map/ppermute | solution.py:46
  165.4 1.4 collective-permute-done.29
  (107 shorter events, 11.3 us)
Async XLA Ops:
  3.2 12.0 %collective-permute-start = (bf16[8,7296]{1,0:T(8,128)(2,1)S(1)}, bf16[8,7296]{1,0:T(8,128)(2,1)S(1)}, u32[]{:S(2)}, u32[]{:S(2)}) collective-permute-start(bf16[8,7296]{1,0:T(8,128)(2,1)S(1)} %token_rows.1), channel_id=1, source_target_pairs={{0,2},{1,7},{2,0},{3,5},{4,6},{5,3},{6,4},{7,1},{8,10},{9,15},{10,... | collective-permute-start | bytes 350216 | tf_op jit(solution)/shard_map/ppermute | solution.py:46
  6.5 13.8 %collective-permute-start.1 = (bf16[8,7296]{1,0:T(8,128)(2,1)S(1)}, bf16[8,7296]{1,0:T(8,128)(2,1)S(1)}, u32[]{:S(2)}, u32[]{:S(2)}) collective-permute-start(bf16[8,7296]{1,0:T(8,128)(2,1)S(1)} %token_rows.1), channel_id=1, source_target_pairs={{0,32},{1,97},{2,34},{3,99},{4,36},{5,101},{6,38},{7,103},{8,40},{... | collective-permute-start | bytes 350216 | tf_op jit(solution)/shard_map/ppermute | solution.py:46
  9.3 11.2 %collective-permute-start.2 = (bf16[8,7296]{1,0:T(8,128)(2,1)S(1)}, bf16[8,7296]{1,0:T(8,128)(2,1)S(1)}, u32[]{:S(2)}, u32[]{:S(2)}) collective-permute-start(bf16[8,7296]{1,0:T(8,128)(2,1)S(1)} %token_rows.1), channel_id=1, source_target_pairs={{0,34},{1,103},{2,32},{3,101},{4,38},{5,99},{6,36},{7,97},{8,42},{... | collective-permute-start | bytes 350216 | tf_op jit(solution)/shard_map/ppermute | solution.py:46
  9.3 11.3 %collective-permute-start.3 = (bf16[8,7296]{1,0:T(8,128)(2,1)S(1)}, bf16[8,7296]{1,0:T(8,128)(2,1)S(1)}, u32[]{:S(2)}, u32[]{:S(2)}) collective-permute-start(bf16[8,7296]{1,0:T(8,128)(2,1)S(1)} %token_rows.1), channel_id=1, source_target_pairs={{0,8},{1,25},{2,10},{3,27},{4,12},{5,29},{6,14},{7,31},{8,0},{9,17... | collective-permute-start | bytes 350216 | tf_op jit(solution)/shard_map/ppermute | solution.py:46
  13.0 8.1 %collective-permute-start.4 = (bf16[8,7296]{1,0:T(8,128)(2,1)S(1)}, bf16[8,7296]{1,0:T(8,128)(2,1)S(1)}, u32[]{:S(2)}, u32[]{:S(2)}) collective-permute-start(bf16[8,7296]{1,0:T(8,128)(2,1)S(1)} %token_rows.1), channel_id=1, source_target_pairs={{0,10},{1,31},{2,8},{3,29},{4,14},{5,27},{6,12},{7,25},{8,2},{9,23... | collective-permute-start | bytes 350216 | tf_op jit(solution)/shard_map/ppermute | solution.py:46
  15.2 7.3 %collective-permute-start.5 = (bf16[8,7296]{1,0:T(8,128)(2,1)S(1)}, bf16[8,7296]{1,0:T(8,128)(2,1)S(1)}, u32[]{:S(2)}, u32[]{:S(2)}) collective-permute-start(bf16[8,7296]{1,0:T(8,128)(2,1)S(1)} %token_rows.1), channel_id=1, source_target_pairs={{0,40},{1,121},{2,42},{3,123},{4,44},{5,125},{6,46},{7,127},{8,32}... | collective-permute-start | bytes 350216 | tf_op jit(solution)/shard_map/ppermute | solution.py:46
  20.3 9.3 %collective-permute-start.6 = (bf16[8,7296]{1,0:T(8,128)(2,1)S(1)}, bf16[8,7296]{1,0:T(8,128)(2,1)S(1)}, u32[]{:S(2)}, u32[]{:S(2)}) collective-permute-start(bf16[8,7296]{1,0:T(8,128)(2,1)S(1)} %token_rows.1), channel_id=1, source_target_pairs={{0,42},{1,127},{2,40},{3,125},{4,46},{5,123},{6,44},{7,121},{8,34}... | collective-permute-start | bytes 350216 | tf_op jit(solution)/shard_map/ppermute | solution.py:46
  20.5 39.9 %collective-permute-start.10 = (bf16[7168,256]{1,0:T(8,128)(2,1)}, bf16[7168,256]{1,0:T(8,128)(2,1)S(1)}, u32[]{:S(2)}, u32[]{:S(2)}) collective-permute-start(bf16[7168,256]{1,0:T(8,128)(2,1)} %bitcast.7), channel_id=1, source_target_pairs={{0,1},{1,0},{2,3},{3,2},{4,5},{5,4},{6,7},{7,6},{8,9},{9,8},{10,11... | collective-permute-start | bytes 11010056 | tf_op jit(solution)/shard_map/ppermute | solution.py:54
  20.6 47.9 %collective-permute-start.11 = (bf16[7168,256]{1,0:T(8,128)(2,1)}, bf16[7168,256]{1,0:T(8,128)(2,1)}, u32[]{:S(2)}, u32[]{:S(2)}) collective-permute-start(bf16[7168,256]{1,0:T(8,128)(2,1)} %bitcast.9), channel_id=1, source_target_pairs={{0,1},{1,0},{2,3},{3,2},{4,5},{5,4},{6,7},{7,6},{8,9},{9,8},{10,11... | collective-permute-start | bytes 11010056 | tf_op jit(solution)/shard_map/ppermute | solution.py:54
  29.7 5.9 %collective-permute-start.15 = (bf16[64,2304]{1,0:T(8,128)(2,1)S(1)}, bf16[64,2304]{1,0:T(8,128)(2,1)S(1)}, u32[]{:S(2)}, u32[]{:S(2)}) collective-permute-start(bf16[64,2304]{1,0:T(8,128)(2,1)S(1)} %slice.111), channel_id=1, source_target_pairs={{0,24},{1,9},{8,16},{9,1},{16,8},{17,25},{24,0},{25,17},{2,26},{3,... | collective-permute-start | bytes 884744 | tf_op jit(solution)/shard_map/ppermute | solution.py:28
  29.8 63.0 %collective-permute-start.18 = (bf16[256,7168]{1,0:T(8,128)(2,1)}, bf16[256,7168]{1,0:T(8,128)(2,1)}, u32[]{:S(2)}, u32[]{:S(2)}) collective-permute-start(bf16[256,7168]{1,0:T(8,128)(2,1)} %bitcast.11), channel_id=1, source_target_pairs={{0,1},{1,0},{2,3},{3,2},{4,5},{5,4},{6,7},{7,6},{8,9},{9,8},{10,11... | collective-permute-start | bytes 11010056 | tf_op jit(solution)/shard_map/ppermute | solution.py:54
  29.9 11.5 %collective-permute-start.7 = (bf16[64,2560]{1,0:T(8,128)(2,1)S(1)}, bf16[64,2560]{1,0:T(8,128)(2,1)S(1)}, u32[]{:S(2)}, u32[]{:S(2)}) collective-permute-start(bf16[64,2560]{1,0:T(8,128)(2,1)S(1)} %slice.109), channel_id=1, source_target_pairs={{0,6},{1,3},{2,4},{3,1},{4,2},{5,7},{6,0},{7,5},{8,14},{9,11},{10,... | collective-permute-start | bytes 983048 | tf_op jit(solution)/shard_map/ppermute | solution.py:28
  35.6 5.7 %collective-permute-start.12 = (bf16[64,2432]{1,0:T(8,128)(2,1)S(1)}, bf16[64,2432]{1,0:T(8,128)(2,1)S(1)}, u32[]{:S(2)}, u32[]{:S(2)}) collective-permute-start(bf16[64,2432]{1,0:T(8,128)(2,1)S(1)} %slice.110), channel_id=1, source_target_pairs={{0,96},{1,33},{32,64},{33,1},{64,32},{65,97},{96,0},{97,65},{2,98}... | collective-permute-start | bytes 933896 | tf_op jit(solution)/shard_map/ppermute | solution.py:28
  35.6 26.6 %copy-start.11 = (bf16[1,256,7168]{2,1,0:T(8,128)(2,1)S(1)}, bf16[1,256,7168]{2,1,0:T(8,128)(2,1)}, u32[]{:S(2)}) copy-start(bf16[1,256,7168]{2,1,0:T(8,128)(2,1)} %param.13) | copy-start | bytes 11010052
  41.4 9.0 %collective-permute-start.16 = (bf16[128,2304]{1,0:T(8,128)(2,1)S(1)}, bf16[128,2304]{1,0:T(8,128)(2,1)S(1)}, u32[]{:S(2)}, u32[]{:S(2)}) collective-permute-start(bf16[128,2304]{1,0:T(8,128)(2,1)S(1)} %pad_maximum_fusion.6), channel_id=1, source_target_pairs={{0,6},{1,3},{2,4},{3,1},{4,2},{5,7},{6,0},{7,5},{8,14},{9,11},{10,... | collective-permute-start | bytes 1769480 | tf_op jit(solution)/shard_map/ppermute | solution.py:28
  41.4 9.5 %collective-permute-start.13 = (bf16[128,2432]{1,0:T(8,128)(2,1)S(1)}, bf16[128,2432]{1,0:T(8,128)(2,1)S(1)}, u32[]{:S(2)}, u32[]{:S(2)}) collective-permute-start(bf16[128,2432]{1,0:T(8,128)(2,1)S(1)} %pad_maximum_fusion.5), channel_id=1, source_target_pairs={{0,24},{1,9},{8,16},{9,1},{16,8},{17,25},{24,0},{25,17},{2,26},{3,... | collective-permute-start | bytes 1867784 | tf_op jit(solution)/shard_map/ppermute | solution.py:28
  50.4 9.7 %collective-permute-start.8 = (bf16[128,2560]{1,0:T(8,128)(2,1)S(1)}, bf16[128,2560]{1,0:T(8,128)(2,1)S(1)}, u32[]{:S(2)}, u32[]{:S(2)}) collective-permute-start(bf16[128,2560]{1,0:T(8,128)(2,1)S(1)} %pad_maximum_fusion.4), channel_id=1, source_target_pairs={{0,96},{1,33},{32,64},{33,1},{64,32},{65,97},{96,0},{97,65},{2,98}... | collective-permute-start | bytes 1966088 | tf_op jit(solution)/shard_map/ppermute | solution.py:28
  50.4 11.8 %copy-start.10 = (bf16[1,7168,256]{2,1,0:T(8,128)(2,1)S(1)}, bf16[1,7168,256]{2,1,0:T(8,128)(2,1)}, u32[]{:S(2)}) copy-start(bf16[1,7168,256]{2,1,0:T(8,128)(2,1)} %param.12) | copy-start | bytes 11010052
  50.9 33.8 %collective-permute-start.17 = (bf16[256,2304]{1,0:T(8,128)(2,1)S(1)}, bf16[256,2304]{1,0:T(8,128)(2,1)}, u32[]{:S(2)}, u32[]{:S(2)}) collective-permute-start(bf16[256,2304]{1,0:T(8,128)(2,1)S(1)} %pad_maximum_fusion.3.x2.near_x2), channel_id=1, source_target_pairs={{0,96},{1,33},{32,64},{33,1},{64,32},{65,97},{96,0},{97,65},{2,98}... | collective-permute-start | bytes 3538952 | tf_op jit(solution)/shard_map/ppermute | solution.py:28
  52.0 10.2 %copy-start.9 = (bf16[1,7168,256]{2,1,0:T(8,128)(2,1)S(1)}, bf16[1,7168,256]{2,1,0:T(8,128)(2,1)}, u32[]{:S(2)}) copy-start(bf16[1,7168,256]{2,1,0:T(8,128)(2,1)} %param.11) | copy-start | bytes 11010052
  60.1 21.8 %collective-permute-start.14 = (bf16[256,2432]{1,0:T(8,128)(2,1)}, bf16[256,2432]{1,0:T(8,128)(2,1)}, u32[]{:S(2)}, u32[]{:S(2)}) collective-permute-start(bf16[256,2432]{1,0:T(8,128)(2,1)} %pad_maximum_fusion.2.x1), channel_id=1, source_target_pairs={{0,6},{1,3},{2,4},{3,1},{4,2},{5,7},{6,0},{7,5},{8,14},{9,11},{10,... | collective-permute-start | bytes 3735560 | tf_op jit(solution)/shard_map/ppermute | solution.py:28
  60.3 1.9 %copy-start.12 = (bf16[7168,256]{1,0:T(8,128)(2,1)}, bf16[7168,256]{1,0:T(8,128)(2,1)S(1)}, u32[]{:S(2)}) copy-start(bf16[7168,256]{1,0:T(8,128)(2,1)S(1)} %collective-permute-done.10.refs_0_) | copy-start | bytes 11010052
  62.2 16.9 %collective-permute-start.9 = (bf16[256,2560]{1,0:T(8,128)(2,1)S(1)}, bf16[256,2560]{1,0:T(8,128)(2,1)}, u32[]{:S(2)}, u32[]{:S(2)}) collective-permute-start(bf16[256,2560]{1,0:T(8,128)(2,1)S(1)} %pad_maximum_fusion.1.x0), channel_id=1, source_target_pairs={{0,24},{1,9},{8,16},{9,1},{16,8},{17,25},{24,0},{25,17},{2,26},{3,... | collective-permute-start | bytes 3932168 | tf_op jit(solution)/shard_map/ppermute | solution.py:28
  63.0 1.8 %copy-start = (bf16[256,7168]{1,0:T(8,128)(2,1)}, bf16[256,7168]{1,0:T(8,128)(2,1)S(1)}, u32[]{:S(2)}) copy-start(bf16[256,7168]{1,0:T(8,128)(2,1)S(1)} %get-tuple-element.15.own) | copy-start | bytes 11010052
  64.8 1.8 %copy-start.2 = (bf16[7168,256]{1,0:T(8,128)(2,1)}, bf16[7168,256]{1,0:T(8,128)(2,1)S(1)}, u32[]{:S(2)}) copy-start(bf16[7168,256]{1,0:T(8,128)(2,1)S(1)} %get-tuple-element.10.w0) | copy-start | bytes 11010052
  66.6 1.9 %copy-start.4 = (bf16[7168,256]{1,0:T(8,128)(2,1)}, bf16[7168,256]{1,0:T(8,128)(2,1)S(1)}, u32[]{:S(2)}) copy-start(bf16[7168,256]{1,0:T(8,128)(2,1)S(1)} %get-tuple-element.12.w2) | copy-start | bytes 11010052
  68.5 2.0 %copy-start.13 = (bf16[7168,256]{1,0:T(8,128)(2,1)S(1)}, bf16[7168,256]{1,0:T(8,128)(2,1)}, u32[]{:S(2)}) copy-start(bf16[7168,256]{1,0:T(8,128)(2,1)} %copy-done.12) | copy-start | bytes 11010052
  70.5 8.6 %copy-start.3 = (bf16[7168,256]{1,0:T(8,128)(2,1)S(1)}, bf16[7168,256]{1,0:T(8,128)(2,1)}, u32[]{:S(2)}) copy-start(bf16[7168,256]{1,0:T(8,128)(2,1)} %copy-done.2) | copy-start | bytes 11010052
  70.5 8.6 %copy-start.5 = (bf16[7168,256]{1,0:T(8,128)(2,1)S(1)}, bf16[7168,256]{1,0:T(8,128)(2,1)}, u32[]{:S(2)}) copy-start(bf16[7168,256]{1,0:T(8,128)(2,1)} %copy-done.4) | copy-start | bytes 11010052
  94.8 2.4 %copy-start.1 = (bf16[256,7168]{1,0:T(8,128)(2,1)S(1)}, bf16[256,7168]{1,0:T(8,128)(2,1)}, u32[]{:S(2)}) copy-start(bf16[256,7168]{1,0:T(8,128)(2,1)} %copy-done) | copy-start | bytes 11010052
  98.0 14.7 %collective-permute-start.19 = (bf16[256,2176]{1,0:T(8,128)(2,1)S(1)}, bf16[256,2176]{1,0:T(8,128)(2,1)S(1)}, u32[]{:S(2)}, u32[]{:S(2)}) collective-permute-start(bf16[256,2176]{1,0:T(8,128)(2,1)S(1)} %shard_map.98), channel_id=1, source_target_pairs={{0,24},{1,9},{8,16},{9,1},{16,8},{17,25},{24,0},{25,17},{2,26},{3,... | collective-permute-start | bytes 3342344 | tf_op jit(solution)/shard_map/ppermute | solution.py:28
  99.0 16.1 %collective-permute-start.22 = (bf16[256,2432]{1,0:T(8,128)(2,1)S(1)}, bf16[256,2432]{1,0:T(8,128)(2,1)S(1)}, u32[]{:S(2)}, u32[]{:S(2)}) collective-permute-start(bf16[256,2432]{1,0:T(8,128)(2,1)S(1)} %shard_map.100), channel_id=1, source_target_pairs={{0,6},{1,3},{2,4},{3,1},{4,2},{5,7},{6,0},{7,5},{8,14},{9,11},{10,... | collective-permute-start | bytes 3735560 | tf_op jit(solution)/shard_map/ppermute | solution.py:28
  100.4 11.4 %collective-permute-start.35 = (s32[1,128]{1,0:T(1,128)S(1)}, s32[1,128]{1,0:T(1,128)S(1)}, u32[]{:S(2)}, u32[]{:S(2)}) collective-permute-start(s32[1,128]{1,0:T(1,128)S(1)} %get-tuple-element.16), channel_id=1, source_target_pairs={{0,1},{1,0},{2,3},{3,2},{4,5},{5,4},{6,7},{7,6},{8,9},{9,8},{10,11... | collective-permute-start | bytes 1544 | tf_op jit(solution)/shard_map/ppermute | solution.py:54
  111.7 16.8 %collective-permute-start.25 = (bf16[256,2560]{1,0:T(8,128)(2,1)S(1)}, bf16[256,2560]{1,0:T(8,128)(2,1)S(1)}, u32[]{:S(2)}, u32[]{:S(2)}) collective-permute-start(bf16[256,2560]{1,0:T(8,128)(2,1)S(1)} %shard_map.102), channel_id=1, source_target_pairs={{0,96},{1,33},{32,64},{33,1},{64,32},{65,97},{96,0},{97,65},{2,98}... | collective-permute-start | bytes 3932168 | tf_op jit(solution)/shard_map/ppermute | solution.py:28
  113.0 21.5 %collective-permute-start.20 = (bf16[128,2176]{1,0:T(8,128)(2,1)S(1)}, bf16[128,2176]{1,0:T(8,128)(2,1)S(1)}, u32[]{:S(2)}, u32[]{:S(2)}) collective-permute-start(bf16[128,2176]{1,0:T(8,128)(2,1)S(1)} %slice.162), channel_id=1, source_target_pairs={{0,96},{1,33},{32,64},{33,1},{64,32},{65,97},{96,0},{97,65},{2,98}... | collective-permute-start | bytes 1671176 | tf_op jit(solution)/shard_map/ppermute | solution.py:28
  115.4 19.3 %collective-permute-start.23 = (bf16[128,2432]{1,0:T(8,128)(2,1)S(1)}, bf16[128,2432]{1,0:T(8,128)(2,1)S(1)}, u32[]{:S(2)}, u32[]{:S(2)}) collective-permute-start(bf16[128,2432]{1,0:T(8,128)(2,1)S(1)} %slice.161), channel_id=1, source_target_pairs={{0,24},{1,9},{8,16},{9,1},{16,8},{17,25},{24,0},{25,17},{2,26},{3,... | collective-permute-start | bytes 1867784 | tf_op jit(solution)/shard_map/ppermute | solution.py:28
  128.9 12.9 %collective-permute-start.26 = (bf16[128,2560]{1,0:T(8,128)(2,1)S(1)}, bf16[128,2560]{1,0:T(8,128)(2,1)S(1)}, u32[]{:S(2)}, u32[]{:S(2)}) collective-permute-start(bf16[128,2560]{1,0:T(8,128)(2,1)S(1)} %slice.160), channel_id=1, source_target_pairs={{0,6},{1,3},{2,4},{3,1},{4,2},{5,7},{6,0},{7,5},{8,14},{9,11},{10,... | collective-permute-start | bytes 1966088 | tf_op jit(solution)/shard_map/ppermute | solution.py:28
  134.6 7.1 %collective-permute-start.21 = (bf16[64,2176]{1,0:T(8,128)(2,1)S(1)}, bf16[64,2176]{1,0:T(8,128)(2,1)S(1)}, u32[]{:S(2)}, u32[]{:S(2)}) collective-permute-start(bf16[64,2176]{1,0:T(8,128)(2,1)S(1)} %slice.165), channel_id=1, source_target_pairs={{0,6},{1,3},{2,4},{3,1},{4,2},{5,7},{6,0},{7,5},{8,14},{9,11},{10,... | collective-permute-start | bytes 835592 | tf_op jit(solution)/shard_map/ppermute | solution.py:28
  134.9 7.2 %collective-permute-start.24 = (bf16[64,2432]{1,0:T(8,128)(2,1)S(1)}, bf16[64,2432]{1,0:T(8,128)(2,1)S(1)}, u32[]{:S(2)}, u32[]{:S(2)}) collective-permute-start(bf16[64,2432]{1,0:T(8,128)(2,1)S(1)} %slice.164), channel_id=1, source_target_pairs={{0,96},{1,33},{32,64},{33,1},{64,32},{65,97},{96,0},{97,65},{2,98}... | collective-permute-start | bytes 933896 | tf_op jit(solution)/shard_map/ppermute | solution.py:28
  141.9 6.0 %collective-permute-start.27 = (bf16[64,2560]{1,0:T(8,128)(2,1)S(1)}, bf16[64,2560]{1,0:T(8,128)(2,1)S(1)}, u32[]{:S(2)}, u32[]{:S(2)}) collective-permute-start(bf16[64,2560]{1,0:T(8,128)(2,1)S(1)} %slice.163), channel_id=1, source_target_pairs={{0,24},{1,9},{8,16},{9,1},{16,8},{17,25},{24,0},{25,17},{2,26},{3,... | collective-permute-start | bytes 983048 | tf_op jit(solution)/shard_map/ppermute | solution.py:28
  148.0 5.9 %copy-start.14 = (f32[16]{0:T(128)S(1)}, f32[16]{0:T(128)}, u32[]{:S(2)}) copy-start(f32[16]{0:T(128)} %param.14) | copy-start | bytes 196
  148.2 13.8 %collective-permute-start.34 = (bf16[8,7168]{1,0:T(8,128)(2,1)S(1)}, bf16[8,7168]{1,0:T(8,128)(2,1)S(1)}, u32[]{:S(2)}, u32[]{:S(2)}) collective-permute-start(bf16[8,7168]{1,0:T(8,128)(2,1)S(1)} %get-tuple-element.20), channel_id=1, source_target_pairs={{0,42},{1,127},{2,40},{3,125},{4,46},{5,123},{6,44},{7,121},{8,34}... | collective-permute-start | bytes 344072 | tf_op jit(solution)/shard_map/ppermute | solution.py:46
  151.6 10.5 %collective-permute-start.33 = (bf16[8,7168]{1,0:T(8,128)(2,1)S(1)}, bf16[8,7168]{1,0:T(8,128)(2,1)S(1)}, u32[]{:S(2)}, u32[]{:S(2)}) collective-permute-start(bf16[8,7168]{1,0:T(8,128)(2,1)S(1)} %get-tuple-element.21), channel_id=1, source_target_pairs={{0,40},{1,121},{2,42},{3,123},{4,44},{5,125},{6,46},{7,127},{8,32}... | collective-permute-start | bytes 344072 | tf_op jit(solution)/shard_map/ppermute | solution.py:46
  154.5 9.1 %collective-permute-start.32 = (bf16[8,7168]{1,0:T(8,128)(2,1)S(1)}, bf16[8,7168]{1,0:T(8,128)(2,1)S(1)}, u32[]{:S(2)}, u32[]{:S(2)}) collective-permute-start(bf16[8,7168]{1,0:T(8,128)(2,1)S(1)} %get-tuple-element.22), channel_id=1, source_target_pairs={{0,10},{1,31},{2,8},{3,29},{4,14},{5,27},{6,12},{7,25},{8,2},{9,23... | collective-permute-start | bytes 344072 | tf_op jit(solution)/shard_map/ppermute | solution.py:46
  156.5 7.2 %collective-permute-start.31 = (bf16[8,7168]{1,0:T(8,128)(2,1)S(1)}, bf16[8,7168]{1,0:T(8,128)(2,1)S(1)}, u32[]{:S(2)}, u32[]{:S(2)}) collective-permute-start(bf16[8,7168]{1,0:T(8,128)(2,1)S(1)} %get-tuple-element.23), channel_id=1, source_target_pairs={{0,8},{1,25},{2,10},{3,27},{4,12},{5,29},{6,14},{7,31},{8,0},{9,17... | collective-permute-start | bytes 344072 | tf_op jit(solution)/shard_map/ppermute | solution.py:46
  158.5 7.0 %collective-permute-start.30 = (bf16[8,7168]{1,0:T(8,128)(2,1)S(1)}, bf16[8,7168]{1,0:T(8,128)(2,1)S(1)}, u32[]{:S(2)}, u32[]{:S(2)}) collective-permute-start(bf16[8,7168]{1,0:T(8,128)(2,1)S(1)} %get-tuple-element.24), channel_id=1, source_target_pairs={{0,34},{1,103},{2,32},{3,101},{4,38},{5,99},{6,36},{7,97},{8,42},{... | collective-permute-start | bytes 344072 | tf_op jit(solution)/shard_map/ppermute | solution.py:46
  162.0 4.9 %collective-permute-start.29 = (bf16[8,7168]{1,0:T(8,128)(2,1)S(1)}, bf16[8,7168]{1,0:T(8,128)(2,1)S(1)}, u32[]{:S(2)}, u32[]{:S(2)}) collective-permute-start(bf16[8,7168]{1,0:T(8,128)(2,1)S(1)} %get-tuple-element.25), channel_id=1, source_target_pairs={{0,32},{1,97},{2,34},{3,99},{4,36},{5,101},{6,38},{7,103},{8,40},{... | collective-permute-start | bytes 344072 | tf_op jit(solution)/shard_map/ppermute | solution.py:46
  162.0 4.9 %collective-permute-start.28 = (bf16[8,7168]{1,0:T(8,128)(2,1)S(1)}, bf16[8,7168]{1,0:T(8,128)(2,1)S(1)}, u32[]{:S(2)}, u32[]{:S(2)}) collective-permute-start(bf16[8,7168]{1,0:T(8,128)(2,1)S(1)} %get-tuple-element.19), channel_id=1, source_target_pairs={{0,2},{1,7},{2,0},{3,5},{4,6},{5,3},{6,4},{7,1},{8,10},{9,15},{10,... | collective-permute-start | bytes 344072 | tf_op jit(solution)/shard_map/ppermute | solution.py:46
  (3 other events, 2.3 us)

commit v6 on v5

--- a/solution.py
+++ b/solution.py
@@ -14,8 +14,8 @@
 EARLY = (X, Y, Z)
 LATE = ((X, Y, Z), (Y, Z, X), (Z, X, Y))
 INFO = 128
-CUTS = (0, 2560, 4992, 7168)
-COL_CUTS = (0, 2176, 4608, 7168)
+CUTS = (0, 2432, 4864, 7168)
+COL_CUTS = (0, 2432, 4864, 7168)
 BF16 = jnp.bfloat16
 F32 = jnp.float32
 
@@ -63,42 +63,30 @@
 SMEM = pl.BlockSpec(memory_space=pltpu.SMEM)
 
 
-def rows_kernel(experts, tokens, ids_in, weights_in, out, ids, weights, sem):
+def rows_kernel(experts, tokens, routes, out):
     width = tokens.shape[1]
-    copies = (
-        pltpu.make_async_copy(ids_in, ids, sem.at[0]),
-        pltpu.make_async_copy(weights_in, weights, sem.at[1]),
-        pltpu.make_async_copy(tokens, out.at[:, pl.ds(0, width)], sem.at[2]),
-    )
-    for c in copies:
-        c.start()
-    copies[0].wait()
-    copies[1].wait()
-    lane = lax.broadcasted_iota(jnp.int32, (tokens.shape[0], INFO), 1)
+    count = routes.shape[1] // 2
+    out[:, :width] = tokens[...]
+    lane = lax.broadcasted_iota(jnp.int32, (tokens.shape[0], INFO), 1).astype(F32)
     info = jnp.zeros((tokens.shape[0], INFO), F32)
-    for k in range(ids.shape[1]):
-        chosen = ids[:, k : k + 1]
-        info += jnp.where(lane == chosen, weights[:, k : k + 1].astype(F32), 0.0)
+    for k in range(count):
+        chosen = routes[:, k : k + 1]
+        info += jnp.where(lane == chosen, routes[:, count + k : count + k + 1], 0.0)
         info += jnp.where(lane == chosen + experts, 1.0, 0.0)
     out[:, width:] = info.astype(BF16)
-    copies[2].wait()
 
 
 def rows_of(tokens, ids, weights, experts):
     rows, width = tokens.shape
+    routes = jnp.concatenate([ids.astype(F32), weights.astype(F32)], axis=1)
     return pl.pallas_call(
         functools.partial(rows_kernel, experts),
         out_shape=jax.ShapeDtypeStruct((rows, width + INFO), BF16),
-        in_specs=[pl.BlockSpec(memory_space=pltpu.HBM)] * 3,
+        in_specs=[VMEM] * 2,
         out_specs=VMEM,
-        scratch_shapes=[
-            pltpu.VMEM(ids.shape, ids.dtype),
-            pltpu.VMEM(weights.shape, weights.dtype),
-            pltpu.SemaphoreType.DMA((3,)),
-        ],
         compiler_params=pltpu.CompilerParams(vmem_limit_bytes=4 << 20),
         name="token_rows",
-    )(tokens, ids, weights)
+    )(tokens, routes)
 
 
 def near_kernel(x0, x1, x2, w0, w1, w2, w3, acc):

time: 168 us -> 161 us (0.958); the launches traced: 168 us -> 158 us
  waiting for transfers between devices: 77.1 us -> 61.2 us
  starting transfers between devices: 46.4 us -> 49.4 us
    ppermute x18, waiting for transfers between devices: 65.4 us -> 50.7 us  [exchange(): return lax.ppermute(value, (axis, 'gz_1'), pairs)]
    ppermute x4, starting transfers between devices: 8.68 us -> 10.9 us  [partner(): return lax.ppermute(value, 'gz_1', [(0, 1), (1, 0)])]
    pallas_call x3, Pallas kernels: 5.26 us -> 7.05 us  [in_vmem(): pl.pallas_call(load_kernel, out_shape=tuple((jax.ShapeDtypeStruct(a.shape...]
    unnamed x37 -> x31, local copies, waits for them, and re-layouts: 12.3 us -> 12.7 us
  transfers between devices with their start and end apart: 36 -> 36, of which waited for: 17 -> 16; matrix products, arithmetic and copies ran while one was open for 2% -> 2% of each run, Pallas kernels for 13% -> 14%
where the time goes in v6:
time: 161 us; the launch traced here: 158 us
  waiting for transfers between devices  61.2 us (38%)
  starting transfers between devices  49.4 us (31%)
  Pallas kernels  27.6 us (17%)
  local copies, waits for them, and re-layouts  13.2 us (8%)
  other arithmetic  5.72 us (4%)
    ppermute x18, waiting for transfers between devices, exchange(): return lax.ppermute(value, (axis, 'gz_1'), pairs)  50.7 us
    ppermute x14, starting transfers between devices, direct(): return lax.ppermute(value, AXES, pairs)  31.9 us
    unnamed x31, local copies, waits for them, and re-layouts  12.7 us
    ppermute x4, starting transfers between devices, partner(): return lax.ppermute(value, 'gz_1', [(0, 1), (1, 0)])  10.9 us
    ppermute x14, waiting for transfers between devices, direct(): return lax.ppermute(value, AXES, pairs)  10.6 us
    pallas_call x3, Pallas kernels, gate_up_far_part(): pl.pallas_call(functools.partial(far_part_kernel, colour), out_shape=jax....  8.28 us
    pallas_call x3, Pallas kernels, in_vmem(): pl.pallas_call(load_kernel, out_shape=tuple((jax.ShapeDtypeStruct(a.shape...  7.05 us
    ppermute x18, starting transfers between devices, exchange(): return lax.ppermute(value, (axis, 'gz_1'), pairs)  6.61 us
  transfers between devices with their start and end apart: 36, of which 16 were waited for; matrix products, arithmetic and copies ran while one was open for 2% of the time, Pallas kernels for 14%

profile of v6, /device:TPU:1, one launch (start us, length us, event | category | flops | bytes accessed | tf_op | source)
XLA Modules:
  0.0 158.3 jit_solution(13042820131585502065)
XLA Ops:
  2.1 0.9 copy-done.6
  3.1 3.4 %collective-permute-start = (bf16[8,7296]{1,0:T(8,128)(2,1)S(1)}, bf16[8,7296]{1,0:T(8,128)(2,1)S(1)}, u32[]{:S(2)}, u32[]{:S(2)}) collective-permute-start(bf16[8,7296]{1,0:T(8,128)(2,1)S(1)} %token_rows.1), channel_id=1, source_target_pairs={{0,2},{1,7},{2,0},{3,5},{4,6},{5,3},{6,4},{7,1},{8,10},{9,15},{10,... | collective-permute-start | bytes 350216 | tf_op jit(solution)/shard_map/ppermute | solution.py:46
  6.5 2.7 %collective-permute-start.1 = (bf16[8,7296]{1,0:T(8,128)(2,1)S(1)}, bf16[8,7296]{1,0:T(8,128)(2,1)S(1)}, u32[]{:S(2)}, u32[]{:S(2)}) collective-permute-start(bf16[8,7296]{1,0:T(8,128)(2,1)S(1)} %token_rows.1), channel_id=1, source_target_pairs={{0,32},{1,97},{2,34},{3,99},{4,36},{5,101},{6,38},{7,103},{8,40},{... | collective-permute-start | bytes 350216 | tf_op jit(solution)/shard_map/ppermute | solution.py:46
  9.2 3.8 %collective-permute-start.3 = (bf16[8,7296]{1,0:T(8,128)(2,1)S(1)}, bf16[8,7296]{1,0:T(8,128)(2,1)S(1)}, u32[]{:S(2)}, u32[]{:S(2)}) collective-permute-start(bf16[8,7296]{1,0:T(8,128)(2,1)S(1)} %token_rows.1), channel_id=1, source_target_pairs={{0,8},{1,25},{2,10},{3,27},{4,12},{5,29},{6,14},{7,31},{8,0},{9,17... | collective-permute-start | bytes 350216 | tf_op jit(solution)/shard_map/ppermute | solution.py:46
  13.0 2.1 %collective-permute-start.4 = (bf16[8,7296]{1,0:T(8,128)(2,1)S(1)}, bf16[8,7296]{1,0:T(8,128)(2,1)S(1)}, u32[]{:S(2)}, u32[]{:S(2)}) collective-permute-start(bf16[8,7296]{1,0:T(8,128)(2,1)S(1)} %token_rows.1), channel_id=1, source_target_pairs={{0,10},{1,31},{2,8},{3,29},{4,14},{5,27},{6,12},{7,25},{8,2},{9,23... | collective-permute-start | bytes 350216 | tf_op jit(solution)/shard_map/ppermute | solution.py:46
  15.1 5.1 %collective-permute-start.5 = (bf16[8,7296]{1,0:T(8,128)(2,1)S(1)}, bf16[8,7296]{1,0:T(8,128)(2,1)S(1)}, u32[]{:S(2)}, u32[]{:S(2)}) collective-permute-start(bf16[8,7296]{1,0:T(8,128)(2,1)S(1)} %token_rows.1), channel_id=1, source_target_pairs={{0,40},{1,121},{2,42},{3,123},{4,44},{5,125},{6,46},{7,127},{8,32}... | collective-permute-start | bytes 350216 | tf_op jit(solution)/shard_map/ppermute | solution.py:46
  21.1 1.3 collective-permute-done.5
  22.5 7.0 %collective-permute-done.6 = bf16[8,7296]{1,0:T(8,128)(2,1)S(1)} collective-permute-done((bf16[8,7296]{1,0:T(8,128)(2,1)S(1)}, bf16[8,7296]{1,0:T(8,128)(2,1)S(1)}, u32[]{:S(2)}, u32[]{:S(2)}) %collective-permute-start.6) | collective-permute-done | bytes 116768 | tf_op jit(solution)/shard_map/ppermute | solution.py:46
  29.8 5.8 %collective-permute-done.7 = bf16[64,2432]{1,0:T(8,128)(2,1)S(1)} collective-permute-done((bf16[64,2432]{1,0:T(8,128)(2,1)S(1)}, bf16[64,2432]{1,0:T(8,128)(2,1)S(1)}, u32[]{:S(2)}, u32[]{:S(2)}) %collective-permute-start.7) | collective-permute-done | bytes 311328 | tf_op jit(solution)/shard_map/ppermute | solution.py:28
  35.9 5.5 %collective-permute-done.15 = bf16[64,2432]{1,0:T(8,128)(2,1)S(1)} collective-permute-done((bf16[64,2432]{1,0:T(8,128)(2,1)S(1)}, bf16[64,2432]{1,0:T(8,128)(2,1)S(1)}, u32[]{:S(2)}, u32[]{:S(2)}) %collective-permute-start.15) | collective-permute-done | bytes 311328 | tf_op jit(solution)/shard_map/ppermute | solution.py:28
  41.7 3.5 %collective-permute-done.8 = bf16[128,2432]{1,0:T(8,128)(2,1)S(1)} collective-permute-done((bf16[128,2432]{1,0:T(8,128)(2,1)S(1)}, bf16[128,2432]{1,0:T(8,128)(2,1)S(1)}, u32[]{:S(2)}, u32[]{:S(2)}) %collective-permute-start.8) | collective-permute-done | bytes 622624 | tf_op jit(solution)/shard_map/ppermute | solution.py:28
  45.2 1.3 collective-permute-start.16
  46.6 3.9 %collective-permute-done.13 = bf16[128,2432]{1,0:T(8,128)(2,1)S(1)} collective-permute-done((bf16[128,2432]{1,0:T(8,128)(2,1)S(1)}, bf16[128,2432]{1,0:T(8,128)(2,1)S(1)}, u32[]{:S(2)}, u32[]{:S(2)}) %collective-permute-start.13) | collective-permute-done | bytes 622624 | tf_op jit(solution)/shard_map/ppermute | solution.py:28
  51.2 1.2 pad_maximum_fusion.2.x1
  52.3 2.2 %collective-permute-done.16 = bf16[128,2432]{1,0:T(8,128)(2,1)S(1)} collective-permute-done((bf16[128,2432]{1,0:T(8,128)(2,1)S(1)}, bf16[128,2432]{1,0:T(8,128)(2,1)S(1)}, u32[]{:S(2)}, u32[]{:S(2)}) %collective-permute-start.16) | collective-permute-done | bytes 622624 | tf_op jit(solution)/shard_map/ppermute | solution.py:28
  54.6 1.3 collective-permute-start.14
  56.0 1.9 %copy-done.9 = bf16[7168,256]{1,0:T(8,128)(2,1)} copy-done((bf16[7168,256]{1,0:T(8,128)(2,1)}, bf16[7168,256]{1,0:T(8,128)(2,1)S(1)}, u32[]{:S(2)}) %copy-start.9) | copy-done | bytes 3670040
  58.0 2.6 %weights_in.3 = (bf16[7168,256]{1,0:T(8,128)(2,1)S(1)}, bf16[7168,256]{1,0:T(8,128)(2,1)S(1)}, bf16[256,7168]{1,0:T(8,128)(2,1)S(1)}) custom-call(bf16[7168,256]{1,0:T(8,128)(2,1)S(1)} %bitcast.8, bf16[7168,256]{1,0:T(8,128)(2,1)S(1)} %bitcast.10, bf16[256,7168]{1,0:T(8,128)(2,1)} %bitcast.3.refs_2_), custom_call_target="tpu_custom_call" | custom-call | flops 8589934592 | tf_op jit(solution)/shard_map/weights_in/pallas_call | solution.py:160
  60.6 1.8 %copy-done = bf16[256,7168]{1,0:T(8,128)(2,1)} copy-done((bf16[256,7168]{1,0:T(8,128)(2,1)}, bf16[256,7168]{1,0:T(8,128)(2,1)S(1)}, u32[]{:S(2)}) %copy-start) | copy-done | bytes 3670040
  62.3 1.8 %copy-done.2 = bf16[7168,256]{1,0:T(8,128)(2,1)} copy-done((bf16[7168,256]{1,0:T(8,128)(2,1)}, bf16[7168,256]{1,0:T(8,128)(2,1)S(1)}, u32[]{:S(2)}) %copy-start.2) | copy-done | bytes 3670040
  64.2 1.9 %copy-done.4 = bf16[7168,256]{1,0:T(8,128)(2,1)} copy-done((bf16[7168,256]{1,0:T(8,128)(2,1)}, bf16[7168,256]{1,0:T(8,128)(2,1)S(1)}, u32[]{:S(2)}) %copy-start.4) | copy-done | bytes 3670040
  66.0 2.0 %copy-done.10 = bf16[7168,256]{1,0:T(8,128)(2,1)S(1)} copy-done((bf16[7168,256]{1,0:T(8,128)(2,1)S(1)}, bf16[7168,256]{1,0:T(8,128)(2,1)}, u32[]{:S(2)}) %copy-start.10) | copy-done | bytes 3670040
  68.1 2.4 %weights_in.4 = (bf16[7168,256]{1,0:T(8,128)(2,1)S(1)}, bf16[7168,256]{1,0:T(8,128)(2,1)S(1)}) custom-call(bf16[7168,256]{1,0:T(8,128)(2,1)S(1)} %copy-done.10, bf16[7168,256]{1,0:T(8,128)(2,1)} %collective-permute-done.11.refs_1_), custom_call_target="tpu_custom_call" | custom-call | flops 8589934592 | tf_op jit(solution)/shard_map/weights_in/pallas_call | solution.py:160
  71.2 1.1 copy-done.5
  72.3 2.8 %shard_map.94.part0 = f32[4,256,256]{2,1,0:T(8,128)S(1)} custom-call(bf16[256,2432]{1,0:T(8,128)(2,1)} %collective-permute-done.9.x, bf16[7168,256]{1,0:T(8,128)(2,1)S(1)} %copy-done.3, bf16[7168,256]{1,0:T(8,128)(2,1)S(1)} %get-tuple-element.11.w1, bf16[7168,256]{1,0:T(8,128)(2,1)S(1)} %copy-done.5, bf16[7168,256]{1,0:T(8,128)(2,1)S(1)} %get-tuple-element.13.w3), custom_call_target="tpu_custom_call" | custom-call | flops 1252524032 | tf_op jit(solution)/shard_map/pallas_call | solution.py:191
  75.1 2.8 %shard_map.95.part1 = f32[4,256,256]{2,1,0:T(8,128)S(1)} custom-call(bf16[256,2432]{1,0:T(8,128)(2,1)} %collective-permute-done.14.x, bf16[7168,256]{1,0:T(8,128)(2,1)S(1)} %copy-done.3, bf16[7168,256]{1,0:T(8,128)(2,1)S(1)} %get-tuple-element.11.w1, bf16[7168,256]{1,0:T(8,128)(2,1)S(1)} %copy-done.5, bf16[7168,256]{1,0:T(8,128)(2,1)S(1)} %get-tuple-element.13.w3), custom_call_target="tpu_custom_call" | custom-call | flops 1252524032 | tf_op jit(solution)/shard_map/pallas_call | solution.py:191
  78.0 2.7 %shard_map.96.part2 = f32[4,256,256]{2,1,0:T(8,128)S(1)} custom-call(bf16[256,2432]{1,0:T(8,128)(2,1)} %collective-permute-done.17.x.x2, bf16[7168,256]{1,0:T(8,128)(2,1)S(1)} %copy-done.3, bf16[7168,256]{1,0:T(8,128)(2,1)S(1)} %get-tuple-element.11.w1, bf16[7168,256]{1,0:T(8,128)(2,1)S(1)} %copy-done.5, bf16[7168,256]{1,0:T(8,128)(2,1)S(1)} %get-tuple-element.13.w3), custom_call_target="tpu_custom_call" | custom-call | flops 1252524032 | tf_op jit(solution)/shard_map/pallas_call | solution.py:191
  80.6 5.4 %gate_up_near.1.acc = f32[4,512,256]{2,1,0:T(8,128)S(1)} custom-call(bf16[256,2432]{1,0:T(8,128)(2,1)S(1)} %pad_maximum_fusion.1.x0, bf16[256,2432]{1,0:T(8,128)(2,1)} %pad_maximum_fusion.2.x1, bf16[256,2432]{1,0:T(8,128)(2,1)S(1)} %pad_maximum_fusion.3.x2.near_x2, bf16[7168,256]{1,0:T(8,128)(2,1)S(1)} %copy-done.3, ...), custom_call_target="tpu_custom_call" | custom-call | flops 3757572096 | tf_op jit(solution)/shard_map/gate_up_near/pallas_call | solution.py:179
  86.0 2.0 %weights_in.5.other = bf16[256,7168]{1,0:T(8,128)(2,1)S(1)} custom-call(bf16[256,7168]{1,0:T(8,128)(2,1)} %collective-permute-done.18.refs_0_), custom_call_target="tpu_custom_call" | custom-call | flops 8589934592 | tf_op jit(solution)/shard_map/weights_in/pallas_call | solution.py:160
  88.1 1.9 %hidden.1 = (bf16[512,512]{1,0:T(8,128)(2,1)S(1)}, s32[1,128]{1,0:T(1,128)S(1)}) custom-call(s32[1]{0:T(128)} %bitcast.expert, f32[4,256,256]{2,1,0:T(8,128)S(1)} %shard_map.94.part0, f32[4,256,256]{2,1,0:T(8,128)S(1)} %shard_map.95.part1, f32[4,256,256]{2,1,0:T(8,128)S(1)} %shard_map.96.part2, bf16[256,2432]{1,0:T(8,128)(2,1)S(1)} %pad_maximum_fusion.3.x2.near_x2, ...), custom_call_target="tpu_custom_call" | custom-call | flops 1252524032 | tf_op jit(solution)/shard_map/hidden/pallas_call | solution.py:202
  91.3 1.4 collective-permute-start.25
  92.7 0.8 shard_map.100
  93.9 10.1 %collective-permute-start.35 = (s32[1,128]{1,0:T(1,128)S(1)}, s32[1,128]{1,0:T(1,128)S(1)}, u32[]{:S(2)}, u32[]{:S(2)}) collective-permute-start(s32[1,128]{1,0:T(1,128)S(1)} %get-tuple-element.16), channel_id=1, source_target_pairs={{0,1},{1,0},{2,3},{3,2},{4,5},{5,4},{6,7},{7,6},{8,9},{9,8},{10,11... | collective-permute-start | bytes 1544 | tf_op jit(solution)/shard_map/ppermute | solution.py:54
  104.0 0.8 shard_map.99
  104.9 0.8 shard_map.97
  105.7 0.8 shard_map.98
  108.1 1.7 %collective-permute-done.22 = bf16[256,2432]{1,0:T(8,128)(2,1)S(1)} collective-permute-done((bf16[256,2432]{1,0:T(8,128)(2,1)S(1)}, bf16[256,2432]{1,0:T(8,128)(2,1)S(1)}, u32[]{:S(2)}, u32[]{:S(2)}) %collective-permute-start.22) | collective-permute-done | bytes 1245216 | tf_op jit(solution)/shard_map/ppermute | solution.py:28
  110.3 13.2 %collective-permute-done.19 = bf16[256,2432]{1,0:T(8,128)(2,1)S(1)} collective-permute-done((bf16[256,2432]{1,0:T(8,128)(2,1)S(1)}, bf16[256,2432]{1,0:T(8,128)(2,1)S(1)}, u32[]{:S(2)}, u32[]{:S(2)}) %collective-permute-start.19) | collective-permute-done | bytes 1245216 | tf_op jit(solution)/shard_map/ppermute | solution.py:28
  124.2 6.0 %collective-permute-done.23 = bf16[128,2432]{1,0:T(8,128)(2,1)S(1)} collective-permute-done((bf16[128,2432]{1,0:T(8,128)(2,1)S(1)}, bf16[128,2432]{1,0:T(8,128)(2,1)S(1)}, u32[]{:S(2)}, u32[]{:S(2)}) %collective-permute-start.23) | collective-permute-done | bytes 622624 | tf_op jit(solution)/shard_map/ppermute | solution.py:28
  130.4 2.9 %collective-permute-done.20 = bf16[128,2432]{1,0:T(8,128)(2,1)S(1)} collective-permute-done((bf16[128,2432]{1,0:T(8,128)(2,1)S(1)}, bf16[128,2432]{1,0:T(8,128)(2,1)S(1)}, u32[]{:S(2)}, u32[]{:S(2)}) %collective-permute-start.20) | collective-permute-done | bytes 622624 | tf_op jit(solution)/shard_map/ppermute | solution.py:28
  133.6 3.0 %collective-permute-done.24 = bf16[64,2432]{1,0:T(8,128)(2,1)S(1)} collective-permute-done((bf16[64,2432]{1,0:T(8,128)(2,1)S(1)}, bf16[64,2432]{1,0:T(8,128)(2,1)S(1)}, u32[]{:S(2)}, u32[]{:S(2)}) %collective-permute-start.24) | collective-permute-done | bytes 311328 | tf_op jit(solution)/shard_map/ppermute | solution.py:28
  136.7 2.9 %collective-permute-done.21 = bf16[64,2432]{1,0:T(8,128)(2,1)S(1)} collective-permute-done((bf16[64,2432]{1,0:T(8,128)(2,1)S(1)}, bf16[64,2432]{1,0:T(8,128)(2,1)S(1)}, u32[]{:S(2)}, u32[]{:S(2)}) %collective-permute-start.21) | collective-permute-done | bytes 311328 | tf_op jit(solution)/shard_map/ppermute | solution.py:28
  139.9 4.7 %collective-permute-start.33 = (bf16[8,7168]{1,0:T(8,128)(2,1)S(1)}, bf16[8,7168]{1,0:T(8,128)(2,1)S(1)}, u32[]{:S(2)}, u32[]{:S(2)}) collective-permute-start(bf16[8,7168]{1,0:T(8,128)(2,1)S(1)} %get-tuple-element.24), channel_id=1, source_target_pairs={{0,40},{1,121},{2,42},{3,123},{4,44},{5,125},{6,46},{7,127},{8,32}... | collective-permute-start | bytes 344072 | tf_op jit(solution)/shard_map/ppermute | solution.py:46
  145.2 2.2 %collective-permute-start.32 = (bf16[8,7168]{1,0:T(8,128)(2,1)S(1)}, bf16[8,7168]{1,0:T(8,128)(2,1)S(1)}, u32[]{:S(2)}, u32[]{:S(2)}) collective-permute-start(bf16[8,7168]{1,0:T(8,128)(2,1)S(1)} %get-tuple-element.25), channel_id=1, source_target_pairs={{0,10},{1,31},{2,8},{3,29},{4,14},{5,27},{6,12},{7,25},{8,2},{9,23... | collective-permute-start | bytes 344072 | tf_op jit(solution)/shard_map/ppermute | solution.py:46
  147.4 2.7 %collective-permute-start.31 = (bf16[8,7168]{1,0:T(8,128)(2,1)S(1)}, bf16[8,7168]{1,0:T(8,128)(2,1)S(1)}, u32[]{:S(2)}, u32[]{:S(2)}) collective-permute-start(bf16[8,7168]{1,0:T(8,128)(2,1)S(1)} %get-tuple-element.26), channel_id=1, source_target_pairs={{0,8},{1,25},{2,10},{3,27},{4,12},{5,29},{6,14},{7,31},{8,0},{9,17... | collective-permute-start | bytes 344072 | tf_op jit(solution)/shard_map/ppermute | solution.py:46
  150.1 2.6 %collective-permute-start.29 = (bf16[8,7168]{1,0:T(8,128)(2,1)S(1)}, bf16[8,7168]{1,0:T(8,128)(2,1)S(1)}, u32[]{:S(2)}, u32[]{:S(2)}) collective-permute-start(bf16[8,7168]{1,0:T(8,128)(2,1)S(1)} %get-tuple-element.28), channel_id=1, source_target_pairs={{0,32},{1,97},{2,34},{3,99},{4,36},{5,101},{6,38},{7,103},{8,40},{... | collective-permute-start | bytes 344072 | tf_op jit(solution)/shard_map/ppermute | solution.py:46
  152.7 2.5 %collective-permute-start.28 = (bf16[8,7168]{1,0:T(8,128)(2,1)S(1)}, bf16[8,7168]{1,0:T(8,128)(2,1)S(1)}, u32[]{:S(2)}, u32[]{:S(2)}) collective-permute-start(bf16[8,7168]{1,0:T(8,128)(2,1)S(1)} %get-tuple-element.22), channel_id=1, source_target_pairs={{0,2},{1,7},{2,0},{3,5},{4,6},{5,3},{6,4},{7,1},{8,10},{9,15},{10,... | collective-permute-start | bytes 344072 | tf_op jit(solution)/shard_map/ppermute | solution.py:46
  155.3 1.7 %collective-permute-done.30 = bf16[8,7168]{1,0:T(8,128)(2,1)S(1)} collective-permute-done((bf16[8,7168]{1,0:T(8,128)(2,1)S(1)}, bf16[8,7168]{1,0:T(8,128)(2,1)S(1)}, u32[]{:S(2)}, u32[]{:S(2)}) %collective-permute-start.30) | collective-permute-done | bytes 114720 | tf_op jit(solution)/shard_map/ppermute | solution.py:46
  (102 shorter events, 12.2 us)
Async XLA Ops:
  2.1 0.9 copy-start.6
  3.1 12.0 %collective-permute-start = (bf16[8,7296]{1,0:T(8,128)(2,1)S(1)}, bf16[8,7296]{1,0:T(8,128)(2,1)S(1)}, u32[]{:S(2)}, u32[]{:S(2)}) collective-permute-start(bf16[8,7296]{1,0:T(8,128)(2,1)S(1)} %token_rows.1), channel_id=1, source_target_pairs={{0,2},{1,7},{2,0},{3,5},{4,6},{5,3},{6,4},{7,1},{8,10},{9,15},{10,... | collective-permute-start | bytes 350216 | tf_op jit(solution)/shard_map/ppermute | solution.py:46
  6.5 13.8 %collective-permute-start.1 = (bf16[8,7296]{1,0:T(8,128)(2,1)S(1)}, bf16[8,7296]{1,0:T(8,128)(2,1)S(1)}, u32[]{:S(2)}, u32[]{:S(2)}) collective-permute-start(bf16[8,7296]{1,0:T(8,128)(2,1)S(1)} %token_rows.1), channel_id=1, source_target_pairs={{0,32},{1,97},{2,34},{3,99},{4,36},{5,101},{6,38},{7,103},{8,40},{... | collective-permute-start | bytes 350216 | tf_op jit(solution)/shard_map/ppermute | solution.py:46
  9.2 11.2 %collective-permute-start.2 = (bf16[8,7296]{1,0:T(8,128)(2,1)S(1)}, bf16[8,7296]{1,0:T(8,128)(2,1)S(1)}, u32[]{:S(2)}, u32[]{:S(2)}) collective-permute-start(bf16[8,7296]{1,0:T(8,128)(2,1)S(1)} %token_rows.1), channel_id=1, source_target_pairs={{0,34},{1,103},{2,32},{3,101},{4,38},{5,99},{6,36},{7,97},{8,42},{... | collective-permute-start | bytes 350216 | tf_op jit(solution)/shard_map/ppermute | solution.py:46
  9.2 11.3 %collective-permute-start.3 = (bf16[8,7296]{1,0:T(8,128)(2,1)S(1)}, bf16[8,7296]{1,0:T(8,128)(2,1)S(1)}, u32[]{:S(2)}, u32[]{:S(2)}) collective-permute-start(bf16[8,7296]{1,0:T(8,128)(2,1)S(1)} %token_rows.1), channel_id=1, source_target_pairs={{0,8},{1,25},{2,10},{3,27},{4,12},{5,29},{6,14},{7,31},{8,0},{9,17... | collective-permute-start | bytes 350216 | tf_op jit(solution)/shard_map/ppermute | solution.py:46
  13.0 8.1 %collective-permute-start.4 = (bf16[8,7296]{1,0:T(8,128)(2,1)S(1)}, bf16[8,7296]{1,0:T(8,128)(2,1)S(1)}, u32[]{:S(2)}, u32[]{:S(2)}) collective-permute-start(bf16[8,7296]{1,0:T(8,128)(2,1)S(1)} %token_rows.1), channel_id=1, source_target_pairs={{0,10},{1,31},{2,8},{3,29},{4,14},{5,27},{6,12},{7,25},{8,2},{9,23... | collective-permute-start | bytes 350216 | tf_op jit(solution)/shard_map/ppermute | solution.py:46
  15.1 7.3 %collective-permute-start.5 = (bf16[8,7296]{1,0:T(8,128)(2,1)S(1)}, bf16[8,7296]{1,0:T(8,128)(2,1)S(1)}, u32[]{:S(2)}, u32[]{:S(2)}) collective-permute-start(bf16[8,7296]{1,0:T(8,128)(2,1)S(1)} %token_rows.1), channel_id=1, source_target_pairs={{0,40},{1,121},{2,42},{3,123},{4,44},{5,125},{6,46},{7,127},{8,32}... | collective-permute-start | bytes 350216 | tf_op jit(solution)/shard_map/ppermute | solution.py:46
  20.3 9.2 %collective-permute-start.6 = (bf16[8,7296]{1,0:T(8,128)(2,1)S(1)}, bf16[8,7296]{1,0:T(8,128)(2,1)S(1)}, u32[]{:S(2)}, u32[]{:S(2)}) collective-permute-start(bf16[8,7296]{1,0:T(8,128)(2,1)S(1)} %token_rows.1), channel_id=1, source_target_pairs={{0,42},{1,127},{2,40},{3,125},{4,46},{5,123},{6,44},{7,121},{8,34}... | collective-permute-start | bytes 350216 | tf_op jit(solution)/shard_map/ppermute | solution.py:46
  20.4 35.6 %collective-permute-start.10 = (bf16[7168,256]{1,0:T(8,128)(2,1)}, bf16[7168,256]{1,0:T(8,128)(2,1)S(1)}, u32[]{:S(2)}, u32[]{:S(2)}) collective-permute-start(bf16[7168,256]{1,0:T(8,128)(2,1)} %bitcast.7), channel_id=1, source_target_pairs={{0,1},{1,0},{2,3},{3,2},{4,5},{5,4},{6,7},{7,6},{8,9},{9,8},{10,11... | collective-permute-start | bytes 11010056 | tf_op jit(solution)/shard_map/ppermute | solution.py:54
  20.5 45.5 %collective-permute-start.11 = (bf16[7168,256]{1,0:T(8,128)(2,1)}, bf16[7168,256]{1,0:T(8,128)(2,1)}, u32[]{:S(2)}, u32[]{:S(2)}) collective-permute-start(bf16[7168,256]{1,0:T(8,128)(2,1)} %bitcast.9), channel_id=1, source_target_pairs={{0,1},{1,0},{2,3},{3,2},{4,5},{5,4},{6,7},{7,6},{8,9},{9,8},{10,11... | collective-permute-start | bytes 11010056 | tf_op jit(solution)/shard_map/ppermute | solution.py:54
  29.5 6.1 %collective-permute-start.7 = (bf16[64,2432]{1,0:T(8,128)(2,1)S(1)}, bf16[64,2432]{1,0:T(8,128)(2,1)S(1)}, u32[]{:S(2)}, u32[]{:S(2)}) collective-permute-start(bf16[64,2432]{1,0:T(8,128)(2,1)S(1)} %get-tuple-element.21), channel_id=1, source_target_pairs={{0,6},{1,3},{2,4},{3,1},{4,2},{5,7},{6,0},{7,5},{8,14},{9,11},{10,... | collective-permute-start | bytes 933896 | tf_op jit(solution)/shard_map/ppermute | solution.py:28
  29.6 56.4 %collective-permute-start.18 = (bf16[256,7168]{1,0:T(8,128)(2,1)}, bf16[256,7168]{1,0:T(8,128)(2,1)}, u32[]{:S(2)}, u32[]{:S(2)}) collective-permute-start(bf16[256,7168]{1,0:T(8,128)(2,1)} %bitcast.3.refs_2_), channel_id=1, source_target_pairs={{0,1},{1,0},{2,3},{3,2},{4,5},{5,4},{6,7},{7,6},{8,9},{9,8},{10,11... | collective-permute-start | bytes 11010056 | tf_op jit(solution)/shard_map/ppermute | solution.py:54
  29.7 6.1 %collective-permute-start.12 = (bf16[64,2432]{1,0:T(8,128)(2,1)S(1)}, bf16[64,2432]{1,0:T(8,128)(2,1)S(1)}, u32[]{:S(2)}, u32[]{:S(2)}) collective-permute-start(bf16[64,2432]{1,0:T(8,128)(2,1)S(1)} %get-tuple-element.20), channel_id=1, source_target_pairs={{0,96},{1,33},{32,64},{33,1},{64,32},{65,97},{96,0},{97,65},{2,98}... | collective-permute-start | bytes 933896 | tf_op jit(solution)/shard_map/ppermute | solution.py:28
  35.6 5.7 %collective-permute-start.15 = (bf16[64,2432]{1,0:T(8,128)(2,1)S(1)}, bf16[64,2432]{1,0:T(8,128)(2,1)S(1)}, u32[]{:S(2)}, u32[]{:S(2)}) collective-permute-start(bf16[64,2432]{1,0:T(8,128)(2,1)S(1)} %get-tuple-element.19), channel_id=1, source_target_pairs={{0,24},{1,9},{8,16},{9,1},{16,8},{17,25},{24,0},{25,17},{2,26},{3,... | collective-permute-start | bytes 933896 | tf_op jit(solution)/shard_map/ppermute | solution.py:28
  35.8 9.4 %collective-permute-start.8 = (bf16[128,2432]{1,0:T(8,128)(2,1)S(1)}, bf16[128,2432]{1,0:T(8,128)(2,1)S(1)}, u32[]{:S(2)}, u32[]{:S(2)}) collective-permute-start(bf16[128,2432]{1,0:T(8,128)(2,1)S(1)} %pad_maximum_fusion.4), channel_id=1, source_target_pairs={{0,96},{1,33},{32,64},{33,1},{64,32},{65,97},{96,0},{97,65},{2,98}... | collective-permute-start | bytes 1867784 | tf_op jit(solution)/shard_map/ppermute | solution.py:28
  41.4 9.1 %collective-permute-start.13 = (bf16[128,2432]{1,0:T(8,128)(2,1)S(1)}, bf16[128,2432]{1,0:T(8,128)(2,1)S(1)}, u32[]{:S(2)}, u32[]{:S(2)}) collective-permute-start(bf16[128,2432]{1,0:T(8,128)(2,1)S(1)} %pad_maximum_fusion.5), channel_id=1, source_target_pairs={{0,24},{1,9},{8,16},{9,1},{16,8},{17,25},{24,0},{25,17},{2,26},{3,... | collective-permute-start | bytes 1867784 | tf_op jit(solution)/shard_map/ppermute | solution.py:28
  45.2 9.4 %collective-permute-start.16 = (bf16[128,2432]{1,0:T(8,128)(2,1)S(1)}, bf16[128,2432]{1,0:T(8,128)(2,1)S(1)}, u32[]{:S(2)}, u32[]{:S(2)}) collective-permute-start(bf16[128,2432]{1,0:T(8,128)(2,1)S(1)} %pad_maximum_fusion.6), channel_id=1, source_target_pairs={{0,6},{1,3},{2,4},{3,1},{4,2},{5,7},{6,0},{7,5},{8,14},{9,11},{10,... | collective-permute-start | bytes 1867784 | tf_op jit(solution)/shard_map/ppermute | solution.py:28
  46.5 11.5 %copy-start.8 = (bf16[1,7168,256]{2,1,0:T(8,128)(2,1)S(1)}, bf16[1,7168,256]{2,1,0:T(8,128)(2,1)}, u32[]{:S(2)}) copy-start(bf16[1,7168,256]{2,1,0:T(8,128)(2,1)} %param.12) | copy-start | bytes 11010052
  50.5 20.0 %collective-permute-start.9 = (bf16[256,2432]{1,0:T(8,128)(2,1)S(1)}, bf16[256,2432]{1,0:T(8,128)(2,1)}, u32[]{:S(2)}, u32[]{:S(2)}) collective-permute-start(bf16[256,2432]{1,0:T(8,128)(2,1)S(1)} %pad_maximum_fusion.1.x0), channel_id=1, source_target_pairs={{0,24},{1,9},{8,16},{9,1},{16,8},{17,25},{24,0},{25,17},{2,26},{3,... | collective-permute-start | bytes 3735560 | tf_op jit(solution)/shard_map/ppermute | solution.py:28
  51.2 6.8 %copy-start.7 = (bf16[1,7168,256]{2,1,0:T(8,128)(2,1)S(1)}, bf16[1,7168,256]{2,1,0:T(8,128)(2,1)}, u32[]{:S(2)}) copy-start(bf16[1,7168,256]{2,1,0:T(8,128)(2,1)} %param.11) | copy-start | bytes 11010052
  54.6 20.5 %collective-permute-start.14 = (bf16[256,2432]{1,0:T(8,128)(2,1)}, bf16[256,2432]{1,0:T(8,128)(2,1)}, u32[]{:S(2)}, u32[]{:S(2)}) collective-permute-start(bf16[256,2432]{1,0:T(8,128)(2,1)} %pad_maximum_fusion.2.x1), channel_id=1, source_target_pairs={{0,6},{1,3},{2,4},{3,1},{4,2},{5,7},{6,0},{7,5},{8,14},{9,11},{10,... | collective-permute-start | bytes 3735560 | tf_op jit(solution)/shard_map/ppermute | solution.py:28
  56.0 1.9 %copy-start.9 = (bf16[7168,256]{1,0:T(8,128)(2,1)}, bf16[7168,256]{1,0:T(8,128)(2,1)S(1)}, u32[]{:S(2)}) copy-start(bf16[7168,256]{1,0:T(8,128)(2,1)S(1)} %collective-permute-done.10.refs_0_) | copy-start | bytes 11010052
  57.9 20.1 %collective-permute-start.17 = (bf16[256,2432]{1,0:T(8,128)(2,1)S(1)}, bf16[256,2432]{1,0:T(8,128)(2,1)}, u32[]{:S(2)}, u32[]{:S(2)}) collective-permute-start(bf16[256,2432]{1,0:T(8,128)(2,1)S(1)} %pad_maximum_fusion.3.x2.near_x2), channel_id=1, source_target_pairs={{0,96},{1,33},{32,64},{33,1},{64,32},{65,97},{96,0},{97,65},{2,98}... | collective-permute-start | bytes 3735560 | tf_op jit(solution)/shard_map/ppermute | solution.py:28
  60.5 1.8 %copy-start = (bf16[256,7168]{1,0:T(8,128)(2,1)}, bf16[256,7168]{1,0:T(8,128)(2,1)S(1)}, u32[]{:S(2)}) copy-start(bf16[256,7168]{1,0:T(8,128)(2,1)S(1)} %get-tuple-element.15.own) | copy-start | bytes 11010052
  62.3 1.8 %copy-start.2 = (bf16[7168,256]{1,0:T(8,128)(2,1)}, bf16[7168,256]{1,0:T(8,128)(2,1)S(1)}, u32[]{:S(2)}) copy-start(bf16[7168,256]{1,0:T(8,128)(2,1)S(1)} %get-tuple-element.10.w0) | copy-start | bytes 11010052
  64.2 1.9 %copy-start.4 = (bf16[7168,256]{1,0:T(8,128)(2,1)}, bf16[7168,256]{1,0:T(8,128)(2,1)S(1)}, u32[]{:S(2)}) copy-start(bf16[7168,256]{1,0:T(8,128)(2,1)S(1)} %get-tuple-element.12.w2) | copy-start | bytes 11010052
  66.0 2.0 %copy-start.10 = (bf16[7168,256]{1,0:T(8,128)(2,1)S(1)}, bf16[7168,256]{1,0:T(8,128)(2,1)}, u32[]{:S(2)}) copy-start(bf16[7168,256]{1,0:T(8,128)(2,1)} %copy-done.9) | copy-start | bytes 11010052
  68.1 3.1 %copy-start.3 = (bf16[7168,256]{1,0:T(8,128)(2,1)S(1)}, bf16[7168,256]{1,0:T(8,128)(2,1)}, u32[]{:S(2)}) copy-start(bf16[7168,256]{1,0:T(8,128)(2,1)} %copy-done.2) | copy-start | bytes 11010052
  68.1 4.3 %copy-start.5 = (bf16[7168,256]{1,0:T(8,128)(2,1)S(1)}, bf16[7168,256]{1,0:T(8,128)(2,1)}, u32[]{:S(2)}) copy-start(bf16[7168,256]{1,0:T(8,128)(2,1)} %copy-done.4) | copy-start | bytes 11010052
  88.1 2.4 %copy-start.1 = (bf16[256,7168]{1,0:T(8,128)(2,1)S(1)}, bf16[256,7168]{1,0:T(8,128)(2,1)}, u32[]{:S(2)}) copy-start(bf16[256,7168]{1,0:T(8,128)(2,1)} %copy-done) | copy-start | bytes 11010052
  91.3 16.2 %collective-permute-start.25 = (bf16[256,2304]{1,0:T(8,128)(2,1)S(1)}, bf16[256,2304]{1,0:T(8,128)(2,1)S(1)}, u32[]{:S(2)}, u32[]{:S(2)}) collective-permute-start(bf16[256,2304]{1,0:T(8,128)(2,1)S(1)} %shard_map.102), channel_id=1, source_target_pairs={{0,96},{1,33},{32,64},{33,1},{64,32},{65,97},{96,0},{97,65},{2,98}... | collective-permute-start | bytes 3538952 | tf_op jit(solution)/shard_map/ppermute | solution.py:28
  93.6 16.1 %collective-permute-start.22 = (bf16[256,2432]{1,0:T(8,128)(2,1)S(1)}, bf16[256,2432]{1,0:T(8,128)(2,1)S(1)}, u32[]{:S(2)}, u32[]{:S(2)}) collective-permute-start(bf16[256,2432]{1,0:T(8,128)(2,1)S(1)} %shard_map.100), channel_id=1, source_target_pairs={{0,6},{1,3},{2,4},{3,1},{4,2},{5,7},{6,0},{7,5},{8,14},{9,11},{10,... | collective-permute-start | bytes 3735560 | tf_op jit(solution)/shard_map/ppermute | solution.py:28
  93.9 13.6 %collective-permute-start.35 = (s32[1,128]{1,0:T(1,128)S(1)}, s32[1,128]{1,0:T(1,128)S(1)}, u32[]{:S(2)}, u32[]{:S(2)}) collective-permute-start(s32[1,128]{1,0:T(1,128)S(1)} %get-tuple-element.16), channel_id=1, source_target_pairs={{0,1},{1,0},{2,3},{3,2},{4,5},{5,4},{6,7},{7,6},{8,9},{9,8},{10,11... | collective-permute-start | bytes 1544 | tf_op jit(solution)/shard_map/ppermute | solution.py:54
  107.3 16.1 %collective-permute-start.19 = (bf16[256,2432]{1,0:T(8,128)(2,1)S(1)}, bf16[256,2432]{1,0:T(8,128)(2,1)S(1)}, u32[]{:S(2)}, u32[]{:S(2)}) collective-permute-start(bf16[256,2432]{1,0:T(8,128)(2,1)S(1)} %shard_map.98), channel_id=1, source_target_pairs={{0,24},{1,9},{8,16},{9,1},{16,8},{17,25},{24,0},{25,17},{2,26},{3,... | collective-permute-start | bytes 3735560 | tf_op jit(solution)/shard_map/ppermute | solution.py:28
  107.7 16.2 %collective-permute-start.26 = (bf16[128,2304]{1,0:T(8,128)(2,1)S(1)}, bf16[128,2304]{1,0:T(8,128)(2,1)S(1)}, u32[]{:S(2)}, u32[]{:S(2)}) collective-permute-start(bf16[128,2304]{1,0:T(8,128)(2,1)S(1)} %slice.162), channel_id=1, source_target_pairs={{0,6},{1,3},{2,4},{3,1},{4,2},{5,7},{6,0},{7,5},{8,14},{9,11},{10,... | collective-permute-start | bytes 1769480 | tf_op jit(solution)/shard_map/ppermute | solution.py:28
  110.0 20.1 %collective-permute-start.23 = (bf16[128,2432]{1,0:T(8,128)(2,1)S(1)}, bf16[128,2432]{1,0:T(8,128)(2,1)S(1)}, u32[]{:S(2)}, u32[]{:S(2)}) collective-permute-start(bf16[128,2432]{1,0:T(8,128)(2,1)S(1)} %slice.160), channel_id=1, source_target_pairs={{0,24},{1,9},{8,16},{9,1},{16,8},{17,25},{24,0},{25,17},{2,26},{3,... | collective-permute-start | bytes 1867784 | tf_op jit(solution)/shard_map/ppermute | solution.py:28
  123.8 9.5 %collective-permute-start.20 = (bf16[128,2432]{1,0:T(8,128)(2,1)S(1)}, bf16[128,2432]{1,0:T(8,128)(2,1)S(1)}, u32[]{:S(2)}, u32[]{:S(2)}) collective-permute-start(bf16[128,2432]{1,0:T(8,128)(2,1)S(1)} %slice.161), channel_id=1, source_target_pairs={{0,96},{1,33},{32,64},{33,1},{64,32},{65,97},{96,0},{97,65},{2,98}... | collective-permute-start | bytes 1867784 | tf_op jit(solution)/shard_map/ppermute | solution.py:28
  124.1 9.5 %collective-permute-start.27 = (bf16[64,2304]{1,0:T(8,128)(2,1)S(1)}, bf16[64,2304]{1,0:T(8,128)(2,1)S(1)}, u32[]{:S(2)}, u32[]{:S(2)}) collective-permute-start(bf16[64,2304]{1,0:T(8,128)(2,1)S(1)} %slice.165), channel_id=1, source_target_pairs={{0,24},{1,9},{8,16},{9,1},{16,8},{17,25},{24,0},{25,17},{2,26},{3,... | collective-permute-start | bytes 884744 | tf_op jit(solution)/shard_map/ppermute | solution.py:28
  130.3 6.3 %collective-permute-start.24 = (bf16[64,2432]{1,0:T(8,128)(2,1)S(1)}, bf16[64,2432]{1,0:T(8,128)(2,1)S(1)}, u32[]{:S(2)}, u32[]{:S(2)}) collective-permute-start(bf16[64,2432]{1,0:T(8,128)(2,1)S(1)} %slice.163), channel_id=1, source_target_pairs={{0,96},{1,33},{32,64},{33,1},{64,32},{65,97},{96,0},{97,65},{2,98}... | collective-permute-start | bytes 933896 | tf_op jit(solution)/shard_map/ppermute | solution.py:28
  133.5 6.1 %collective-permute-start.21 = (bf16[64,2432]{1,0:T(8,128)(2,1)S(1)}, bf16[64,2432]{1,0:T(8,128)(2,1)S(1)}, u32[]{:S(2)}, u32[]{:S(2)}) collective-permute-start(bf16[64,2432]{1,0:T(8,128)(2,1)S(1)} %slice.164), channel_id=1, source_target_pairs={{0,6},{1,3},{2,4},{3,1},{4,2},{5,7},{6,0},{7,5},{8,14},{9,11},{10,... | collective-permute-start | bytes 933896 | tf_op jit(solution)/shard_map/ppermute | solution.py:28
  139.7 5.0 %copy-start.11 = (f32[16]{0:T(128)S(1)}, f32[16]{0:T(128)}, u32[]{:S(2)}) copy-start(f32[16]{0:T(128)} %param.14) | copy-start | bytes 196
  139.8 10.3 %collective-permute-start.34 = (bf16[8,7168]{1,0:T(8,128)(2,1)S(1)}, bf16[8,7168]{1,0:T(8,128)(2,1)S(1)}, u32[]{:S(2)}, u32[]{:S(2)}) collective-permute-start(bf16[8,7168]{1,0:T(8,128)(2,1)S(1)} %get-tuple-element.23), channel_id=1, source_target_pairs={{0,42},{1,127},{2,40},{3,125},{4,46},{5,123},{6,44},{7,121},{8,34}... | collective-permute-start | bytes 344072 | tf_op jit(solution)/shard_map/ppermute | solution.py:46
  139.9 12.8 %collective-permute-start.33 = (bf16[8,7168]{1,0:T(8,128)(2,1)S(1)}, bf16[8,7168]{1,0:T(8,128)(2,1)S(1)}, u32[]{:S(2)}, u32[]{:S(2)}) collective-permute-start(bf16[8,7168]{1,0:T(8,128)(2,1)S(1)} %get-tuple-element.24), channel_id=1, source_target_pairs={{0,40},{1,121},{2,42},{3,123},{4,44},{5,125},{6,46},{7,127},{8,32}... | collective-permute-start | bytes 344072 | tf_op jit(solution)/shard_map/ppermute | solution.py:46
  145.2 10.1 %collective-permute-start.32 = (bf16[8,7168]{1,0:T(8,128)(2,1)S(1)}, bf16[8,7168]{1,0:T(8,128)(2,1)S(1)}, u32[]{:S(2)}, u32[]{:S(2)}) collective-permute-start(bf16[8,7168]{1,0:T(8,128)(2,1)S(1)} %get-tuple-element.25), channel_id=1, source_target_pairs={{0,10},{1,31},{2,8},{3,29},{4,14},{5,27},{6,12},{7,25},{8,2},{9,23... | collective-permute-start | bytes 344072 | tf_op jit(solution)/shard_map/ppermute | solution.py:46
  147.4 7.9 %collective-permute-start.31 = (bf16[8,7168]{1,0:T(8,128)(2,1)S(1)}, bf16[8,7168]{1,0:T(8,128)(2,1)S(1)}, u32[]{:S(2)}, u32[]{:S(2)}) collective-permute-start(bf16[8,7168]{1,0:T(8,128)(2,1)S(1)} %get-tuple-element.26), channel_id=1, source_target_pairs={{0,8},{1,25},{2,10},{3,27},{4,12},{5,29},{6,14},{7,31},{8,0},{9,17... | collective-permute-start | bytes 344072 | tf_op jit(solution)/shard_map/ppermute | solution.py:46
  150.1 7.0 %collective-permute-start.30 = (bf16[8,7168]{1,0:T(8,128)(2,1)S(1)}, bf16[8,7168]{1,0:T(8,128)(2,1)S(1)}, u32[]{:S(2)}, u32[]{:S(2)}) collective-permute-start(bf16[8,7168]{1,0:T(8,128)(2,1)S(1)} %get-tuple-element.27), channel_id=1, source_target_pairs={{0,34},{1,103},{2,32},{3,101},{4,38},{5,99},{6,36},{7,97},{8,42},{... | collective-permute-start | bytes 344072 | tf_op jit(solution)/shard_map/ppermute | solution.py:46
  150.1 7.0 %collective-permute-start.29 = (bf16[8,7168]{1,0:T(8,128)(2,1)S(1)}, bf16[8,7168]{1,0:T(8,128)(2,1)S(1)}, u32[]{:S(2)}, u32[]{:S(2)}) collective-permute-start(bf16[8,7168]{1,0:T(8,128)(2,1)S(1)} %get-tuple-element.28), channel_id=1, source_target_pairs={{0,32},{1,97},{2,34},{3,99},{4,36},{5,101},{6,38},{7,103},{8,40},{... | collective-permute-start | bytes 344072 | tf_op jit(solution)/shard_map/ppermute | solution.py:46
  152.7 4.9 %collective-permute-start.28 = (bf16[8,7168]{1,0:T(8,128)(2,1)S(1)}, bf16[8,7168]{1,0:T(8,128)(2,1)S(1)}, u32[]{:S(2)}, u32[]{:S(2)}) collective-permute-start(bf16[8,7168]{1,0:T(8,128)(2,1)S(1)} %get-tuple-element.22), channel_id=1, source_target_pairs={{0,2},{1,7},{2,0},{3,5},{4,6},{5,3},{6,4},{7,1},{8,10},{9,15},{10,... | collective-permute-start | bytes 344072 | tf_op jit(solution)/shard_map/ppermute | solution.py:46

commit v7 on v6

--- a/solution.py
+++ b/solution.py
@@ -11,11 +11,10 @@
 AXES = ("gx", "gy", "gz_0", "gz_1")
 GZ = ("gz_0", "gz_1")
 X, Y, Z = "gz_0", "gx", "gy"
-EARLY = (X, Y, Z)
 LATE = ((X, Y, Z), (Y, Z, X), (Z, X, Y))
 INFO = 128
 CUTS = (0, 2432, 4864, 7168)
-COL_CUTS = (0, 2432, 4864, 7168)
+COL_CUTS = (0, 2304, 4736, 7168)
 BF16 = jnp.bfloat16
 F32 = jnp.float32
 
@@ -28,26 +27,24 @@
     return lax.ppermute(value, (axis, "gz_1"), pairs)
 
 
-def direct(value, hops):
-    masks = (1, 3)
-    pairs = []
+def cubes():
+    index, groups, seen = lambda a, b, x, c: ((a * 4 + b) * 4 + x) * 2 + c, [], set()
     for a in range(4):
         for b in range(4):
             for x in range(4):
-                for c in range(2):
-                    m = masks[c]
-                    far = (
-                        a ^ (m if Y in hops else 0),
-                        b ^ (m if Z in hops else 0),
-                        x ^ (m if X in hops else 0),
-                    )
-                    here = ((a * 4 + b) * 4 + x) * 2 + c
-                    pairs.append((here, ((far[0] * 4 + far[1]) * 4 + far[2]) * 2 + c))
-    return lax.ppermute(value, AXES, pairs)
-
-
-def hops_of(n):
-    return [axis for k, axis in enumerate(EARLY) if n >> k & 1]
+                for c, m in enumerate((1, 3)):
+                    if index(a, b, x, c) not in seen:
+                        group = [
+                            index(a ^ (m * (n >> 2 & 1)), b ^ (m * (n >> 1 & 1)), x ^ (m * (n & 1)), c)
+                            for n in range(8)
+                        ]
+                        groups.append(group)
+                        seen.update(group)
+    return groups
+
+
+def swap(blocks):
+    return lax.all_to_all(blocks, AXES, 0, 0, axis_index_groups=cubes(), tiled=True)
 
 
 def partner(value):
@@ -255,10 +252,7 @@
     gate_ups = (gate_own, gate_far, up_own, up_far)
 
     rows = rows_of(tokens, expert_ids, route_weight, experts)
-    blocks = [rows]
-    for n in range(1, 8):
-        blocks.append(direct(rows, hops_of(n)))
-    rows = jnp.concatenate(blocks, axis=0)
+    rows = swap(jnp.broadcast_to(rows[None], (8, *rows.shape))).reshape(64, width + INFO)
     ends = (*CUTS[:3], width + INFO)
     pieces = [rows[:, ends[i] : ends[i + 1]] for i in range(3)]
     for step in range(3):
@@ -296,11 +290,8 @@
             sent = [t[half:].astype(BF16) for t in totals]
             kept = [t[:half] for t in totals]
     total = jnp.concatenate(totals, axis=1)
-    combined = total[:tok_rows]
-    for n in range(1, 8):
-        block = total[n * tok_rows : (n + 1) * tok_rows].astype(BF16)
-        block = direct(block, hops_of(n))
-        combined = combined + block.astype(F32)
+    blocks = swap(total.astype(BF16).reshape(8, tok_rows, width))
+    combined = jnp.sum(blocks.astype(F32), axis=0)
 
     other_marks = partner(marks)
     expert_load = (marks + other_marks)[0, experts : 2 * experts]

time: 161 us -> 154 us (0.957)
  the two profiles are of different devices: /device:TPU:1 before, /device:TPU:0 now
where the time goes in v7:
time: 154 us
  waiting for transfers between devices  66.3 us (43%)
  starting transfers between devices  43.2 us (28%)
  Pallas kernels  26.7 us (17%)
  local copies, waits for them, and re-layouts  10.3 us (7%)
  other arithmetic  6.37 us (4%)
    ppermute x18, waiting for transfers between devices, exchange(): return lax.ppermute(value, (axis, 'gz_1'), pairs)  50.3 us
    ppermute x18, starting transfers between devices, exchange(): return lax.ppermute(value, (axis, 'gz_1'), pairs)  24.8 us
    all_to_all x2, waiting for transfers between devices, swap(): lax.all_to_all(blocks, AXES, 0, 0, axis_index_groups=cubes(), tiled=True)  14.8 us
    ppermute x4, starting transfers between devices, partner(): return lax.ppermute(value, 'gz_1', [(0, 1), (1, 0)])  9.64 us
    unnamed x22, local copies, waits for them, and re-layouts  8.88 us
    all_to_all x2, starting transfers between devices, swap(): lax.all_to_all(blocks, AXES, 0, 0, axis_index_groups=cubes(), tiled=True)  8.8 us
    pallas_call x3, Pallas kernels, gate_up_far_part(): pl.pallas_call(functools.partial(far_part_kernel, colour), out_shape=jax....  8.27 us
    pallas_call x3, Pallas kernels, in_vmem(): pl.pallas_call(load_kernel, out_shape=tuple((jax.ShapeDtypeStruct(a.shape...  6.12 us
  transfers between devices with their start and end apart: 24, of which 18 were waited for; matrix products, arithmetic and copies ran while one was open for 2% of the time, Pallas kernels for 14%

profile of v7, /device:TPU:0, one launch (start us, length us, event | category | flops | bytes accessed | tf_op | source)
XLA Modules:
  0.0 153.8 jit_solution(13311230409009300456)
XLA Ops:
  2.1 0.9 copy-done.6
  3.1 1.0 broadcast_in_dim.10
  4.1 5.2 %all-to-all-start = ((bf16[8,8,7296]{2,1,0:T(8,128)(2,1)}), bf16[8,8,7296]{2,1,0:T(8,128)(2,1)S(1)}, u32[]{:S(2)}, u32[]{:S(2)}) async-start(bf16[8,8,7296]{2,1,0:T(8,128)(2,1)} %broadcast_in_dim.10), calls=%async_computation | async-start | bytes 1867776 | tf_op jit(solution)/shard_map/all_to_all | solution.py:47
  9.3 4.4 %collective-permute-start.3 = (bf16[7168,256]{1,0:T(8,128)(2,1)}, bf16[7168,256]{1,0:T(8,128)(2,1)}, u32[]{:S(2)}, u32[]{:S(2)}) collective-permute-start(bf16[7168,256]{1,0:T(8,128)(2,1)} %bitcast.14), channel_id=1, source_target_pairs={{0,1},{1,0},{2,3},{3,2},{4,5},{5,4},{6,7},{7,6},{8,9},{9,8},{10,11... | collective-permute-start | bytes 11010056 | tf_op jit(solution)/shard_map/ppermute | solution.py:51
  13.8 6.1 %all-to-all-done = bf16[8,8,7296]{2,1,0:T(8,128)(2,1)S(1)} async-done(((bf16[8,8,7296]{2,1,0:T(8,128)(2,1)}), bf16[8,8,7296]{2,1,0:T(8,128)(2,1)S(1)}, u32[]{:S(2)}, u32[]{:S(2)}) %all-to-all-start) | async-done | bytes 933920 | tf_op jit(solution)/shard_map/all_to_all | solution.py:47
  20.0 1.9 %collective-permute-start = (bf16[64,2432]{1,0:T(8,128)(2,1)S(1)}, bf16[64,2432]{1,0:T(8,128)(2,1)S(1)}, u32[]{:S(2)}, u32[]{:S(2)}) collective-permute-start(bf16[64,2432]{1,0:T(8,128)(2,1)S(1)} %get-tuple-element.21), channel_id=1, source_target_pairs={{0,6},{1,3},{2,4},{3,1},{4,2},{5,7},{6,0},{7,5},{8,14},{9,11},{10,... | collective-permute-start | bytes 933896 | tf_op jit(solution)/shard_map/ppermute | solution.py:27
  21.9 5.1 %collective-permute-start.11 = (bf16[256,7168]{1,0:T(8,128)(2,1)}, bf16[256,7168]{1,0:T(8,128)(2,1)}, u32[]{:S(2)}, u32[]{:S(2)}) collective-permute-start(bf16[256,7168]{1,0:T(8,128)(2,1)} %bitcast.18), channel_id=1, source_target_pairs={{0,1},{1,0},{2,3},{3,2},{4,5},{5,4},{6,7},{7,6},{8,9},{9,8},{10,11... | collective-permute-start | bytes 11010056 | tf_op jit(solution)/shard_map/ppermute | solution.py:51
  28.2 2.7 %collective-permute-start.8 = (bf16[64,2432]{1,0:T(8,128)(2,1)S(1)}, bf16[64,2432]{1,0:T(8,128)(2,1)S(1)}, u32[]{:S(2)}, u32[]{:S(2)}) collective-permute-start(bf16[64,2432]{1,0:T(8,128)(2,1)S(1)} %get-tuple-element.19), channel_id=1, source_target_pairs={{0,24},{1,9},{8,16},{9,1},{16,8},{17,25},{24,0},{25,17},{2,26},{3,... | collective-permute-start | bytes 933896 | tf_op jit(solution)/shard_map/ppermute | solution.py:27
  31.0 4.1 %collective-permute-done.5 = bf16[64,2432]{1,0:T(8,128)(2,1)S(1)} collective-permute-done((bf16[64,2432]{1,0:T(8,128)(2,1)S(1)}, bf16[64,2432]{1,0:T(8,128)(2,1)S(1)}, u32[]{:S(2)}, u32[]{:S(2)}) %collective-permute-start.5) | collective-permute-done | bytes 311328 | tf_op jit(solution)/shard_map/ppermute | solution.py:27
  36.3 2.7 %collective-permute-start.6 = (bf16[128,2432]{1,0:T(8,128)(2,1)S(1)}, bf16[128,2432]{1,0:T(8,128)(2,1)S(1)}, u32[]{:S(2)}, u32[]{:S(2)}) collective-permute-start(bf16[128,2432]{1,0:T(8,128)(2,1)S(1)} %pad_maximum_fusion.5), channel_id=1, source_target_pairs={{0,24},{1,9},{8,16},{9,1},{16,8},{17,25},{24,0},{25,17},{2,26},{3,... | collective-permute-start | bytes 1867784 | tf_op jit(solution)/shard_map/ppermute | solution.py:27
  39.1 7.5 %collective-permute-done.1 = bf16[128,2432]{1,0:T(8,128)(2,1)S(1)} collective-permute-done((bf16[128,2432]{1,0:T(8,128)(2,1)S(1)}, bf16[128,2432]{1,0:T(8,128)(2,1)S(1)}, u32[]{:S(2)}, u32[]{:S(2)}) %collective-permute-start.1) | collective-permute-done | bytes 622624 | tf_op jit(solution)/shard_map/ppermute | solution.py:27
  46.7 1.1 collective-permute-done.6
  47.8 2.7 %collective-permute-start.2 = (bf16[256,2432]{1,0:T(8,128)(2,1)S(1)}, bf16[256,2432]{1,0:T(8,128)(2,1)}, u32[]{:S(2)}, u32[]{:S(2)}) collective-permute-start(bf16[256,2432]{1,0:T(8,128)(2,1)S(1)} %pad_maximum_fusion.x0), channel_id=1, source_target_pairs={{0,24},{1,9},{8,16},{9,1},{16,8},{17,25},{24,0},{25,17},{2,26},{3,... | collective-permute-start | bytes 3735560 | tf_op jit(solution)/shard_map/ppermute | solution.py:27
  50.5 1.1 pad_maximum_fusion.1.x1
  51.6 6.4 %collective-permute-done.9 = bf16[128,2432]{1,0:T(8,128)(2,1)S(1)} collective-permute-done((bf16[128,2432]{1,0:T(8,128)(2,1)S(1)}, bf16[128,2432]{1,0:T(8,128)(2,1)S(1)}, u32[]{:S(2)}, u32[]{:S(2)}) %collective-permute-start.9) | collective-permute-done | bytes 622624 | tf_op jit(solution)/shard_map/ppermute | solution.py:27
  58.1 1.2 collective-permute-start.10
  60.1 1.8 %copy-done = bf16[256,7168]{1,0:T(8,128)(2,1)} copy-done((bf16[256,7168]{1,0:T(8,128)(2,1)}, bf16[256,7168]{1,0:T(8,128)(2,1)S(1)}, u32[]{:S(2)}) %copy-start) | copy-done | bytes 3670040
  61.9 1.8 %copy-done.2 = bf16[7168,256]{1,0:T(8,128)(2,1)} copy-done((bf16[7168,256]{1,0:T(8,128)(2,1)}, bf16[7168,256]{1,0:T(8,128)(2,1)S(1)}, u32[]{:S(2)}) %copy-start.2) | copy-done | bytes 3670040
  63.7 1.8 %copy-done.4 = bf16[7168,256]{1,0:T(8,128)(2,1)} copy-done((bf16[7168,256]{1,0:T(8,128)(2,1)}, bf16[7168,256]{1,0:T(8,128)(2,1)S(1)}, u32[]{:S(2)}) %copy-start.4) | copy-done | bytes 3670040
  65.6 3.3 %weights_in.4 = (bf16[7168,256]{1,0:T(8,128)(2,1)S(1)}, bf16[7168,256]{1,0:T(8,128)(2,1)S(1)}) custom-call(bf16[7168,256]{1,0:T(8,128)(2,1)} %collective-permute-done.3.refs_0_, bf16[7168,256]{1,0:T(8,128)(2,1)} %collective-permute-done.4.refs_1_), custom_call_target="tpu_custom_call" | custom-call | flops 8589934592 | tf_op jit(solution)/shard_map/weights_in/pallas_call | solution.py:157
  68.9 0.9 copy-done.3
  69.8 1.1 copy-done.5
  70.9 2.8 %shard_map.94.part0 = f32[4,256,256]{2,1,0:T(8,128)S(1)} custom-call(bf16[256,2432]{1,0:T(8,128)(2,1)} %collective-permute-done.2.x, bf16[7168,256]{1,0:T(8,128)(2,1)S(1)} %copy-done.3, bf16[7168,256]{1,0:T(8,128)(2,1)S(1)} %get-tuple-element.11.w1, bf16[7168,256]{1,0:T(8,128)(2,1)S(1)} %copy-done.5, bf16[7168,256]{1,0:T(8,128)(2,1)S(1)} %get-tuple-element.13.w3), custom_call_target="tpu_custom_call" | custom-call | flops 1252524032 | tf_op jit(solution)/shard_map/pallas_call | solution.py:188
  73.7 2.8 %collective-permute-done.7.x = bf16[256,2432]{1,0:T(8,128)(2,1)} collective-permute-done((bf16[256,2432]{1,0:T(8,128)(2,1)}, bf16[256,2432]{1,0:T(8,128)(2,1)}, u32[]{:S(2)}, u32[]{:S(2)}) %collective-permute-start.7) | collective-permute-done | bytes 1245216 | tf_op jit(solution)/shard_map/ppermute | solution.py:27
  76.5 2.8 %shard_map.95.part1 = f32[4,256,256]{2,1,0:T(8,128)S(1)} custom-call(bf16[256,2432]{1,0:T(8,128)(2,1)} %collective-permute-done.7.x, bf16[7168,256]{1,0:T(8,128)(2,1)S(1)} %copy-done.3, bf16[7168,256]{1,0:T(8,128)(2,1)S(1)} %get-tuple-element.11.w1, bf16[7168,256]{1,0:T(8,128)(2,1)S(1)} %copy-done.5, bf16[7168,256]{1,0:T(8,128)(2,1)S(1)} %get-tuple-element.13.w3), custom_call_target="tpu_custom_call" | custom-call | flops 1252524032 | tf_op jit(solution)/shard_map/pallas_call | solution.py:188
  79.3 2.7 %shard_map.96.part2 = f32[4,256,256]{2,1,0:T(8,128)S(1)} custom-call(bf16[256,2432]{1,0:T(8,128)(2,1)} %collective-permute-done.10.x.x2, bf16[7168,256]{1,0:T(8,128)(2,1)S(1)} %copy-done.3, bf16[7168,256]{1,0:T(8,128)(2,1)S(1)} %get-tuple-element.11.w1, bf16[7168,256]{1,0:T(8,128)(2,1)S(1)} %copy-done.5, bf16[7168,256]{1,0:T(8,128)(2,1)S(1)} %get-tuple-element.13.w3), custom_call_target="tpu_custom_call" | custom-call | flops 1252524032 | tf_op jit(solution)/shard_map/pallas_call | solution.py:188
  82.0 5.4 %gate_up_near.1.acc = f32[4,512,256]{2,1,0:T(8,128)S(1)} custom-call(bf16[256,2432]{1,0:T(8,128)(2,1)S(1)} %pad_maximum_fusion.x0, bf16[256,2432]{1,0:T(8,128)(2,1)} %pad_maximum_fusion.1.x1, bf16[256,2432]{1,0:T(8,128)(2,1)S(1)} %pad_maximum_fusion.2.x2.near_x2, bf16[7168,256]{1,0:T(8,128)(2,1)S(1)} %copy-done.3, ...), custom_call_target="tpu_custom_call" | custom-call | flops 3757572096 | tf_op jit(solution)/shard_map/gate_up_near/pallas_call | solution.py:176
  87.3 2.0 %weights_in.5.other = bf16[256,7168]{1,0:T(8,128)(2,1)S(1)} custom-call(bf16[256,7168]{1,0:T(8,128)(2,1)} %collective-permute-done.11.refs_0_), custom_call_target="tpu_custom_call" | custom-call | flops 8589934592 | tf_op jit(solution)/shard_map/weights_in/pallas_call | solution.py:157
  89.4 1.9 %hidden.1 = (bf16[512,512]{1,0:T(8,128)(2,1)S(1)}, s32[1,128]{1,0:T(1,128)S(1)}) custom-call(s32[1]{0:T(128)} %bitcast.expert, f32[4,256,256]{2,1,0:T(8,128)S(1)} %shard_map.94.part0, f32[4,256,256]{2,1,0:T(8,128)S(1)} %shard_map.95.part1, f32[4,256,256]{2,1,0:T(8,128)S(1)} %shard_map.96.part2, bf16[256,2432]{1,0:T(8,128)(2,1)S(1)} %pad_maximum_fusion.2.x2.near_x2, ...), custom_call_target="tpu_custom_call" | custom-call | flops 1252524032 | tf_op jit(solution)/shard_map/hidden/pallas_call | solution.py:199
  92.9 0.8 shard_map.102
  93.7 1.2 collective-permute-start.18
  94.9 0.8 shard_map.100
  95.8 1.6 %collective-permute-start.15 = (bf16[256,2432]{1,0:T(8,128)(2,1)S(1)}, bf16[256,2432]{1,0:T(8,128)(2,1)S(1)}, u32[]{:S(2)}, u32[]{:S(2)}) collective-permute-start(bf16[256,2432]{1,0:T(8,128)(2,1)S(1)} %shard_map.100), channel_id=1, source_target_pairs={{0,6},{1,3},{2,4},{3,1},{4,2},{5,7},{6,0},{7,5},{8,14},{9,11},{10,... | collective-permute-start | bytes 3735560 | tf_op jit(solution)/shard_map/ppermute | solution.py:27
  98.1 0.8 shard_map.101
  99.0 0.8 shard_map.99
  99.8 10.4 %collective-permute-done.12 = bf16[256,2304]{1,0:T(8,128)(2,1)S(1)} collective-permute-done((bf16[256,2304]{1,0:T(8,128)(2,1)S(1)}, bf16[256,2304]{1,0:T(8,128)(2,1)S(1)}, u32[]{:S(2)}, u32[]{:S(2)}) %collective-permute-start.12) | collective-permute-done | bytes 1179680 | tf_op jit(solution)/shard_map/ppermute | solution.py:27
  112.2 1.4 collective-permute-start.19
  114.3 2.8 %collective-permute-start.16 = (bf16[128,2432]{1,0:T(8,128)(2,1)S(1)}, bf16[128,2432]{1,0:T(8,128)(2,1)S(1)}, u32[]{:S(2)}, u32[]{:S(2)}) collective-permute-start(bf16[128,2432]{1,0:T(8,128)(2,1)S(1)} %slice.111), channel_id=1, source_target_pairs={{0,24},{1,9},{8,16},{9,1},{16,8},{17,25},{24,0},{25,17},{2,26},{3,... | collective-permute-start | bytes 1867784 | tf_op jit(solution)/shard_map/ppermute | solution.py:27
  117.0 4.7 %collective-permute-done.13 = bf16[128,2304]{1,0:T(8,128)(2,1)S(1)} collective-permute-done((bf16[128,2304]{1,0:T(8,128)(2,1)S(1)}, bf16[128,2304]{1,0:T(8,128)(2,1)S(1)}, u32[]{:S(2)}, u32[]{:S(2)}) %collective-permute-start.13) | collective-permute-done | bytes 589856 | tf_op jit(solution)/shard_map/ppermute | solution.py:27
  122.3 1.4 collective-permute-done.19
  123.9 3.3 %collective-permute-start.20 = (bf16[64,2432]{1,0:T(8,128)(2,1)S(1)}, bf16[64,2432]{1,0:T(8,128)(2,1)S(1)}, u32[]{:S(2)}, u32[]{:S(2)}) collective-permute-start(bf16[64,2432]{1,0:T(8,128)(2,1)S(1)} %slice.113), channel_id=1, source_target_pairs={{0,24},{1,9},{8,16},{9,1},{16,8},{17,25},{24,0},{25,17},{2,26},{3,... | collective-permute-start | bytes 933896 | tf_op jit(solution)/shard_map/ppermute | solution.py:27
  128.1 2.9 %collective-permute-done.14 = bf16[64,2304]{1,0:T(8,128)(2,1)S(1)} collective-permute-done((bf16[64,2304]{1,0:T(8,128)(2,1)S(1)}, bf16[64,2304]{1,0:T(8,128)(2,1)S(1)}, u32[]{:S(2)}, u32[]{:S(2)}) %collective-permute-start.14) | collective-permute-done | bytes 294944 | tf_op jit(solution)/shard_map/ppermute | solution.py:27
  131.1 4.7 %collective-permute-done.20 = bf16[64,2432]{1,0:T(8,128)(2,1)S(1)} collective-permute-done((bf16[64,2432]{1,0:T(8,128)(2,1)S(1)}, bf16[64,2432]{1,0:T(8,128)(2,1)S(1)}, u32[]{:S(2)}, u32[]{:S(2)}) %collective-permute-start.20) | collective-permute-done | bytes 311328 | tf_op jit(solution)/shard_map/ppermute | solution.py:27
  135.8 2.1 %collective-permute-done.17 = bf16[64,2432]{1,0:T(8,128)(2,1)S(1)} collective-permute-done((bf16[64,2432]{1,0:T(8,128)(2,1)S(1)}, bf16[64,2432]{1,0:T(8,128)(2,1)S(1)}, u32[]{:S(2)}, u32[]{:S(2)}) %collective-permute-start.17) | collective-permute-done | bytes 311328 | tf_op jit(solution)/shard_map/ppermute | solution.py:27
  138.0 1.0 pad_maximum_fusion.3
  139.0 3.6 %all-to-all-start.1 = ((bf16[8,8,7168]{2,1,0:T(8,128)(2,1)}), bf16[8,8,7168]{2,1,0:T(8,128)(2,1)S(1)}, u32[]{:S(2)}, u32[]{:S(2)}) async-start(bf16[8,8,7168]{2,1,0:T(8,128)(2,1)} %pad_maximum_fusion.3), calls=%async_computation.1 | async-start | bytes 1835008 | tf_op jit(solution)/shard_map/all_to_all | solution.py:47
  142.6 1.1 collective-permute-done.21
  144.4 8.6 %all-to-all-done.1 = bf16[8,8,7168]{2,1,0:T(8,128)(2,1)S(1)} async-done(((bf16[8,8,7168]{2,1,0:T(8,128)(2,1)}), bf16[8,8,7168]{2,1,0:T(8,128)(2,1)S(1)}, u32[]{:S(2)}, u32[]{:S(2)}) %all-to-all-start.1) | async-done | bytes 917536 | tf_op jit(solution)/shard_map/all_to_all | solution.py:47
  (67 shorter events, 13.4 us)
Async XLA Ops:
  2.1 0.9 copy-start.6
  4.1 15.9 %all-to-all-start = ((bf16[8,8,7296]{2,1,0:T(8,128)(2,1)}), bf16[8,8,7296]{2,1,0:T(8,128)(2,1)S(1)}, u32[]{:S(2)}, u32[]{:S(2)}) async-start(bf16[8,8,7296]{2,1,0:T(8,128)(2,1)} %broadcast_in_dim.10), calls=%async_computation | async-start | bytes 1867776 | tf_op jit(solution)/shard_map/all_to_all | solution.py:47
  9.3 48.8 %collective-permute-start.3 = (bf16[7168,256]{1,0:T(8,128)(2,1)}, bf16[7168,256]{1,0:T(8,128)(2,1)}, u32[]{:S(2)}, u32[]{:S(2)}) collective-permute-start(bf16[7168,256]{1,0:T(8,128)(2,1)} %bitcast.14), channel_id=1, source_target_pairs={{0,1},{1,0},{2,3},{3,2},{4,5},{5,4},{6,7},{7,6},{8,9},{9,8},{10,11... | collective-permute-start | bytes 11010056 | tf_op jit(solution)/shard_map/ppermute | solution.py:51
  13.7 51.9 %collective-permute-start.4 = (bf16[7168,256]{1,0:T(8,128)(2,1)}, bf16[7168,256]{1,0:T(8,128)(2,1)}, u32[]{:S(2)}, u32[]{:S(2)}) collective-permute-start(bf16[7168,256]{1,0:T(8,128)(2,1)} %bitcast.16), channel_id=1, source_target_pairs={{0,1},{1,0},{2,3},{3,2},{4,5},{5,4},{6,7},{7,6},{8,9},{9,8},{10,11... | collective-permute-start | bytes 11010056 | tf_op jit(solution)/shard_map/ppermute | solution.py:51
  20.0 8.2 %collective-permute-start = (bf16[64,2432]{1,0:T(8,128)(2,1)S(1)}, bf16[64,2432]{1,0:T(8,128)(2,1)S(1)}, u32[]{:S(2)}, u32[]{:S(2)}) collective-permute-start(bf16[64,2432]{1,0:T(8,128)(2,1)S(1)} %get-tuple-element.21), channel_id=1, source_target_pairs={{0,6},{1,3},{2,4},{3,1},{4,2},{5,7},{6,0},{7,5},{8,14},{9,11},{10,... | collective-permute-start | bytes 933896 | tf_op jit(solution)/shard_map/ppermute | solution.py:27
  21.9 65.4 %collective-permute-start.11 = (bf16[256,7168]{1,0:T(8,128)(2,1)}, bf16[256,7168]{1,0:T(8,128)(2,1)}, u32[]{:S(2)}, u32[]{:S(2)}) collective-permute-start(bf16[256,7168]{1,0:T(8,128)(2,1)} %bitcast.18), channel_id=1, source_target_pairs={{0,1},{1,0},{2,3},{3,2},{4,5},{5,4},{6,7},{7,6},{8,9},{9,8},{10,11... | collective-permute-start | bytes 11010056 | tf_op jit(solution)/shard_map/ppermute | solution.py:51
  27.0 8.1 %collective-permute-start.5 = (bf16[64,2432]{1,0:T(8,128)(2,1)S(1)}, bf16[64,2432]{1,0:T(8,128)(2,1)S(1)}, u32[]{:S(2)}, u32[]{:S(2)}) collective-permute-start(bf16[64,2432]{1,0:T(8,128)(2,1)S(1)} %get-tuple-element.20), channel_id=1, source_target_pairs={{0,96},{1,33},{32,64},{33,1},{64,32},{65,97},{96,0},{97,65},{2,98}... | collective-permute-start | bytes 933896 | tf_op jit(solution)/shard_map/ppermute | solution.py:27
  28.2 8.1 %collective-permute-start.8 = (bf16[64,2432]{1,0:T(8,128)(2,1)S(1)}, bf16[64,2432]{1,0:T(8,128)(2,1)S(1)}, u32[]{:S(2)}, u32[]{:S(2)}) collective-permute-start(bf16[64,2432]{1,0:T(8,128)(2,1)S(1)} %get-tuple-element.19), channel_id=1, source_target_pairs={{0,24},{1,9},{8,16},{9,1},{16,8},{17,25},{24,0},{25,17},{2,26},{3,... | collective-permute-start | bytes 933896 | tf_op jit(solution)/shard_map/ppermute | solution.py:27
  31.0 28.4 %copy-start.9 = (bf16[1,256,7168]{2,1,0:T(8,128)(2,1)S(1)}, bf16[1,256,7168]{2,1,0:T(8,128)(2,1)}, u32[]{:S(2)}) copy-start(bf16[1,256,7168]{2,1,0:T(8,128)(2,1)} %param.13) | copy-start | bytes 11010052
  35.1 11.4 %collective-permute-start.1 = (bf16[128,2432]{1,0:T(8,128)(2,1)S(1)}, bf16[128,2432]{1,0:T(8,128)(2,1)S(1)}, u32[]{:S(2)}, u32[]{:S(2)}) collective-permute-start(bf16[128,2432]{1,0:T(8,128)(2,1)S(1)} %pad_maximum_fusion.4), channel_id=1, source_target_pairs={{0,96},{1,33},{32,64},{33,1},{64,32},{65,97},{96,0},{97,65},{2,98}... | collective-permute-start | bytes 1867784 | tf_op jit(solution)/shard_map/ppermute | solution.py:27
  36.3 11.4 %collective-permute-start.6 = (bf16[128,2432]{1,0:T(8,128)(2,1)S(1)}, bf16[128,2432]{1,0:T(8,128)(2,1)S(1)}, u32[]{:S(2)}, u32[]{:S(2)}) collective-permute-start(bf16[128,2432]{1,0:T(8,128)(2,1)S(1)} %pad_maximum_fusion.5), channel_id=1, source_target_pairs={{0,24},{1,9},{8,16},{9,1},{16,8},{17,25},{24,0},{25,17},{2,26},{3,... | collective-permute-start | bytes 1867784 | tf_op jit(solution)/shard_map/ppermute | solution.py:27
  46.6 11.4 %collective-permute-start.9 = (bf16[128,2432]{1,0:T(8,128)(2,1)S(1)}, bf16[128,2432]{1,0:T(8,128)(2,1)S(1)}, u32[]{:S(2)}, u32[]{:S(2)}) collective-permute-start(bf16[128,2432]{1,0:T(8,128)(2,1)S(1)} %pad_maximum_fusion.6), channel_id=1, source_target_pairs={{0,6},{1,3},{2,4},{3,1},{4,2},{5,7},{6,0},{7,5},{8,14},{9,11},{10,... | collective-permute-start | bytes 1867784 | tf_op jit(solution)/shard_map/ppermute | solution.py:27
  46.6 12.8 %copy-start.8 = (bf16[1,7168,256]{2,1,0:T(8,128)(2,1)S(1)}, bf16[1,7168,256]{2,1,0:T(8,128)(2,1)}, u32[]{:S(2)}) copy-start(bf16[1,7168,256]{2,1,0:T(8,128)(2,1)} %param.12) | copy-start | bytes 11010052
  47.8 21.1 %collective-permute-start.2 = (bf16[256,2432]{1,0:T(8,128)(2,1)S(1)}, bf16[256,2432]{1,0:T(8,128)(2,1)}, u32[]{:S(2)}, u32[]{:S(2)}) collective-permute-start(bf16[256,2432]{1,0:T(8,128)(2,1)S(1)} %pad_maximum_fusion.x0), channel_id=1, source_target_pairs={{0,24},{1,9},{8,16},{9,1},{16,8},{17,25},{24,0},{25,17},{2,26},{3,... | collective-permute-start | bytes 3735560 | tf_op jit(solution)/shard_map/ppermute | solution.py:27
  50.5 8.8 %copy-start.7 = (bf16[1,7168,256]{2,1,0:T(8,128)(2,1)S(1)}, bf16[1,7168,256]{2,1,0:T(8,128)(2,1)}, u32[]{:S(2)}) copy-start(bf16[1,7168,256]{2,1,0:T(8,128)(2,1)} %param.11) | copy-start | bytes 11010052
  58.0 18.4 %collective-permute-start.7 = (bf16[256,2432]{1,0:T(8,128)(2,1)}, bf16[256,2432]{1,0:T(8,128)(2,1)}, u32[]{:S(2)}, u32[]{:S(2)}) collective-permute-start(bf16[256,2432]{1,0:T(8,128)(2,1)} %pad_maximum_fusion.1.x1), channel_id=1, source_target_pairs={{0,6},{1,3},{2,4},{3,1},{4,2},{5,7},{6,0},{7,5},{8,14},{9,11},{10,... | collective-permute-start | bytes 3735560 | tf_op jit(solution)/shard_map/ppermute | solution.py:27
  58.1 21.1 %collective-permute-start.10 = (bf16[256,2432]{1,0:T(8,128)(2,1)S(1)}, bf16[256,2432]{1,0:T(8,128)(2,1)}, u32[]{:S(2)}, u32[]{:S(2)}) collective-permute-start(bf16[256,2432]{1,0:T(8,128)(2,1)S(1)} %pad_maximum_fusion.2.x2.near_x2), channel_id=1, source_target_pairs={{0,96},{1,33},{32,64},{33,1},{64,32},{65,97},{96,0},{97,65},{2,98}... | collective-permute-start | bytes 3735560 | tf_op jit(solution)/shard_map/ppermute | solution.py:27
  60.1 1.8 %copy-start = (bf16[256,7168]{1,0:T(8,128)(2,1)}, bf16[256,7168]{1,0:T(8,128)(2,1)S(1)}, u32[]{:S(2)}) copy-start(bf16[256,7168]{1,0:T(8,128)(2,1)S(1)} %get-tuple-element.15.own) | copy-start | bytes 11010052
  61.9 1.8 %copy-start.2 = (bf16[7168,256]{1,0:T(8,128)(2,1)}, bf16[7168,256]{1,0:T(8,128)(2,1)S(1)}, u32[]{:S(2)}) copy-start(bf16[7168,256]{1,0:T(8,128)(2,1)S(1)} %get-tuple-element.10.w0) | copy-start | bytes 11010052
  63.7 1.8 %copy-start.4 = (bf16[7168,256]{1,0:T(8,128)(2,1)}, bf16[7168,256]{1,0:T(8,128)(2,1)S(1)}, u32[]{:S(2)}) copy-start(bf16[7168,256]{1,0:T(8,128)(2,1)S(1)} %get-tuple-element.12.w2) | copy-start | bytes 11010052
  65.6 4.2 %copy-start.3 = (bf16[7168,256]{1,0:T(8,128)(2,1)S(1)}, bf16[7168,256]{1,0:T(8,128)(2,1)}, u32[]{:S(2)}) copy-start(bf16[7168,256]{1,0:T(8,128)(2,1)} %copy-done.2) | copy-start | bytes 11010052
  65.6 5.3 %copy-start.5 = (bf16[7168,256]{1,0:T(8,128)(2,1)S(1)}, bf16[7168,256]{1,0:T(8,128)(2,1)}, u32[]{:S(2)}) copy-start(bf16[7168,256]{1,0:T(8,128)(2,1)} %copy-done.4) | copy-start | bytes 11010052
  89.4 2.4 %copy-start.1 = (bf16[256,7168]{1,0:T(8,128)(2,1)S(1)}, bf16[256,7168]{1,0:T(8,128)(2,1)}, u32[]{:S(2)}) copy-start(bf16[256,7168]{1,0:T(8,128)(2,1)} %copy-done) | copy-start | bytes 11010052
  92.6 17.7 %collective-permute-start.12 = (bf16[256,2304]{1,0:T(8,128)(2,1)S(1)}, bf16[256,2304]{1,0:T(8,128)(2,1)S(1)}, u32[]{:S(2)}, u32[]{:S(2)}) collective-permute-start(bf16[256,2304]{1,0:T(8,128)(2,1)S(1)} %shard_map.98), channel_id=1, source_target_pairs={{0,24},{1,9},{8,16},{9,1},{16,8},{17,25},{24,0},{25,17},{2,26},{3,... | collective-permute-start | bytes 3538952 | tf_op jit(solution)/shard_map/ppermute | solution.py:27
  93.7 18.2 %collective-permute-start.18 = (bf16[256,2432]{1,0:T(8,128)(2,1)S(1)}, bf16[256,2432]{1,0:T(8,128)(2,1)S(1)}, u32[]{:S(2)}, u32[]{:S(2)}) collective-permute-start(bf16[256,2432]{1,0:T(8,128)(2,1)S(1)} %shard_map.102), channel_id=1, source_target_pairs={{0,96},{1,33},{32,64},{33,1},{64,32},{65,97},{96,0},{97,65},{2,98}... | collective-permute-start | bytes 3735560 | tf_op jit(solution)/shard_map/ppermute | solution.py:27
  95.8 18.2 %collective-permute-start.15 = (bf16[256,2432]{1,0:T(8,128)(2,1)S(1)}, bf16[256,2432]{1,0:T(8,128)(2,1)S(1)}, u32[]{:S(2)}, u32[]{:S(2)}) collective-permute-start(bf16[256,2432]{1,0:T(8,128)(2,1)S(1)} %shard_map.100), channel_id=1, source_target_pairs={{0,6},{1,3},{2,4},{3,1},{4,2},{5,7},{6,0},{7,5},{8,14},{9,11},{10,... | collective-permute-start | bytes 3735560 | tf_op jit(solution)/shard_map/ppermute | solution.py:27
  110.5 11.2 %collective-permute-start.13 = (bf16[128,2304]{1,0:T(8,128)(2,1)S(1)}, bf16[128,2304]{1,0:T(8,128)(2,1)S(1)}, u32[]{:S(2)}, u32[]{:S(2)}) collective-permute-start(bf16[128,2304]{1,0:T(8,128)(2,1)S(1)} %slice.112), channel_id=1, source_target_pairs={{0,96},{1,33},{32,64},{33,1},{64,32},{65,97},{96,0},{97,65},{2,98}... | collective-permute-start | bytes 1769480 | tf_op jit(solution)/shard_map/ppermute | solution.py:27
  112.2 11.5 %collective-permute-start.19 = (bf16[128,2432]{1,0:T(8,128)(2,1)S(1)}, bf16[128,2432]{1,0:T(8,128)(2,1)S(1)}, u32[]{:S(2)}, u32[]{:S(2)}) collective-permute-start(bf16[128,2432]{1,0:T(8,128)(2,1)S(1)} %slice.110), channel_id=1, source_target_pairs={{0,6},{1,3},{2,4},{3,1},{4,2},{5,7},{6,0},{7,5},{8,14},{9,11},{10,... | collective-permute-start | bytes 1867784 | tf_op jit(solution)/shard_map/ppermute | solution.py:27
  114.3 12.9 %collective-permute-start.16 = (bf16[128,2432]{1,0:T(8,128)(2,1)S(1)}, bf16[128,2432]{1,0:T(8,128)(2,1)S(1)}, u32[]{:S(2)}, u32[]{:S(2)}) collective-permute-start(bf16[128,2432]{1,0:T(8,128)(2,1)S(1)} %slice.111), channel_id=1, source_target_pairs={{0,24},{1,9},{8,16},{9,1},{16,8},{17,25},{24,0},{25,17},{2,26},{3,... | collective-permute-start | bytes 1867784 | tf_op jit(solution)/shard_map/ppermute | solution.py:27
  121.9 9.2 %collective-permute-start.14 = (bf16[64,2304]{1,0:T(8,128)(2,1)S(1)}, bf16[64,2304]{1,0:T(8,128)(2,1)S(1)}, u32[]{:S(2)}, u32[]{:S(2)}) collective-permute-start(bf16[64,2304]{1,0:T(8,128)(2,1)S(1)} %slice.115), channel_id=1, source_target_pairs={{0,6},{1,3},{2,4},{3,1},{4,2},{5,7},{6,0},{7,5},{8,14},{9,11},{10,... | collective-permute-start | bytes 884744 | tf_op jit(solution)/shard_map/ppermute | solution.py:27
  123.9 11.9 %collective-permute-start.20 = (bf16[64,2432]{1,0:T(8,128)(2,1)S(1)}, bf16[64,2432]{1,0:T(8,128)(2,1)S(1)}, u32[]{:S(2)}, u32[]{:S(2)}) collective-permute-start(bf16[64,2432]{1,0:T(8,128)(2,1)S(1)} %slice.113), channel_id=1, source_target_pairs={{0,24},{1,9},{8,16},{9,1},{16,8},{17,25},{24,0},{25,17},{2,26},{3,... | collective-permute-start | bytes 933896 | tf_op jit(solution)/shard_map/ppermute | solution.py:27
  127.3 10.5 %collective-permute-start.17 = (bf16[64,2432]{1,0:T(8,128)(2,1)S(1)}, bf16[64,2432]{1,0:T(8,128)(2,1)S(1)}, u32[]{:S(2)}, u32[]{:S(2)}) collective-permute-start(bf16[64,2432]{1,0:T(8,128)(2,1)S(1)} %slice.114), channel_id=1, source_target_pairs={{0,96},{1,33},{32,64},{33,1},{64,32},{65,97},{96,0},{97,65},{2,98}... | collective-permute-start | bytes 933896 | tf_op jit(solution)/shard_map/ppermute | solution.py:27
  138.0 5.8 %copy-start.10 = (f32[16]{0:T(128)S(1)}, f32[16]{0:T(128)}, u32[]{:S(2)}) copy-start(f32[16]{0:T(128)} %param.14) | copy-start | bytes 196
  139.0 14.0 %all-to-all-start.1 = ((bf16[8,8,7168]{2,1,0:T(8,128)(2,1)}), bf16[8,8,7168]{2,1,0:T(8,128)(2,1)S(1)}, u32[]{:S(2)}, u32[]{:S(2)}) async-start(bf16[8,8,7168]{2,1,0:T(8,128)(2,1)} %pad_maximum_fusion.3), calls=%async_computation.1 | async-start | bytes 1835008 | tf_op jit(solution)/shard_map/all_to_all | solution.py:47
  142.5 1.2 collective-permute-start.21
